TPU v7x, 32 devices: a whole 2x2x4 slice. The times are simulated.
32 devices in a mesh: batch: 8 (over z, x), seq: 4 (over y, core).
Axes of the slice: x: 2, y: 2, z: 4, core: 2. Of those that a mesh axis runs over, the one named last changes fastest.
Arguments:
- acoustic_sequence: bfloat16 [16, 1024, 1024], P('batch', 'seq'), may hold values from -6 to 6
- utterance_durations: int32 [16], P('batch'), may hold values from 1 to 1024, 12288 in all
- chosen_entry_number: int32 [16, 1024], P('batch', 'seq'), may hold values from 0 to 1023
- discretizer_score_perturbation: bfloat16 [16, 1024, 1024], P('batch', 'seq'), may hold values from -6 to 6
- softmax_heat: float32 [], replicated, may hold values from 0.7 to 2
- normalizer_affine_rows: bfloat16 [14, 1024], P(None, 'batch'), may hold values from -0.5 to 1.3
- discretizer_score_projection: bfloat16 [1024, 1024], P('batch'), may hold values from -0.1875 to 0.1875
- lexicon_vectors: bfloat16 [1024, 1024], P('batch'), may hold values from -6 to 6
- opening_dense_entry_projection: bfloat16 [1024, 4096], P('batch'), may hold values from -0.1875 to 0.1875
- opening_dense_exit_projection: bfloat16 [4096, 1024], P('batch'), may hold values from -0.1875 to 0.1875
- request_projection: bfloat16 [1024, 1024], P('batch'), may hold values from -0.1875 to 0.1875
- lookup_projection: bfloat16 [1024, 1024], P('batch'), may hold values from -0.1875 to 0.1875
- content_projection_kernel: bfloat16 [1024, 1024], P('batch'), may hold values from -0.1875 to 0.1875
- relative_offset_projection: bfloat16 [1024, 1024], P('batch'), may hold values from -0.25 to 0.25
- mixing_exit_projection: bfloat16 [1024, 1024], P('batch'), may hold values from -1 to 1
- unit_kernel_before_gating: bfloat16 [1024, 2048], P('batch'), may hold values from -0.1875 to 0.1875
- channelwise_filter_coefficients: bfloat16 [5, 1024], P(None, 'batch'), may hold values from -2.5 to 2.5
- unit_kernel_after_normalizing: bfloat16 [1024, 1024], P('batch'), may hold values from -0.1875 to 0.1875
- closing_dense_entry_projection: bfloat16 [1024, 4096], P('batch'), may hold values from -0.1875 to 0.1875
- closing_dense_exit_projection: bfloat16 [4096, 1024], P('batch'), may hold values from -0.1875 to 0.1875
- result_adjoint: bfloat16 [16, 1024, 1024], P('batch', 'seq'), may hold values from -6 to 6
- discrete_label_adjoint: bfloat16 [16, 1024, 1024], P('batch', 'seq'), may hold values from -6 to 6
Outputs:
- output: bfloat16 [16, 1024, 1024], P('batch', 'seq')
- codes: bfloat16 [16, 1024, 1024], P('batch', 'seq')
- frames_grad: bfloat16 [16, 1024, 1024], P('batch', 'seq')
- vectors_grad: float32 [14, 1024], P(None, 'batch')
- quant_proj_grad: float32 [1024, 1024], P('batch', 'seq')
- codebook_grad: float32 [1024, 1024], P('batch', 'seq')
- macaron_in_grad: float32 [1024, 4096], P('batch', 'seq')
- macaron_out_grad: float32 [4096, 1024], P('batch', 'seq')
- query_grad: float32 [1024, 1024], P('batch', 'seq')
- key_grad: float32 [1024, 1024], P('batch', 'seq')
- value_grad: float32 [1024, 1024], P('batch', 'seq')
- pos_grad: float32 [1024, 1024], P('batch', 'seq')
- out_proj_grad: float32 [1024, 1024], P('batch', 'seq')
- conv_in_grad: float32 [1024, 2048], P('batch', 'seq')
- depth_grad: float32 [5, 1024], P(None, 'batch')
- conv_out_grad: float32 [1024, 1024], P('batch', 'seq')
- closing_in_grad: float32 [1024, 4096], P('batch', 'seq')
- closing_out_grad: float32 [4096, 1024], P('batch', 'seq')
Inputs may be any that keep to these rules, and one draw needn't show every extreme that they name: `utterance_durations`: frames at or past an utterance's length are padding. Some utterance has exactly 1024 frames.
All inputs are finite; a program needn't handle non-finite values. No bound on the sum of `utterance_durations` on one device may be relied on, other than what follows from the above.
Results may differ from a plain program's by a relative error of at most 0.028.
Values may be sent and summed in bfloat16 or wider, within the bound.
No kernel may reach another device: no remote copies, remote signals or barrier semaphores. Data moves between devices by JAX's collectives and lax.ppermute only.
A program may use at most 320 MiB of HBM per device.

v0:
```python
from functools import partial
import math

import jax
import jax.numpy as jnp
from jax import lax
from jax.sharding import PartitionSpec as P

HEADS = 8


epsilon = 1e-05


def extended(value, sides, width):
    for axis, dim in sides:
        size, length = (lax.axis_size(axis), value.shape[dim])
        up = [(i, (i + 1) % size) for i in range(size - 1)]
        down = [(j, i) for i, j in up]
        last = lax.slice_in_dim(value, length - width, length, axis=dim)
        initial = lax.slice_in_dim(value, 0, width, axis=dim)
        before = lax.ppermute(last, axis, up)
        after = lax.ppermute(initial, axis, down)
        value = jnp.concatenate([before, value, after], axis=dim)
    return value


def layer_norm(values, scale_row, shift_row):
    center = values - jnp.mean(values, axis=-1, keepdims=True)
    spread = jnp.mean(center * center, axis=-1, keepdims=True)
    return center * lax.rsqrt(spread + epsilon) * scale_row + shift_row


def glu_gate(gated_rows):
    half_width = gated_rows.shape[-1] // 2
    return gated_rows[..., :half_width] * jax.nn.sigmoid(gated_rows[..., half_width:])


def batch_norm(conv_value, sum_first, sum_second, scale_row, shift_row, count_all):
    center = sum_first / count_all
    spread = sum_second / count_all - center * center
    return (conv_value - center) * lax.rsqrt(spread + epsilon) * scale_row + shift_row


def position_table(length, model_width):
    offsets = (jnp.arange(2 * length - 1, dtype=jnp.int32) - (length - 1)).astype(jnp.float32)
    pairs = jnp.arange(model_width // 2, dtype=jnp.int32).astype(jnp.float32)
    rates = jnp.exp(pairs * (-2.0 * math.log(10000.0) / model_width))
    angles = offsets[:, None] * rates[None, :]
    return jnp.stack([jnp.sin(angles), jnp.cos(angles)], axis=-1).reshape(
        2 * length - 1, model_width
    )


def relative_shift(relative):
    head_count, row_count, span_len = relative.shape
    flat_rows = relative.reshape(head_count, row_count * span_len)
    moved_rows = lax.slice_in_dim(
        flat_rows, row_count - 1, row_count - 1 + row_count * (span_len - 1), axis=1
    )
    return moved_rows.reshape(head_count, row_count, span_len - 1)[:, :, :row_count]


def depth_conv(padded, kernel_rows, length):
    result = kernel_rows[0] * padded[:, 0:length]
    for offset in range(1, kernel_rows.shape[0]):
        result = result + kernel_rows[offset] * padded[:, offset : offset + length]
    return result


def depth_conv_back(padded_grad, kernel_rows, length):
    last_tap = kernel_rows.shape[0] - 1
    result = kernel_rows[0] * padded_grad[:, last_tap : last_tap + length]
    for offset in range(1, last_tap + 1):
        result = (
            result
            + kernel_rows[offset] * padded_grad[:, last_tap - offset : last_tap - offset + length]
        )
    return result


def matmul_rows(left_side, right_side):
    return jnp.dot(left_side, right_side, preferred_element_type=jnp.float32)


def times_transpose(left_side, right_side):
    return lax.dot_general(
        left_side, right_side, (((1,), (1,)), ((), ())), preferred_element_type=jnp.float32
    )


def transpose_times(left_side, right_side):
    return lax.dot_general(
        left_side, right_side, (((0,), (0,)), ((), ())), preferred_element_type=jnp.float32
    )


def linear_back(grad_rows, weight):
    grad_low = grad_rows.astype(jnp.bfloat16)
    return (times_transpose(grad_low, weight), grad_low)


def ffn_forward(values, scale_row, shift_row, weight_in, weight_out):
    normed_low = layer_norm(values, scale_row, shift_row).astype(jnp.bfloat16)
    hidden_pre = matmul_rows(normed_low, weight_in)
    hidden_low = jax.nn.silu(hidden_pre).astype(jnp.bfloat16)
    return (matmul_rows(hidden_low, weight_out), (normed_low, hidden_pre, hidden_low))


def ffn_backward(grad_rows, values, scale_row, shift_row, weight_in, weight_out, saved_parts):
    normed_low, hidden_pre, hidden_low = saved_parts
    grad_hidden, grad_out_low = linear_back(grad_rows, weight_out)
    silu_value, silu_back = jax.vjp(jax.nn.silu, hidden_pre)
    grad_pre = silu_back(grad_hidden)[0]
    grad_normed, grad_pre_low = linear_back(grad_pre, weight_in)
    norm_value, norm_back = jax.vjp(layer_norm, values, scale_row, shift_row)
    grad_values, grad_scale, grad_shift = norm_back(grad_normed)
    return (grad_values, grad_scale, grad_shift, grad_pre_low, grad_out_low)


def attention_logits(query_rows, key_rows, position_rows, content_bias, position_bias, length_one):
    query_float = query_rows.astype(jnp.float32)
    content_query = (query_float + content_bias).astype(jnp.bfloat16)
    position_query = (query_float + position_bias).astype(jnp.bfloat16)
    content = jnp.einsum(
        "ihd,jhd->hij", content_query, key_rows, preferred_element_type=jnp.float32
    )
    relative = jnp.einsum(
        "ihd,nhd->hin", position_query, position_rows, preferred_element_type=jnp.float32
    )
    raw_scores = content + relative_shift(relative)
    key_valid = jnp.arange(key_rows.shape[0], dtype=jnp.int32)[None, None, :] < length_one
    discretizer_scores = jnp.where(
        key_valid, raw_scores * (1.0 / math.sqrt(key_rows.shape[2])), -1e30
    )
    return (discretizer_scores, key_valid, content_query, position_query, relative.shape)


def sum_small_seq(smalls):
    small_sums = (
        lax.psum(smalls[0].astype(jnp.bfloat16), "seq").astype(jnp.float32),
        lax.psum(smalls[1].astype(jnp.bfloat16), "seq").astype(jnp.float32),
    )
    return tuple(small_sums)


def sum_over_seq(matrices, smalls):
    (
        grad_one,
        grad_two,
        grad_three,
        grad_four,
        grad_five,
        grad_six,
        grad_seven,
        grad_eight,
        grad_nine,
        grad_ten,
        grad_eleven,
        grad_twelve,
        grad_thirteen,
    ) = matrices
    reduced = (
        lax.psum_scatter(
            grad_one.astype(jnp.bfloat16), "seq", scatter_dimension=1, tiled=True
        ).astype(jnp.float32),
        lax.psum_scatter(
            grad_two.astype(jnp.bfloat16), "seq", scatter_dimension=1, tiled=True
        ).astype(jnp.float32),
        lax.psum_scatter(
            grad_three.astype(jnp.bfloat16), "seq", scatter_dimension=1, tiled=True
        ).astype(jnp.float32),
        lax.psum_scatter(
            grad_four.astype(jnp.bfloat16), "seq", scatter_dimension=1, tiled=True
        ).astype(jnp.float32),
        lax.psum_scatter(
            grad_five.astype(jnp.bfloat16), "seq", scatter_dimension=1, tiled=True
        ).astype(jnp.float32),
        lax.psum_scatter(
            grad_six.astype(jnp.bfloat16), "seq", scatter_dimension=1, tiled=True
        ).astype(jnp.float32),
        lax.psum_scatter(
            grad_seven.astype(jnp.bfloat16), "seq", scatter_dimension=1, tiled=True
        ).astype(jnp.float32),
        lax.psum_scatter(
            grad_eight.astype(jnp.bfloat16), "seq", scatter_dimension=1, tiled=True
        ).astype(jnp.float32),
        lax.psum_scatter(
            grad_nine.astype(jnp.bfloat16), "seq", scatter_dimension=1, tiled=True
        ).astype(jnp.float32),
        lax.psum_scatter(
            grad_ten.astype(jnp.bfloat16), "seq", scatter_dimension=1, tiled=True
        ).astype(jnp.float32),
        lax.psum_scatter(
            grad_eleven.astype(jnp.bfloat16), "seq", scatter_dimension=1, tiled=True
        ).astype(jnp.float32),
        lax.psum_scatter(
            grad_twelve.astype(jnp.bfloat16), "seq", scatter_dimension=1, tiled=True
        ).astype(jnp.float32),
        lax.psum_scatter(
            grad_thirteen.astype(jnp.bfloat16), "seq", scatter_dimension=1, tiled=True
        ).astype(jnp.float32),
    )
    return (tuple(reduced), sum_small_seq(smalls))


def sum_over_batch(matrices, smalls):
    (
        grad_one,
        grad_two,
        grad_three,
        grad_four,
        grad_five,
        grad_six,
        grad_seven,
        grad_eight,
        grad_nine,
        grad_ten,
        grad_eleven,
        grad_twelve,
        grad_thirteen,
    ) = matrices
    small_one, small_two = smalls
    reduced = (
        lax.psum_scatter(
            grad_one.astype(jnp.bfloat16), "batch", scatter_dimension=0, tiled=True
        ).astype(jnp.float32),
        lax.psum_scatter(
            grad_two.astype(jnp.bfloat16), "batch", scatter_dimension=0, tiled=True
        ).astype(jnp.float32),
        lax.psum_scatter(
            grad_three.astype(jnp.bfloat16), "batch", scatter_dimension=0, tiled=True
        ).astype(jnp.float32),
        lax.psum_scatter(
            grad_four.astype(jnp.bfloat16), "batch", scatter_dimension=0, tiled=True
        ).astype(jnp.float32),
        lax.psum_scatter(
            grad_five.astype(jnp.bfloat16), "batch", scatter_dimension=0, tiled=True
        ).astype(jnp.float32),
        lax.psum_scatter(
            grad_six.astype(jnp.bfloat16), "batch", scatter_dimension=0, tiled=True
        ).astype(jnp.float32),
        lax.psum_scatter(
            grad_seven.astype(jnp.bfloat16), "batch", scatter_dimension=0, tiled=True
        ).astype(jnp.float32),
        lax.psum_scatter(
            grad_eight.astype(jnp.bfloat16), "batch", scatter_dimension=0, tiled=True
        ).astype(jnp.float32),
        lax.psum_scatter(
            grad_nine.astype(jnp.bfloat16), "batch", scatter_dimension=0, tiled=True
        ).astype(jnp.float32),
        lax.psum_scatter(
            grad_ten.astype(jnp.bfloat16), "batch", scatter_dimension=0, tiled=True
        ).astype(jnp.float32),
        lax.psum_scatter(
            grad_eleven.astype(jnp.bfloat16), "batch", scatter_dimension=0, tiled=True
        ).astype(jnp.float32),
        lax.psum_scatter(
            grad_twelve.astype(jnp.bfloat16), "batch", scatter_dimension=0, tiled=True
        ).astype(jnp.float32),
        lax.psum_scatter(
            grad_thirteen.astype(jnp.bfloat16), "batch", scatter_dimension=0, tiled=True
        ).astype(jnp.float32),
        lax.psum_scatter(
            small_one.astype(jnp.bfloat16), "batch", scatter_dimension=1, tiled=True
        ).astype(jnp.float32),
        lax.psum_scatter(
            small_two.astype(jnp.bfloat16), "batch", scatter_dimension=1, tiled=True
        ).astype(jnp.float32),
    )
    return (tuple(reduced[:13]), tuple(reduced[13:]))


def per_device(
    acoustic_sequence,
    utterance_durations,
    chosen_entry_number,
    discretizer_score_perturbation,
    softmax_heat,
    normalizer_affine_rows,
    discretizer_score_projection,
    lexicon_vectors,
    opening_dense_entry_projection,
    opening_dense_exit_projection,
    request_projection,
    lookup_projection,
    content_projection_kernel,
    relative_offset_projection,
    mixing_exit_projection,
    unit_kernel_before_gating,
    channelwise_filter_coefficients,
    unit_kernel_after_normalizing,
    closing_dense_entry_projection,
    closing_dense_exit_projection,
    result_adjoint,
    discrete_label_adjoint,
):
    (
        vectors_all,
        quant_all,
        codebook_all,
        macaron_in_all,
        macaron_out_all,
        query_all,
        key_all,
        value_all,
        pos_all,
        out_all,
        conv_in_all,
        depth_all,
        conv_out_all,
        closing_in_all,
        closing_out_all,
    ) = (
        lax.all_gather(normalizer_affine_rows, "batch", axis=1, tiled=True),
        lax.all_gather(discretizer_score_projection, "batch", axis=0, tiled=True),
        lax.all_gather(lexicon_vectors, "batch", axis=0, tiled=True),
        lax.all_gather(opening_dense_entry_projection, "batch", axis=0, tiled=True),
        lax.all_gather(opening_dense_exit_projection, "batch", axis=0, tiled=True),
        lax.all_gather(request_projection, "batch", axis=0, tiled=True),
        lax.all_gather(lookup_projection, "batch", axis=0, tiled=True),
        lax.all_gather(content_projection_kernel, "batch", axis=0, tiled=True),
        lax.all_gather(relative_offset_projection, "batch", axis=0, tiled=True),
        lax.all_gather(mixing_exit_projection, "batch", axis=0, tiled=True),
        lax.all_gather(unit_kernel_before_gating, "batch", axis=0, tiled=True),
        lax.all_gather(channelwise_filter_coefficients, "batch", axis=1, tiled=True),
        lax.all_gather(unit_kernel_after_normalizing, "batch", axis=0, tiled=True),
        lax.all_gather(closing_dense_entry_projection, "batch", axis=0, tiled=True),
        lax.all_gather(closing_dense_exit_projection, "batch", axis=0, tiled=True),
    )
    groups, local_len, model_width = acoustic_sequence.shape
    seq_count = lax.axis_size("seq")
    seq_place = lax.axis_index("seq")
    full_len = local_len * seq_count
    entries = codebook_all.shape[0]
    total_rows = groups * local_len
    heads_local = HEADS // seq_count
    head_width = model_width // HEADS
    local_width = model_width // seq_count
    kernel_size = depth_all.shape[0]
    rim_width = kernel_size // 2
    params_f = vectors_all.astype(jnp.float32)
    depth_f = depth_all.astype(jnp.float32)
    positions = seq_place * local_len + jnp.arange(local_len, dtype=jnp.int32)
    valid_mask = (positions[None, :] < utterance_durations[:, None]).astype(jnp.float32)
    valid_rows = valid_mask.reshape(total_rows, 1)
    inputs_low = acoustic_sequence.reshape(total_rows, model_width)
    inputs_f = inputs_low.astype(jnp.float32)
    quant_logits = matmul_rows(inputs_low, quant_all)
    scaled_logits = (
        quant_logits
        + discretizer_score_perturbation.reshape(total_rows, entries).astype(jnp.float32)
    ) / softmax_heat
    relaxed_assignments = jax.nn.softmax(scaled_logits, axis=-1)
    soft_low = relaxed_assignments.astype(jnp.bfloat16)
    one_hot = (
        chosen_entry_number.reshape(total_rows, 1) == jnp.arange(entries, dtype=jnp.int32)[None, :]
    ).astype(jnp.bfloat16)
    codes_value = valid_rows * (
        matmul_rows(one_hot, codebook_all) + matmul_rows(soft_low, codebook_all)
    )
    macaron_value, macaron_saved = ffn_forward(
        inputs_f, params_f[0], params_f[5], macaron_in_all, macaron_out_all
    )
    first_mid = inputs_f + 0.5 * macaron_value
    attn_normed = layer_norm(first_mid, params_f[1], params_f[6]).astype(jnp.bfloat16)
    stacked = (
        jnp.stack(
            [
                matmul_rows(attn_normed, query_all),
                matmul_rows(attn_normed, key_all),
                matmul_rows(attn_normed, value_all),
            ]
        )
        .astype(jnp.bfloat16)
        .reshape(3, groups, local_len, model_width)
    )
    by_heads = lax.all_to_all(stacked, "seq", split_axis=3, concat_axis=2, tiled=True)
    head_shape = (groups, full_len, heads_local, head_width)
    query_heads = by_heads[0].reshape(head_shape)
    key_heads = by_heads[1].reshape(head_shape)
    value_heads = by_heads[2].reshape(head_shape)
    table_low = position_table(full_len, model_width).astype(jnp.bfloat16)
    pos_columns = lax.dynamic_slice_in_dim(pos_all, seq_place * local_width, local_width, 1)
    position_low = (
        matmul_rows(table_low, pos_columns)
        .astype(jnp.bfloat16)
        .reshape(2 * full_len - 1, heads_local, head_width)
    )
    content_bias = lax.dynamic_slice_in_dim(
        params_f[12], seq_place * local_width, local_width, 0
    ).reshape(heads_local, head_width)
    position_bias = lax.dynamic_slice_in_dim(
        params_f[13], seq_place * local_width, local_width, 0
    ).reshape(heads_local, head_width)

    def attend_forward(items):
        query_rows, key_rows, value_rows, length_one = items
        discretizer_scores = attention_logits(
            query_rows, key_rows, position_low, content_bias, position_bias, length_one
        )[0]
        row_top = jnp.max(discretizer_scores, axis=-1, keepdims=True)
        weights_exp = jnp.exp(discretizer_scores - row_top)
        totals = jnp.sum(weights_exp, axis=-1, keepdims=True)
        weights_low = (weights_exp / totals).astype(jnp.bfloat16)
        attended = jnp.einsum(
            "hij,jhd->ihd", weights_low, value_rows, preferred_element_type=jnp.float32
        )
        return (attended.astype(jnp.bfloat16), (row_top + jnp.log(totals))[..., 0])

    attended_low, log_totals = lax.map(
        attend_forward, (query_heads, key_heads, value_heads, utterance_durations)
    )
    back_time = lax.all_to_all(
        attended_low.reshape(groups, full_len, local_width),
        "seq",
        split_axis=1,
        concat_axis=2,
        tiled=True,
    )
    attended_rows = back_time.reshape(total_rows, model_width)
    second_mid = first_mid + matmul_rows(attended_rows, out_all)
    conv_normed = layer_norm(second_mid, params_f[2], params_f[7]).astype(jnp.bfloat16)
    gated_rows = matmul_rows(conv_normed, conv_in_all)
    glu_low = (
        (valid_rows * glu_gate(gated_rows))
        .astype(jnp.bfloat16)
        .reshape(groups, local_len, model_width)
    )
    padded_glu = extended(glu_low, (("seq", 1),), rim_width)
    conv_value = depth_conv(padded_glu, depth_f, local_len).reshape(total_rows, model_width)
    masked_conv = valid_rows * conv_value
    sum_first, sum_second, count_all = lax.psum(
        (
            jnp.sum(masked_conv, axis=0),
            jnp.sum(masked_conv * conv_value, axis=0),
            jnp.sum(valid_mask),
        ),
        ("batch", "seq"),
    )
    bound_norm = partial(batch_norm, count_all=count_all)
    normalized = bound_norm(conv_value, sum_first, sum_second, params_f[10], params_f[11])
    act_low = jax.nn.silu(normalized).astype(jnp.bfloat16)
    third_mid = second_mid + matmul_rows(act_low, conv_out_all)
    closing_value, closing_saved = ffn_forward(
        third_mid, params_f[3], params_f[8], closing_in_all, closing_out_all
    )
    fourth_mid = third_mid + 0.5 * closing_value
    final_value, final_back = jax.vjp(layer_norm, fourth_mid, params_f[4], params_f[9])
    output = (valid_rows * final_value).astype(jnp.bfloat16).reshape(groups, local_len, model_width)
    codes = codes_value.astype(jnp.bfloat16).reshape(groups, local_len, model_width)
    grad_final = valid_rows * result_adjoint.reshape(total_rows, model_width).astype(jnp.float32)
    grad_fourth, scale_four, shift_four = final_back(grad_final)
    grad_closing, scale_three, shift_three, close_pre_low, close_out_low = ffn_backward(
        0.5 * grad_fourth,
        third_mid,
        params_f[3],
        params_f[8],
        closing_in_all,
        closing_out_all,
        closing_saved,
    )
    grad_third = grad_fourth + grad_closing
    grad_act, grad_third_low = linear_back(grad_third, conv_out_all)
    silu_value, silu_back = jax.vjp(jax.nn.silu, normalized)
    grad_normalized = silu_back(grad_act)[0]
    norm_value, norm_back = jax.vjp(
        bound_norm, conv_value, sum_first, sum_second, params_f[10], params_f[11]
    )
    grad_conv_direct, part_first, part_second, grad_bn_scale, grad_bn_shift = norm_back(
        grad_normalized
    )
    total_first, total_second = lax.psum((part_first, part_second), ("batch", "seq"))
    grad_conv = grad_conv_direct + valid_rows * (total_first + 2.0 * conv_value * total_second)
    grad_conv_low = grad_conv.astype(jnp.bfloat16).reshape(groups, local_len, model_width)
    padded_grad = extended(grad_conv_low, (("seq", 1),), rim_width)
    grad_glu = valid_rows * depth_conv_back(padded_grad, depth_f, local_len).reshape(
        total_rows, model_width
    )
    grad_conv_float = grad_conv_low.astype(jnp.float32)
    grad_depth = jnp.stack(
        [
            jnp.sum(
                padded_glu[:, offset : offset + local_len].astype(jnp.float32) * grad_conv_float,
                axis=(0, 1),
            )
            for offset in range(kernel_size)
        ]
    )
    glu_value, glu_back = jax.vjp(glu_gate, gated_rows)
    grad_gated = glu_back(grad_glu)[0]
    grad_conv_normed, grad_gated_low = linear_back(grad_gated, conv_in_all)
    conv_norm_value, conv_norm_back = jax.vjp(layer_norm, second_mid, params_f[2], params_f[7])
    grad_from_conv, scale_two, shift_two = conv_norm_back(grad_conv_normed)
    grad_second = grad_third + grad_from_conv
    grad_attended, grad_second_low = linear_back(grad_second, out_all)
    grad_heads = lax.all_to_all(
        grad_second_low_heads(grad_attended, groups, local_len, model_width),
        "seq",
        split_axis=2,
        concat_axis=1,
        tiled=True,
    ).reshape(head_shape)

    def attend_backward(items):
        query_rows, key_rows, value_rows, length_one, log_total, grad_rows = items
        discretizer_scores, key_valid, content_query, position_query, relative_shape = (
            attention_logits(
                query_rows, key_rows, position_low, content_bias, position_bias, length_one
            )
        )
        weights_soft = jnp.exp(discretizer_scores - log_total[..., None])
        weights_low = weights_soft.astype(jnp.bfloat16)
        grad_weights = jnp.einsum(
            "ihd,jhd->hij", grad_rows, value_rows, preferred_element_type=jnp.float32
        )
        grad_value = jnp.einsum(
            "hij,ihd->jhd", weights_low, grad_rows, preferred_element_type=jnp.float32
        )
        grad_logits = weights_soft * (
            grad_weights - jnp.sum(grad_weights * weights_soft, axis=-1, keepdims=True)
        )
        grad_raw = (
            jnp.where(key_valid, grad_logits, 0.0) * (1.0 / math.sqrt(key_rows.shape[2]))
        ).astype(jnp.bfloat16)
        grad_content_query = jnp.einsum(
            "hij,jhd->ihd", grad_raw, key_rows, preferred_element_type=jnp.float32
        )
        grad_key = jnp.einsum(
            "hij,ihd->jhd", grad_raw, content_query, preferred_element_type=jnp.float32
        )
        shift_value, shift_back = jax.vjp(relative_shift, jnp.zeros(relative_shape, jnp.float32))
        grad_relative = shift_back(grad_raw.astype(jnp.float32))[0].astype(jnp.bfloat16)
        grad_position_query = jnp.einsum(
            "hin,nhd->ihd", grad_relative, position_low, preferred_element_type=jnp.float32
        )
        grad_position = jnp.einsum(
            "hin,ihd->nhd", grad_relative, position_query, preferred_element_type=jnp.float32
        )
        return (
            grad_content_query + grad_position_query,
            grad_key,
            grad_value,
            grad_position,
            jnp.sum(grad_content_query, axis=0),
            jnp.sum(grad_position_query, axis=0),
        )

    grad_query, grad_key, grad_value, grad_positions, grad_content_bias, grad_position_bias = (
        lax.map(
            attend_backward,
            (query_heads, key_heads, value_heads, utterance_durations, log_totals, grad_heads),
        )
    )
    grad_stack = (
        jnp.stack([grad_query, grad_key, grad_value])
        .astype(jnp.bfloat16)
        .reshape(3, groups, full_len, local_width)
    )
    grad_time = lax.all_to_all(grad_stack, "seq", split_axis=2, concat_axis=3, tiled=True).reshape(
        3, total_rows, model_width
    )
    grad_attn_normed = (
        times_transpose(grad_time[0], query_all)
        + times_transpose(grad_time[1], key_all)
        + times_transpose(grad_time[2], value_all)
    )
    attn_norm_value, attn_norm_back = jax.vjp(layer_norm, first_mid, params_f[1], params_f[6])
    grad_from_attn, scale_one, shift_one = attn_norm_back(grad_attn_normed)
    grad_first = grad_second + grad_from_attn
    grad_position_low = (
        jnp.sum(grad_positions, axis=0).astype(jnp.bfloat16).reshape(2 * full_len - 1, local_width)
    )
    grad_pos_columns = transpose_times(table_low, grad_position_low)
    content_full = lax.dynamic_update_slice_in_dim(
        jnp.zeros((model_width,), jnp.float32),
        jnp.sum(grad_content_bias, axis=0).reshape(local_width),
        seq_place * local_width,
        0,
    )
    position_full = lax.dynamic_update_slice_in_dim(
        jnp.zeros((model_width,), jnp.float32),
        jnp.sum(grad_position_bias, axis=0).reshape(local_width),
        seq_place * local_width,
        0,
    )
    grad_macaron, scale_zero, shift_zero, mac_pre_low, mac_out_low = ffn_backward(
        0.5 * grad_first,
        inputs_f,
        params_f[0],
        params_f[5],
        macaron_in_all,
        macaron_out_all,
        macaron_saved,
    )
    grad_layer_in = grad_first + grad_macaron
    grad_codes = (
        valid_rows * discrete_label_adjoint.reshape(total_rows, model_width).astype(jnp.float32)
    ).astype(jnp.bfloat16)
    grad_soft = times_transpose(grad_codes, codebook_all)
    rescaled_derivative = relaxed_assignments * (
        grad_soft - jnp.sum(grad_soft * relaxed_assignments, axis=-1, keepdims=True)
    )
    score_derivative_lowprecision = (rescaled_derivative / softmax_heat).astype(jnp.bfloat16)
    grad_quant_in = times_transpose(score_derivative_lowprecision, quant_all)
    frames_grad = (
        (grad_layer_in + grad_quant_in).astype(jnp.bfloat16).reshape(groups, local_len, model_width)
    )
    vectors_grad = jnp.stack(
        [
            scale_zero,
            scale_one,
            scale_two,
            scale_three,
            scale_four,
            shift_zero,
            shift_one,
            shift_two,
            shift_three,
            shift_four,
            grad_bn_scale,
            grad_bn_shift,
            content_full,
            position_full,
        ]
    )
    smalls = (vectors_grad, grad_depth)
    mac_normed, mac_pre, mac_hidden = macaron_saved
    close_normed, close_pre, close_hidden = closing_saved
    grad_pos_w = lax.dynamic_update_slice_in_dim(
        jnp.zeros((model_width, model_width), jnp.float32),
        grad_pos_columns,
        seq_place * local_width,
        1,
    )
    matrices = (
        transpose_times(inputs_low, score_derivative_lowprecision),
        transpose_times(one_hot, grad_codes) + transpose_times(soft_low, grad_codes),
        transpose_times(mac_normed, mac_pre_low),
        transpose_times(mac_hidden, mac_out_low),
        transpose_times(attn_normed, grad_time[0]),
        transpose_times(attn_normed, grad_time[1]),
        transpose_times(attn_normed, grad_time[2]),
        grad_pos_w,
        transpose_times(attended_rows, grad_second_low),
        transpose_times(conv_normed, grad_gated_low),
        transpose_times(act_low, grad_third_low),
        transpose_times(close_normed, close_pre_low),
        transpose_times(close_hidden, close_out_low),
    )
    matrices, smalls = sum_over_seq(matrices, smalls)
    matrices, smalls = sum_over_batch(matrices, smalls)
    (
        quant_sum,
        codebook_sum,
        macaron_in_sum,
        macaron_out_sum,
        query_sum,
        key_sum,
        value_sum,
        pos_sum,
        out_sum,
        conv_in_sum,
        conv_out_sum,
        closing_in_sum,
        closing_out_sum,
    ) = matrices
    vectors_sum, depth_sum = smalls
    return (
        output,
        codes,
        frames_grad,
        vectors_sum,
        quant_sum,
        codebook_sum,
        macaron_in_sum,
        macaron_out_sum,
        query_sum,
        key_sum,
        value_sum,
        pos_sum,
        out_sum,
        conv_in_sum,
        depth_sum,
        conv_out_sum,
        closing_in_sum,
        closing_out_sum,
    )


def grad_second_low_heads(grad_attended, groups, local_len, model_width):
    return grad_attended.astype(jnp.bfloat16).reshape(groups, local_len, model_width)


def flat_rows(blocks):
    return blocks.reshape(blocks.shape[0] * blocks.shape[1], blocks.shape[2])


def solution(mesh):
    placed = (
        P("batch", "seq", None),
        P("batch"),
        P("batch", "seq"),
        P("batch", "seq", None),
        P(),
        P(None, "batch"),
        P("batch", None),
        P("batch", None),
        P("batch", None),
        P("batch", None),
        P("batch", None),
        P("batch", None),
        P("batch", None),
        P("batch", None),
        P("batch", None),
        P("batch", None),
        P(None, "batch"),
        P("batch", None),
        P("batch", None),
        P("batch", None),
        P("batch", "seq", None),
        P("batch", "seq", None),
    )
    return jax.shard_map(
        per_device,
        mesh=mesh,
        in_specs=placed,
        out_specs=(
            P("batch", "seq", None),
            P("batch", "seq", None),
            P("batch", "seq", None),
            P(None, "batch"),
            P("batch", "seq"),
            P("batch", "seq"),
            P("batch", "seq"),
            P("batch", "seq"),
            P("batch", "seq"),
            P("batch", "seq"),
            P("batch", "seq"),
            P("batch", "seq"),
            P("batch", "seq"),
            P("batch", "seq"),
            P(None, "batch"),
            P("batch", "seq"),
            P("batch", "seq"),
            P("batch", "seq"),
        ),
        check_vma=False,
    )
```

profile of v0, /device:TPU:0, one launch (start us, length us, event | category | flops | bytes accessed | tf_op | source)
XLA Modules:
  0.0 3309.3 jit_solution(17030341335038590570)
XLA Ops:
  16.1 28.5 all_gather.45
  46.4 91.9 %all-gather.14.cloned.1.call-done = bf16[1024,4096]{1,0:T(8,128)(2,1)} async-done(((bf16[128,4096]{1,0:T(8,128)(2,1)}), bf16[1024,4096]{1,0:T(8,128)(2,1)}) %all-gather.14.cloned.1.call-update) | async-done | bytes 8388624 | tf_op jit(solution)/shard_map/all_gather | solution.py:318
  148.5 115.1 %all-gather.16.cloned.1.call-done = bf16[4096,1024]{1,0:T(8,128)(2,1)} async-done(((bf16[512,1024]{1,0:T(8,128)(2,1)}), bf16[4096,1024]{1,0:T(8,128)(2,1)}) %all-gather.16.cloned.1.call-update) | async-done | bytes 8388624 | tf_op jit(solution)/shard_map/all_gather | solution.py:319
  275.0 38.3 %all-gather.18.cloned.1.call-done = bf16[1024,1024]{1,0:T(8,128)(2,1)} async-done(((bf16[128,1024]{1,0:T(8,128)(2,1)}), bf16[1024,1024]{1,0:T(8,128)(2,1)}) %all-gather.18.cloned.1.call-update) | async-done | bytes 2097168 | tf_op jit(solution)/shard_map/all_gather | solution.py:320
  317.1 46.0 %all-gather.20.cloned.1.call-done = bf16[1024,1024]{1,0:T(8,128)(2,1)} async-done(((bf16[128,1024]{1,0:T(8,128)(2,1)}), bf16[1024,1024]{1,0:T(8,128)(2,1)}) %all-gather.20.cloned.1.call-update) | async-done | bytes 2097168 | tf_op jit(solution)/shard_map/all_gather | solution.py:321
  369.4 43.5 %all-gather.22.cloned.1.call-done = bf16[1024,1024]{1,0:T(8,128)(2,1)} async-done(((bf16[128,1024]{1,0:T(8,128)(2,1)}), bf16[1024,1024]{1,0:T(8,128)(2,1)}) %all-gather.22.cloned.1.call-update) | async-done | bytes 2097168 | tf_op jit(solution)/shard_map/all_gather | solution.py:322
  429.5 121.7 %multiply_sine_fusion = (bf16[2047,512,1]{0,2,1:T(2,128)(2,1)}, bf16[2047,512,1]{0,2,1:T(2,128)(2,1)}) fusion(f32[2047]{0:T(1024)S(1)} %add_convert_fusion.8, f32[512]{0:T(512)S(1)} %multiply_exponential_fusion), kind=kLoop, calls=%fused_computation.80 | loop fusion | flops 3144192 | bytes 4202492 | tf_op jit(solution)/shard_map/sin | solution.py:50
  572.5 27.1 all_gather.53
  622.2 339.9 %while.32 = (s32[]{:T(128)}, bf16[2,1024,2,128]{1,3,2,0:T(8,128)(2,1)}, f32[2,2,1024]{2,1,0:T(2,128)S(1)}, bf16[2,1024,2,128]{3,2,1,0:T(2,128)(2,1)}, s32[2]{0:T...) while((s32[]{:T(128)}, ...), condition=%wide.region_7.8_spmd, body=%wide.region_4.7_spmd.sunk | while | flops 2167667712 | bytes 291958944 | solution.py:411
  632.8 23.3 reshape.627
  656.1 24.1 reshape.628
  680.3 21.0 slice.344
  701.3 37.8 %reshape.629 = f32[4190208]{0:T(1024)} reshape(f32[2,2095104]{1,0:T(2,128)} %slice.344) | data formatting | bytes 33521664 | tf_op jit(solution)/shard_map/while
  739.1 17.0 reshape.630
  799.4 23.5 reshape.627
  823.0 24.1 reshape.628
  847.1 21.2 slice.344
  868.3 37.5 %reshape.629 = f32[4190208]{0:T(1024)} reshape(f32[2,2095104]{1,0:T(2,128)} %slice.344) | data formatting | bytes 33521664 | tf_op jit(solution)/shard_map/while
  905.8 16.7 reshape.630
  1009.7 39.7 %all-reduce.5 = (f32[1024]{0:T(1024)S(1)}, f32[]{:T(128)}, f32[1024]{0:T(1024)S(1)}) all-reduce(f32[1024]{0:T(1024)S(1)} %get-tuple-element.404, f32[]{:T(128)} %fusion.118, f32[1024]{0:T(1024)S(1)} %get-tuple-element.403), channel_id=1, replica_groups=mesh['batch'=8,'seq'=4] {'batch','seq'}, use_global_device_ids=true, to_apply=%region_15.16 | all-reduce | flops 2049 | bytes 16392 | tf_op jit(solution)/shard_map/psum | solution.py:433
  1058.9 11.9 fusion.128
  1102.6 11.2 fusion.48
  1132.4 41.1 %all-reduce.4 = (f32[1024]{0:T(1024)S(1)}, f32[1024]{0:T(1024)S(1)}) all-reduce(f32[1024]{0:T(1024)S(1)} %get-tuple-element.528, f32[1024]{0:T(1024)S(1)} %get-tuple-element.527), channel_id=1, replica_groups=mesh['batch'=8,'seq'=4] {'batch','seq'}, use_global_device_ids=true, to_apply=%region_29.30 | all-reduce | flops 2048 | bytes 16384 | tf_op jit(solution)/shard_map/psum | solution.py:473
  1233.8 556.6 %while.33 = (s32[]{:T(128)}, bf16[2,1024,2,128]{1,3,2,0:T(8,128)(2,1)}, bf16[2,1024,2,128]{1,3,2,0:T(8,128)(2,1)}, bf16[2,1024,2,128]{1,3,2,0:T(8,128)(2,1)}, f3...) while((s32[]{:T(128)}, ...), condition=%wide.region_36.37_spmd, body=%wide.region_32.36_spmd.sunk | while | flops 6467883008 | bytes 473258496 | solution.py:550
  1244.5 23.5 reshape.631
  1268.0 24.1 reshape.632
  1292.2 21.0 slice.346
  1313.2 37.6 %reshape.633 = f32[4190208]{0:T(1024)} reshape(f32[2,2095104]{1,0:T(2,128)} %slice.346) | data formatting | bytes 33521664 | tf_op jit(solution)/shard_map/while
  1350.7 16.7 reshape.634
  1417.1 15.0 reshape.635
  1440.8 13.9 pad.139
  1454.7 11.9 reshape.637
  1466.6 17.5 convert_element_type.699
  1519.1 23.2 reshape.631
  1542.3 24.1 reshape.632
  1566.4 21.0 slice.346
  1587.5 37.6 %reshape.633 = f32[4190208]{0:T(1024)} reshape(f32[2,2095104]{1,0:T(2,128)} %slice.346) | data formatting | bytes 33521664 | tf_op jit(solution)/shard_map/while
  1625.1 16.7 reshape.634
  1691.4 15.0 reshape.635
  1715.1 13.9 pad.139
  1729.0 11.9 reshape.637
  1740.9 17.5 convert_element_type.699
  1809.6 50.7 %all_to_all.60 = bf16[3,2,1024,256]{3,1,0,2:T(2,128)(2,1)S(1)} all-to-all(bf16[3,2,1024,256]{3,1,0,2:T(2,128)(2,1)S(1)} %pad_maximum_fusion.1), channel_id=1, replica_groups=mesh['batch'=8,'seq'=4] {'seq'}, dimensions={2} | all-to-all | bytes 6291456 | tf_op jit(solution)/shard_map/all_to_all | solution.py:560
  1924.7 11.2 fusion.51
  1966.0 44.1 %reduce-scatter.69.cloned.1.call-done = bf16[1024,512]{1,0:T(8,128)(2,1)} async-done(((bf16[1024,2048]{1,0:T(8,128)(2,1)}), bf16[1024,512]{1,0:T(8,128)(2,1)}) %reduce-scatter.69.cloned.1.call-update) | async-done | bytes 1048592 | tf_op jit(solution)/shard_map/reduce_scatter | solution.py:191
  2010.2 74.4 %reduce-scatter.81.cloned.1.call-done = bf16[4096,256]{1,0:T(8,128)(2,1)} async-done(((bf16[4096,1024]{1,0:T(8,128)(2,1)}), bf16[4096,256]{1,0:T(8,128)(2,1)}) %reduce-scatter.81.cloned.1.call-update) | async-done | bytes 2097168 | tf_op jit(solution)/shard_map/reduce_scatter | solution.py:200
  2084.7 74.1 %reduce-scatter.77.cloned.1.call-done = bf16[1024,1024]{1,0:T(8,128)(2,1)} async-done(((bf16[1024,4096]{1,0:T(8,128)(2,1)}), bf16[1024,1024]{1,0:T(8,128)(2,1)}) %reduce-scatter.77.cloned.1.call-update) | async-done | bytes 2097168 | tf_op jit(solution)/shard_map/reduce_scatter | solution.py:197
  2158.9 74.4 %reduce-scatter.45.cloned.1.call-done = bf16[4096,256]{1,0:T(8,128)(2,1)} async-done(((bf16[4096,1024]{1,0:T(8,128)(2,1)}), bf16[4096,256]{1,0:T(8,128)(2,1)}) %reduce-scatter.45.cloned.1.call-update) | async-done | bytes 2097168 | tf_op jit(solution)/shard_map/reduce_scatter | solution.py:173
  2233.5 73.9 %reduce-scatter.41.cloned.1.call-done = bf16[1024,1024]{1,0:T(8,128)(2,1)} async-done(((bf16[1024,4096]{1,0:T(8,128)(2,1)}), bf16[1024,1024]{1,0:T(8,128)(2,1)}) %reduce-scatter.41.cloned.1.call-update) | async-done | bytes 2097168 | tf_op jit(solution)/shard_map/reduce_scatter | solution.py:170
  2313.1 59.8 %reduce-scatter.89.cloned.1.call-done = bf16[128,5]{1,0:T(8,128)(2,1)} async-done(((bf16[1024,5]{1,0:T(8,128)(2,1)}), bf16[128,5]{1,0:T(8,128)(2,1)}) %reduce-scatter.89.cloned.1.call-update) | async-done | bytes 1296
  2378.6 58.9 %reduce-scatter.87.cloned.1.call-done = bf16[128,14]{1,0:T(8,128)(2,1)} async-done(((bf16[1024,14]{1,0:T(8,128)(2,1)}), bf16[128,14]{1,0:T(8,128)(2,1)}) %reduce-scatter.87.cloned.1.call-update) | async-done | bytes 3600
  2445.2 57.5 %reduce-scatter.85.cloned.1.call-done = bf16[128,256]{1,0:T(8,128)(2,1)} async-done(((bf16[1024,256]{1,0:T(8,128)(2,1)}), bf16[128,256]{1,0:T(8,128)(2,1)}) %reduce-scatter.85.cloned.1.call-update) | async-done | bytes 65552
  2504.4 62.3 %reduce-scatter.39.cloned.1.call-done = bf16[128,256]{1,0:T(8,128)(2,1)} async-done(((bf16[1024,256]{1,0:T(8,128)(2,1)}), bf16[128,256]{1,0:T(8,128)(2,1)}) %reduce-scatter.39.cloned.1.call-update) | async-done | bytes 65552 | tf_op jit(solution)/shard_map/reduce_scatter | solution.py:228
  2568.3 63.2 %reduce-scatter.75.cloned.1.call-done = bf16[128,256]{1,0:T(8,128)(2,1)} async-done(((bf16[1024,256]{1,0:T(8,128)(2,1)}), bf16[128,256]{1,0:T(8,128)(2,1)}) %reduce-scatter.75.cloned.1.call-update) | async-done | bytes 65552 | tf_op jit(solution)/shard_map/reduce_scatter | solution.py:255
  2633.0 62.8 %reduce-scatter.67.cloned.1.call-done = bf16[128,256]{1,0:T(8,128)(2,1)} async-done(((bf16[1024,256]{1,0:T(8,128)(2,1)}), bf16[128,256]{1,0:T(8,128)(2,1)}) %reduce-scatter.67.cloned.1.call-update) | async-done | bytes 65552 | tf_op jit(solution)/shard_map/reduce_scatter | solution.py:249
  2697.4 63.0 %reduce-scatter.63.cloned.1.call-done = bf16[128,256]{1,0:T(8,128)(2,1)} async-done(((bf16[1024,256]{1,0:T(8,128)(2,1)}), bf16[128,256]{1,0:T(8,128)(2,1)}) %reduce-scatter.63.cloned.1.call-update) | async-done | bytes 65552 | tf_op jit(solution)/shard_map/reduce_scatter | solution.py:246
  2761.9 62.8 %reduce-scatter.51.cloned.1.call-done = bf16[128,256]{1,0:T(8,128)(2,1)} async-done(((bf16[1024,256]{1,0:T(8,128)(2,1)}), bf16[128,256]{1,0:T(8,128)(2,1)}) %reduce-scatter.51.cloned.1.call-update) | async-done | bytes 65552 | tf_op jit(solution)/shard_map/reduce_scatter | solution.py:237
  2826.2 63.2 %reduce-scatter.55.cloned.1.call-done = bf16[128,256]{1,0:T(8,128)(2,1)} async-done(((bf16[1024,256]{1,0:T(8,128)(2,1)}), bf16[128,256]{1,0:T(8,128)(2,1)}) %reduce-scatter.55.cloned.1.call-update) | async-done | bytes 65552 | tf_op jit(solution)/shard_map/reduce_scatter | solution.py:240
  2890.9 62.7 %reduce-scatter.59.cloned.1.call-done = bf16[128,256]{1,0:T(8,128)(2,1)} async-done(((bf16[1024,256]{1,0:T(8,128)(2,1)}), bf16[128,256]{1,0:T(8,128)(2,1)}) %reduce-scatter.59.cloned.1.call-update) | async-done | bytes 65552 | tf_op jit(solution)/shard_map/reduce_scatter | solution.py:243
  2955.0 64.7 %reduce-scatter.71.cloned.1.call-done = bf16[128,512]{1,0:T(8,128)(2,1)} async-done(((bf16[1024,512]{1,0:T(8,128)(2,1)}), bf16[128,512]{1,0:T(8,128)(2,1)}) %reduce-scatter.71.cloned.1.call-update) | async-done | bytes 131088 | tf_op jit(solution)/shard_map/reduce_scatter | solution.py:252
  3021.3 68.6 %reduce-scatter.83.cloned.1.call-done = bf16[512,256]{1,0:T(8,128)(2,1)} async-done(((bf16[4096,256]{1,0:T(8,128)(2,1)}), bf16[512,256]{1,0:T(8,128)(2,1)}) %reduce-scatter.83.cloned.1.call-update) | async-done | bytes 262160 | tf_op jit(solution)/shard_map/reduce_scatter | solution.py:261
  3091.7 68.3 %reduce-scatter.79.cloned.1.call-done = bf16[128,1024]{1,0:T(8,128)(2,1)} async-done(((bf16[1024,1024]{1,0:T(8,128)(2,1)}), bf16[128,1024]{1,0:T(8,128)(2,1)}) %reduce-scatter.79.cloned.1.call-update) | async-done | bytes 262160 | tf_op jit(solution)/shard_map/reduce_scatter | solution.py:258
  3161.8 68.5 %reduce-scatter.47.cloned.1.call-done = bf16[512,256]{1,0:T(8,128)(2,1)} async-done(((bf16[4096,256]{1,0:T(8,128)(2,1)}), bf16[512,256]{1,0:T(8,128)(2,1)}) %reduce-scatter.47.cloned.1.call-update) | async-done | bytes 262160 | tf_op jit(solution)/shard_map/reduce_scatter | solution.py:234
  3232.0 68.4 %reduce-scatter.43.cloned.1.call-done = bf16[128,1024]{1,0:T(8,128)(2,1)} async-done(((bf16[1024,1024]{1,0:T(8,128)(2,1)}), bf16[128,1024]{1,0:T(8,128)(2,1)}) %reduce-scatter.43.cloned.1.call-update) | async-done | bytes 262160 | tf_op jit(solution)/shard_map/reduce_scatter | solution.py:231
  (665 shorter events, 693.4 us)
Async XLA Ops:
  7.2 131.2 %all-gather.14.cloned.1.call-start = ((), (), s32[]{:S(2)}) async-start(), calls=%async_computation.32 | async-start | bytes 9437184 | tf_op jit(solution)/shard_map/all_gather | solution.py:318
  7.9 255.7 %all-gather.16.cloned.1.call-start = ((), (), s32[]{:S(2)}) async-start(), calls=%async_computation.33 | async-start | bytes 9437184 | tf_op jit(solution)/shard_map/all_gather | solution.py:319
  8.7 304.6 %all-gather.18.cloned.1.call-start = ((), (), s32[]{:S(2)}) async-start(), calls=%async_computation.34 | async-start | bytes 2359296 | tf_op jit(solution)/shard_map/all_gather | solution.py:320
  9.4 353.7 %all-gather.20.cloned.1.call-start = ((), (), s32[]{:S(2)}) async-start(), calls=%async_computation.35 | async-start | bytes 2359296 | tf_op jit(solution)/shard_map/all_gather | solution.py:321
  10.0 402.9 %all-gather.22.cloned.1.call-start = ((), (), s32[]{:S(2)}) async-start(), calls=%async_computation.36 | async-start | bytes 2359296 | tf_op jit(solution)/shard_map/all_gather | solution.py:322
  10.6 590.4 %all-gather.24.cloned.1.call-start = ((), (), s32[]{:S(2)}) async-start(), calls=%async_computation.37 | async-start | bytes 2359296 | tf_op jit(solution)/shard_map/all_gather | solution.py:323
  11.2 959.0 %all-gather.38.cloned.1.call-start = ((), (), s32[]{:S(2)}) async-start(), calls=%async_computation.44 | async-start | bytes 2359296 | tf_op jit(solution)/shard_map/all_gather | solution.py:316
  11.9 976.1 %all-gather.26.cloned.1.call-start = ((), (), s32[]{:S(2)}) async-start(), calls=%async_computation.38 | async-start | bytes 2359296 | tf_op jit(solution)/shard_map/all_gather | solution.py:324
  12.7 980.9 %all-gather.28.cloned.1.call-start = ((), (), s32[]{:S(2)}) async-start(), calls=%async_computation.39 | async-start | bytes 4718592 | tf_op jit(solution)/shard_map/all_gather | solution.py:325
  13.4 1039.9 %all-gather.30.cloned.1.call-start = ((), (), s32[]{:S(2)}) async-start(), calls=%async_computation.40 | async-start | bytes 2359296 | tf_op jit(solution)/shard_map/all_gather | solution.py:327
  14.0 1044.9 %all-gather.32.cloned.1.call-start = ((), (), s32[]{:S(2)}) async-start(), calls=%async_computation.41 | async-start | bytes 9437184 | tf_op jit(solution)/shard_map/all_gather | solution.py:328
  14.7 1056.1 %all-gather.34.cloned.1.call-start = ((), (), s32[]{:S(2)}) async-start(), calls=%async_computation.42 | async-start | bytes 9437184 | tf_op jit(solution)/shard_map/all_gather | solution.py:329
  15.3 1072.3 %all-gather.36.cloned.1.call-start = ((), (), s32[]{:S(2)}) async-start(), calls=%async_computation.43 | async-start | bytes 2359296 | tf_op jit(solution)/shard_map/all_gather | solution.py:317
  45.2 229.3 %copy-start.64 = (f32[1,1024]{1,0:T(1,128)}, f32[1,1024]{1,0:T(1,128)S(1)}, u32[]{:S(2)}) copy-start(f32[1,1024]{1,0:T(1,128)S(1)} %get-tuple-element.518) | copy-start | bytes 12292
  45.9 102.6 %copy-start.78 = (f32[1,2,2,128]{3,1,2,0:T(2,128)}, f32[1,2,2,128]{3,1,2,0:T(2,128)S(1)}, u32[]{:S(2)}) copy-start(f32[1,2,2,128]{3,1,2,0:T(2,128)S(1)} %copy.222) | copy-start | bytes 6148
  45.9 102.6 %copy-start.80 = (f32[512]{0:T(512)}, f32[512]{0:T(512)S(1)}, u32[]{:S(2)}) copy-start(f32[512]{0:T(512)S(1)} %rsqrt.58) | copy-start | bytes 6148
  45.9 102.5 %copy-start.82 = (f32[1,2,2,128]{3,1,2,0:T(2,128)}, f32[1,2,2,128]{3,1,2,0:T(2,128)S(1)}, u32[]{:S(2)}) copy-start(f32[1,2,2,128]{3,1,2,0:T(2,128)S(1)} %copy.221) | copy-start | bytes 6148
  46.4 102.1 %copy-start.45 = (bf16[512,1024]{1,0:T(8,128)(2,1)}, bf16[512,1024]{1,0:T(8,128)(2,1)S(1)}, u32[]{:S(2)}) copy-start(bf16[512,1024]{1,0:T(8,128)(2,1)S(1)} %fusion.58) | copy-start | bytes 3145732
  275.0 137.9 %copy-start.47 = (bf16[512,1024]{1,0:T(8,128)(2,1)}, bf16[512,1024]{1,0:T(8,128)(2,1)S(1)}, u32[]{:S(2)}) copy-start(bf16[512,1024]{1,0:T(8,128)(2,1)S(1)} %add_convert_fusion.5) | copy-start | bytes 3145732
  424.6 180.7 %all-to-all-start = ((bf16[3,2,256,1024]{2,1,0,3:T(2,128)(2,1)}), bf16[3,2,256,1024]{2,1,0,3:T(2,128)(2,1)}, u32[]{:S(2)}, u32[]{:S(2)}) async-start(bf16[3,2,256,1024]{2,1,0,3:T(2,128)(2,1)} %pad_maximum_fusion), calls=%async_computation | async-start | bytes 6291456 | tf_op jit(solution)/shard_map/all_to_all | solution.py:378
  965.8 18.8 all-to-all-start.1
  970.1 989.0 %reduce-scatter.35.cloned.1.call-start = ((), (), s32[]{:S(2)}) async-start(), calls=%async_computation.45 | async-start | bytes 2621440 | tf_op jit(solution)/shard_map/reduce_scatter | solution.py:164
  974.9 124.6 %copy-start.105 = (f32[512]{0:T(512)}, f32[512]{0:T(512)S(1)}, u32[]{:S(2)}) copy-start(f32[512]{0:T(512)S(1)} %get-tuple-element.546) | copy-start | bytes 6148
  991.9 206.3 %copy-start.84 = (f32[512]{0:T(512)}, f32[512]{0:T(512)S(1)}, u32[]{:S(2)}) copy-start(f32[512]{0:T(512)S(1)} %broadcast_multiply_fusion.3) | copy-start | bytes 6148
  993.5 204.7 %copy-start.98 = (f32[512]{0:T(512)}, f32[512]{0:T(512)S(1)}, u32[]{:S(2)}) copy-start(f32[512]{0:T(512)S(1)} %fusion.114) | copy-start | bytes 6148
  1001.0 3.5 collective-permute-start
  1002.7 3.4 collective-permute-start.1
  1004.5 95.0 %copy-start.107 = (f32[512]{0:T(512)}, f32[512]{0:T(512)S(1)}, u32[]{:S(2)}) copy-start(f32[512]{0:T(512)S(1)} %fusion.93) | copy-start | bytes 6148
  1057.2 66.2 %copy-start.86 = (f32[512]{0:T(512)}, f32[512]{0:T(512)S(1)}, u32[]{:S(2)}) copy-start(f32[512]{0:T(512)S(1)} %broadcast_multiply_fusion.2) | copy-start | bytes 6148
  1058.9 64.6 %copy-start.100 = (f32[512]{0:T(512)}, f32[512]{0:T(512)S(1)}, u32[]{:S(2)}) copy-start(f32[512]{0:T(512)S(1)} %fusion.115) | copy-start | bytes 6148
  1096.0 865.2 %reduce-scatter.37.cloned.1.call-start = ((), (), s32[]{:S(2)}) async-start(), calls=%async_computation.46 | async-start | bytes 2621440 | tf_op jit(solution)/shard_map/reduce_scatter | solution.py:167
  1102.5 859.3 %reduce-scatter.73.cloned.1.call-start = ((), (), s32[]{:S(2)}) async-start(), calls=%async_computation.64 | async-start | bytes 2621440 | tf_op jit(solution)/shard_map/reduce_scatter | solution.py:194
  1183.5 4.3 collective-permute-start.2
  1184.8 3.8 collective-permute-start.3
  1207.4 19.7 all-to-all-start.2
  1212.5 750.1 %reduce-scatter.65.cloned.1.call-start = ((), (), s32[]{:S(2)}) async-start(), calls=%async_computation.60 | async-start | bytes 2621440 | tf_op jit(solution)/shard_map/reduce_scatter | solution.py:188
  1217.1 746.2 %reduce-scatter.61.cloned.1.call-start = ((), (), s32[]{:S(2)}) async-start(), calls=%async_computation.58 | async-start | bytes 2621440 | tf_op jit(solution)/shard_map/reduce_scatter | solution.py:185
  1234.0 152.2 %copy-start.3 = (bf16[2,1024,2,128]{3,1,2,0:T(8,128)(2,1)}, bf16[2,1024,2,128]{3,1,2,0:T(8,128)(2,1)S(1)}, u32[]{:S(2)}) copy-start(bf16[2,1024,2,128]{3,1,2,0:T(8,128)(2,1)S(1)} %get-tuple-element.813) | copy-start | bytes 3145732 | tf_op jit(solution)/shard_map/while
  1508.6 152.0 %copy-start.3 = (bf16[2,1024,2,128]{3,1,2,0:T(8,128)(2,1)}, bf16[2,1024,2,128]{3,1,2,0:T(8,128)(2,1)S(1)}, u32[]{:S(2)}) copy-start(bf16[2,1024,2,128]{3,1,2,0:T(8,128)(2,1)S(1)} %get-tuple-element.813) | copy-start | bytes 3145732 | tf_op jit(solution)/shard_map/while
  1798.3 165.6 %reduce-scatter.49.cloned.1.call-start = ((), (), s32[]{:S(2)}) async-start(), calls=%async_computation.52 | async-start | bytes 2621440 | tf_op jit(solution)/shard_map/reduce_scatter | solution.py:176
  1865.6 99.0 %reduce-scatter.53.cloned.1.call-start = ((), (), s32[]{:S(2)}) async-start(), calls=%async_computation.54 | async-start | bytes 2621440 | tf_op jit(solution)/shard_map/reduce_scatter | solution.py:179
  1869.4 96.0 %reduce-scatter.57.cloned.1.call-start = ((), (), s32[]{:S(2)}) async-start(), calls=%async_computation.56 | async-start | bytes 2621440 | tf_op jit(solution)/shard_map/reduce_scatter | solution.py:182
  1873.3 136.8 %reduce-scatter.69.cloned.1.call-start = ((), (), s32[]{:S(2)}) async-start(), calls=%async_computation.62 | async-start | bytes 5242880 | tf_op jit(solution)/shard_map/reduce_scatter | solution.py:191
  1881.8 202.8 %reduce-scatter.81.cloned.1.call-start = ((), (), s32[]{:S(2)}) async-start(), calls=%async_computation.68 | async-start | bytes 10485760 | tf_op jit(solution)/shard_map/reduce_scatter | solution.py:200
  1894.6 264.2 %reduce-scatter.77.cloned.1.call-start = ((), (), s32[]{:S(2)}) async-start(), calls=%async_computation.66 | async-start | bytes 10485760 | tf_op jit(solution)/shard_map/reduce_scatter | solution.py:197
  1905.5 327.8 %reduce-scatter.45.cloned.1.call-start = ((), (), s32[]{:S(2)}) async-start(), calls=%async_computation.50 | async-start | bytes 10485760 | tf_op jit(solution)/shard_map/reduce_scatter | solution.py:173
  1924.2 383.3 %reduce-scatter.41.cloned.1.call-start = ((), (), s32[]{:S(2)}) async-start(), calls=%async_computation.48 | async-start | bytes 10485760 | tf_op jit(solution)/shard_map/reduce_scatter | solution.py:170
  1945.0 427.9 %reduce-scatter.89.cloned.1.call-start = ((), (), s32[]{:S(2)}) async-start(), calls=%async_computation.72 | async-start | bytes 294912
  1949.0 488.4 %reduce-scatter.87.cloned.1.call-start = ((), (), s32[]{:S(2)}) async-start(), calls=%async_computation.71 | async-start | bytes 294912
  1959.1 543.7 %reduce-scatter.85.cloned.1.call-start = ((), (), s32[]{:S(2)}) async-start(), calls=%async_computation.70 | async-start | bytes 589824
  1961.2 605.6 %reduce-scatter.39.cloned.1.call-start = ((), (), s32[]{:S(2)}) async-start(), calls=%async_computation.47 | async-start | bytes 589824 | tf_op jit(solution)/shard_map/reduce_scatter | solution.py:228
  1961.8 669.7 %reduce-scatter.75.cloned.1.call-start = ((), (), s32[]{:S(2)}) async-start(), calls=%async_computation.65 | async-start | bytes 589824 | tf_op jit(solution)/shard_map/reduce_scatter | solution.py:255
  1962.5 733.3 %reduce-scatter.67.cloned.1.call-start = ((), (), s32[]{:S(2)}) async-start(), calls=%async_computation.61 | async-start | bytes 589824 | tf_op jit(solution)/shard_map/reduce_scatter | solution.py:249
  1963.3 797.1 %reduce-scatter.63.cloned.1.call-start = ((), (), s32[]{:S(2)}) async-start(), calls=%async_computation.59 | async-start | bytes 589824 | tf_op jit(solution)/shard_map/reduce_scatter | solution.py:246
  1963.8 860.9 %reduce-scatter.51.cloned.1.call-start = ((), (), s32[]{:S(2)}) async-start(), calls=%async_computation.53 | async-start | bytes 589824 | tf_op jit(solution)/shard_map/reduce_scatter | solution.py:237
  1964.6 924.8 %reduce-scatter.55.cloned.1.call-start = ((), (), s32[]{:S(2)}) async-start(), calls=%async_computation.55 | async-start | bytes 589824 | tf_op jit(solution)/shard_map/reduce_scatter | solution.py:240
  1965.3 988.2 %reduce-scatter.59.cloned.1.call-start = ((), (), s32[]{:S(2)}) async-start(), calls=%async_computation.57 | async-start | bytes 589824 | tf_op jit(solution)/shard_map/reduce_scatter | solution.py:243
  1965.9 1053.8 %reduce-scatter.71.cloned.1.call-start = ((), (), s32[]{:S(2)}) async-start(), calls=%async_computation.63 | async-start | bytes 1179648 | tf_op jit(solution)/shard_map/reduce_scatter | solution.py:252
  2010.1 1079.8 %reduce-scatter.83.cloned.1.call-start = ((), (), s32[]{:S(2)}) async-start(), calls=%async_computation.69 | async-start | bytes 2359296 | tf_op jit(solution)/shard_map/reduce_scatter | solution.py:261
  2084.6 1075.4 %reduce-scatter.79.cloned.1.call-start = ((), (), s32[]{:S(2)}) async-start(), calls=%async_computation.67 | async-start | bytes 2359296 | tf_op jit(solution)/shard_map/reduce_scatter | solution.py:258
  2158.8 1071.4 %reduce-scatter.47.cloned.1.call-start = ((), (), s32[]{:S(2)}) async-start(), calls=%async_computation.51 | async-start | bytes 2359296 | tf_op jit(solution)/shard_map/reduce_scatter | solution.py:234
  2233.3 74.2 %copy-start.124 = (s32[1,2,2,128]{3,1,2,0:T(2,128)S(1)}, s32[1,2,2,128]{3,1,2,0:T(2,128)}, u32[]{:S(2)}) copy-start(s32[1,2,2,128]{3,1,2,0:T(2,128)} %copy-done.123) | copy-start | bytes 6148
  2233.3 1067.1 %reduce-scatter.43.cloned.1.call-start = ((), (), s32[]{:S(2)}) async-start(), calls=%async_computation.49 | async-start | bytes 2359296 | tf_op jit(solution)/shard_map/reduce_scatter | solution.py:231
  2310.7 63.0 %copy-start.79 = (f32[1,2,2,128]{3,1,2,0:T(2,128)S(1)}, f32[1,2,2,128]{3,1,2,0:T(2,128)}, u32[]{:S(2)}) copy-start(f32[1,2,2,128]{3,1,2,0:T(2,128)} %copy-done.78) | copy-start | bytes 6148
  (130 other events, 597.4 us)
Sparse Core Ops, SparseCore 0:
  10.1 128.1 all-gather.13
  140.5 123.1 all-gather.15
  265.8 47.4 all-gather.17
  315.3 47.7 all-gather.19
  365.0 47.7 all-gather.21
  414.8 47.7 all-gather.23
  464.8 47.8 all-gather.37
  514.8 47.7 all-gather.25
  564.7 72.1 all-gather.27
  638.9 47.5 all-gather.29
  688.6 123.4 all-gather.31
  814.0 123.1 all-gather.33
  939.3 47.4 all-gather.35
  1096.1 32.0 reduce-scatter.34
  1130.8 31.5 reduce-scatter.36
  1178.2 30.4 reduce-scatter.72
  1217.3 31.3 reduce-scatter.64
  1798.4 40.6 reduce-scatter.60
  1865.7 29.2 reduce-scatter.48
  1897.4 31.4 reduce-scatter.52
  1931.6 31.3 reduce-scatter.56
  1965.5 44.5 reduce-scatter.68
  2012.9 71.6 reduce-scatter.80
  2087.0 71.7 reduce-scatter.76
  2161.5 71.6 reduce-scatter.44
  2235.7 71.7 reduce-scatter.40
  2311.6 61.2 reduce-scatter.88
  2377.1 60.2 reduce-scatter.86
  2441.7 60.9 reduce-scatter.84
  2505.9 60.8 reduce-scatter.38
  2570.5 60.9 reduce-scatter.74
  2634.8 60.9 reduce-scatter.66
  2699.4 60.9 reduce-scatter.62
  2763.7 60.9 reduce-scatter.50
  2828.4 60.9 reduce-scatter.54
  2892.6 60.9 reduce-scatter.58
  2957.2 62.4 reduce-scatter.70
  3023.2 66.6 reduce-scatter.82
  3093.3 66.6 reduce-scatter.78
  3163.5 66.6 reduce-scatter.46
  3233.8 66.6 reduce-scatter.42
where the time goes:
time: 3320 us; the launch traced here: 3310 us
  waiting for transfers between devices  1670 us (50%)
  local copies, waits for them, and re-layouts  844 us (25%)
  matrix products  345 us (10%)
  other arithmetic  204 us (6%)
  blocking collectives  193 us (6%)
    while x62, local copies, waits for them, and re-layouts  353 us
    unnamed x44, waiting for transfers between devices  189 us
    sin x1, other arithmetic, position_table(): jnp.sin(angles)  122 us
    all_gather x1, waiting for transfers between devices, per_device(): lax.all_gather(opening_dense_exit_projection, 'batch', axis=0, tiled=True)  115 us
    reshape x4, local copies, waits for them, and re-layouts, relative_shift(): flat_rows = relative.reshape(head_count, row_count * span_len)  96.5 us
    all_gather x1, waiting for transfers between devices, per_device(): lax.all_gather(opening_dense_entry_projection, 'batch', axis=0, tiled=True)  91.9 us
    reshape x6, local copies, waits for them, and re-layouts, relative_shift(): moved_rows.reshape(head_count, row_count, span_len - 1)[:, :, :row_count]  84.4 us
    slice x4, local copies, waits for them, and re-layouts, relative_shift(): lax.slice_in_dim(flat_rows, row_count - 1, row_count - 1 + row_count * (s...  84.3 us
  transfers between devices with their start and end apart: 48, of which 29 were waited for; matrix products, arithmetic and copies ran while one was open for 41% of the time, Pallas kernels for 0%

commit v1 on v0

--- a/solution.py
+++ b/solution.py
@@ -4,12 +4,169 @@
 import jax
 import jax.numpy as jnp
 from jax import lax
+from jax.experimental import pallas as pl
+from jax.experimental.pallas import tpu as pltpu
 from jax.sharding import PartitionSpec as P
 
-HEADS = 8
+HEAD_WIDTH = 128
 
 
 epsilon = 1e-05
+
+F32, BF16 = jnp.float32, jnp.bfloat16
+
+def dot(a, b, ca, cb):
+    return lax.dot_general(a, b, (((ca,), (cb,)), ((), ())), preferred_element_type=F32)
+
+def _fwd_body(len_ref, q_ref, k_ref, v_ref, pos_ref, bias_ref, o_ref, p_ref, *, rows, full, scale):
+    block = pl.program_id(2)
+    length = len_ref[pl.program_id(0)]
+    query = q_ref[0, 0].astype(F32)
+    content_query = (query + bias_ref[0:1, :]).astype(BF16)
+    position_query = (query + bias_ref[1:2, :]).astype(BF16)
+    content = dot(content_query, k_ref[0, 0], 1, 1)
+    span = full + rows
+    start = pl.multiple_of(full - rows - block * rows, rows)
+    relative = dot(position_query, pos_ref[pl.ds(start, span), :], 1, 1)
+    relative = pltpu.roll(relative, span - (rows - 1), 1, stride=1, stride_axis=0)
+    raw = content + relative[:, :full]
+    seen = lax.broadcasted_iota(jnp.int32, raw.shape, 1) < length
+    scores = jnp.where(seen, raw * scale, -1e30)
+    top = jnp.max(scores, axis=-1, keepdims=True)
+    weights = jnp.exp(scores - top)
+    total = jnp.sum(weights, axis=-1, keepdims=True)
+    low = (weights * (1.0 / total)).astype(BF16)
+    p_ref[0, 0] = low
+    o_ref[0] = dot(low, v_ref[0, 0], 1, 0).astype(BF16)
+
+def attend_forward(by_heads, position, bias, lengths, rows=256):
+    _, groups, full, width = by_heads.shape
+    depth = HEAD_WIDTH
+    heads = width // depth
+    body = partial(_fwd_body, rows=rows, full=full, scale=1.0 / math.sqrt(depth))
+    flops = groups * heads * full * (2 * full * depth * 3 + 2 * rows * depth)
+    return pl.pallas_call(
+        body,
+        grid_spec=pltpu.PrefetchScalarGridSpec(
+            num_scalar_prefetch=1,
+            grid=(groups, heads, full // rows),
+            in_specs=[
+                pl.BlockSpec((1, 1, rows, depth), lambda u, h, i, n: (0, u, i, h)),
+                pl.BlockSpec((1, 1, full, depth), lambda u, h, i, n: (1, u, 0, h)),
+                pl.BlockSpec((1, 1, full, depth), lambda u, h, i, n: (2, u, 0, h)),
+                pl.BlockSpec((2 * full, depth), lambda u, h, i, n: (0, h)),
+                pl.BlockSpec((2, depth), lambda u, h, i, n: (0, h)),
+            ],
+            out_specs=[
+                pl.BlockSpec((1, rows, depth), lambda u, h, i, n: (u, i, h)),
+                pl.BlockSpec((1, 1, rows, full), lambda u, h, i, n: (u, h, i, 0)),
+            ],
+        ),
+        out_shape=[
+            jax.ShapeDtypeStruct((groups, full, width), BF16),
+            jax.ShapeDtypeStruct((groups, heads, full, full), BF16),
+        ],
+        compiler_params=pltpu.CompilerParams(vmem_limit_bytes=48 << 20),
+        cost_estimate=pl.CostEstimate(flops=flops, transcendentals=groups * heads * full * full, bytes_accessed=groups * heads * full * full * 2 + 5 * groups * full * width * 2),
+        name="attend_forward",
+    )(lengths, by_heads, by_heads, by_heads, position, bias)
+
+def _bwd_body(p_ref, q_ref, k_ref, v_ref, g_ref, pos_ref, bias_ref, d_ref, dpos_ref, dbias_ref,
+              key_acc, value_acc, pos_acc, bias_acc, *, rows, full, scale):
+    group, block = pl.program_id(1), pl.program_id(2)
+    last_block = block == pl.num_programs(2) - 1
+
+    @pl.when((group == 0) & (block == 0))
+    def _():
+        pos_acc[...] = jnp.zeros_like(pos_acc)
+        bias_acc[...] = jnp.zeros_like(bias_acc)
+
+    @pl.when(block == 0)
+    def _():
+        key_acc[...] = jnp.zeros_like(key_acc)
+        value_acc[...] = jnp.zeros_like(value_acc)
+
+    query = q_ref[0, 0].astype(F32)
+    content_query = (query + bias_ref[0:1, :]).astype(BF16)
+    position_query = (query + bias_ref[1:2, :]).astype(BF16)
+    keys, grad = k_ref[0, 0], g_ref[0]
+    low = p_ref[0, 0]
+    weights = low.astype(F32)
+    grad_weights = dot(grad, v_ref[0, 0], 1, 1)
+    value_acc[...] += dot(grad, low, 0, 0)
+    inner = jnp.sum(grad_weights * weights, axis=-1, keepdims=True)
+    grad_raw = (weights * (grad_weights - inner) * scale).astype(BF16)
+    key_acc[...] += dot(content_query, grad_raw, 0, 0)
+    grad_content = dot(grad_raw, keys, 1, 0)
+    row = lax.broadcasted_iota(jnp.int32, (rows, rows), 0)
+    column = lax.broadcasted_iota(jnp.int32, (rows, rows), 1)
+    flip = jnp.where(row + column == rows - 1, 1.0, 0.0).astype(BF16)
+    span = full + rows
+    start = pl.multiple_of(full - rows - block * rows, rows)
+    turned = jnp.concatenate([dot(flip, grad_raw, 1, 0).astype(BF16), jnp.zeros((rows, rows), BF16)], axis=1)
+    turned = pltpu.roll(turned, 0, 1, stride=1, stride_axis=0)
+    turned_query = dot(flip, position_query, 1, 0).astype(BF16)
+    pos_acc[:, pl.ds(start, span)] += dot(turned_query, turned, 0, 0)
+    grad_turned = dot(turned, pos_ref[pl.ds(start, span), :], 1, 0)
+    high = grad_turned.astype(BF16)
+    rest = (grad_turned - high.astype(F32)).astype(BF16)
+    grad_position = dot(flip, high, 1, 0) + dot(flip, rest, 1, 0)
+    here = pl.ds(pl.multiple_of(block * rows, rows), rows)
+    d_ref[0, 0, here, :] = (grad_content + grad_position).astype(BF16)
+    bias_acc[0:1, :] += jnp.sum(grad_content, axis=0, keepdims=True)
+    bias_acc[1:2, :] += jnp.sum(grad_position, axis=0, keepdims=True)
+
+    @pl.when(last_block)
+    def _():
+        d_ref[1, 0] = key_acc[...].T.astype(BF16)
+        d_ref[2, 0] = value_acc[...].T.astype(BF16)
+
+    @pl.when(last_block & (group == pl.num_programs(1) - 1))
+    def _():
+        dpos_ref[...] = pos_acc[...].T.astype(BF16)
+        dbias_ref[...] = bias_acc[...]
+
+def attend_backward(probs, by_heads, grad_heads, position, bias, rows=256):
+    _, groups, full, width = by_heads.shape
+    depth = HEAD_WIDTH
+    heads = width // depth
+    body = partial(_bwd_body, rows=rows, full=full, scale=1.0 / math.sqrt(depth))
+    flops = groups * heads * full * (2 * full * depth * 7 + 6 * rows * depth)
+    return pl.pallas_call(
+        body,
+        grid_spec=pltpu.PrefetchScalarGridSpec(
+            num_scalar_prefetch=0,
+            grid=(heads, groups, full // rows),
+            in_specs=[
+                pl.BlockSpec((1, 1, rows, full), lambda h, u, i: (u, h, i, 0)),
+                pl.BlockSpec((1, 1, rows, depth), lambda h, u, i: (0, u, i, h)),
+                pl.BlockSpec((1, 1, full, depth), lambda h, u, i: (1, u, 0, h)),
+                pl.BlockSpec((1, 1, full, depth), lambda h, u, i: (2, u, 0, h)),
+                pl.BlockSpec((1, rows, depth), lambda h, u, i: (u, i, h)),
+                pl.BlockSpec((2 * full, depth), lambda h, u, i: (0, h)),
+                pl.BlockSpec((2, depth), lambda h, u, i: (0, h)),
+            ],
+            out_specs=[
+                pl.BlockSpec((3, 1, full, depth), lambda h, u, i: (0, u, 0, h)),
+                pl.BlockSpec((2 * full, depth), lambda h, u, i: (0, h)),
+                pl.BlockSpec((2, depth), lambda h, u, i: (0, h)),
+            ],
+            scratch_shapes=[
+                pltpu.VMEM((depth, full), F32),
+                pltpu.VMEM((depth, full), F32),
+                pltpu.VMEM((depth, 2 * full), F32),
+                pltpu.VMEM((2, depth), F32),
+            ],
+        ),
+        out_shape=[
+            jax.ShapeDtypeStruct((3, groups, full, width), BF16),
+            jax.ShapeDtypeStruct((2 * full, width), BF16),
+            jax.ShapeDtypeStruct((2, width), F32),
+        ],
+        compiler_params=pltpu.CompilerParams(vmem_limit_bytes=48 << 20),
+        cost_estimate=pl.CostEstimate(flops=flops, transcendentals=0, bytes_accessed=groups * heads * full * full * 2 + 8 * groups * full * width * 2),
+        name="attend_backward",
+    )(probs, by_heads, by_heads, by_heads, grad_heads, position, bias)
 
 
 def extended(value, sides, width):
@@ -43,22 +200,19 @@
 
 
 def position_table(length, model_width):
-    offsets = (jnp.arange(2 * length - 1, dtype=jnp.int32) - (length - 1)).astype(jnp.float32)
-    pairs = jnp.arange(model_width // 2, dtype=jnp.int32).astype(jnp.float32)
-    rates = jnp.exp(pairs * (-2.0 * math.log(10000.0) / model_width))
-    angles = offsets[:, None] * rates[None, :]
-    return jnp.stack([jnp.sin(angles), jnp.cos(angles)], axis=-1).reshape(
-        2 * length - 1, model_width
-    )
-
-
-def relative_shift(relative):
-    head_count, row_count, span_len = relative.shape
-    flat_rows = relative.reshape(head_count, row_count * span_len)
-    moved_rows = lax.slice_in_dim(
-        flat_rows, row_count - 1, row_count - 1 + row_count * (span_len - 1), axis=1
-    )
-    return moved_rows.reshape(head_count, row_count, span_len - 1)[:, :, :row_count]
+    fine = 64
+    coarse = 2 * length // fine
+    column = jnp.arange(model_width, dtype=jnp.int32)
+    rates = jnp.exp((column // 2).astype(jnp.float32) * (-2.0 * math.log(10000.0) / model_width))
+    odd = (column % 2 == 1)[None, :]
+    start = (jnp.arange(coarse, dtype=jnp.int32) * fine - (length - 1)).astype(jnp.float32)
+    large = start[:, None] * rates[None, :]
+    small = jnp.arange(fine, dtype=jnp.int32).astype(jnp.float32)[:, None] * rates[None, :]
+    sin_large, cos_large = jnp.sin(large), jnp.cos(large)
+    first = jnp.where(odd, cos_large, sin_large)[:, None, :]
+    second = jnp.where(odd, -sin_large, cos_large)[:, None, :]
+    table = first * jnp.cos(small)[None] + second * jnp.sin(small)[None]
+    return table.astype(jnp.bfloat16).reshape(2 * length, model_width)
 
 
 def depth_conv(padded, kernel_rows, length):
@@ -118,22 +272,13 @@
     return (grad_values, grad_scale, grad_shift, grad_pre_low, grad_out_low)
 
 
-def attention_logits(query_rows, key_rows, position_rows, content_bias, position_bias, length_one):
-    query_float = query_rows.astype(jnp.float32)
-    content_query = (query_float + content_bias).astype(jnp.bfloat16)
-    position_query = (query_float + position_bias).astype(jnp.bfloat16)
-    content = jnp.einsum(
-        "ihd,jhd->hij", content_query, key_rows, preferred_element_type=jnp.float32
-    )
-    relative = jnp.einsum(
-        "ihd,nhd->hin", position_query, position_rows, preferred_element_type=jnp.float32
-    )
-    raw_scores = content + relative_shift(relative)
-    key_valid = jnp.arange(key_rows.shape[0], dtype=jnp.int32)[None, None, :] < length_one
-    discretizer_scores = jnp.where(
-        key_valid, raw_scores * (1.0 / math.sqrt(key_rows.shape[2])), -1e30
-    )
-    return (discretizer_scores, key_valid, content_query, position_query, relative.shape)
+def sum_everywhere(value):
+    for axis in ("seq", "batch"):
+        size, step = lax.axis_size(axis), 1
+        while step < size:
+            value = value + lax.ppermute(value, axis, [(i, i ^ step) for i in range(size)])
+            step *= 2
+    return value
 
 
 def sum_small_seq(smalls):
@@ -334,8 +479,6 @@
     full_len = local_len * seq_count
     entries = codebook_all.shape[0]
     total_rows = groups * local_len
-    heads_local = HEADS // seq_count
-    head_width = model_width // HEADS
     local_width = model_width // seq_count
     kernel_size = depth_all.shape[0]
     rim_width = kernel_size // 2
@@ -376,43 +519,13 @@
         .reshape(3, groups, local_len, model_width)
     )
     by_heads = lax.all_to_all(stacked, "seq", split_axis=3, concat_axis=2, tiled=True)
-    head_shape = (groups, full_len, heads_local, head_width)
-    query_heads = by_heads[0].reshape(head_shape)
-    key_heads = by_heads[1].reshape(head_shape)
-    value_heads = by_heads[2].reshape(head_shape)
-    table_low = position_table(full_len, model_width).astype(jnp.bfloat16)
+    table_low = position_table(full_len, model_width)
     pos_columns = lax.dynamic_slice_in_dim(pos_all, seq_place * local_width, local_width, 1)
-    position_low = (
-        matmul_rows(table_low, pos_columns)
-        .astype(jnp.bfloat16)
-        .reshape(2 * full_len - 1, heads_local, head_width)
-    )
-    content_bias = lax.dynamic_slice_in_dim(
-        params_f[12], seq_place * local_width, local_width, 0
-    ).reshape(heads_local, head_width)
-    position_bias = lax.dynamic_slice_in_dim(
-        params_f[13], seq_place * local_width, local_width, 0
-    ).reshape(heads_local, head_width)
-
-    def attend_forward(items):
-        query_rows, key_rows, value_rows, length_one = items
-        discretizer_scores = attention_logits(
-            query_rows, key_rows, position_low, content_bias, position_bias, length_one
-        )[0]
-        row_top = jnp.max(discretizer_scores, axis=-1, keepdims=True)
-        weights_exp = jnp.exp(discretizer_scores - row_top)
-        totals = jnp.sum(weights_exp, axis=-1, keepdims=True)
-        weights_low = (weights_exp / totals).astype(jnp.bfloat16)
-        attended = jnp.einsum(
-            "hij,jhd->ihd", weights_low, value_rows, preferred_element_type=jnp.float32
-        )
-        return (attended.astype(jnp.bfloat16), (row_top + jnp.log(totals))[..., 0])
-
-    attended_low, log_totals = lax.map(
-        attend_forward, (query_heads, key_heads, value_heads, utterance_durations)
-    )
+    position_low = matmul_rows(table_low, pos_columns).astype(jnp.bfloat16)
+    biases = lax.dynamic_slice_in_dim(params_f[12:14], seq_place * local_width, local_width, 1)
+    attended_low, probs = attend_forward(by_heads, position_low, biases, utterance_durations)
     back_time = lax.all_to_all(
-        attended_low.reshape(groups, full_len, local_width),
+        attended_low,
         "seq",
         split_axis=1,
         concat_axis=2,
@@ -430,14 +543,16 @@
     padded_glu = extended(glu_low, (("seq", 1),), rim_width)
     conv_value = depth_conv(padded_glu, depth_f, local_len).reshape(total_rows, model_width)
     masked_conv = valid_rows * conv_value
-    sum_first, sum_second, count_all = lax.psum(
-        (
-            jnp.sum(masked_conv, axis=0),
-            jnp.sum(masked_conv * conv_value, axis=0),
-            jnp.sum(valid_mask),
-        ),
-        ("batch", "seq"),
-    )
+    sums = sum_everywhere(
+        jnp.stack(
+            [
+                jnp.sum(masked_conv, axis=0),
+                jnp.sum(masked_conv * conv_value, axis=0),
+                jnp.broadcast_to(jnp.sum(valid_mask), (model_width,)),
+            ]
+        )
+    )
+    sum_first, sum_second, count_all = sums[0], sums[1], sums[2]
     bound_norm = partial(batch_norm, count_all=count_all)
     normalized = bound_norm(conv_value, sum_first, sum_second, params_f[10], params_f[11])
     act_low = jax.nn.silu(normalized).astype(jnp.bfloat16)
@@ -470,7 +585,7 @@
     grad_conv_direct, part_first, part_second, grad_bn_scale, grad_bn_shift = norm_back(
         grad_normalized
     )
-    total_first, total_second = lax.psum((part_first, part_second), ("batch", "seq"))
+    total_first, total_second = sum_everywhere(jnp.stack([part_first, part_second]))
     grad_conv = grad_conv_direct + valid_rows * (total_first + 2.0 * conv_value * total_second)
     grad_conv_low = grad_conv.astype(jnp.bfloat16).reshape(groups, local_len, model_width)
     padded_grad = extended(grad_conv_low, (("seq", 1),), rim_width)
@@ -500,62 +615,10 @@
         split_axis=2,
         concat_axis=1,
         tiled=True,
-    ).reshape(head_shape)
-
-    def attend_backward(items):
-        query_rows, key_rows, value_rows, length_one, log_total, grad_rows = items
-        discretizer_scores, key_valid, content_query, position_query, relative_shape = (
-            attention_logits(
-                query_rows, key_rows, position_low, content_bias, position_bias, length_one
-            )
-        )
-        weights_soft = jnp.exp(discretizer_scores - log_total[..., None])
-        weights_low = weights_soft.astype(jnp.bfloat16)
-        grad_weights = jnp.einsum(
-            "ihd,jhd->hij", grad_rows, value_rows, preferred_element_type=jnp.float32
-        )
-        grad_value = jnp.einsum(
-            "hij,ihd->jhd", weights_low, grad_rows, preferred_element_type=jnp.float32
-        )
-        grad_logits = weights_soft * (
-            grad_weights - jnp.sum(grad_weights * weights_soft, axis=-1, keepdims=True)
-        )
-        grad_raw = (
-            jnp.where(key_valid, grad_logits, 0.0) * (1.0 / math.sqrt(key_rows.shape[2]))
-        ).astype(jnp.bfloat16)
-        grad_content_query = jnp.einsum(
-            "hij,jhd->ihd", grad_raw, key_rows, preferred_element_type=jnp.float32
-        )
-        grad_key = jnp.einsum(
-            "hij,ihd->jhd", grad_raw, content_query, preferred_element_type=jnp.float32
-        )
-        shift_value, shift_back = jax.vjp(relative_shift, jnp.zeros(relative_shape, jnp.float32))
-        grad_relative = shift_back(grad_raw.astype(jnp.float32))[0].astype(jnp.bfloat16)
-        grad_position_query = jnp.einsum(
-            "hin,nhd->ihd", grad_relative, position_low, preferred_element_type=jnp.float32
-        )
-        grad_position = jnp.einsum(
-            "hin,ihd->nhd", grad_relative, position_query, preferred_element_type=jnp.float32
-        )
-        return (
-            grad_content_query + grad_position_query,
-            grad_key,
-            grad_value,
-            grad_position,
-            jnp.sum(grad_content_query, axis=0),
-            jnp.sum(grad_position_query, axis=0),
-        )
-
-    grad_query, grad_key, grad_value, grad_positions, grad_content_bias, grad_position_bias = (
-        lax.map(
-            attend_backward,
-            (query_heads, key_heads, value_heads, utterance_durations, log_totals, grad_heads),
-        )
-    )
-    grad_stack = (
-        jnp.stack([grad_query, grad_key, grad_value])
-        .astype(jnp.bfloat16)
-        .reshape(3, groups, full_len, local_width)
+    )
+
+    grad_stack, grad_position_low, grad_biases = attend_backward(
+        probs, by_heads, grad_heads, position_low, biases
     )
     grad_time = lax.all_to_all(grad_stack, "seq", split_axis=2, concat_axis=3, tiled=True).reshape(
         3, total_rows, model_width
@@ -568,21 +631,9 @@
     attn_norm_value, attn_norm_back = jax.vjp(layer_norm, first_mid, params_f[1], params_f[6])
     grad_from_attn, scale_one, shift_one = attn_norm_back(grad_attn_normed)
     grad_first = grad_second + grad_from_attn
-    grad_position_low = (
-        jnp.sum(grad_positions, axis=0).astype(jnp.bfloat16).reshape(2 * full_len - 1, local_width)
-    )
     grad_pos_columns = transpose_times(table_low, grad_position_low)
-    content_full = lax.dynamic_update_slice_in_dim(
-        jnp.zeros((model_width,), jnp.float32),
-        jnp.sum(grad_content_bias, axis=0).reshape(local_width),
-        seq_place * local_width,
-        0,
-    )
-    position_full = lax.dynamic_update_slice_in_dim(
-        jnp.zeros((model_width,), jnp.float32),
-        jnp.sum(grad_position_bias, axis=0).reshape(local_width),
-        seq_place * local_width,
-        0,
+    content_full, position_full = lax.dynamic_update_slice_in_dim(
+        jnp.zeros((2, model_width), jnp.float32), grad_biases, seq_place * local_width, 1
     )
     grad_macaron, scale_zero, shift_zero, mac_pre_low, mac_out_low = ffn_backward(
         0.5 * grad_first,

time: 3320 us -> 2660 us (0.80)
  local copies, waits for them, and re-layouts: 844 us -> 70.4 us
  waiting for transfers between devices: 1670 us -> 2080 us
  other arithmetic: 204 us -> 57.3 us
  matrix products: 345 us -> 205 us
  Pallas kernels: 0 us -> 55.1 us
  blocking collectives: 193 us -> 140 us
    while x64 -> x0, local copies, waits for them, and re-layouts: 355 us -> none
    reshape x12 -> x0, local copies, waits for them, and re-layouts: 187 us -> none  [the longest x4 96.5 us: relative_shift(): flat_rows = relative.reshape(head_count, row_count * span_len)]
    slice x14 -> x1, local copies, waits for them, and re-layouts: 127 us -> 0.01 us  [per_device(): params_f[12:14]]
    sin x1 -> x0, other arithmetic: 122 us -> none  [position_table(): jnp.sin(angles)]
    all_gather x1, waiting for transfers between devices: 0.02 us -> 120 us  [per_device(): lax.all_gather(closing_dense_entry_projection, 'batch', axis=0, tiled=True)]
    all_gather x1, waiting for transfers between devices: 0.01 us -> 113 us  [per_device(): lax.all_gather(closing_dense_exit_projection, 'batch', axis=0, tiled=True)]
    dot_general x20 -> x0, matrix products: 111 us -> none  [the longest x4 32.8 us: attention_logits(): jnp.einsum('ihd,nhd->hin', position_query, position_rows, preferred_eleme...]
    psum x2 -> x0, blocking collectives: 80.8 us -> none  [the longest x1 41.1 us: per_device(): lax.psum((part_first, part_second), ('batch', 'seq'))]
  transfers between devices with their start and end apart: 48 -> 57, of which waited for: 29 -> 42; matrix products, arithmetic and copies ran while one was open for 41% -> 11% of each run, Pallas kernels for 0% -> 2%
where the time goes in v1:
time: 2660 us; the launch traced here: 2650 us
  waiting for transfers between devices  2080 us (78%)
  matrix products  205 us (8%)
  blocking collectives  140 us (5%)
  local copies, waits for them, and re-layouts  70.4 us (3%)
  other arithmetic  57.3 us (2%)
  Pallas kernels  55.1 us (2%)
  starting transfers between devices  30.2 us (1%)
    unnamed x44, waiting for transfers between devices  188 us
    all_gather x1, waiting for transfers between devices, per_device(): lax.all_gather(closing_dense_entry_projection, 'batch', axis=0, tiled=True)  120 us
    all_gather x1, waiting for transfers between devices, per_device(): lax.all_gather(opening_dense_exit_projection, 'batch', axis=0, tiled=True)  115 us
    all_gather x1, waiting for transfers between devices, per_device(): lax.all_gather(closing_dense_exit_projection, 'batch', axis=0, tiled=True)  113 us
    all_gather x1, waiting for transfers between devices, per_device(): lax.all_gather(opening_dense_entry_projection, 'batch', axis=0, tiled=True)  92.7 us
    dot_general x14, matrix products, matmul_rows(): return jnp.dot(left_side, right_side, preferred_element_type=jnp.float32)  78.5 us
    reduce_scatter x1, waiting for transfers between devices, sum_over_seq(): lax.psum_scatter(grad_thirteen.astype(jnp.bfloat16), 'seq', scatter_dimen...  74.5 us
    reduce_scatter x1, waiting for transfers between devices, sum_over_seq(): lax.psum_scatter(grad_four.astype(jnp.bfloat16), 'seq', scatter_dimension...  74.5 us
  transfers between devices with their start and end apart: 57, of which 42 were waited for; matrix products, arithmetic and copies ran while one was open for 11% of the time, Pallas kernels for 2%

profile of v1, /device:TPU:0, one launch (start us, length us, event | category | flops | bytes accessed | tf_op | source)
XLA Modules:
  0.0 2651.0 jit_solution(1555139756119696919)
XLA Ops:
  15.3 28.6 %all_gather.45 = bf16[14,1024]{1,0:T(8,128)(2,1)S(1)} all-gather(bf16[14,128]{1,0:T(8,128)(2,1)S(1)} %copy-done.85), channel_id=1, replica_groups=mesh['batch'=8,'seq'=4] {'batch'}, dimensions={1}, use_global_device_ids=true | all-gather | bytes 32256 | tf_op jit(solution)/shard_map/all_gather | solution.py:460
  45.6 92.7 %all-gather.14.cloned.1.call-done = bf16[1024,4096]{1,0:T(8,128)(2,1)} async-done(((bf16[128,4096]{1,0:T(8,128)(2,1)}), bf16[1024,4096]{1,0:T(8,128)(2,1)}) %all-gather.14.cloned.1.call-update) | async-done | bytes 8388624 | tf_op jit(solution)/shard_map/all_gather | solution.py:463
  138.3 10.1 fusion.120
  148.4 115.2 %all-gather.16.cloned.1.call-done = bf16[4096,1024]{1,0:T(8,128)(2,1)} async-done(((bf16[512,1024]{1,0:T(8,128)(2,1)}), bf16[4096,1024]{1,0:T(8,128)(2,1)}) %all-gather.16.cloned.1.call-update) | async-done | bytes 8388624 | tf_op jit(solution)/shard_map/all_gather | solution.py:464
  263.6 9.6 fusion.115
  275.0 38.2 %all-gather.18.cloned.1.call-done = bf16[1024,1024]{1,0:T(8,128)(2,1)} async-done(((bf16[128,1024]{1,0:T(8,128)(2,1)}), bf16[1024,1024]{1,0:T(8,128)(2,1)}) %all-gather.18.cloned.1.call-update) | async-done | bytes 2097168 | tf_op jit(solution)/shard_map/all_gather | solution.py:465
  317.0 46.0 %all-gather.20.cloned.1.call-done = bf16[1024,1024]{1,0:T(8,128)(2,1)} async-done(((bf16[128,1024]{1,0:T(8,128)(2,1)}), bf16[1024,1024]{1,0:T(8,128)(2,1)}) %all-gather.20.cloned.1.call-update) | async-done | bytes 2097168 | tf_op jit(solution)/shard_map/all_gather | solution.py:466
  363.0 3.8 convolution_convert_fusion.13
  369.3 43.5 %all-gather.22.cloned.1.call-done = bf16[1024,1024]{1,0:T(8,128)(2,1)} async-done(((bf16[128,1024]{1,0:T(8,128)(2,1)}), bf16[1024,1024]{1,0:T(8,128)(2,1)}) %all-gather.22.cloned.1.call-update) | async-done | bytes 2097168 | tf_op jit(solution)/shard_map/all_gather | solution.py:467
  412.8 3.8 convolution_convert_fusion.12
  419.1 5.4 pad_maximum_fusion
  424.5 3.9 all-to-all-start
  433.3 29.2 %all-gather.24.cloned.1.call-done = bf16[1024,1024]{1,0:T(8,128)(2,1)} async-done(((bf16[128,1024]{1,0:T(8,128)(2,1)}), bf16[1024,1024]{1,0:T(8,128)(2,1)}) %all-gather.24.cloned.1.call-update) | async-done | bytes 2097168 | tf_op jit(solution)/shard_map/all_gather | solution.py:468
  462.6 4.5 convolution_convert_fusion.5.pos_ref
  474.4 20.7 attend_forward.1
  497.2 3.5 all-to-all-start.1
  500.9 26.2 all_gather.53
  533.3 53.3 %all-gather.28.cloned.1.call-done = bf16[1024,2048]{1,0:T(8,128)(2,1)} async-done(((bf16[128,2048]{1,0:T(8,128)(2,1)}), bf16[1024,2048]{1,0:T(8,128)(2,1)}) %all-gather.28.cloned.1.call-update) | async-done | bytes 4194320 | tf_op jit(solution)/shard_map/all_gather | solution.py:470
  586.6 5.3 fusion.96
  614.4 21.9 all-gather.38.cloned.1.call-done
  646.0 40.1 %all-gather.30.cloned.1.call-done = bf16[1024,1024]{1,0:T(8,128)(2,1)} async-done(((bf16[128,1024]{1,0:T(8,128)(2,1)}), bf16[1024,1024]{1,0:T(8,128)(2,1)}) %all-gather.30.cloned.1.call-update) | async-done | bytes 2097168 | tf_op jit(solution)/shard_map/all_gather | solution.py:472
  686.1 3.9 fusion.117
  691.7 120.0 %all-gather.32.cloned.1.call-done = bf16[1024,4096]{1,0:T(8,128)(2,1)} async-done(((bf16[128,4096]{1,0:T(8,128)(2,1)}), bf16[1024,4096]{1,0:T(8,128)(2,1)}) %all-gather.32.cloned.1.call-update) | async-done | bytes 8388624 | tf_op jit(solution)/shard_map/all_gather | solution.py:473
  811.7 11.9 fusion.97
  823.6 113.2 %all-gather.34.cloned.1.call-done = bf16[4096,1024]{1,0:T(8,128)(2,1)} async-done(((bf16[512,1024]{1,0:T(8,128)(2,1)}), bf16[4096,1024]{1,0:T(8,128)(2,1)}) %all-gather.34.cloned.1.call-update) | async-done | bytes 8388624 | tf_op jit(solution)/shard_map/all_gather | solution.py:474
  936.9 11.1 fusion.118
  953.5 32.9 %all-gather.36.cloned.1.call-done = bf16[1024,1024]{1,0:T(8,128)(2,1)} async-done(((bf16[128,1024]{1,0:T(8,128)(2,1)}), bf16[1024,1024]{1,0:T(8,128)(2,1)}) %all-gather.36.cloned.1.call-update) | async-done | bytes 2097168 | tf_op jit(solution)/shard_map/all_gather | solution.py:462
  986.5 4.1 multiply_reduce_fusion.8
  1000.7 10.9 fusion.2
  1011.6 9.6 multiply_reduce_fusion.5
  1024.4 4.5 multiply_reduce_fusion.2
  1046.1 4.7 multiply_reduce_fusion.1
  1074.3 28.7 %all_to_all.66 = bf16[2,256,1024]{1,0,2:T(2,128)(2,1)S(1)} all-to-all(bf16[2,256,1024]{1,0,2:T(2,128)(2,1)S(1)} %copy.57), channel_id=1, replica_groups=mesh['batch'=8,'seq'=4] {'seq'}, dimensions={2} | all-to-all | bytes 2097152 | tf_op jit(solution)/shard_map/all_to_all | solution.py:612
  1104.2 34.4 %attend_backward.1 = (bf16[3,2,1024,256]{3,2,1,0:T(8,128)(2,1)}, bf16[2048,256]{1,0:T(8,128)(2,1)S(1)}, f32[2,256]{1,0:T(2,128)S(1)}) custom-call(bf16[2,2,1024,1024]{3,2,1,0:T(8,128)(2,1)} %get-tuple-element.24.p_ref, bf16[3,2,1024,256]{3,2,1,0:T(8,128)(2,1)} %bitcast.196, bf16[3,2,1024,256]{3,2,1,0:T(8,128)(2,1)} %bitcast.197, ...), custom_call_target="tpu_custom_call" | custom-call | flops 8321499136 | bytes 16777216 | tf_op jit(solution)/shard_map/attend_backward/pallas_call | solution.py:135
  1141.8 5.1 copy.60
  1146.9 50.7 %all_to_all.67 = bf16[3,2,1024,256]{3,1,0,2:T(2,128)(2,1)S(1)} all-to-all(bf16[3,2,1024,256]{3,1,0,2:T(2,128)(2,1)S(1)} %copy.60), channel_id=1, replica_groups=mesh['batch'=8,'seq'=4] {'seq'}, dimensions={2} | all-to-all | bytes 6291456 | tf_op jit(solution)/shard_map/all_to_all | solution.py:623
  1214.0 7.0 convolution_convert_fusion.4
  1222.8 11.2 convolution_convert_fusion
  1235.6 9.3 convolution_convert_fusion.1
  1256.7 7.0 convolution_convert_fusion.2
  1264.0 11.3 fusion.5
  1277.3 6.9 convolution_convert_fusion.3
  1288.5 9.1 fusion.13
  1305.6 46.0 %reduce-scatter.69.cloned.1.call-done = bf16[1024,512]{1,0:T(8,128)(2,1)} async-done(((bf16[1024,2048]{1,0:T(8,128)(2,1)}), bf16[1024,512]{1,0:T(8,128)(2,1)}) %reduce-scatter.69.cloned.1.call-update) | async-done | bytes 1048592 | tf_op jit(solution)/shard_map/reduce_scatter | solution.py:336
  1351.6 74.5 %reduce-scatter.81.cloned.1.call-done = bf16[4096,256]{1,0:T(8,128)(2,1)} async-done(((bf16[4096,1024]{1,0:T(8,128)(2,1)}), bf16[4096,256]{1,0:T(8,128)(2,1)}) %reduce-scatter.81.cloned.1.call-update) | async-done | bytes 2097168 | tf_op jit(solution)/shard_map/reduce_scatter | solution.py:345
  1426.1 74.1 %reduce-scatter.77.cloned.1.call-done = bf16[1024,1024]{1,0:T(8,128)(2,1)} async-done(((bf16[1024,4096]{1,0:T(8,128)(2,1)}), bf16[1024,1024]{1,0:T(8,128)(2,1)}) %reduce-scatter.77.cloned.1.call-update) | async-done | bytes 2097168 | tf_op jit(solution)/shard_map/reduce_scatter | solution.py:342
  1500.3 74.5 %reduce-scatter.45.cloned.1.call-done = bf16[4096,256]{1,0:T(8,128)(2,1)} async-done(((bf16[4096,1024]{1,0:T(8,128)(2,1)}), bf16[4096,256]{1,0:T(8,128)(2,1)}) %reduce-scatter.45.cloned.1.call-update) | async-done | bytes 2097168 | tf_op jit(solution)/shard_map/reduce_scatter | solution.py:318
  1575.0 73.9 %reduce-scatter.41.cloned.1.call-done = bf16[1024,1024]{1,0:T(8,128)(2,1)} async-done(((bf16[1024,4096]{1,0:T(8,128)(2,1)}), bf16[1024,1024]{1,0:T(8,128)(2,1)}) %reduce-scatter.41.cloned.1.call-update) | async-done | bytes 2097168 | tf_op jit(solution)/shard_map/reduce_scatter | solution.py:315
  1654.5 59.8 %reduce-scatter.89.cloned.1.call-done = bf16[128,5]{1,0:T(8,128)(2,1)} async-done(((bf16[1024,5]{1,0:T(8,128)(2,1)}), bf16[128,5]{1,0:T(8,128)(2,1)}) %reduce-scatter.89.cloned.1.call-update) | async-done | bytes 1296
  1720.0 58.8 %reduce-scatter.87.cloned.1.call-done = bf16[128,14]{1,0:T(8,128)(2,1)} async-done(((bf16[1024,14]{1,0:T(8,128)(2,1)}), bf16[128,14]{1,0:T(8,128)(2,1)}) %reduce-scatter.87.cloned.1.call-update) | async-done | bytes 3600
  1779.7 5.8 all-reduce.2
  1786.6 57.4 %reduce-scatter.85.cloned.1.call-done = bf16[128,256]{1,0:T(8,128)(2,1)} async-done(((bf16[1024,256]{1,0:T(8,128)(2,1)}), bf16[128,256]{1,0:T(8,128)(2,1)}) %reduce-scatter.85.cloned.1.call-update) | async-done | bytes 65552
  1845.8 62.5 %reduce-scatter.39.cloned.1.call-done = bf16[128,256]{1,0:T(8,128)(2,1)} async-done(((bf16[1024,256]{1,0:T(8,128)(2,1)}), bf16[128,256]{1,0:T(8,128)(2,1)}) %reduce-scatter.39.cloned.1.call-update) | async-done | bytes 65552 | tf_op jit(solution)/shard_map/reduce_scatter | solution.py:373
  1909.8 63.2 %reduce-scatter.75.cloned.1.call-done = bf16[128,256]{1,0:T(8,128)(2,1)} async-done(((bf16[1024,256]{1,0:T(8,128)(2,1)}), bf16[128,256]{1,0:T(8,128)(2,1)}) %reduce-scatter.75.cloned.1.call-update) | async-done | bytes 65552 | tf_op jit(solution)/shard_map/reduce_scatter | solution.py:400
  1974.5 62.8 %reduce-scatter.67.cloned.1.call-done = bf16[128,256]{1,0:T(8,128)(2,1)} async-done(((bf16[1024,256]{1,0:T(8,128)(2,1)}), bf16[128,256]{1,0:T(8,128)(2,1)}) %reduce-scatter.67.cloned.1.call-update) | async-done | bytes 65552 | tf_op jit(solution)/shard_map/reduce_scatter | solution.py:394
  2038.7 63.0 %reduce-scatter.63.cloned.1.call-done = bf16[128,256]{1,0:T(8,128)(2,1)} async-done(((bf16[1024,256]{1,0:T(8,128)(2,1)}), bf16[128,256]{1,0:T(8,128)(2,1)}) %reduce-scatter.63.cloned.1.call-update) | async-done | bytes 65552 | tf_op jit(solution)/shard_map/reduce_scatter | solution.py:391
  2103.3 62.8 %reduce-scatter.51.cloned.1.call-done = bf16[128,256]{1,0:T(8,128)(2,1)} async-done(((bf16[1024,256]{1,0:T(8,128)(2,1)}), bf16[128,256]{1,0:T(8,128)(2,1)}) %reduce-scatter.51.cloned.1.call-update) | async-done | bytes 65552 | tf_op jit(solution)/shard_map/reduce_scatter | solution.py:382
  2167.6 63.2 %reduce-scatter.55.cloned.1.call-done = bf16[128,256]{1,0:T(8,128)(2,1)} async-done(((bf16[1024,256]{1,0:T(8,128)(2,1)}), bf16[128,256]{1,0:T(8,128)(2,1)}) %reduce-scatter.55.cloned.1.call-update) | async-done | bytes 65552 | tf_op jit(solution)/shard_map/reduce_scatter | solution.py:385
  2232.3 62.7 %reduce-scatter.59.cloned.1.call-done = bf16[128,256]{1,0:T(8,128)(2,1)} async-done(((bf16[1024,256]{1,0:T(8,128)(2,1)}), bf16[128,256]{1,0:T(8,128)(2,1)}) %reduce-scatter.59.cloned.1.call-update) | async-done | bytes 65552 | tf_op jit(solution)/shard_map/reduce_scatter | solution.py:388
  2296.5 64.5 %reduce-scatter.71.cloned.1.call-done = bf16[128,512]{1,0:T(8,128)(2,1)} async-done(((bf16[1024,512]{1,0:T(8,128)(2,1)}), bf16[128,512]{1,0:T(8,128)(2,1)}) %reduce-scatter.71.cloned.1.call-update) | async-done | bytes 131088 | tf_op jit(solution)/shard_map/reduce_scatter | solution.py:397
  2362.6 68.7 %reduce-scatter.83.cloned.1.call-done = bf16[512,256]{1,0:T(8,128)(2,1)} async-done(((bf16[4096,256]{1,0:T(8,128)(2,1)}), bf16[512,256]{1,0:T(8,128)(2,1)}) %reduce-scatter.83.cloned.1.call-update) | async-done | bytes 262160 | tf_op jit(solution)/shard_map/reduce_scatter | solution.py:406
  2433.1 68.3 %reduce-scatter.79.cloned.1.call-done = bf16[128,1024]{1,0:T(8,128)(2,1)} async-done(((bf16[1024,1024]{1,0:T(8,128)(2,1)}), bf16[128,1024]{1,0:T(8,128)(2,1)}) %reduce-scatter.79.cloned.1.call-update) | async-done | bytes 262160 | tf_op jit(solution)/shard_map/reduce_scatter | solution.py:403
  2503.2 68.5 %reduce-scatter.47.cloned.1.call-done = bf16[512,256]{1,0:T(8,128)(2,1)} async-done(((bf16[4096,256]{1,0:T(8,128)(2,1)}), bf16[512,256]{1,0:T(8,128)(2,1)}) %reduce-scatter.47.cloned.1.call-update) | async-done | bytes 262160 | tf_op jit(solution)/shard_map/reduce_scatter | solution.py:379
  2573.5 68.7 %reduce-scatter.43.cloned.1.call-done = bf16[128,1024]{1,0:T(8,128)(2,1)} async-done(((bf16[1024,1024]{1,0:T(8,128)(2,1)}), bf16[128,1024]{1,0:T(8,128)(2,1)}) %reduce-scatter.43.cloned.1.call-update) | async-done | bytes 262160 | tf_op jit(solution)/shard_map/reduce_scatter | solution.py:376
  (499 shorter events, 217.2 us)
Async XLA Ops:
  7.2 131.1 %all-gather.14.cloned.1.call-start = ((), (), s32[]{:S(2)}) async-start(), calls=%async_computation.32 | async-start | bytes 9437184 | tf_op jit(solution)/shard_map/all_gather | solution.py:463
  7.9 255.6 %all-gather.16.cloned.1.call-start = ((), (), s32[]{:S(2)}) async-start(), calls=%async_computation.33 | async-start | bytes 9437184 | tf_op jit(solution)/shard_map/all_gather | solution.py:464
  8.7 304.5 %all-gather.18.cloned.1.call-start = ((), (), s32[]{:S(2)}) async-start(), calls=%async_computation.34 | async-start | bytes 2359296 | tf_op jit(solution)/shard_map/all_gather | solution.py:465
  9.4 353.6 %all-gather.20.cloned.1.call-start = ((), (), s32[]{:S(2)}) async-start(), calls=%async_computation.35 | async-start | bytes 2359296 | tf_op jit(solution)/shard_map/all_gather | solution.py:466
  10.0 402.8 %all-gather.22.cloned.1.call-start = ((), (), s32[]{:S(2)}) async-start(), calls=%async_computation.36 | async-start | bytes 2359296 | tf_op jit(solution)/shard_map/all_gather | solution.py:467
  10.6 452.0 %all-gather.24.cloned.1.call-start = ((), (), s32[]{:S(2)}) async-start(), calls=%async_computation.37 | async-start | bytes 2359296 | tf_op jit(solution)/shard_map/all_gather | solution.py:468
  11.2 517.0 %all-gather.26.cloned.1.call-start = ((), (), s32[]{:S(2)}) async-start(), calls=%async_computation.38 | async-start | bytes 2359296 | tf_op jit(solution)/shard_map/all_gather | solution.py:469
  11.9 574.7 %all-gather.28.cloned.1.call-start = ((), (), s32[]{:S(2)}) async-start(), calls=%async_computation.39 | async-start | bytes 4718592 | tf_op jit(solution)/shard_map/all_gather | solution.py:470
  12.7 623.7 %all-gather.38.cloned.1.call-start = ((), (), s32[]{:S(2)}) async-start(), calls=%async_computation.44 | async-start | bytes 2359296 | tf_op jit(solution)/shard_map/all_gather | solution.py:461
  13.4 672.7 %all-gather.30.cloned.1.call-start = ((), (), s32[]{:S(2)}) async-start(), calls=%async_computation.40 | async-start | bytes 2359296 | tf_op jit(solution)/shard_map/all_gather | solution.py:472
  14.0 797.7 %all-gather.32.cloned.1.call-start = ((), (), s32[]{:S(2)}) async-start(), calls=%async_computation.41 | async-start | bytes 9437184 | tf_op jit(solution)/shard_map/all_gather | solution.py:473
  14.7 922.1 %all-gather.34.cloned.1.call-start = ((), (), s32[]{:S(2)}) async-start(), calls=%async_computation.42 | async-start | bytes 9437184 | tf_op jit(solution)/shard_map/all_gather | solution.py:474
  44.7 229.7 %copy-start.58 = (f32[1,1024]{1,0:T(1,128)}, f32[1,1024]{1,0:T(1,128)S(1)}, u32[]{:S(2)}) copy-start(f32[1,1024]{1,0:T(1,128)S(1)} %get-tuple-element.147) | copy-start | bytes 12292
  44.7 542.0 %copy-start.88 = (f32[1,1024]{1,0:T(1,128)}, f32[1,1024]{1,0:T(1,128)S(1)}, u32[]{:S(2)}) copy-start(f32[1,1024]{1,0:T(1,128)S(1)} %get-tuple-element.146) | copy-start | bytes 12292
  44.7 767.0 %copy-start.86 = (f32[1,1024]{1,0:T(1,128)}, f32[1,1024]{1,0:T(1,128)S(1)}, u32[]{:S(2)}) copy-start(f32[1,1024]{1,0:T(1,128)S(1)} %get-tuple-element.142) | copy-start | bytes 12292
  274.9 137.8 %copy-start.46 = (bf16[512,1024]{1,0:T(8,128)(2,1)}, bf16[512,1024]{1,0:T(8,128)(2,1)S(1)}, u32[]{:S(2)}) copy-start(bf16[512,1024]{1,0:T(8,128)(2,1)S(1)} %add_convert_fusion.6) | copy-start | bytes 3145732
  424.5 42.6 %all-to-all-start = ((bf16[3,2,256,1024]{2,1,0,3:T(2,128)(2,1)}), bf16[3,2,256,1024]{2,1,0,3:T(2,128)(2,1)S(1)}, u32[]{:S(2)}, u32[]{:S(2)}) async-start(bf16[3,2,256,1024]{2,1,0,3:T(2,128)(2,1)} %pad_maximum_fusion), calls=%async_computation | async-start | bytes 6291456 | tf_op jit(solution)/shard_map/all_to_all | solution.py:521
  497.2 29.8 %all-to-all-start.1 = ((bf16[2,1024,256]{2,0,1:T(2,128)(2,1)}), bf16[2,1024,256]{2,0,1:T(2,128)(2,1)S(1)}, u32[]{:S(2)}, u32[]{:S(2)}) async-start(bf16[2,1024,256]{2,0,1:T(2,128)(2,1)} %copy.55), calls=%async_computation.1 | async-start | bytes 2097152 | tf_op jit(solution)/shard_map/all_to_all | solution.py:527
  500.8 485.7 %all-gather.36.cloned.1.call-start = ((), (), s32[]{:S(2)}) async-start(), calls=%async_computation.43 | async-start | bytes 2359296 | tf_op jit(solution)/shard_map/all_gather | solution.py:462
  500.9 556.6 %copy-start.56 = (f32[1,2,2,128]{3,1,2,0:T(2,128)}, f32[1,2,2,128]{3,1,2,0:T(2,128)S(1)}, u32[]{:S(2)}) copy-start(f32[1,2,2,128]{3,1,2,0:T(2,128)S(1)} %copy.69) | copy-start | bytes 6148
  594.0 4.0 collective-permute-start
  595.3 4.8 collective-permute-start.1
  602.7 3.3 collective-permute-start.2
  606.0 3.7 collective-permute-start.3
  609.9 3.7 collective-permute-start.4
  610.5 688.3 %reduce-scatter.35.cloned.1.call-start = ((), (), s32[]{:S(2)}) async-start(), calls=%async_computation.45 | async-start | bytes 2621440 | tf_op jit(solution)/shard_map/reduce_scatter | solution.py:309
  613.6 26.0 collective-permute-start.5
  639.6 357.9 %copy-start.80 = (f32[512]{0:T(512)}, f32[512]{0:T(512)S(1)}, u32[]{:S(2)}) copy-start(f32[512]{0:T(512)S(1)} %get-tuple-element.175) | copy-start | bytes 6148
  639.7 4.7 collective-permute-start.6
  642.0 355.5 %copy-start.82 = (f32[512]{0:T(512)}, f32[512]{0:T(512)S(1)}, u32[]{:S(2)}) copy-start(f32[512]{0:T(512)S(1)} %fusion.47) | copy-start | bytes 6148
  994.9 306.0 %reduce-scatter.37.cloned.1.call-start = ((), (), s32[]{:S(2)}) async-start(), calls=%async_computation.46 | async-start | bytes 2621440 | tf_op jit(solution)/shard_map/reduce_scatter | solution.py:312
  1000.6 300.8 %reduce-scatter.73.cloned.1.call-start = ((), (), s32[]{:S(2)}) async-start(), calls=%async_computation.64 | async-start | bytes 2621440 | tf_op jit(solution)/shard_map/reduce_scatter | solution.py:339
  1029.0 1.2 collective-permute-start.7
  1030.2 3.7 collective-permute-start.8
  1034.0 3.7 collective-permute-start.9
  1037.7 3.7 collective-permute-start.10
  1041.3 4.7 collective-permute-start.11
  1046.0 256.1 %reduce-scatter.65.cloned.1.call-start = ((), (), s32[]{:S(2)}) async-start(), calls=%async_computation.60 | async-start | bytes 2621440 | tf_op jit(solution)/shard_map/reduce_scatter | solution.py:333
  1050.9 4.7 collective-permute-start.12
  1052.2 3.8 collective-permute-start.13
  1070.3 232.6 %reduce-scatter.61.cloned.1.call-start = ((), (), s32[]{:S(2)}) async-start(), calls=%async_computation.58 | async-start | bytes 2621440 | tf_op jit(solution)/shard_map/reduce_scatter | solution.py:330
  1141.6 161.9 %reduce-scatter.49.cloned.1.call-start = ((), (), s32[]{:S(2)}) async-start(), calls=%async_computation.52 | async-start | bytes 2621440 | tf_op jit(solution)/shard_map/reduce_scatter | solution.py:321
  1205.1 99.1 %reduce-scatter.53.cloned.1.call-start = ((), (), s32[]{:S(2)}) async-start(), calls=%async_computation.54 | async-start | bytes 2621440 | tf_op jit(solution)/shard_map/reduce_scatter | solution.py:324
  1209.1 95.9 %reduce-scatter.57.cloned.1.call-start = ((), (), s32[]{:S(2)}) async-start(), calls=%async_computation.56 | async-start | bytes 2621440 | tf_op jit(solution)/shard_map/reduce_scatter | solution.py:327
  1212.1 139.5 %reduce-scatter.69.cloned.1.call-start = ((), (), s32[]{:S(2)}) async-start(), calls=%async_computation.62 | async-start | bytes 5242880 | tf_op jit(solution)/shard_map/reduce_scatter | solution.py:336
  1221.0 205.1 %reduce-scatter.81.cloned.1.call-start = ((), (), s32[]{:S(2)}) async-start(), calls=%async_computation.68 | async-start | bytes 10485760 | tf_op jit(solution)/shard_map/reduce_scatter | solution.py:345
  1234.0 266.2 %reduce-scatter.77.cloned.1.call-start = ((), (), s32[]{:S(2)}) async-start(), calls=%async_computation.66 | async-start | bytes 10485760 | tf_op jit(solution)/shard_map/reduce_scatter | solution.py:342
  1244.9 329.9 %reduce-scatter.45.cloned.1.call-start = ((), (), s32[]{:S(2)}) async-start(), calls=%async_computation.50 | async-start | bytes 10485760 | tf_op jit(solution)/shard_map/reduce_scatter | solution.py:318
  1263.7 385.2 %reduce-scatter.41.cloned.1.call-start = ((), (), s32[]{:S(2)}) async-start(), calls=%async_computation.48 | async-start | bytes 10485760 | tf_op jit(solution)/shard_map/reduce_scatter | solution.py:315
  1284.3 430.0 %reduce-scatter.89.cloned.1.call-start = ((), (), s32[]{:S(2)}) async-start(), calls=%async_computation.72 | async-start | bytes 294912
  1288.4 490.5 %reduce-scatter.87.cloned.1.call-start = ((), (), s32[]{:S(2)}) async-start(), calls=%async_computation.71 | async-start | bytes 294912
  1298.6 545.4 %reduce-scatter.85.cloned.1.call-start = ((), (), s32[]{:S(2)}) async-start(), calls=%async_computation.70 | async-start | bytes 589824
  1300.8 607.5 %reduce-scatter.39.cloned.1.call-start = ((), (), s32[]{:S(2)}) async-start(), calls=%async_computation.47 | async-start | bytes 589824 | tf_op jit(solution)/shard_map/reduce_scatter | solution.py:373
  1301.4 671.6 %reduce-scatter.75.cloned.1.call-start = ((), (), s32[]{:S(2)}) async-start(), calls=%async_computation.65 | async-start | bytes 589824 | tf_op jit(solution)/shard_map/reduce_scatter | solution.py:400
  1302.1 735.1 %reduce-scatter.67.cloned.1.call-start = ((), (), s32[]{:S(2)}) async-start(), calls=%async_computation.61 | async-start | bytes 589824 | tf_op jit(solution)/shard_map/reduce_scatter | solution.py:394
  1302.9 798.9 %reduce-scatter.63.cloned.1.call-start = ((), (), s32[]{:S(2)}) async-start(), calls=%async_computation.59 | async-start | bytes 589824 | tf_op jit(solution)/shard_map/reduce_scatter | solution.py:391
  1303.4 862.7 %reduce-scatter.51.cloned.1.call-start = ((), (), s32[]{:S(2)}) async-start(), calls=%async_computation.53 | async-start | bytes 589824 | tf_op jit(solution)/shard_map/reduce_scatter | solution.py:382
  1304.2 926.6 %reduce-scatter.55.cloned.1.call-start = ((), (), s32[]{:S(2)}) async-start(), calls=%async_computation.55 | async-start | bytes 589824 | tf_op jit(solution)/shard_map/reduce_scatter | solution.py:385
  1304.9 990.1 %reduce-scatter.59.cloned.1.call-start = ((), (), s32[]{:S(2)}) async-start(), calls=%async_computation.57 | async-start | bytes 589824 | tf_op jit(solution)/shard_map/reduce_scatter | solution.py:388
  1305.5 1055.5 %reduce-scatter.71.cloned.1.call-start = ((), (), s32[]{:S(2)}) async-start(), calls=%async_computation.63 | async-start | bytes 1179648 | tf_op jit(solution)/shard_map/reduce_scatter | solution.py:397
  1351.5 1079.8 %reduce-scatter.83.cloned.1.call-start = ((), (), s32[]{:S(2)}) async-start(), calls=%async_computation.69 | async-start | bytes 2359296 | tf_op jit(solution)/shard_map/reduce_scatter | solution.py:406
  1426.1 1075.4 %reduce-scatter.79.cloned.1.call-start = ((), (), s32[]{:S(2)}) async-start(), calls=%async_computation.67 | async-start | bytes 2359296 | tf_op jit(solution)/shard_map/reduce_scatter | solution.py:403
  1500.2 1071.5 %reduce-scatter.47.cloned.1.call-start = ((), (), s32[]{:S(2)}) async-start(), calls=%async_computation.51 | async-start | bytes 2359296 | tf_op jit(solution)/shard_map/reduce_scatter | solution.py:379
  1574.8 1067.4 %reduce-scatter.43.cloned.1.call-start = ((), (), s32[]{:S(2)}) async-start(), calls=%async_computation.49 | async-start | bytes 2359296 | tf_op jit(solution)/shard_map/reduce_scatter | solution.py:376
  (100 other events, 1018.0 us)
Sparse Core Ops, SparseCore 0:
  10.1 128.0 all-gather.13
  140.4 123.1 all-gather.15
  265.7 47.4 all-gather.17
  315.2 47.7 all-gather.19
  365.0 47.7 all-gather.21
  414.8 47.7 all-gather.23
  464.7 47.7 all-gather.25
  514.6 71.9 all-gather.27
  588.8 47.5 all-gather.37
  638.3 47.7 all-gather.29
  688.3 123.4 all-gather.31
  813.7 123.1 all-gather.33
  939.0 47.4 all-gather.35
  995.0 29.8 reduce-scatter.34
  1027.5 31.5 reduce-scatter.36
  1061.4 41.3 reduce-scatter.72
  1105.4 32.4 reduce-scatter.64
  1141.7 42.4 reduce-scatter.60
  1205.3 31.1 reduce-scatter.48
  1238.8 31.4 reduce-scatter.52
  1273.0 31.3 reduce-scatter.56
  1307.0 44.4 reduce-scatter.68
  1354.3 71.7 reduce-scatter.80
  1428.5 71.6 reduce-scatter.76
  1503.0 71.7 reduce-scatter.44
  1577.2 71.6 reduce-scatter.40
  1653.0 61.2 reduce-scatter.88
  1718.6 60.2 reduce-scatter.86
  1783.1 60.8 reduce-scatter.84
  1847.3 60.9 reduce-scatter.38
  1912.0 60.9 reduce-scatter.74
  1976.3 60.8 reduce-scatter.66
  2040.8 60.9 reduce-scatter.62
  2105.1 60.9 reduce-scatter.50
  2169.8 60.9 reduce-scatter.54
  2234.0 60.9 reduce-scatter.58
  2298.6 62.2 reduce-scatter.70
  2364.5 66.7 reduce-scatter.82
  2434.7 66.6 reduce-scatter.78
  2505.0 66.7 reduce-scatter.46
  2575.3 66.8 reduce-scatter.42

commit v2 on v1

--- a/solution.py
+++ b/solution.py
@@ -182,6 +182,263 @@
     return value
 
 
+def line_factors(line):
+    places = [(*device.coords, device.core_on_chip) for device in line]
+    moving = [first != second for first, second in zip(places[0], places[1])].index(True)
+    inner = len({place[moving] for place in places})
+    return len(places) // inner, inner
+
+
+class Grid:
+    def __init__(self, mesh):
+        devices = mesh.devices
+        self.a, self.b = line_factors(list(devices[:, 0]))
+        self.y, self.c = line_factors(list(devices[0, :]))
+        self.size = {"a": self.a, "b": self.b, "y": self.y, "c": self.c}
+
+    def places(self):
+        batch, seq = lax.axis_index("batch"), lax.axis_index("seq")
+        return jnp.stack([batch // self.b, batch % self.b, seq // self.c, seq % self.c]).astype(jnp.int32)
+
+    def shift(self, value, axis, step):
+        name = "batch" if axis in "ab" else "seq"
+        outer, inner = (self.a, self.b) if axis in "ab" else (self.y, self.c)
+        pairs = []
+        for i in range(outer):
+            for j in range(inner):
+                if axis in "ay":
+                    pairs.append((i * inner + j, (i + step) % outer * inner + j))
+                else:
+                    pairs.append((i * inner + j, i * inner + (j + step) % inner))
+        return lax.ppermute(value, name, pairs)
+
+
+def after(value, *tokens):
+    return lax.optimization_barrier((value, *tokens))[0]
+
+
+def spread(grid, value, axis):
+    parts = [value] + [grid.shift(value, axis, k) for k in range(1, grid.size[axis])]
+    return parts
+
+
+def pieces(weights, place, count, width):
+    rows = []
+    for weight in weights:
+        wide = weight.shape[1] // count
+        piece = lax.dynamic_slice_in_dim(weight, place * wide, wide, 1)
+        rows += [piece[:, i : i + width] for i in range(0, wide, width)]
+    return jnp.concatenate(rows, axis=0)
+
+
+def _assemble_body(place_ref, mine_ref, theirs_ref, *outs, grid, plan, split):
+    y, c = place_ref[2], place_ref[3]
+    for out, (row, height, blocks, width) in zip(outs, plan):
+        for step in range(grid.y):
+            side = lax.rem(y - step + grid.y, grid.y) if split else step
+            for other, source in enumerate((mine_ref, theirs_ref)):
+                column = side * grid.c + lax.rem(c + other, grid.c)
+                for block in range(blocks):
+                    place = pl.multiple_of((column * blocks + block) * width, width)
+                    out[:, pl.ds(place, width)] = source[step, 0, pl.ds(row + block * height, height), :]
+
+
+def assemble(grid, places, mine, theirs, shapes, width, split, name):
+    plan, row = [], 0
+    columns = grid.y * grid.c
+    batches = grid.a * grid.b
+    for height, wide in shapes:
+        blocks = wide // (columns * width)
+        rows = height // batches
+        plan.append((row, rows, blocks, width))
+        row += rows * blocks
+
+    def slot(i, p):
+        step_a = lax.rem(p[0] - lax.div(i, grid.b) + grid.a, grid.a)
+        step_b = lax.rem(p[1] - lax.rem(i, grid.b) + grid.b, grid.b)
+        return (0, step_b * grid.a + step_a, 0, 0)
+
+    piece = pl.BlockSpec((grid.y, 1, row, width), slot)
+    return pl.pallas_call(
+        partial(_assemble_body, grid=grid, plan=plan, split=split),
+        grid_spec=pltpu.PrefetchScalarGridSpec(
+            num_scalar_prefetch=1,
+            grid=(batches,),
+            in_specs=[piece, piece],
+            out_specs=[pl.BlockSpec((h // batches, w), lambda i, p: (i, 0)) for h, w in shapes],
+        ),
+        out_shape=[jax.ShapeDtypeStruct(shape, BF16) for shape in shapes],
+        compiler_params=pltpu.CompilerParams(vmem_limit_bytes=48 << 20),
+        cost_estimate=pl.CostEstimate(flops=0, transcendentals=0, bytes_accessed=4 * sum(h * w for h, w in shapes)),
+        name=name,
+    )(places, mine, theirs)
+
+
+def gather_weights(grid, places, weights, width, split, name, token=None):
+    seq = lax.axis_index("seq")
+    columns = grid.y * grid.c
+    if split:
+        value = pieces(weights, seq, columns, width)[None]
+    else:
+        core = lax.rem(seq, grid.c)
+        value = jnp.stack([pieces(weights, i * grid.c + core, columns, width) for i in range(grid.y)])
+    if token is not None:
+        value = after(value, token)
+    first = spread(grid, value, "a")
+    token = first[-1]
+    rows = value.shape[1]
+    value = jnp.stack(first, axis=1)
+    value = jnp.concatenate([v[:, None] for v in spread(grid, value, "b")], axis=1)
+    if split:
+        value = jnp.concatenate(spread(grid, value, "y"), axis=0)
+    mine = value.reshape(grid.y, grid.b * grid.a, rows, width)
+    theirs = grid.shift(mine, "c", 1)
+    shapes = [(w.shape[0] * grid.a * grid.b, w.shape[1]) for w in weights]
+    return assemble(grid, places, mine, theirs, shapes, width, split, name), token
+
+
+def _weight_grad_body(place_ref, *refs, grid, height, first, have_sum, aliased, split, blocks):
+    left_ref, right_ref = refs[:2]
+    refs = refs[2:]
+    sum_ref = None
+    if have_sum:
+        sum_ref, refs = refs[0], refs[1:]
+    refs = refs[aliased:]
+    outs, turned, product = refs[:-2], refs[-2], refs[-1]
+    a, b = place_ref[0], place_ref[1]
+    side, block = pl.program_id(0), pl.program_id(1)
+
+    @pl.when((side == 0) & (block == 0))
+    def _():
+        turned[...] = left_ref[...].T
+
+    product[...] = jnp.dot(turned[...], right_ref[...], preferred_element_type=F32)
+    for step_b in range(grid.b):
+        for step_a in range(grid.a):
+            owner = lax.rem(a + step_a, grid.a) * grid.b + lax.rem(b + step_b, grid.b)
+            part = product[pl.ds(pl.multiple_of(owner * height, height), height), :]
+            if have_sum:
+                part = part + sum_ref[0, step_b, step_a].astype(F32)
+            part = part.astype(BF16)
+            if split == "b":
+                outs[step_b][0, step_a] = part
+            elif split == "y":
+                for k, out in enumerate(outs):
+
+                    @pl.when(side == k)
+                    def _(out=out, part=part):
+                        out[step_b, step_a] = part
+            else:
+                outs[0][0, step_b, step_a] = part
+
+
+def weight_grad(grid, places, left, right, width, core_step, total_rows, row, buffers, split, received=None, name="weight_grad", local=False, sub=None):
+    samples, depth = left.shape
+    height = depth // (grid.a * grid.b)
+    sides = 1 if local else grid.y
+    columns = 1 if local else grid.y * grid.c
+    blocks = right.shape[1] // (columns * width)
+    lo, count = (0, blocks) if sub is None else sub
+    first = row // height
+
+    def right_index(k, i, p):
+        if local:
+            return (0, 0)
+        side = lax.rem(p[2] + k, grid.y)
+        core = lax.rem(p[3] + core_step, grid.c)
+        return (0, (side * grid.c + core) * blocks + lo + i)
+
+    if split == "b":
+        shape = (sides, grid.a, total_rows, width)
+        specs = [pl.BlockSpec((1, grid.a, height, width), lambda k, i, p: (k, 0, first + i, 0))] * grid.b
+        number = grid.b
+    elif split == "y":
+        shape = (grid.b, grid.a, total_rows, width)
+
+        def index_of(which):
+            def index(k, i, p):
+                return (0, 0, first + jnp.where(k < which, 0, jnp.where(k > which, count - 1, i)), 0)
+
+            return index
+
+        specs = [pl.BlockSpec((grid.b, grid.a, height, width), index_of(k)) for k in range(sides)]
+        number = sides
+    else:
+        shape = (sides, grid.b, grid.a, total_rows, width)
+        specs = [pl.BlockSpec((1, grid.b, grid.a, height, width), lambda k, i, p: (k, 0, 0, first + i, 0))]
+        number = 1
+    in_specs = [
+        pl.BlockSpec((samples, depth), lambda k, i, p: (0, 0), pipeline_mode=pl.Buffered(1)),
+        pl.BlockSpec((samples, width), right_index),
+    ]
+    operands = [left, right]
+    if received is not None:
+        in_specs.append(pl.BlockSpec((1, grid.b, grid.a, height, width), lambda k, i, p: (k, 0, 0, first + i, 0)))
+        operands.append(received)
+    aliases = {}
+    if buffers is not None:
+        for i, buffer in enumerate(buffers):
+            aliases[1 + len(operands)] = i
+            in_specs.append(pl.BlockSpec(memory_space=pl.ANY))
+            operands.append(buffer)
+    body = partial(
+        _weight_grad_body, grid=grid, height=height, first=first, have_sum=received is not None,
+        aliased=0 if buffers is None else len(buffers), split=split, blocks=count,
+    )
+    work = sides * count * width
+    return pl.pallas_call(
+        body,
+        grid_spec=pltpu.PrefetchScalarGridSpec(
+            num_scalar_prefetch=1,
+            grid=(sides, count),
+            in_specs=in_specs,
+            out_specs=specs,
+            scratch_shapes=[pltpu.VMEM((depth, samples), BF16), pltpu.VMEM((depth, width), F32)],
+        ),
+        out_shape=[jax.ShapeDtypeStruct(shape, BF16)] * number,
+        input_output_aliases=aliases,
+        compiler_params=pltpu.CompilerParams(vmem_limit_bytes=48 << 20),
+        cost_estimate=pl.CostEstimate(flops=2 * samples * depth * work, transcendentals=0, bytes_accessed=2 * (samples * (depth + work) + depth * work)),
+        name=name,
+    )(places, *operands)
+
+
+def added(parts):
+    total = parts[0].astype(F32)
+    for part in parts[1:]:
+        total = total + part.astype(F32)
+    return total
+
+
+def reduce_group(grid, places, pairs, width, order, name, extra=None, sub=None):
+    heights = [left.shape[1] // (grid.a * grid.b) for left, _ in pairs]
+    columns = grid.y * grid.c
+    counts = [right.shape[1] // (columns * width) if sub is None else sub[1] for _, right in pairs]
+    total = sum(h * n for h, n in zip(heights, counts))
+
+    def products(core_step, split, received):
+        buffers, row = None, 0
+        for i, ((left, right), h, n) in enumerate(zip(pairs, heights, counts)):
+            buffers = weight_grad(
+                grid, places, left, right, width, core_step, total, row, buffers, split, received,
+                name=f"{name}_{i}_{core_step}", sub=sub,
+            )
+            row += h * n
+        return buffers
+
+    sent = products(1, None, None)[0]
+    received = grid.shift(sent, "c", 1)
+    near = products(0, order, received)
+    for stage, axis in enumerate(("y", "b") if order == "y" else ("b", "y")):
+        if extra is not None and axis == "b":
+            near = [jnp.concatenate([p, q], axis=-2) for p, q in zip(near, extra)]
+        parts = [near[0]] + [grid.shift(near[k], axis, k) for k in range(1, grid.size[axis])]
+        following = grid.a if stage == 1 else grid.size["b" if axis == "y" else "y"]
+        near = [added([p[k] for p in parts]).astype(BF16) for k in range(following)]
+    parts = [near[0]] + [grid.shift(near[k], "a", k) for k in range(1, grid.a)]
+    return added(parts)
+
+
 def layer_norm(values, scale_row, shift_row):
     center = values - jnp.mean(values, axis=-1, keepdims=True)
     spread = jnp.mean(center * center, axis=-1, keepdims=True)
@@ -281,142 +538,19 @@
     return value
 
 
-def sum_small_seq(smalls):
-    small_sums = (
-        lax.psum(smalls[0].astype(jnp.bfloat16), "seq").astype(jnp.float32),
-        lax.psum(smalls[1].astype(jnp.bfloat16), "seq").astype(jnp.float32),
-    )
-    return tuple(small_sums)
-
-
-def sum_over_seq(matrices, smalls):
-    (
-        grad_one,
-        grad_two,
-        grad_three,
-        grad_four,
-        grad_five,
-        grad_six,
-        grad_seven,
-        grad_eight,
-        grad_nine,
-        grad_ten,
-        grad_eleven,
-        grad_twelve,
-        grad_thirteen,
-    ) = matrices
-    reduced = (
-        lax.psum_scatter(
-            grad_one.astype(jnp.bfloat16), "seq", scatter_dimension=1, tiled=True
-        ).astype(jnp.float32),
-        lax.psum_scatter(
-            grad_two.astype(jnp.bfloat16), "seq", scatter_dimension=1, tiled=True
-        ).astype(jnp.float32),
-        lax.psum_scatter(
-            grad_three.astype(jnp.bfloat16), "seq", scatter_dimension=1, tiled=True
-        ).astype(jnp.float32),
-        lax.psum_scatter(
-            grad_four.astype(jnp.bfloat16), "seq", scatter_dimension=1, tiled=True
-        ).astype(jnp.float32),
-        lax.psum_scatter(
-            grad_five.astype(jnp.bfloat16), "seq", scatter_dimension=1, tiled=True
-        ).astype(jnp.float32),
-        lax.psum_scatter(
-            grad_six.astype(jnp.bfloat16), "seq", scatter_dimension=1, tiled=True
-        ).astype(jnp.float32),
-        lax.psum_scatter(
-            grad_seven.astype(jnp.bfloat16), "seq", scatter_dimension=1, tiled=True
-        ).astype(jnp.float32),
-        lax.psum_scatter(
-            grad_eight.astype(jnp.bfloat16), "seq", scatter_dimension=1, tiled=True
-        ).astype(jnp.float32),
-        lax.psum_scatter(
-            grad_nine.astype(jnp.bfloat16), "seq", scatter_dimension=1, tiled=True
-        ).astype(jnp.float32),
-        lax.psum_scatter(
-            grad_ten.astype(jnp.bfloat16), "seq", scatter_dimension=1, tiled=True
-        ).astype(jnp.float32),
-        lax.psum_scatter(
-            grad_eleven.astype(jnp.bfloat16), "seq", scatter_dimension=1, tiled=True
-        ).astype(jnp.float32),
-        lax.psum_scatter(
-            grad_twelve.astype(jnp.bfloat16), "seq", scatter_dimension=1, tiled=True
-        ).astype(jnp.float32),
-        lax.psum_scatter(
-            grad_thirteen.astype(jnp.bfloat16), "seq", scatter_dimension=1, tiled=True
-        ).astype(jnp.float32),
-    )
-    return (tuple(reduced), sum_small_seq(smalls))
-
-
-def sum_over_batch(matrices, smalls):
-    (
-        grad_one,
-        grad_two,
-        grad_three,
-        grad_four,
-        grad_five,
-        grad_six,
-        grad_seven,
-        grad_eight,
-        grad_nine,
-        grad_ten,
-        grad_eleven,
-        grad_twelve,
-        grad_thirteen,
-    ) = matrices
-    small_one, small_two = smalls
-    reduced = (
-        lax.psum_scatter(
-            grad_one.astype(jnp.bfloat16), "batch", scatter_dimension=0, tiled=True
-        ).astype(jnp.float32),
-        lax.psum_scatter(
-            grad_two.astype(jnp.bfloat16), "batch", scatter_dimension=0, tiled=True
-        ).astype(jnp.float32),
-        lax.psum_scatter(
-            grad_three.astype(jnp.bfloat16), "batch", scatter_dimension=0, tiled=True
-        ).astype(jnp.float32),
-        lax.psum_scatter(
-            grad_four.astype(jnp.bfloat16), "batch", scatter_dimension=0, tiled=True
-        ).astype(jnp.float32),
-        lax.psum_scatter(
-            grad_five.astype(jnp.bfloat16), "batch", scatter_dimension=0, tiled=True
-        ).astype(jnp.float32),
-        lax.psum_scatter(
-            grad_six.astype(jnp.bfloat16), "batch", scatter_dimension=0, tiled=True
-        ).astype(jnp.float32),
-        lax.psum_scatter(
-            grad_seven.astype(jnp.bfloat16), "batch", scatter_dimension=0, tiled=True
-        ).astype(jnp.float32),
-        lax.psum_scatter(
-            grad_eight.astype(jnp.bfloat16), "batch", scatter_dimension=0, tiled=True
-        ).astype(jnp.float32),
-        lax.psum_scatter(
-            grad_nine.astype(jnp.bfloat16), "batch", scatter_dimension=0, tiled=True
-        ).astype(jnp.float32),
-        lax.psum_scatter(
-            grad_ten.astype(jnp.bfloat16), "batch", scatter_dimension=0, tiled=True
-        ).astype(jnp.float32),
-        lax.psum_scatter(
-            grad_eleven.astype(jnp.bfloat16), "batch", scatter_dimension=0, tiled=True
-        ).astype(jnp.float32),
-        lax.psum_scatter(
-            grad_twelve.astype(jnp.bfloat16), "batch", scatter_dimension=0, tiled=True
-        ).astype(jnp.float32),
-        lax.psum_scatter(
-            grad_thirteen.astype(jnp.bfloat16), "batch", scatter_dimension=0, tiled=True
-        ).astype(jnp.float32),
-        lax.psum_scatter(
-            small_one.astype(jnp.bfloat16), "batch", scatter_dimension=1, tiled=True
-        ).astype(jnp.float32),
-        lax.psum_scatter(
-            small_two.astype(jnp.bfloat16), "batch", scatter_dimension=1, tiled=True
-        ).astype(jnp.float32),
-    )
-    return (tuple(reduced[:13]), tuple(reduced[13:]))
+def gather_small(grid, places, shard):
+    value = jnp.stack(spread(grid, shard, "a"))
+    value = jnp.concatenate(spread(grid, value[None], "b"))
+    value = value.reshape(grid.b * grid.a, *shard.shape)
+    owner = jnp.arange(grid.a * grid.b, dtype=jnp.int32)
+    step_a = (places[0] - owner // grid.b) % grid.a
+    step_b = (places[1] - owner % grid.b) % grid.b
+    value = jnp.take(value, step_b * grid.a + step_a, axis=0)
+    return value.transpose(1, 0, 2).reshape(shard.shape[0], -1)
 
 
 def per_device(
+    grid,
     acoustic_sequence,
     utterance_durations,
     chosen_entry_number,
@@ -440,38 +574,48 @@
     result_adjoint,
     discrete_label_adjoint,
 ):
-    (
-        vectors_all,
-        quant_all,
-        codebook_all,
-        macaron_in_all,
-        macaron_out_all,
-        query_all,
-        key_all,
-        value_all,
-        pos_all,
-        out_all,
-        conv_in_all,
-        depth_all,
-        conv_out_all,
-        closing_in_all,
-        closing_out_all,
-    ) = (
-        lax.all_gather(normalizer_affine_rows, "batch", axis=1, tiled=True),
-        lax.all_gather(discretizer_score_projection, "batch", axis=0, tiled=True),
-        lax.all_gather(lexicon_vectors, "batch", axis=0, tiled=True),
-        lax.all_gather(opening_dense_entry_projection, "batch", axis=0, tiled=True),
-        lax.all_gather(opening_dense_exit_projection, "batch", axis=0, tiled=True),
-        lax.all_gather(request_projection, "batch", axis=0, tiled=True),
-        lax.all_gather(lookup_projection, "batch", axis=0, tiled=True),
-        lax.all_gather(content_projection_kernel, "batch", axis=0, tiled=True),
-        lax.all_gather(relative_offset_projection, "batch", axis=0, tiled=True),
-        lax.all_gather(mixing_exit_projection, "batch", axis=0, tiled=True),
-        lax.all_gather(unit_kernel_before_gating, "batch", axis=0, tiled=True),
-        lax.all_gather(channelwise_filter_coefficients, "batch", axis=1, tiled=True),
-        lax.all_gather(unit_kernel_after_normalizing, "batch", axis=0, tiled=True),
-        lax.all_gather(closing_dense_entry_projection, "batch", axis=0, tiled=True),
-        lax.all_gather(closing_dense_exit_projection, "batch", axis=0, tiled=True),
+    places = grid.places()
+    small_all = gather_small(
+        grid,
+        places,
+        jnp.concatenate([normalizer_affine_rows, channelwise_filter_coefficients], axis=0),
+    )
+    vector_rows = normalizer_affine_rows.shape[0]
+    vectors_all, depth_all = small_all[:vector_rows], small_all[vector_rows:]
+    piece_width = acoustic_sequence.shape[2] // (grid.y * grid.c)
+    gather = partial(gather_weights, grid, places)
+    (macaron_in_all,), token = gather(
+        [opening_dense_entry_projection], piece_width, True, "gather_opening_entry"
+    )
+    (macaron_out_all,), token = gather(
+        [opening_dense_exit_projection], piece_width, True, "gather_opening_exit", token
+    )
+    (query_all, key_all, value_all, pos_all), token = gather(
+        [request_projection, lookup_projection, content_projection_kernel, relative_offset_projection],
+        piece_width,
+        True,
+        "gather_attention",
+        token,
+    )
+    (out_all, conv_in_all, conv_out_all, quant_all, codebook_all), token = gather(
+        [
+            mixing_exit_projection,
+            unit_kernel_before_gating,
+            unit_kernel_after_normalizing,
+            discretizer_score_projection,
+            lexicon_vectors,
+        ],
+        piece_width,
+        True,
+        "gather_convolution",
+        token,
+    )
+    (closing_in_all, closing_out_all), token = gather(
+        [closing_dense_entry_projection, closing_dense_exit_projection],
+        piece_width,
+        False,
+        "gather_closing",
+        token,
     )
     groups, local_len, model_width = acoustic_sequence.shape
     seq_count = lax.axis_size("seq")
@@ -631,7 +775,6 @@
     attn_norm_value, attn_norm_back = jax.vjp(layer_norm, first_mid, params_f[1], params_f[6])
     grad_from_attn, scale_one, shift_one = attn_norm_back(grad_attn_normed)
     grad_first = grad_second + grad_from_attn
-    grad_pos_columns = transpose_times(table_low, grad_position_low)
     content_full, position_full = lax.dynamic_update_slice_in_dim(
         jnp.zeros((2, model_width), jnp.float32), grad_biases, seq_place * local_width, 1
     )
@@ -675,48 +818,59 @@
             position_full,
         ]
     )
-    smalls = (vectors_grad, grad_depth)
+    small_sums = sum_everywhere(jnp.concatenate([vectors_grad, grad_depth], axis=0))
+    small_width = model_width // (grid.a * grid.b)
+    small_sums = lax.dynamic_slice_in_dim(
+        small_sums, lax.axis_index("batch") * small_width, small_width, 1
+    )
+    vectors_sum, depth_sum = small_sums[:vector_rows], small_sums[vector_rows:]
     mac_normed, mac_pre, mac_hidden = macaron_saved
     close_normed, close_pre, close_hidden = closing_saved
-    grad_pos_w = lax.dynamic_update_slice_in_dim(
-        jnp.zeros((model_width, model_width), jnp.float32),
-        grad_pos_columns,
-        seq_place * local_width,
-        1,
-    )
-    matrices = (
-        transpose_times(inputs_low, score_derivative_lowprecision),
-        transpose_times(one_hot, grad_codes) + transpose_times(soft_low, grad_codes),
-        transpose_times(mac_normed, mac_pre_low),
-        transpose_times(mac_hidden, mac_out_low),
-        transpose_times(attn_normed, grad_time[0]),
-        transpose_times(attn_normed, grad_time[1]),
-        transpose_times(attn_normed, grad_time[2]),
-        grad_pos_w,
-        transpose_times(attended_rows, grad_second_low),
-        transpose_times(conv_normed, grad_gated_low),
-        transpose_times(act_low, grad_third_low),
-        transpose_times(close_normed, close_pre_low),
-        transpose_times(close_hidden, close_out_low),
-    )
-    matrices, smalls = sum_over_seq(matrices, smalls)
-    matrices, smalls = sum_over_batch(matrices, smalls)
-    (
-        quant_sum,
-        codebook_sum,
-        macaron_in_sum,
-        macaron_out_sum,
-        query_sum,
-        key_sum,
-        value_sum,
-        pos_sum,
-        out_sum,
-        conv_in_sum,
-        conv_out_sum,
-        closing_in_sum,
-        closing_out_sum,
-    ) = matrices
-    vectors_sum, depth_sum = smalls
+    reduce = partial(reduce_group, grid, places)
+    height = model_width // (grid.a * grid.b)
+    closing_out_sum = reduce([(close_hidden, close_out_low)], piece_width, "y", "closing_exit")
+    closing_in_sum = reduce([(close_normed, close_pre_low)], piece_width, "b", "closing_entry")
+    chosen_soft = one_hot + soft_low
+    first_sums = reduce(
+        [
+            (inputs_low, score_derivative_lowprecision),
+            (chosen_soft, grad_codes),
+            (act_low, grad_third_low),
+        ],
+        piece_width,
+        "y",
+        "quantizer",
+    )
+    quant_sum, codebook_sum, conv_out_sum = (first_sums[i * height : (i + 1) * height] for i in range(3))
+    second_sums = reduce(
+        [(conv_normed, grad_gated_low), (attended_rows, grad_second_low)], piece_width, "b", "convolution"
+    )
+    conv_in_sum, out_sum = second_sums[: 2 * height], second_sums[2 * height :]
+    position_parts = weight_grad(
+        grid, places, table_low, grad_position_low, piece_width, 0, height, 0, None, "b",
+        name="position_grad", local=True,
+    )
+    third_sums = reduce(
+        [(attn_normed, grad_time[i]) for i in range(3)],
+        piece_width,
+        "y",
+        "attention",
+        extra=[part[0] for part in position_parts],
+    )
+    query_sum, key_sum, value_sum, pos_sum = (third_sums[i * height : (i + 1) * height] for i in range(4))
+    macaron_out_sum = reduce([(mac_hidden, mac_out_low)], piece_width, "b", "opening_exit")
+    macaron_in_sum = reduce([(mac_normed, mac_pre_low)], piece_width, "y", "opening_entry")
+
+    def side_by_side(blocks):
+        return jnp.concatenate(
+            [blocks[i : i + height] for i in range(0, blocks.shape[0], height)], axis=1
+        )
+
+    closing_in_sum, conv_in_sum, macaron_in_sum = (
+        side_by_side(closing_in_sum),
+        side_by_side(conv_in_sum),
+        side_by_side(macaron_in_sum),
+    )
     return (
         output,
         codes,
@@ -743,10 +897,6 @@
     return grad_attended.astype(jnp.bfloat16).reshape(groups, local_len, model_width)
 
 
-def flat_rows(blocks):
-    return blocks.reshape(blocks.shape[0] * blocks.shape[1], blocks.shape[2])
-
-
 def solution(mesh):
     placed = (
         P("batch", "seq", None),
@@ -773,7 +923,7 @@
         P("batch", "seq", None),
     )
     return jax.shard_map(
-        per_device,
+        partial(per_device, Grid(mesh)),
         mesh=mesh,
         in_specs=placed,
         out_specs=(

time: 2660 us -> 1130 us (0.42)
  waiting for transfers between devices: 2080 us -> 402 us
  Pallas kernels: 55.1 us -> 234 us
  blocking collectives: 140 us -> 0 us
  starting transfers between devices: 30.2 us -> 137 us
  matrix products: 205 us -> 119 us
  other arithmetic: 57.3 us -> 122 us
  local copies, waits for them, and re-layouts: 70.4 us -> 97.3 us
    reduce_scatter x25 -> x0, waiting for transfers between devices: 1120 us -> none  [the longest x1 74.5 us: sum_over_seq(): lax.psum_scatter(grad_thirteen.astype(jnp.bfloat16), 'seq', scatter_dimen...]
    all_gather x13 -> x0, waiting for transfers between devices: 746 us -> none  [the longest x1 120 us: per_device(): lax.all_gather(closing_dense_entry_projection, 'batch', axis=0, tiled=True)]
    ppermute x0 -> x75, waiting for transfers between devices: none -> 347 us  [shift(): return lax.ppermute(value, name, pairs)]
    unnamed x44 -> x0, waiting for transfers between devices: 188 us -> none
    pallas_call x0 -> x30, Pallas kernels: none -> 180 us  [the longest x25 127 us: weight_grad(): pl.pallas_call(body, grid_spec=pltpu.PrefetchScalarGridSpec(num_scalar_pr...]
    ppermute x0 -> x75, starting transfers between devices: none -> 93.2 us  [shift(): return lax.ppermute(value, name, pairs)]
    all_to_all x2 -> x0, blocking collectives: 79.4 us -> none  [the longest x1 50.7 us: per_device(): lax.all_to_all(grad_stack, 'seq', split_axis=2, concat_axis=3, tiled=True)]
    dot_general x14 -> x0, matrix products: 62.8 us -> none  [transpose_times(): lax.dot_general(left_side, right_side, (((0,), (0,)), ((), ())), preferre...]
  transfers between devices with their start and end apart: 57 -> 98, of which waited for: 42 -> 41; matrix products, arithmetic and copies ran while one was open for 11% -> 22% of each run, Pallas kernels for 2% -> 20%
where the time goes in v2:
time: 1130 us; the launch traced here: 1120 us
  waiting for transfers between devices  402 us (36%)
  Pallas kernels  234 us (21%)
  starting transfers between devices  137 us (12%)
  other arithmetic  122 us (11%)
  matrix products  119 us (11%)
  local copies, waits for them, and re-layouts  97.3 us (9%)
    ppermute x75, waiting for transfers between devices, shift(): return lax.ppermute(value, name, pairs)  347 us
    pallas_call x25, Pallas kernels, weight_grad(): pl.pallas_call(body, grid_spec=pltpu.PrefetchScalarGridSpec(num_scalar_pr...  127 us
    ppermute x75, starting transfers between devices, shift(): return lax.ppermute(value, name, pairs)  93.2 us
    dot_general x14, matrix products, matmul_rows(): return jnp.dot(left_side, right_side, preferred_element_type=jnp.float32)  62.1 us
    dot_general x12, matrix products, times_transpose(): lax.dot_general(left_side, right_side, (((1,), (1,)), ((), ())), preferre...  57.2 us
    pallas_call x5, Pallas kernels, assemble(): pl.pallas_call(partial(_assemble_body, grid=grid, plan=plan, split=split)...  52.5 us
    unnamed x292, local copies, waits for them, and re-layouts  38.6 us
    pallas_call x1, Pallas kernels, attend_backward(): pl.pallas_call(body, grid_spec=pltpu.PrefetchScalarGridSpec(num_scalar_pr...  34.2 us
  transfers between devices with their start and end apart: 98, of which 41 were waited for; matrix products, arithmetic and copies ran while one was open for 22% of the time, Pallas kernels for 20%

profile of v2, /device:TPU:0, one launch (start us, length us, event | category | flops | bytes accessed | tf_op | source)
XLA Modules:
  0.0 1116.4 jit_solution(17947605682636245535)
XLA Ops:
  1.8 5.1 collective-permute-start.6
  7.9 5.7 collective-permute-done.6
  13.6 15.6 %collective-permute-done.5 = bf16[1,512,256]{2,1,0:T(8,128)(2,1)S(1)} collective-permute-done((bf16[1,512,256]{2,1,0:T(8,128)(2,1)S(1)}, bf16[1,512,256]{2,1,0:T(8,128)(2,1)S(1)}, u32[]{:S(2)}, u32[]{:S(2)}) %collective-permute-start.5) | collective-permute-done | bytes 262176 | tf_op jit(solution)/shard_map/ppermute | solution.py:213
  36.7 17.9 %collective-permute-done.7 = bf16[1,4,512,256]{3,2,1,0:T(8,128)(2,1)S(1)} collective-permute-done((bf16[1,4,512,256]{3,2,1,0:T(8,128)(2,1)}, bf16[1,4,512,256]{3,2,1,0:T(8,128)(2,1)S(1)}, u32[]{:S(2)}, u32[]{:S(2)}) %collective-permute-start.7) | collective-permute-done | bytes 1048608 | tf_op jit(solution)/shard_map/ppermute | solution.py:213
  68.9 10.5 collective-permute-done.18
  79.4 6.4 collective-permute-start.23
  88.5 5.3 collective-permute-done.24
  93.8 18.7 %collective-permute-start.1 = (bf16[19,128]{1,0:T(8,128)(2,1)S(1)}, bf16[19,128]{1,0:T(8,128)(2,1)S(1)}, u32[]{:S(2)}, u32[]{:S(2)}) collective-permute-start(bf16[19,128]{1,0:T(8,128)(2,1)S(1)} %get-tuple-element.268), channel_id=1, source_target_pairs={{0,16},{4,20},{8,24},{12,28},{16,0},{20,4},{24,8},{28,12},{1,17},{... | collective-permute-start | bytes 14600 | tf_op jit(solution)/shard_map/ppermute | solution.py:213
  112.5 13.6 %collective-permute-done.23 = bf16[1,768,256]{2,1,0:T(8,128)(2,1)S(1)} collective-permute-done((bf16[1,768,256]{2,1,0:T(8,128)(2,1)}, bf16[1,768,256]{2,1,0:T(8,128)(2,1)S(1)}, u32[]{:S(2)}, u32[]{:S(2)}) %collective-permute-start.23) | collective-permute-done | bytes 393248 | tf_op jit(solution)/shard_map/ppermute | solution.py:213
  147.4 17.6 %collective-permute-done.25 = bf16[1,4,768,256]{3,2,1,0:T(8,128)(2,1)S(1)} collective-permute-done((bf16[1,4,768,256]{3,2,1,0:T(8,128)(2,1)S(1)}, bf16[1,4,768,256]{3,2,1,0:T(8,128)(2,1)S(1)}, u32[]{:S(2)}, u32[]{:S(2)}) %collective-permute-start.25) | collective-permute-done | bytes 1572896 | tf_op jit(solution)/shard_map/ppermute | solution.py:213
  168.2 12.1 %collective-permute-done.19 = bf16[1,4,512,256]{3,2,1,0:T(8,128)(2,1)} collective-permute-done((bf16[1,4,512,256]{3,2,1,0:T(8,128)(2,1)}, bf16[1,4,512,256]{3,2,1,0:T(8,128)(2,1)}, u32[]{:S(2)}, u32[]{:S(2)}) %collective-permute-start.19) | collective-permute-done | bytes 1048608 | tf_op jit(solution)/shard_map/ppermute | solution.py:213
  188.9 57.4 %collective-permute-done.36 = bf16[2,1024,256]{2,1,0:T(8,128)(2,1)} collective-permute-done((bf16[2,1024,256]{2,1,0:T(8,128)(2,1)}, bf16[2,1024,256]{2,1,0:T(8,128)(2,1)}, u32[]{:S(2)}, u32[]{:S(2)}) %collective-permute-start.36) | collective-permute-done | bytes 1048608 | tf_op jit(solution)/shard_map/ppermute | solution.py:213
  246.9 5.3 fusion.180
  253.2 33.1 %collective-permute-done.20 = bf16[1,2,4,512,256]{4,3,2,1,0:T(8,128)(2,1)} collective-permute-done((bf16[1,2,4,512,256]{4,3,2,1,0:T(8,128)(2,1)}, bf16[1,2,4,512,256]{4,3,2,1,0:T(8,128)(2,1)}, u32[]{:S(2)}, u32[]{:S(2)}) %collective-permute-start.20) | collective-permute-done | bytes 2097184 | tf_op jit(solution)/shard_map/ppermute | solution.py:213
  289.9 5.0 pad_maximum_fusion.1
  295.4 9.6 gather_opening_entry.1
  305.0 10.4 multiply_convert_fusion.1
  315.4 8.7 gather_opening_exit.1
  324.1 7.0 fusion.204
  332.5 8.5 gather_attention.1
  364.8 7.3 pad_maximum_fusion.6
  372.1 5.1 all-to-all-start
  378.8 7.5 pad_maximum_fusion
  386.4 7.4 copy.76
  399.9 14.3 %all-to-all-done = bf16[3,2,256,1024]{2,1,0,3:T(2,128)(2,1)} async-done(((bf16[3,2,256,1024]{2,1,0,3:T(2,128)(2,1)}), bf16[3,2,256,1024]{2,1,0,3:T(2,128)(2,1)}, u32[]{:S(2)}, u32[]{:S(2)}) %all-to-all-start) | async-done | bytes 3145760 | tf_op jit(solution)/shard_map/all_to_all | solution.py:665
  418.2 4.7 copy.73
  424.7 20.7 %attend_forward.1 = (bf16[2,1024,256]{2,1,0:T(8,128)(2,1)S(1)}, bf16[2,2,1024,1024]{3,2,1,0:T(8,128)(2,1)}) custom-call(s32[2]{0:T(128)S(1)} %copy-done.54, bf16[3,2,1024,256]{3,2,1,0:T(8,128)(2,1)S(1)} %bitcast.504, bf16[3,2,1024,256]{3,2,1,0:T(8,128)(2,1)S(1)} %bitcast.505, bf16[3,2,1024,256]{3,2,1,0:T(8,128)(2,1)S(1)} %bitcast.506, ...), custom_call_target="tpu_custom_call" | custom-call | flops 3489660928 | bytes 13631488 | tf_op jit(solution)/shard_map/attend_forward/pallas_call | solution.py:48
  452.5 12.9 %all-to-all-done.1 = bf16[2,1024,256]{2,0,1:T(2,128)(2,1)S(1)} async-done(((bf16[2,1024,256]{2,0,1:T(2,128)(2,1)}), bf16[2,1024,256]{2,0,1:T(2,128)(2,1)S(1)}, u32[]{:S(2)}, u32[]{:S(2)}) %all-to-all-start.1) | async-done | bytes 1048608 | tf_op jit(solution)/shard_map/all_to_all | solution.py:671
  466.5 11.1 gather_convolution.1
  517.5 14.6 %gather_closing.1 = (bf16[1024,4096]{1,0:T(8,128)(2,1)}, bf16[4096,1024]{1,0:T(8,128)(2,1)}) custom-call(s32[4]{0:T(128)S(1)} %pad_add_fusion.place_ref, bf16[2,8,1024,256]{3,2,1,0:T(8,128)(2,1)} %bitcast.512, bf16[2,8,1024,256]{3,2,1,0:T(8,128)(2,1)} %collective-permute-done.39.theirs_ref), custom_call_target="tpu_custom_call" | custom-call | bytes 33554432 | tf_op jit(solution)/shard_map/gather_closing/pallas_call | solution.py:262
  532.1 10.5 multiply_convert_fusion
  542.6 4.7 fusion.207
  552.6 11.3 %fusion.2.refs_1_ = bf16[512,4096]{1,0:T(8,128)(2,1)S(1)} fusion(f32[512,4096]{1,0:T(8,128)} %get-tuple-element.287, bf16[512,1024]{1,0:T(8,128)(2,1)S(1)} %multiply_convert_fusion.3.refs_1_, bf16[4096,1024]{1,0:T(8,128)(2,1)} %get-tuple-element.77), kind=kOutput, calls=%fused_computation.5 | convolution fusion | flops 4315938816 | bytes 22020096 | tf_op jit(solution)/shard_map/dot_general | solution.py:498
  564.9 9.4 multiply_reduce_fusion.5
  624.9 4.4 all-to-all-start.2
  650.9 34.2 %attend_backward.1 = (bf16[3,2,1024,256]{3,2,1,0:T(8,128)(2,1)}, bf16[2048,256]{1,0:T(8,128)(2,1)S(1)}, f32[2,256]{1,0:T(2,128)S(1)}) custom-call(bf16[2,2,1024,1024]{3,2,1,0:T(8,128)(2,1)} %get-tuple-element.80.p_ref, bf16[3,2,1024,256]{3,2,1,0:T(8,128)(2,1)} %bitcast.501, bf16[3,2,1024,256]{3,2,1,0:T(8,128)(2,1)} %bitcast.502, ...), custom_call_target="tpu_custom_call" | custom-call | flops 8321499136 | bytes 16777216 | tf_op jit(solution)/shard_map/attend_backward/pallas_call | solution.py:135
  686.1 6.8 copy.81
  692.9 4.9 all-to-all-start.3
  699.0 8.2 closing_exit_0_1.1
  707.7 8.8 closing_entry_0_1.1
  716.8 4.2 convolution_0_1.1.refs_2_
  733.7 4.4 quantizer_2_0.1
  741.1 4.3 copy.93
  757.0 5.8 convolution_0_0.1
  762.8 4.2 convolution_1_0.1
  771.4 11.7 %fusion.5.refs_1_ = bf16[512,4096]{1,0:T(8,128)(2,1)S(1)} fusion(f32[512,4096]{1,0:T(8,128)} %get-tuple-element.279, bf16[512,1024]{1,0:T(8,128)(2,1)S(1)} %get-tuple-element.141.refs_1_, bf16[4096,1024]{1,0:T(8,128)(2,1)} %gather_opening_exit.1), kind=kOutput, calls=%fused_computation.8 | convolution fusion | flops 4315938816 | bytes 22020096 | tf_op jit(solution)/shard_map/dot_general | solution.py:498
  783.2 6.3 fusion.13
  789.7 5.0 fusion.88
  799.2 8.8 opening_entry_0_1.1
  808.6 8.4 opening_exit_0_1.1
  844.3 13.1 %collective-permute-done.78 = bf16[4,384,256]{2,1,0:T(8,128)(2,1)} collective-permute-done((bf16[4,384,256]{2,1,0:T(8,128)(2,1)}, bf16[4,384,256]{2,1,0:T(8,128)(2,1)}, u32[]{:S(2)}, u32[]{:S(2)}) %collective-permute-start.78) | collective-permute-done | bytes 786464 | tf_op jit(solution)/shard_map/ppermute | solution.py:213
  858.7 9.8 closing_entry_0_0.1
  870.4 9.6 closing_exit_0_0.1
  892.3 24.4 %collective-permute-done.83 = bf16[2,4,512,256]{3,2,1,0:T(8,128)(2,1)} collective-permute-done((bf16[2,4,512,256]{3,2,1,0:T(8,128)(2,1)}, bf16[2,4,512,256]{3,2,1,0:T(8,128)(2,1)}, u32[]{:S(2)}, u32[]{:S(2)}) %collective-permute-start.83) | collective-permute-done | bytes 2097184 | tf_op jit(solution)/shard_map/ppermute | solution.py:213
  943.5 8.9 opening_entry_0_0.1
  952.8 8.2 opening_exit_0_0.1
  971.7 22.7 %collective-permute-done.71 = bf16[2,4,384,256]{3,2,1,0:T(8,128)(2,1)} collective-permute-done((bf16[2,4,384,256]{3,2,1,0:T(8,128)(2,1)S(1)}, bf16[2,4,384,256]{3,2,1,0:T(8,128)(2,1)}, u32[]{:S(2)}, u32[]{:S(2)}) %collective-permute-start.71) | collective-permute-done | bytes 1572896 | tf_op jit(solution)/shard_map/ppermute | solution.py:213
  1003.1 7.1 collective-permute-done.86
  1012.7 23.1 %collective-permute-done.59 = bf16[2,4,512,256]{3,2,1,0:T(8,128)(2,1)} collective-permute-done((bf16[2,4,512,256]{3,2,1,0:T(8,128)(2,1)S(1)}, bf16[2,4,512,256]{3,2,1,0:T(8,128)(2,1)}, u32[]{:S(2)}, u32[]{:S(2)}) %collective-permute-start.59) | collective-permute-done | bytes 2097184 | tf_op jit(solution)/shard_map/ppermute | solution.py:213
  1046.2 11.0 collective-permute-done.92
  1059.2 10.4 collective-permute-done.74
  1081.1 5.9 collective-permute-done.63
  1087.0 19.8 %collective-permute-done.62 = bf16[512,256]{1,0:T(8,128)(2,1)S(1)} collective-permute-done((bf16[512,256]{1,0:T(8,128)(2,1)S(1)}, bf16[512,256]{1,0:T(8,128)(2,1)S(1)}, u32[]{:S(2)}, u32[]{:S(2)}) %collective-permute-start.62) | collective-permute-done | bytes 262176 | tf_op jit(solution)/shard_map/ppermute | solution.py:213
  1107.8 7.5 collective-permute-done.68
  (658 shorter events, 385.7 us)
Async XLA Ops:
  6.9 22.3 %collective-permute-start.5 = (bf16[1,512,256]{2,1,0:T(8,128)(2,1)S(1)}, bf16[1,512,256]{2,1,0:T(8,128)(2,1)S(1)}, u32[]{:S(2)}, u32[]{:S(2)}) collective-permute-start(bf16[1,512,256]{2,1,0:T(8,128)(2,1)S(1)} %get-tuple-element.247), channel_id=1, source_target_pairs={{0,16},{4,20},{8,24},{12,28},{16,0},{20,4},{24,8},{28,12},{1,17},{... | collective-permute-start | bytes 786440 | tf_op jit(solution)/shard_map/ppermute | solution.py:213
  6.9 22.3 %collective-permute-start.4 = (bf16[1,512,256]{2,1,0:T(8,128)(2,1)S(1)}, bf16[1,512,256]{2,1,0:T(8,128)(2,1)S(1)}, u32[]{:S(2)}, u32[]{:S(2)}) collective-permute-start(bf16[1,512,256]{2,1,0:T(8,128)(2,1)S(1)} %get-tuple-element.247), channel_id=1, source_target_pairs={{0,8},{4,12},{8,16},{12,20},{16,24},{20,28},{24,0},{28,4},{1,9},{5... | collective-permute-start | bytes 786440 | tf_op jit(solution)/shard_map/ppermute | solution.py:213
  30.3 24.2 %collective-permute-start.7 = (bf16[1,4,512,256]{3,2,1,0:T(8,128)(2,1)}, bf16[1,4,512,256]{3,2,1,0:T(8,128)(2,1)S(1)}, u32[]{:S(2)}, u32[]{:S(2)}) collective-permute-start(bf16[1,4,512,256]{3,2,1,0:T(8,128)(2,1)} %get-tuple-element.223), channel_id=1, source_target_pairs={{0,4},{4,0},{8,12},{12,8},{16,20},{20,16},{24,28},{28,24},{1,5},{5... | collective-permute-start | bytes 3145736 | tf_op jit(solution)/shard_map/ppermute | solution.py:213
  36.6 25.8 %collective-permute-start.12 = (bf16[1,512,256]{2,1,0:T(8,128)(2,1)S(1)}, bf16[1,512,256]{2,1,0:T(8,128)(2,1)S(1)}, u32[]{:S(2)}, u32[]{:S(2)}) collective-permute-start(bf16[1,512,256]{2,1,0:T(8,128)(2,1)S(1)} %dynamic-slice_bitcast_fusion), channel_id=1, source_target_pairs={{0,24},{4,28},{8,0},{12,4},{16,8},{20,12},{24,16},{28,20},{1,25},{... | collective-permute-start | bytes 786440 | tf_op jit(solution)/shard_map/ppermute | solution.py:213
  56.3 76.4 %collective-permute-start.8 = (bf16[1,2,4,512,256]{4,3,2,1,0:T(8,128)(2,1)}, bf16[1,2,4,512,256]{4,3,2,1,0:T(8,128)(2,1)}, u32[]{:S(2)}, u32[]{:S(2)}) collective-permute-start(bf16[1,2,4,512,256]{4,3,2,1,0:T(8,128)(2,1)} %pad_maximum_fusion.8), channel_id=1, source_target_pairs={{0,2},{1,3},{2,0},{3,1},{4,6},{5,7},{6,4},{7,5},{8,10},{9,11},{10,... | collective-permute-start | bytes 6291464 | tf_op jit(solution)/shard_map/ppermute | solution.py:213
  59.3 26.5 %collective-permute-start.11 = (bf16[1,512,256]{2,1,0:T(8,128)(2,1)S(1)}, bf16[1,512,256]{2,1,0:T(8,128)(2,1)S(1)}, u32[]{:S(2)}, u32[]{:S(2)}) collective-permute-start(bf16[1,512,256]{2,1,0:T(8,128)(2,1)S(1)} %dynamic-slice_bitcast_fusion), channel_id=1, source_target_pairs={{0,16},{4,20},{8,24},{12,28},{16,0},{20,4},{24,8},{28,12},{1,17},{... | collective-permute-start | bytes 786440 | tf_op jit(solution)/shard_map/ppermute | solution.py:213
  62.4 16.9 %collective-permute-start.18 = (bf16[1,512,256]{2,1,0:T(8,128)(2,1)S(1)}, bf16[1,512,256]{2,1,0:T(8,128)(2,1)S(1)}, u32[]{:S(2)}, u32[]{:S(2)}) collective-permute-start(bf16[1,512,256]{2,1,0:T(8,128)(2,1)S(1)} %maximum_bitcast_fusion), channel_id=1, source_target_pairs={{0,24},{4,28},{8,0},{12,4},{16,8},{20,12},{24,16},{28,20},{1,25},{... | collective-permute-start | bytes 786440 | tf_op jit(solution)/shard_map/ppermute | solution.py:213
  64.3 21.5 %collective-permute-start.10 = (bf16[1,512,256]{2,1,0:T(8,128)(2,1)S(1)}, bf16[1,512,256]{2,1,0:T(8,128)(2,1)S(1)}, u32[]{:S(2)}, u32[]{:S(2)}) collective-permute-start(bf16[1,512,256]{2,1,0:T(8,128)(2,1)S(1)} %dynamic-slice_bitcast_fusion), channel_id=1, source_target_pairs={{0,8},{4,12},{8,16},{12,20},{16,24},{20,28},{24,0},{28,4},{1,9},{5... | collective-permute-start | bytes 786440 | tf_op jit(solution)/shard_map/ppermute | solution.py:213
  79.4 46.7 %collective-permute-start.23 = (bf16[1,768,256]{2,1,0:T(8,128)(2,1)}, bf16[1,768,256]{2,1,0:T(8,128)(2,1)S(1)}, u32[]{:S(2)}, u32[]{:S(2)}) collective-permute-start(bf16[1,768,256]{2,1,0:T(8,128)(2,1)} %bitcast.51), channel_id=1, source_target_pairs={{0,16},{4,20},{8,24},{12,28},{16,0},{20,4},{24,8},{28,12},{1,17},{... | collective-permute-start | bytes 1179656 | tf_op jit(solution)/shard_map/ppermute | solution.py:213
  85.8 40.3 %collective-permute-start.22 = (bf16[1,768,256]{2,1,0:T(8,128)(2,1)}, bf16[1,768,256]{2,1,0:T(8,128)(2,1)}, u32[]{:S(2)}, u32[]{:S(2)}) collective-permute-start(bf16[1,768,256]{2,1,0:T(8,128)(2,1)} %bitcast.51), channel_id=1, source_target_pairs={{0,8},{4,12},{8,16},{12,20},{16,24},{20,28},{24,0},{28,4},{1,9},{5... | collective-permute-start | bytes 1179656 | tf_op jit(solution)/shard_map/ppermute | solution.py:213
  87.0 42.8 %collective-permute-start.13 = (bf16[1,4,512,256]{3,2,1,0:T(8,128)(2,1)}, bf16[1,4,512,256]{3,2,1,0:T(8,128)(2,1)}, u32[]{:S(2)}, u32[]{:S(2)}) collective-permute-start(bf16[1,4,512,256]{3,2,1,0:T(8,128)(2,1)} %get-tuple-element.221), channel_id=1, source_target_pairs={{0,4},{4,0},{8,12},{12,8},{16,20},{20,16},{24,28},{28,24},{1,5},{5... | collective-permute-start | bytes 3145736 | tf_op jit(solution)/shard_map/ppermute | solution.py:213
  93.8 47.4 %collective-permute-start.1 = (bf16[19,128]{1,0:T(8,128)(2,1)S(1)}, bf16[19,128]{1,0:T(8,128)(2,1)S(1)}, u32[]{:S(2)}, u32[]{:S(2)}) collective-permute-start(bf16[19,128]{1,0:T(8,128)(2,1)S(1)} %get-tuple-element.268), channel_id=1, source_target_pairs={{0,16},{4,20},{8,24},{12,28},{16,0},{20,4},{24,8},{28,12},{1,17},{... | collective-permute-start | bytes 14600 | tf_op jit(solution)/shard_map/ppermute | solution.py:213
  127.6 37.4 %collective-permute-start.25 = (bf16[1,4,768,256]{3,2,1,0:T(8,128)(2,1)S(1)}, bf16[1,4,768,256]{3,2,1,0:T(8,128)(2,1)S(1)}, u32[]{:S(2)}, u32[]{:S(2)}) collective-permute-start(bf16[1,4,768,256]{3,2,1,0:T(8,128)(2,1)S(1)} %get-tuple-element.205), channel_id=1, source_target_pairs={{0,4},{4,0},{8,12},{12,8},{16,20},{20,16},{24,28},{28,24},{1,5},{5... | collective-permute-start | bytes 4718600 | tf_op jit(solution)/shard_map/ppermute | solution.py:213
  132.7 53.7 %collective-permute-start.14 = (bf16[1,2,4,512,256]{4,3,2,1,0:T(8,128)(2,1)}, bf16[1,2,4,512,256]{4,3,2,1,0:T(8,128)(2,1)}, u32[]{:S(2)}, u32[]{:S(2)}) collective-permute-start(bf16[1,2,4,512,256]{4,3,2,1,0:T(8,128)(2,1)} %pad_maximum_fusion.9), channel_id=1, source_target_pairs={{0,2},{1,3},{2,0},{3,1},{4,6},{5,7},{6,4},{7,5},{8,10},{9,11},{10,... | collective-permute-start | bytes 6291464 | tf_op jit(solution)/shard_map/ppermute | solution.py:213
  140.1 155.3 %collective-permute-start.9 = (bf16[2,8,512,256]{3,2,1,0:T(8,128)(2,1)}, bf16[2,8,512,256]{3,2,1,0:T(8,128)(2,1)}, u32[]{:S(2)}, u32[]{:S(2)}) collective-permute-start(bf16[2,8,512,256]{3,2,1,0:T(8,128)(2,1)} %bitcast.22.mine_ref), channel_id=1, source_target_pairs={{0,1},{1,0},{2,3},{3,2},{4,5},{5,4},{6,7},{7,6},{8,9},{9,8},{10,11... | collective-permute-start | bytes 12582920 | tf_op jit(solution)/shard_map/ppermute | solution.py:213
  141.2 39.0 %collective-permute-start.19 = (bf16[1,4,512,256]{3,2,1,0:T(8,128)(2,1)}, bf16[1,4,512,256]{3,2,1,0:T(8,128)(2,1)}, u32[]{:S(2)}, u32[]{:S(2)}) collective-permute-start(bf16[1,4,512,256]{3,2,1,0:T(8,128)(2,1)} %get-tuple-element.219), channel_id=1, source_target_pairs={{0,4},{4,0},{8,12},{12,8},{16,20},{20,16},{24,28},{28,24},{1,5},{5... | collective-permute-start | bytes 3145736 | tf_op jit(solution)/shard_map/ppermute | solution.py:213
  145.3 21.9 %collective-permute-start.2 = (bf16[19,128]{1,0:T(8,128)(2,1)S(1)}, bf16[19,128]{1,0:T(8,128)(2,1)S(1)}, u32[]{:S(2)}, u32[]{:S(2)}) collective-permute-start(bf16[19,128]{1,0:T(8,128)(2,1)S(1)} %get-tuple-element.268), channel_id=1, source_target_pairs={{0,24},{4,28},{8,0},{12,4},{16,8},{20,12},{24,16},{28,20},{1,25},{... | collective-permute-start | bytes 14600 | tf_op jit(solution)/shard_map/ppermute | solution.py:213
  165.0 19.5 %collective-permute-start.37 = (bf16[2,1024,256]{2,1,0:T(8,128)(2,1)}, bf16[2,1024,256]{2,1,0:T(8,128)(2,1)}, u32[]{:S(2)}, u32[]{:S(2)}) collective-permute-start(bf16[2,1024,256]{2,1,0:T(8,128)(2,1)} %pad_maximum_fusion.19), channel_id=1, source_target_pairs={{0,24},{4,28},{8,0},{12,4},{16,8},{20,12},{24,16},{28,20},{1,25},{... | collective-permute-start | bytes 3145736 | tf_op jit(solution)/shard_map/ppermute | solution.py:213
  167.2 122.6 %collective-permute-start.26 = (bf16[1,2,4,768,256]{4,3,2,1,0:T(8,128)(2,1)}, bf16[1,2,4,768,256]{4,3,2,1,0:T(8,128)(2,1)}, u32[]{:S(2)}, u32[]{:S(2)}) collective-permute-start(bf16[1,2,4,768,256]{4,3,2,1,0:T(8,128)(2,1)} %pad_maximum_fusion.7), channel_id=1, source_target_pairs={{0,2},{1,3},{2,0},{3,1},{4,6},{5,7},{6,4},{7,5},{8,10},{9,11},{10,... | collective-permute-start | bytes 9437192 | tf_op jit(solution)/shard_map/ppermute | solution.py:213
  184.5 61.8 %collective-permute-start.36 = (bf16[2,1024,256]{2,1,0:T(8,128)(2,1)}, bf16[2,1024,256]{2,1,0:T(8,128)(2,1)}, u32[]{:S(2)}, u32[]{:S(2)}) collective-permute-start(bf16[2,1024,256]{2,1,0:T(8,128)(2,1)} %pad_maximum_fusion.19), channel_id=1, source_target_pairs={{0,16},{4,20},{8,24},{12,28},{16,0},{20,4},{24,8},{28,12},{1,17},{... | collective-permute-start | bytes 3145736 | tf_op jit(solution)/shard_map/ppermute | solution.py:213
  184.5 101.8 %collective-permute-start.20 = (bf16[1,2,4,512,256]{4,3,2,1,0:T(8,128)(2,1)}, bf16[1,2,4,512,256]{4,3,2,1,0:T(8,128)(2,1)}, u32[]{:S(2)}, u32[]{:S(2)}) collective-permute-start(bf16[1,2,4,512,256]{4,3,2,1,0:T(8,128)(2,1)} %pad_maximum_fusion.10), channel_id=1, source_target_pairs={{0,2},{1,3},{2,0},{3,1},{4,6},{5,7},{6,4},{7,5},{8,10},{9,11},{10,... | collective-permute-start | bytes 6291464 | tf_op jit(solution)/shard_map/ppermute | solution.py:213
  186.4 60.4 %collective-permute-start.35 = (bf16[2,1024,256]{2,1,0:T(8,128)(2,1)}, bf16[2,1024,256]{2,1,0:T(8,128)(2,1)S(1)}, u32[]{:S(2)}, u32[]{:S(2)}) collective-permute-start(bf16[2,1024,256]{2,1,0:T(8,128)(2,1)} %pad_maximum_fusion.19), channel_id=1, source_target_pairs={{0,8},{4,12},{8,16},{12,20},{16,24},{20,28},{24,0},{28,4},{1,9},{5... | collective-permute-start | bytes 3145736 | tf_op jit(solution)/shard_map/ppermute | solution.py:213
  246.3 69.1 %collective-permute-start.15 = (bf16[2,8,512,256]{3,2,1,0:T(8,128)(2,1)S(1)}, bf16[2,8,512,256]{3,2,1,0:T(8,128)(2,1)}, u32[]{:S(2)}, u32[]{:S(2)}) collective-permute-start(bf16[2,8,512,256]{3,2,1,0:T(8,128)(2,1)S(1)} %bitcast.488), channel_id=1, source_target_pairs={{0,1},{1,0},{2,3},{3,2},{4,5},{5,4},{6,7},{7,6},{8,9},{9,8},{10,11... | collective-permute-start | bytes 12582920 | tf_op jit(solution)/shard_map/ppermute | solution.py:213
  252.2 126.6 %collective-permute-start.38 = (bf16[2,4,1024,256]{3,2,0,1:T(8,128)(2,1)}, bf16[2,4,1024,256]{3,2,0,1:T(8,128)(2,1)}, u32[]{:S(2)}, u32[]{:S(2)}) collective-permute-start(bf16[2,4,1024,256]{3,2,0,1:T(8,128)(2,1)} %get-tuple-element.172), channel_id=1, source_target_pairs={{0,4},{4,0},{8,12},{12,8},{16,20},{20,16},{24,28},{28,24},{1,5},{5... | collective-permute-start | bytes 12582920 | tf_op jit(solution)/shard_map/ppermute | solution.py:213
  289.9 42.6 %collective-permute-start.21 = (bf16[2,8,512,256]{3,2,1,0:T(8,128)(2,1)}, bf16[2,8,512,256]{3,2,1,0:T(8,128)(2,1)}, u32[]{:S(2)}, u32[]{:S(2)}) collective-permute-start(bf16[2,8,512,256]{3,2,1,0:T(8,128)(2,1)} %bitcast.40.mine_ref), channel_id=1, source_target_pairs={{0,1},{1,0},{2,3},{3,2},{4,5},{5,4},{6,7},{7,6},{8,9},{9,8},{10,11... | collective-permute-start | bytes 12582920 | tf_op jit(solution)/shard_map/ppermute | solution.py:213
  294.9 171.6 %collective-permute-start.27 = (bf16[2,8,768,256]{3,2,1,0:T(8,128)(2,1)}, bf16[2,8,768,256]{3,2,1,0:T(8,128)(2,1)}, u32[]{:S(2)}, u32[]{:S(2)}) collective-permute-start(bf16[2,8,768,256]{3,2,1,0:T(8,128)(2,1)} %bitcast.58.mine_ref), channel_id=1, source_target_pairs={{0,1},{1,0},{2,3},{3,2},{4,5},{5,4},{6,7},{7,6},{8,9},{9,8},{10,11... | collective-permute-start | bytes 18874376 | tf_op jit(solution)/shard_map/ppermute | solution.py:213
  372.1 42.1 %all-to-all-start = ((bf16[3,2,256,1024]{2,1,0,3:T(2,128)(2,1)}), bf16[3,2,256,1024]{2,1,0,3:T(2,128)(2,1)}, u32[]{:S(2)}, u32[]{:S(2)}) async-start(bf16[3,2,256,1024]{2,1,0,3:T(2,128)(2,1)} %pad_maximum_fusion.6), calls=%async_computation | async-start | bytes 6291456 | tf_op jit(solution)/shard_map/all_to_all | solution.py:665
  393.8 123.7 %collective-permute-start.39 = (bf16[2,8,1024,256]{3,2,1,0:T(8,128)(2,1)}, bf16[2,8,1024,256]{3,2,1,0:T(8,128)(2,1)}, u32[]{:S(2)}, u32[]{:S(2)}) collective-permute-start(bf16[2,8,1024,256]{3,2,1,0:T(8,128)(2,1)} %bitcast.511), channel_id=1, source_target_pairs={{0,1},{1,0},{2,3},{3,2},{4,5},{5,4},{6,7},{7,6},{8,9},{9,8},{10,11... | collective-permute-start | bytes 25165832 | tf_op jit(solution)/shard_map/ppermute | solution.py:213
  447.5 18.0 %all-to-all-start.1 = ((bf16[2,1024,256]{2,0,1:T(2,128)(2,1)}), bf16[2,1024,256]{2,0,1:T(2,128)(2,1)S(1)}, u32[]{:S(2)}, u32[]{:S(2)}) async-start(bf16[2,1024,256]{2,0,1:T(2,128)(2,1)} %copy.74), calls=%async_computation.1 | async-start | bytes 2097152 | tf_op jit(solution)/shard_map/all_to_all | solution.py:671
  624.9 18.9 %all-to-all-start.2 = ((bf16[2,256,1024]{1,0,2:T(2,128)(2,1)}), bf16[2,256,1024]{1,0,2:T(2,128)(2,1)}, u32[]{:S(2)}, u32[]{:S(2)}) async-start(bf16[2,256,1024]{1,0,2:T(2,128)(2,1)} %copy.78), calls=%async_computation.2 | async-start | bytes 2097152 | tf_op jit(solution)/shard_map/all_to_all | solution.py:756
  641.7 83.9 %collective-permute-start.52 = (bf16[2,2,4,384,256]{4,3,2,1,0:T(8,128)(2,1)}, bf16[2,2,4,384,256]{4,3,2,1,0:T(8,128)(2,1)}, u32[]{:S(2)}, u32[]{:S(2)}) collective-permute-start(bf16[2,2,4,384,256]{4,3,2,1,0:T(8,128)(2,1)} %quantizer_2_1.1), channel_id=1, source_target_pairs={{0,1},{1,0},{2,3},{3,2},{4,5},{5,4},{6,7},{7,6},{8,9},{9,8},{10,11... | collective-permute-start | bytes 9437192 | tf_op jit(solution)/shard_map/ppermute | solution.py:213
  692.9 48.3 %all-to-all-start.3 = ((bf16[3,2,1024,256]{3,1,0,2:T(2,128)(2,1)}), bf16[3,2,1024,256]{3,1,0,2:T(2,128)(2,1)}, u32[]{:S(2)}, u32[]{:S(2)}) async-start(bf16[3,2,1024,256]{3,1,0,2:T(2,128)(2,1)} %copy.81), calls=%async_computation.3 | async-start | bytes 6291456 | tf_op jit(solution)/shard_map/all_to_all | solution.py:767
  707.2 129.8 %collective-permute-start.88 = (bf16[2,2,4,512,256]{4,3,2,1,0:T(8,128)(2,1)}, bf16[2,2,4,512,256]{4,3,2,1,0:T(8,128)(2,1)}, u32[]{:S(2)}, u32[]{:S(2)}) collective-permute-start(bf16[2,2,4,512,256]{4,3,2,1,0:T(8,128)(2,1)} %closing_exit_0_1.1), channel_id=1, source_target_pairs={{0,1},{1,0},{2,3},{3,2},{4,5},{5,4},{6,7},{7,6},{8,9},{9,8},{10,11... | collective-permute-start | bytes 12582920 | tf_op jit(solution)/shard_map/ppermute | solution.py:213
  716.4 127.8 %collective-permute-start.82 = (bf16[2,2,4,512,256]{4,3,2,1,0:T(8,128)(2,1)}, bf16[2,2,4,512,256]{4,3,2,1,0:T(8,128)(2,1)}, u32[]{:S(2)}, u32[]{:S(2)}) collective-permute-start(bf16[2,2,4,512,256]{4,3,2,1,0:T(8,128)(2,1)} %closing_entry_0_1.1), channel_id=1, source_target_pairs={{0,1},{1,0},{2,3},{3,2},{4,5},{5,4},{6,7},{7,6},{8,9},{9,8},{10,11... | collective-permute-start | bytes 12582920 | tf_op jit(solution)/shard_map/ppermute | solution.py:213
  723.8 33.2 %collective-permute-start.76 = (bf16[2,2,4,384,256]{4,3,2,1,0:T(8,128)(2,1)}, bf16[2,2,4,384,256]{4,3,2,1,0:T(8,128)(2,1)}, u32[]{:S(2)}, u32[]{:S(2)}) collective-permute-start(bf16[2,2,4,384,256]{4,3,2,1,0:T(8,128)(2,1)} %convolution_1_1.1), channel_id=1, source_target_pairs={{0,1},{1,0},{2,3},{3,2},{4,5},{5,4},{6,7},{7,6},{8,9},{9,8},{10,11... | collective-permute-start | bytes 9437192 | tf_op jit(solution)/shard_map/ppermute | solution.py:213
  739.2 55.7 %collective-permute-start.53 = (bf16[2,4,384,256]{3,2,1,0:T(8,128)(2,1)}, bf16[2,4,384,256]{3,2,1,0:T(8,128)(2,1)}, u32[]{:S(2)}, u32[]{:S(2)}) collective-permute-start(bf16[2,4,384,256]{3,2,1,0:T(8,128)(2,1)} %get-tuple-element.88), channel_id=1, source_target_pairs={{0,2},{1,3},{2,0},{3,1},{4,6},{5,7},{6,4},{7,5},{8,10},{9,11},{10,... | collective-permute-start | bytes 4718600 | tf_op jit(solution)/shard_map/ppermute | solution.py:213
  767.0 61.9 %collective-permute-start.77 = (bf16[2,4,384,256]{3,2,1,0:T(8,128)(2,1)}, bf16[2,4,384,256]{3,2,1,0:T(8,128)(2,1)}, u32[]{:S(2)}, u32[]{:S(2)}) collective-permute-start(bf16[2,4,384,256]{3,2,1,0:T(8,128)(2,1)} %get-tuple-element.105), channel_id=1, source_target_pairs={{0,4},{4,0},{8,12},{12,8},{16,20},{20,16},{24,28},{28,24},{1,5},{5... | collective-permute-start | bytes 4718600 | tf_op jit(solution)/shard_map/ppermute | solution.py:213
  797.7 39.7 %collective-permute-start.54 = (bf16[4,384,256]{2,1,0:T(8,128)(2,1)}, bf16[4,384,256]{2,1,0:T(8,128)(2,1)}, u32[]{:S(2)}, u32[]{:S(2)}) collective-permute-start(bf16[4,384,256]{2,1,0:T(8,128)(2,1)} %get-tuple-element.178), channel_id=1, source_target_pairs={{0,4},{4,0},{8,12},{12,8},{16,20},{20,16},{24,28},{28,24},{1,5},{5... | collective-permute-start | bytes 2359304 | tf_op jit(solution)/shard_map/ppermute | solution.py:213
  828.8 88.6 %collective-permute-start.70 = (bf16[2,2,4,384,256]{4,3,2,1,0:T(8,128)(2,1)S(1)}, bf16[2,2,4,384,256]{4,3,2,1,0:T(8,128)(2,1)}, u32[]{:S(2)}, u32[]{:S(2)}) collective-permute-start(bf16[2,2,4,384,256]{4,3,2,1,0:T(8,128)(2,1)S(1)} %attention_2_1.1), channel_id=1, source_target_pairs={{0,1},{1,0},{2,3},{3,2},{4,5},{5,4},{6,7},{7,6},{8,9},{9,8},{10,11... | collective-permute-start | bytes 9437192 | tf_op jit(solution)/shard_map/ppermute | solution.py:213
  836.9 115.9 %collective-permute-start.64 = (bf16[2,2,4,512,256]{4,3,2,1,0:T(8,128)(2,1)}, bf16[2,2,4,512,256]{4,3,2,1,0:T(8,128)(2,1)}, u32[]{:S(2)}, u32[]{:S(2)}) collective-permute-start(bf16[2,2,4,512,256]{4,3,2,1,0:T(8,128)(2,1)} %opening_exit_0_1.1), channel_id=1, source_target_pairs={{0,1},{1,0},{2,3},{3,2},{4,5},{5,4},{6,7},{7,6},{8,9},{9,8},{10,11... | collective-permute-start | bytes 12582920 | tf_op jit(solution)/shard_map/ppermute | solution.py:213
  837.0 106.5 %collective-permute-start.58 = (bf16[2,2,4,512,256]{4,3,2,1,0:T(8,128)(2,1)}, bf16[2,2,4,512,256]{4,3,2,1,0:T(8,128)(2,1)}, u32[]{:S(2)}, u32[]{:S(2)}) collective-permute-start(bf16[2,2,4,512,256]{4,3,2,1,0:T(8,128)(2,1)} %opening_entry_0_1.1), channel_id=1, source_target_pairs={{0,1},{1,0},{2,3},{3,2},{4,5},{5,4},{6,7},{7,6},{8,9},{9,8},{10,11... | collective-permute-start | bytes 12582920 | tf_op jit(solution)/shard_map/ppermute | solution.py:213
  837.4 19.9 %collective-permute-start.78 = (bf16[4,384,256]{2,1,0:T(8,128)(2,1)}, bf16[4,384,256]{2,1,0:T(8,128)(2,1)}, u32[]{:S(2)}, u32[]{:S(2)}) collective-permute-start(bf16[4,384,256]{2,1,0:T(8,128)(2,1)} %get-tuple-element.174), channel_id=1, source_target_pairs={{0,2},{1,3},{2,0},{3,1},{4,6},{5,7},{6,4},{7,5},{8,10},{9,11},{10,... | collective-permute-start | bytes 2359304 | tf_op jit(solution)/shard_map/ppermute | solution.py:213
  844.3 25.6 %collective-permute-start.55 = (bf16[384,256]{1,0:T(8,128)(2,1)}, bf16[384,256]{1,0:T(8,128)(2,1)}, u32[]{:S(2)}, u32[]{:S(2)}) collective-permute-start(bf16[384,256]{1,0:T(8,128)(2,1)} %get-tuple-element.201), channel_id=1, source_target_pairs={{0,8},{4,12},{8,16},{12,20},{16,24},{20,28},{24,0},{28,4},{1,9},{5... | collective-permute-start | bytes 589832 | tf_op jit(solution)/shard_map/ppermute | solution.py:213
  869.9 46.9 %collective-permute-start.83 = (bf16[2,4,512,256]{3,2,1,0:T(8,128)(2,1)}, bf16[2,4,512,256]{3,2,1,0:T(8,128)(2,1)}, u32[]{:S(2)}, u32[]{:S(2)}) collective-permute-start(bf16[2,4,512,256]{3,2,1,0:T(8,128)(2,1)} %get-tuple-element.107), channel_id=1, source_target_pairs={{0,4},{4,0},{8,12},{12,8},{16,20},{20,16},{24,28},{28,24},{1,5},{5... | collective-permute-start | bytes 6291464 | tf_op jit(solution)/shard_map/ppermute | solution.py:213
  881.1 53.5 %collective-permute-start.89 = (bf16[2,4,512,256]{3,2,1,0:T(8,128)(2,1)}, bf16[2,4,512,256]{3,2,1,0:T(8,128)(2,1)}, u32[]{:S(2)}, u32[]{:S(2)}) collective-permute-start(bf16[2,4,512,256]{3,2,1,0:T(8,128)(2,1)} %get-tuple-element.109), channel_id=1, source_target_pairs={{0,2},{1,3},{2,0},{3,1},{4,6},{5,7},{6,4},{7,5},{8,10},{9,11},{10,... | collective-permute-start | bytes 6291464 | tf_op jit(solution)/shard_map/ppermute | solution.py:213
  916.7 17.4 %collective-permute-start.79 = (bf16[384,256]{1,0:T(8,128)(2,1)S(1)}, bf16[384,256]{1,0:T(8,128)(2,1)S(1)}, u32[]{:S(2)}, u32[]{:S(2)}) collective-permute-start(bf16[384,256]{1,0:T(8,128)(2,1)S(1)} %get-tuple-element.198), channel_id=1, source_target_pairs={{0,8},{4,12},{8,16},{12,20},{16,24},{20,28},{24,0},{28,4},{1,9},{5... | collective-permute-start | bytes 589832 | tf_op jit(solution)/shard_map/ppermute | solution.py:213
  934.2 29.8 %collective-permute-start.84 = (bf16[4,512,256]{2,1,0:T(8,128)(2,1)}, bf16[4,512,256]{2,1,0:T(8,128)(2,1)}, u32[]{:S(2)}, u32[]{:S(2)}) collective-permute-start(bf16[4,512,256]{2,1,0:T(8,128)(2,1)} %get-tuple-element.166), channel_id=1, source_target_pairs={{0,2},{1,3},{2,0},{3,1},{4,6},{5,7},{6,4},{7,5},{8,10},{9,11},{10,... | collective-permute-start | bytes 3145736 | tf_op jit(solution)/shard_map/ppermute | solution.py:213
  934.6 59.8 %collective-permute-start.71 = (bf16[2,4,384,256]{3,2,1,0:T(8,128)(2,1)S(1)}, bf16[2,4,384,256]{3,2,1,0:T(8,128)(2,1)}, u32[]{:S(2)}, u32[]{:S(2)}) collective-permute-start(bf16[2,4,384,256]{3,2,1,0:T(8,128)(2,1)S(1)} %get-tuple-element.98), channel_id=1, source_target_pairs={{0,2},{1,3},{2,0},{3,1},{4,6},{5,7},{6,4},{7,5},{8,10},{9,11},{10,... | collective-permute-start | bytes 4718600 | tf_op jit(solution)/shard_map/ppermute | solution.py:213
  941.9 26.4 %collective-permute-start.90 = (bf16[4,512,256]{2,1,0:T(8,128)(2,1)}, bf16[4,512,256]{2,1,0:T(8,128)(2,1)}, u32[]{:S(2)}, u32[]{:S(2)}) collective-permute-start(bf16[4,512,256]{2,1,0:T(8,128)(2,1)} %get-tuple-element.164), channel_id=1, source_target_pairs={{0,4},{4,0},{8,12},{12,8},{16,20},{20,16},{24,28},{28,24},{1,5},{5... | collective-permute-start | bytes 3145736 | tf_op jit(solution)/shard_map/ppermute | solution.py:213
  952.5 83.4 %collective-permute-start.59 = (bf16[2,4,512,256]{3,2,1,0:T(8,128)(2,1)S(1)}, bf16[2,4,512,256]{3,2,1,0:T(8,128)(2,1)}, u32[]{:S(2)}, u32[]{:S(2)}) collective-permute-start(bf16[2,4,512,256]{3,2,1,0:T(8,128)(2,1)S(1)} %get-tuple-element.90), channel_id=1, source_target_pairs={{0,2},{1,3},{2,0},{3,1},{4,6},{5,7},{6,4},{7,5},{8,10},{9,11},{10,... | collective-permute-start | bytes 6291464 | tf_op jit(solution)/shard_map/ppermute | solution.py:213
  961.1 79.4 %collective-permute-start.65 = (bf16[2,4,512,256]{3,2,1,0:T(8,128)(2,1)S(1)}, bf16[2,4,512,256]{3,2,1,0:T(8,128)(2,1)S(1)}, u32[]{:S(2)}, u32[]{:S(2)}) collective-permute-start(bf16[2,4,512,256]{3,2,1,0:T(8,128)(2,1)S(1)} %get-tuple-element.92), channel_id=1, source_target_pairs={{0,4},{4,0},{8,12},{12,8},{16,20},{20,16},{24,28},{28,24},{1,5},{5... | collective-permute-start | bytes 6291464 | tf_op jit(solution)/shard_map/ppermute | solution.py:213
  965.4 33.8 %collective-permute-start.85 = (bf16[512,256]{1,0:T(8,128)(2,1)S(1)}, bf16[512,256]{1,0:T(8,128)(2,1)S(1)}, u32[]{:S(2)}, u32[]{:S(2)}) collective-permute-start(bf16[512,256]{1,0:T(8,128)(2,1)S(1)} %get-tuple-element.186), channel_id=1, source_target_pairs={{0,8},{4,12},{8,16},{12,20},{16,24},{20,28},{24,0},{28,4},{1,9},{5... | collective-permute-start | bytes 786440 | tf_op jit(solution)/shard_map/ppermute | solution.py:213
  968.3 30.9 %collective-permute-start.87 = (bf16[512,256]{1,0:T(8,128)(2,1)S(1)}, bf16[512,256]{1,0:T(8,128)(2,1)S(1)}, u32[]{:S(2)}, u32[]{:S(2)}) collective-permute-start(bf16[512,256]{1,0:T(8,128)(2,1)S(1)} %get-tuple-element.187), channel_id=1, source_target_pairs={{0,24},{4,28},{8,0},{12,4},{16,8},{20,12},{24,16},{28,20},{1,25},{... | collective-permute-start | bytes 786440 | tf_op jit(solution)/shard_map/ppermute | solution.py:213
  999.2 43.1 %collective-permute-start.91 = (bf16[512,256]{1,0:T(8,128)(2,1)S(1)}, bf16[512,256]{1,0:T(8,128)(2,1)S(1)}, u32[]{:S(2)}, u32[]{:S(2)}) collective-permute-start(bf16[512,256]{1,0:T(8,128)(2,1)S(1)} %get-tuple-element.183), channel_id=1, source_target_pairs={{0,8},{4,12},{8,16},{12,20},{16,24},{20,28},{24,0},{28,4},{1,9},{5... | collective-permute-start | bytes 786440 | tf_op jit(solution)/shard_map/ppermute | solution.py:213
  999.3 43.1 %collective-permute-start.93 = (bf16[512,256]{1,0:T(8,128)(2,1)S(1)}, bf16[512,256]{1,0:T(8,128)(2,1)S(1)}, u32[]{:S(2)}, u32[]{:S(2)}) collective-permute-start(bf16[512,256]{1,0:T(8,128)(2,1)S(1)} %get-tuple-element.184), channel_id=1, source_target_pairs={{0,24},{4,28},{8,0},{12,4},{16,8},{20,12},{24,16},{28,20},{1,25},{... | collective-permute-start | bytes 786440 | tf_op jit(solution)/shard_map/ppermute | solution.py:213
  1010.2 31.6 %collective-permute-start.72 = (bf16[4,512,256]{2,1,0:T(8,128)(2,1)S(1)}, bf16[4,512,256]{2,1,0:T(8,128)(2,1)S(1)}, u32[]{:S(2)}, u32[]{:S(2)}) collective-permute-start(bf16[4,512,256]{2,1,0:T(8,128)(2,1)S(1)} %pad_maximum_fusion.20), channel_id=1, source_target_pairs={{0,4},{4,0},{8,12},{12,8},{16,20},{20,16},{24,28},{28,24},{1,5},{5... | collective-permute-start | bytes 3145736 | tf_op jit(solution)/shard_map/ppermute | solution.py:213
  1035.8 21.4 %collective-permute-start.92 = (bf16[512,256]{1,0:T(8,128)(2,1)S(1)}, bf16[512,256]{1,0:T(8,128)(2,1)S(1)}, u32[]{:S(2)}, u32[]{:S(2)}) collective-permute-start(bf16[512,256]{1,0:T(8,128)(2,1)S(1)} %get-tuple-element.185), channel_id=1, source_target_pairs={{0,16},{4,20},{8,24},{12,28},{16,0},{20,4},{24,8},{28,12},{1,17},{... | collective-permute-start | bytes 786440 | tf_op jit(solution)/shard_map/ppermute | solution.py:213
  1040.5 29.2 %collective-permute-start.60 = (bf16[4,512,256]{2,1,0:T(8,128)(2,1)S(1)}, bf16[4,512,256]{2,1,0:T(8,128)(2,1)S(1)}, u32[]{:S(2)}, u32[]{:S(2)}) collective-permute-start(bf16[4,512,256]{2,1,0:T(8,128)(2,1)S(1)} %get-tuple-element.170), channel_id=1, source_target_pairs={{0,4},{4,0},{8,12},{12,8},{16,20},{20,16},{24,28},{28,24},{1,5},{5... | collective-permute-start | bytes 3145736 | tf_op jit(solution)/shard_map/ppermute | solution.py:213
  1041.7 32.9 %collective-permute-start.66 = (bf16[4,512,256]{2,1,0:T(8,128)(2,1)S(1)}, bf16[4,512,256]{2,1,0:T(8,128)(2,1)S(1)}, u32[]{:S(2)}, u32[]{:S(2)}) collective-permute-start(bf16[4,512,256]{2,1,0:T(8,128)(2,1)S(1)} %get-tuple-element.168), channel_id=1, source_target_pairs={{0,2},{1,3},{2,0},{3,1},{4,6},{5,7},{6,4},{7,5},{8,10},{9,11},{10,... | collective-permute-start | bytes 3145736 | tf_op jit(solution)/shard_map/ppermute | solution.py:213
  1070.0 16.9 %collective-permute-start.63 = (bf16[512,256]{1,0:T(8,128)(2,1)S(1)}, bf16[512,256]{1,0:T(8,128)(2,1)S(1)}, u32[]{:S(2)}, u32[]{:S(2)}) collective-permute-start(bf16[512,256]{1,0:T(8,128)(2,1)S(1)} %get-tuple-element.196), channel_id=1, source_target_pairs={{0,24},{4,28},{8,0},{12,4},{16,8},{20,12},{24,16},{28,20},{1,25},{... | collective-permute-start | bytes 786440 | tf_op jit(solution)/shard_map/ppermute | solution.py:213
  1073.9 32.9 %collective-permute-start.62 = (bf16[512,256]{1,0:T(8,128)(2,1)S(1)}, bf16[512,256]{1,0:T(8,128)(2,1)S(1)}, u32[]{:S(2)}, u32[]{:S(2)}) collective-permute-start(bf16[512,256]{1,0:T(8,128)(2,1)S(1)} %get-tuple-element.197), channel_id=1, source_target_pairs={{0,16},{4,20},{8,24},{12,28},{16,0},{20,4},{24,8},{28,12},{1,17},{... | collective-permute-start | bytes 786440 | tf_op jit(solution)/shard_map/ppermute | solution.py:213
  1074.8 33.0 %collective-permute-start.67 = (bf16[512,256]{1,0:T(8,128)(2,1)S(1)}, bf16[512,256]{1,0:T(8,128)(2,1)S(1)}, u32[]{:S(2)}, u32[]{:S(2)}) collective-permute-start(bf16[512,256]{1,0:T(8,128)(2,1)S(1)} %get-tuple-element.192), channel_id=1, source_target_pairs={{0,8},{4,12},{8,16},{12,20},{16,24},{20,28},{24,0},{28,4},{1,9},{5... | collective-permute-start | bytes 786440 | tf_op jit(solution)/shard_map/ppermute | solution.py:213
  1075.5 32.4 %collective-permute-start.69 = (bf16[512,256]{1,0:T(8,128)(2,1)S(1)}, bf16[512,256]{1,0:T(8,128)(2,1)S(1)}, u32[]{:S(2)}, u32[]{:S(2)}) collective-permute-start(bf16[512,256]{1,0:T(8,128)(2,1)S(1)} %get-tuple-element.193), channel_id=1, source_target_pairs={{0,24},{4,28},{8,0},{12,4},{16,8},{20,12},{24,16},{28,20},{1,25},{... | collective-permute-start | bytes 786440 | tf_op jit(solution)/shard_map/ppermute | solution.py:213
  1081.1 34.2 %collective-permute-start.68 = (bf16[512,256]{1,0:T(8,128)(2,1)S(1)}, bf16[512,256]{1,0:T(8,128)(2,1)S(1)}, u32[]{:S(2)}, u32[]{:S(2)}) collective-permute-start(bf16[512,256]{1,0:T(8,128)(2,1)S(1)} %get-tuple-element.194), channel_id=1, source_target_pairs={{0,16},{4,20},{8,24},{12,28},{16,0},{20,4},{24,8},{28,12},{1,17},{... | collective-permute-start | bytes 786440 | tf_op jit(solution)/shard_map/ppermute | solution.py:213
  (171 other events, 1622.6 us)

commit v3 on v2

--- a/solution.py
+++ b/solution.py
@@ -21,10 +21,10 @@
 def _fwd_body(len_ref, q_ref, k_ref, v_ref, pos_ref, bias_ref, o_ref, p_ref, *, rows, full, scale):
     block = pl.program_id(2)
     length = len_ref[pl.program_id(0)]
-    query = q_ref[0, 0].astype(F32)
+    query = q_ref[0, 0, 0].astype(F32)
     content_query = (query + bias_ref[0:1, :]).astype(BF16)
     position_query = (query + bias_ref[1:2, :]).astype(BF16)
-    content = dot(content_query, k_ref[0, 0], 1, 1)
+    content = dot(content_query, k_ref[:, 0, 0].reshape(full, -1), 1, 1)
     span = full + rows
     start = pl.multiple_of(full - rows - block * rows, rows)
     relative = dot(position_query, pos_ref[pl.ds(start, span), :], 1, 1)
@@ -37,11 +37,11 @@
     total = jnp.sum(weights, axis=-1, keepdims=True)
     low = (weights * (1.0 / total)).astype(BF16)
     p_ref[0, 0] = low
-    o_ref[0] = dot(low, v_ref[0, 0], 1, 0).astype(BF16)
-
-def attend_forward(by_heads, position, bias, lengths, rows=256):
-    _, groups, full, width = by_heads.shape
-    depth = HEAD_WIDTH
+    o_ref[0, 0] = dot(low, v_ref[:, 0, 0].reshape(full, -1), 1, 0).astype(BF16)
+
+def attend_forward(by_heads, position, bias, lengths):
+    parts, _, groups, rows, width = by_heads.shape
+    depth, full = HEAD_WIDTH, parts * rows
     heads = width // depth
     body = partial(_fwd_body, rows=rows, full=full, scale=1.0 / math.sqrt(depth))
     flops = groups * heads * full * (2 * full * depth * 3 + 2 * rows * depth)
@@ -49,21 +49,21 @@
         body,
         grid_spec=pltpu.PrefetchScalarGridSpec(
             num_scalar_prefetch=1,
-            grid=(groups, heads, full // rows),
+            grid=(groups, heads, parts),
             in_specs=[
-                pl.BlockSpec((1, 1, rows, depth), lambda u, h, i, n: (0, u, i, h)),
-                pl.BlockSpec((1, 1, full, depth), lambda u, h, i, n: (1, u, 0, h)),
-                pl.BlockSpec((1, 1, full, depth), lambda u, h, i, n: (2, u, 0, h)),
+                pl.BlockSpec((1, 1, 1, rows, depth), lambda u, h, i, n: (i, 0, u, 0, h)),
+                pl.BlockSpec((parts, 1, 1, rows, depth), lambda u, h, i, n: (0, 1, u, 0, h)),
+                pl.BlockSpec((parts, 1, 1, rows, depth), lambda u, h, i, n: (0, 2, u, 0, h)),
                 pl.BlockSpec((2 * full, depth), lambda u, h, i, n: (0, h)),
                 pl.BlockSpec((2, depth), lambda u, h, i, n: (0, h)),
             ],
             out_specs=[
-                pl.BlockSpec((1, rows, depth), lambda u, h, i, n: (u, i, h)),
+                pl.BlockSpec((1, 1, rows, depth), lambda u, h, i, n: (i, u, 0, h)),
                 pl.BlockSpec((1, 1, rows, full), lambda u, h, i, n: (u, h, i, 0)),
             ],
         ),
         out_shape=[
-            jax.ShapeDtypeStruct((groups, full, width), BF16),
+            jax.ShapeDtypeStruct((parts, groups, rows, width), BF16),
             jax.ShapeDtypeStruct((groups, heads, full, full), BF16),
         ],
         compiler_params=pltpu.CompilerParams(vmem_limit_bytes=48 << 20),
@@ -86,13 +86,13 @@
         key_acc[...] = jnp.zeros_like(key_acc)
         value_acc[...] = jnp.zeros_like(value_acc)
 
-    query = q_ref[0, 0].astype(F32)
+    query = q_ref[0, 0, 0].astype(F32)
     content_query = (query + bias_ref[0:1, :]).astype(BF16)
     position_query = (query + bias_ref[1:2, :]).astype(BF16)
-    keys, grad = k_ref[0, 0], g_ref[0]
+    keys, values, grad = k_ref[:, 0, 0].reshape(full, -1), v_ref[:, 0, 0].reshape(full, -1), g_ref[0, 0]
     low = p_ref[0, 0]
     weights = low.astype(F32)
-    grad_weights = dot(grad, v_ref[0, 0], 1, 1)
+    grad_weights = dot(grad, values, 1, 1)
     value_acc[...] += dot(grad, low, 0, 0)
     inner = jnp.sum(grad_weights * weights, axis=-1, keepdims=True)
     grad_raw = (weights * (grad_weights - inner) * scale).astype(BF16)
@@ -111,24 +111,23 @@
     high = grad_turned.astype(BF16)
     rest = (grad_turned - high.astype(F32)).astype(BF16)
     grad_position = dot(flip, high, 1, 0) + dot(flip, rest, 1, 0)
-    here = pl.ds(pl.multiple_of(block * rows, rows), rows)
-    d_ref[0, 0, here, :] = (grad_content + grad_position).astype(BF16)
+    d_ref[block, 0, 0] = (grad_content + grad_position).astype(BF16)
     bias_acc[0:1, :] += jnp.sum(grad_content, axis=0, keepdims=True)
     bias_acc[1:2, :] += jnp.sum(grad_position, axis=0, keepdims=True)
 
     @pl.when(last_block)
     def _():
-        d_ref[1, 0] = key_acc[...].T.astype(BF16)
-        d_ref[2, 0] = value_acc[...].T.astype(BF16)
+        d_ref[:, 1, 0] = key_acc[...].T.astype(BF16).reshape(full // rows, rows, -1)
+        d_ref[:, 2, 0] = value_acc[...].T.astype(BF16).reshape(full // rows, rows, -1)
 
     @pl.when(last_block & (group == pl.num_programs(1) - 1))
     def _():
         dpos_ref[...] = pos_acc[...].T.astype(BF16)
         dbias_ref[...] = bias_acc[...]
 
-def attend_backward(probs, by_heads, grad_heads, position, bias, rows=256):
-    _, groups, full, width = by_heads.shape
-    depth = HEAD_WIDTH
+def attend_backward(probs, by_heads, grad_heads, position, bias):
+    parts, _, groups, rows, width = by_heads.shape
+    depth, full = HEAD_WIDTH, parts * rows
     heads = width // depth
     body = partial(_bwd_body, rows=rows, full=full, scale=1.0 / math.sqrt(depth))
     flops = groups * heads * full * (2 * full * depth * 7 + 6 * rows * depth)
@@ -136,18 +135,18 @@
         body,
         grid_spec=pltpu.PrefetchScalarGridSpec(
             num_scalar_prefetch=0,
-            grid=(heads, groups, full // rows),
+            grid=(heads, groups, parts),
             in_specs=[
                 pl.BlockSpec((1, 1, rows, full), lambda h, u, i: (u, h, i, 0)),
-                pl.BlockSpec((1, 1, rows, depth), lambda h, u, i: (0, u, i, h)),
-                pl.BlockSpec((1, 1, full, depth), lambda h, u, i: (1, u, 0, h)),
-                pl.BlockSpec((1, 1, full, depth), lambda h, u, i: (2, u, 0, h)),
-                pl.BlockSpec((1, rows, depth), lambda h, u, i: (u, i, h)),
+                pl.BlockSpec((1, 1, 1, rows, depth), lambda h, u, i: (i, 0, u, 0, h)),
+                pl.BlockSpec((parts, 1, 1, rows, depth), lambda h, u, i: (0, 1, u, 0, h)),
+                pl.BlockSpec((parts, 1, 1, rows, depth), lambda h, u, i: (0, 2, u, 0, h)),
+                pl.BlockSpec((1, 1, rows, depth), lambda h, u, i: (i, u, 0, h)),
                 pl.BlockSpec((2 * full, depth), lambda h, u, i: (0, h)),
                 pl.BlockSpec((2, depth), lambda h, u, i: (0, h)),
             ],
             out_specs=[
-                pl.BlockSpec((3, 1, full, depth), lambda h, u, i: (0, u, 0, h)),
+                pl.BlockSpec((parts, 3, 1, rows, depth), lambda h, u, i: (0, 0, u, 0, h)),
                 pl.BlockSpec((2 * full, depth), lambda h, u, i: (0, h)),
                 pl.BlockSpec((2, depth), lambda h, u, i: (0, h)),
             ],
@@ -159,7 +158,7 @@
             ],
         ),
         out_shape=[
-            jax.ShapeDtypeStruct((3, groups, full, width), BF16),
+            jax.ShapeDtypeStruct((parts, 3, groups, rows, width), BF16),
             jax.ShapeDtypeStruct((2 * full, width), BF16),
             jax.ShapeDtypeStruct((2, width), F32),
         ],
@@ -182,6 +181,81 @@
     return value
 
 
+def _project_body(left_ref, *refs):
+    out = refs[-1]
+    for i, weight in enumerate(refs[:-1]):
+        out[0, i] = dot(left_ref[...], weight[...], 1, 0).astype(BF16).reshape(out.shape[2:])
+
+
+def project_heads(left, weights, groups, parts):
+    rows, depth = left.shape
+    width = weights[0].shape[1] // parts
+    shape = (parts, len(weights), groups, rows // groups, width)
+    return pl.pallas_call(
+        _project_body,
+        grid=(parts,),
+        in_specs=[pl.BlockSpec((rows, depth), lambda s: (0, 0))]
+        + [pl.BlockSpec((depth, width), lambda s: (0, s))] * len(weights),
+        out_specs=pl.BlockSpec((1, *shape[1:]), lambda s: (s, 0, 0, 0, 0)),
+        out_shape=jax.ShapeDtypeStruct(shape, BF16),
+        compiler_params=pltpu.CompilerParams(vmem_limit_bytes=48 << 20),
+        cost_estimate=pl.CostEstimate(flops=2 * rows * depth * width * parts * len(weights), transcendentals=0, bytes_accessed=2 * len(weights) * (rows + depth) * width * parts + 2 * rows * depth),
+        name="project_heads",
+    )(left, *weights)
+
+
+def _unproject_body(left_ref, weight_ref, out_ref):
+    out_ref[0] = dot(left_ref[...], weight_ref[...], 1, 1).astype(BF16).reshape(out_ref.shape[1:])
+
+
+def unproject_heads(left, weight, groups, parts):
+    rows, depth = left.shape
+    width = weight.shape[0] // parts
+    shape = (parts, groups, rows // groups, width)
+    return pl.pallas_call(
+        _unproject_body,
+        grid=(parts,),
+        in_specs=[
+            pl.BlockSpec((rows, depth), lambda s: (0, 0)),
+            pl.BlockSpec((width, depth), lambda s: (s, 0)),
+        ],
+        out_specs=pl.BlockSpec((1, *shape[1:]), lambda s: (s, 0, 0, 0)),
+        out_shape=jax.ShapeDtypeStruct(shape, BF16),
+        compiler_params=pltpu.CompilerParams(vmem_limit_bytes=48 << 20),
+        cost_estimate=pl.CostEstimate(flops=2 * rows * depth * width * parts, transcendentals=0, bytes_accessed=2 * (rows + depth) * width * parts + 2 * rows * depth),
+        name="unproject_heads",
+    )(left, weight)
+
+
+def _join_body(grad_ref, *refs):
+    out = refs[-1]
+
+    @pl.when(pl.program_id(0) == 0)
+    def _():
+        out[...] = jnp.zeros_like(out)
+
+    total = out[...]
+    for i, weight in enumerate(refs[:-1]):
+        total = total + dot(grad_ref[0, i].reshape(out.shape[0], -1), weight[...], 1, 1)
+    out[...] = total
+
+
+def join_heads(grads, weights):
+    parts, count, groups, frames, width = grads.shape
+    rows, depth = groups * frames, weights[0].shape[0]
+    return pl.pallas_call(
+        _join_body,
+        grid=(parts,),
+        in_specs=[pl.BlockSpec((1, count, groups, frames, width), lambda s: (s, 0, 0, 0, 0))]
+        + [pl.BlockSpec((depth, width), lambda s: (0, s))] * count,
+        out_specs=pl.BlockSpec((rows, depth), lambda s: (0, 0)),
+        out_shape=jax.ShapeDtypeStruct((rows, depth), F32),
+        compiler_params=pltpu.CompilerParams(vmem_limit_bytes=48 << 20),
+        cost_estimate=pl.CostEstimate(flops=2 * rows * depth * width * parts * count, transcendentals=0, bytes_accessed=2 * count * (rows + depth) * width * parts + 4 * rows * depth),
+        name="join_heads",
+    )(grads, *weights)
+
+
 def line_factors(line):
     places = [(*device.coords, device.core_on_chip) for device in line]
     moving = [first != second for first, second in zip(places[0], places[1])].index(True)
@@ -195,6 +269,7 @@
         self.a, self.b = line_factors(list(devices[:, 0]))
         self.y, self.c = line_factors(list(devices[0, :]))
         self.size = {"a": self.a, "b": self.b, "y": self.y, "c": self.c}
+        self.bits = self.a.bit_length() - 1
 
     def places(self):
         batch, seq = lax.axis_index("batch"), lax.axis_index("seq")
@@ -212,14 +287,35 @@
                     pairs.append((i * inner + j, i * inner + (j + step) % inner))
         return lax.ppermute(value, name, pairs)
 
+    def swap(self, value, step):
+        pairs = [
+            (i * self.b + j, (i ^ step) * self.b + j) for i in range(self.a) for j in range(self.b)
+        ]
+        return lax.ppermute(value, "batch", pairs)
+
 
 def after(value, *tokens):
     return lax.optimization_barrier((value, *tokens))[0]
 
 
+def settle(jobs, *tokens, hold=()):
+    flights = tuple(tuple(job.flight) for job in jobs)
+    parts = tuple(tuple(job.parts) for job in hold)
+    landed, tokens, parts = lax.optimization_barrier((flights, tokens, parts))
+    for job, held in zip(hold, parts):
+        job.parts = list(held)
+    for job, flight in zip(jobs, landed):
+        job.flight = list(flight)
+        job.land()
+    return tokens[0] if len(tokens) == 1 else tokens
+
+
+def bit_reversed(value, bits):
+    return sum((value >> i & 1) << (bits - 1 - i) for i in range(bits))
+
+
 def spread(grid, value, axis):
-    parts = [value] + [grid.shift(value, axis, k) for k in range(1, grid.size[axis])]
-    return parts
+    return [value] + [grid.shift(value, axis, k) for k in range(1, grid.size[axis])]
 
 
 def pieces(weights, place, count, width):
@@ -274,62 +370,83 @@
     )(places, mine, theirs)
 
 
-def gather_weights(grid, places, weights, width, split, name, token=None):
-    seq = lax.axis_index("seq")
-    columns = grid.y * grid.c
-    if split:
-        value = pieces(weights, seq, columns, width)[None]
-    else:
-        core = lax.rem(seq, grid.c)
-        value = jnp.stack([pieces(weights, i * grid.c + core, columns, width) for i in range(grid.y)])
-    if token is not None:
-        value = after(value, token)
-    first = spread(grid, value, "a")
-    token = first[-1]
-    rows = value.shape[1]
-    value = jnp.stack(first, axis=1)
-    value = jnp.concatenate([v[:, None] for v in spread(grid, value, "b")], axis=1)
-    if split:
-        value = jnp.concatenate(spread(grid, value, "y"), axis=0)
-    mine = value.reshape(grid.y, grid.b * grid.a, rows, width)
-    theirs = grid.shift(mine, "c", 1)
-    shapes = [(w.shape[0] * grid.a * grid.b, w.shape[1]) for w in weights]
-    return assemble(grid, places, mine, theirs, shapes, width, split, name), token
-
-
-def _weight_grad_body(place_ref, *refs, grid, height, first, have_sum, aliased, split, blocks):
+class Gather:
+    def __init__(self, grid, places, weights, width, split, name):
+        self.grid, self.places, self.width, self.split, self.name = grid, places, width, split, name
+        self.shapes = [(w.shape[0] * grid.a * grid.b, w.shape[1]) for w in weights]
+        seq, columns = lax.axis_index("seq"), grid.y * grid.c
+        if split:
+            self.value = pieces(weights, seq, columns, width)[None]
+        else:
+            core = lax.rem(seq, grid.c)
+            self.value = jnp.stack(
+                [pieces(weights, i * grid.c + core, columns, width) for i in range(grid.y)]
+            )
+
+    def send(self, axis):
+        self.axis = axis
+        self.flight = spread(self.grid, self.value, axis)[1:]
+
+    def land(self):
+        parts = [self.value, *self.flight]
+        if self.axis == "y":
+            self.value = jnp.concatenate(parts, axis=0)
+        else:
+            self.value = jnp.stack(parts, axis=1)
+
+    def whole(self):
+        grid = self.grid
+        mine = self.value.reshape(grid.y, grid.b * grid.a, *self.value.shape[-2:])
+        theirs = grid.shift(mine, "c", 1)
+        return assemble(
+            grid, self.places, mine, theirs, self.shapes, self.width, self.split, self.name
+        )
+
+
+def _weight_grad_body(place_ref, *refs, grid, height, have_sum, aliased, split):
     left_ref, right_ref = refs[:2]
     refs = refs[2:]
     sum_ref = None
     if have_sum:
         sum_ref, refs = refs[0], refs[1:]
     refs = refs[aliased:]
-    outs, turned, product = refs[:-2], refs[-2], refs[-1]
+    direct = height % 128 == 0
+    outs, turned, natural = (refs[:-1], refs[-1], None) if direct else (refs[:-2], refs[-2], refs[-1])
     a, b = place_ref[0], place_ref[1]
     side, block = pl.program_id(0), pl.program_id(1)
 
     @pl.when((side == 0) & (block == 0))
     def _():
-        turned[...] = left_ref[...].T
-
-    product[...] = jnp.dot(turned[...], right_ref[...], preferred_element_type=F32)
+        if not direct:
+            natural[...] = left_ref[...].T
+        for step_b in range(grid.b):
+            for step_a in range(grid.a):
+                other = lax.bitwise_xor(a, jnp.int32(bit_reversed(step_a, grid.bits)))
+                owner = other * grid.b + lax.rem(b + step_b, grid.b)
+                here = pl.ds(pl.multiple_of(owner * height, height), height)
+                turned[step_b, step_a] = left_ref[:, here].T if direct else natural[here, :]
+
+    samples = turned.shape[-1]
+    half = grid.a * height
     for step_b in range(grid.b):
-        for step_a in range(grid.a):
-            owner = lax.rem(a + step_a, grid.a) * grid.b + lax.rem(b + step_b, grid.b)
-            part = product[pl.ds(pl.multiple_of(owner * height, height), height), :]
-            if have_sum:
-                part = part + sum_ref[0, step_b, step_a].astype(F32)
-            part = part.astype(BF16)
-            if split == "b":
-                outs[step_b][0, step_a] = part
-            elif split == "y":
-                for k, out in enumerate(outs):
-
-                    @pl.when(side == k)
-                    def _(out=out, part=part):
-                        out[step_b, step_a] = part
-            else:
-                outs[0][0, step_b, step_a] = part
+        part = jnp.dot(
+            turned[step_b].reshape(half, samples),
+            right_ref[...].reshape(samples, -1),
+            preferred_element_type=F32,
+        ).reshape(grid.a, height, -1)
+        if have_sum:
+            part = part + sum_ref[0, step_b].astype(F32)
+        part = part.astype(BF16)
+        if split == "b":
+            outs[step_b][0] = part
+        elif split == "y":
+            for k, out in enumerate(outs):
+
+                @pl.when(side == k)
+                def _(out=out, part=part):
+                    out[step_b] = part
+        else:
+            outs[0][0, step_b] = part
 
 
 def weight_grad(grid, places, left, right, width, core_step, total_rows, row, buffers, split, received=None, name="weight_grad", local=False, sub=None):
@@ -337,7 +454,8 @@
     height = depth // (grid.a * grid.b)
     sides = 1 if local else grid.y
     columns = 1 if local else grid.y * grid.c
-    blocks = right.shape[1] // (columns * width)
+    many = right.ndim == 5
+    blocks = right.shape[1] if many else right.shape[1] // (columns * width)
     lo, count = (0, blocks) if sub is None else sub
     first = row // height
 
@@ -346,6 +464,8 @@
             return (0, 0)
         side = lax.rem(p[2] + k, grid.y)
         core = lax.rem(p[3] + core_step, grid.c)
+        if many:
+            return (side * grid.c + core, lo + i, 0, 0, 0)
         return (0, (side * grid.c + core) * blocks + lo + i)
 
     if split == "b":
@@ -369,7 +489,7 @@
         number = 1
     in_specs = [
         pl.BlockSpec((samples, depth), lambda k, i, p: (0, 0), pipeline_mode=pl.Buffered(1)),
-        pl.BlockSpec((samples, width), right_index),
+        pl.BlockSpec((1, 1, *right.shape[2:]) if many else (samples, width), right_index),
     ]
     operands = [left, right]
     if received is not None:
@@ -382,8 +502,8 @@
             in_specs.append(pl.BlockSpec(memory_space=pl.ANY))
             operands.append(buffer)
     body = partial(
-        _weight_grad_body, grid=grid, height=height, first=first, have_sum=received is not None,
-        aliased=0 if buffers is None else len(buffers), split=split, blocks=count,
+        _weight_grad_body, grid=grid, height=height, have_sum=received is not None,
+        aliased=0 if buffers is None else len(buffers), split=split,
     )
     work = sides * count * width
     return pl.pallas_call(
@@ -393,7 +513,8 @@
             grid=(sides, count),
             in_specs=in_specs,
             out_specs=specs,
-            scratch_shapes=[pltpu.VMEM((depth, samples), BF16), pltpu.VMEM((depth, width), F32)],
+            scratch_shapes=[pltpu.VMEM((grid.b, grid.a, height, samples), BF16)]
+            + ([] if height % 128 == 0 else [pltpu.VMEM((depth, samples), BF16)]),
         ),
         out_shape=[jax.ShapeDtypeStruct(shape, BF16)] * number,
         input_output_aliases=aliases,
@@ -410,33 +531,124 @@
     return total
 
 
-def reduce_group(grid, places, pairs, width, order, name, extra=None, sub=None):
-    heights = [left.shape[1] // (grid.a * grid.b) for left, _ in pairs]
-    columns = grid.y * grid.c
-    counts = [right.shape[1] // (columns * width) if sub is None else sub[1] for _, right in pairs]
-    total = sum(h * n for h, n in zip(heights, counts))
-
-    def products(core_step, split, received):
+class Reduce:
+    def __init__(self, grid, places, pairs, width, order, name, sub=None):
+        self.grid, self.places, self.pairs, self.width = grid, places, pairs, width
+        self.axes, self.name, self.sub = tuple(order), name, sub
+        self.extra = None
+        self.heights = [left.shape[1] // (grid.a * grid.b) for left, _ in pairs]
+        columns = grid.y * grid.c
+        self.counts = [
+            right.shape[1] if right.ndim == 5 else right.shape[1] // (columns * width) if sub is None else sub[1]
+            for _, right in pairs
+        ]
+
+    def _products(self, core_step, split, received, tokens):
         buffers, row = None, 0
-        for i, ((left, right), h, n) in enumerate(zip(pairs, heights, counts)):
+        total = sum(h * n for h, n in zip(self.heights, self.counts))
+        for i, ((left, right), h, n) in enumerate(zip(self.pairs, self.heights, self.counts)):
+            if i == 0 and tokens:
+                right = after(right, *tokens)
             buffers = weight_grad(
-                grid, places, left, right, width, core_step, total, row, buffers, split, received,
-                name=f"{name}_{i}_{core_step}", sub=sub,
+                self.grid, self.places, left, right, self.width, core_step, total, row, buffers, split,
+                received, name=f"{self.name}_{i}_{core_step}", sub=self.sub,
             )
             row += h * n
         return buffers
 
-    sent = products(1, None, None)[0]
-    received = grid.shift(sent, "c", 1)
-    near = products(0, order, received)
-    for stage, axis in enumerate(("y", "b") if order == "y" else ("b", "y")):
-        if extra is not None and axis == "b":
-            near = [jnp.concatenate([p, q], axis=-2) for p, q in zip(near, extra)]
-        parts = [near[0]] + [grid.shift(near[k], axis, k) for k in range(1, grid.size[axis])]
-        following = grid.a if stage == 1 else grid.size["b" if axis == "y" else "y"]
-        near = [added([p[k] for p in parts]).astype(BF16) for k in range(following)]
-    parts = [near[0]] + [grid.shift(near[k], "a", k) for k in range(1, grid.a)]
-    return added(parts)
+    def far(self, *tokens):
+        self.parts = self._products(1, None, None, tokens)
+
+    def ship(self):
+        self.received = self.grid.shift(self.parts[0], "c", 1)
+
+    def near(self, *tokens):
+        self.parts = self._products(0, self.axes[0], self.received, tokens)
+        return self.parts[0]
+
+    def send(self, stage, *tokens):
+        grid, axis = self.grid, self.axes[stage]
+        self.stage = stage
+        if tokens:
+            self.parts = list(lax.optimization_barrier((tuple(self.parts), tokens))[0])
+        if self.extra is not None and axis == "b":
+            self.parts = [jnp.concatenate([p, q], axis=-2) for p, q in zip(self.parts, self.extra)]
+        self.flight = [grid.shift(self.parts[k], axis, k) for k in range(1, grid.size[axis])]
+
+    def land(self):
+        parts = [self.parts[0], *self.flight]
+        if self.stage == 1:
+            half = self.grid.a // 2
+            self.parts = [added([p[k * half : (k + 1) * half] for p in parts]).astype(BF16) for k in range(2)]
+        else:
+            following = self.grid.size[self.axes[1]]
+            self.parts = [added([p[k] for p in parts]).astype(BF16) for k in range(following)]
+
+
+class Bundle:
+    def __init__(self, *jobs):
+        self.jobs, self.stage = jobs, 0
+        self.grid = jobs[0].grid
+        self.near, self.away = (
+            jnp.concatenate([job.parts[k] for job in jobs], axis=1) for k in range(2)
+        )
+
+    def send(self):
+        self.flight = [self.grid.swap(self.away, 1 << self.stage)]
+
+    def land(self):
+        total = [self.near, self.flight[0]]
+        self.stage += 1
+        if self.stage < self.grid.bits:
+            half = self.near.shape[0] // 2
+            self.near, self.away = (
+                added([part[k * half : (k + 1) * half] for part in total]).astype(BF16)
+                for k in range(2)
+            )
+            return
+        row = 0
+        for job in self.jobs:
+            height = job.parts[0].shape[1]
+            job.result = added([part[0, row : row + height] for part in total])
+            row += height
+
+
+def gather_everywhere(shard):
+    rows = shard.shape[0] // lax.axis_size("seq")
+    part = lax.dynamic_slice_in_dim(shard, lax.axis_index("seq") * rows, rows, 0)
+    return lax.all_gather(part, ("batch", "seq"), axis=0, tiled=True)
+
+
+class Share:
+    def __init__(self, grid, value):
+        self.grid, self.value = grid, value
+
+    def send(self, axis):
+        self.flight = spread(self.grid, self.value, axis)[1:]
+
+    def land(self):
+        self.value = added([self.value, *self.flight])
+
+
+class Collect:
+    def __init__(self, grid, places, shard):
+        self.grid, self.places, self.shape, self.value = grid, places, shard.shape, shard[None, None]
+
+    def send(self, axis):
+        self.axis = axis
+        self.flight = spread(self.grid, self.value, axis)[1:]
+
+    def land(self):
+        self.value = jnp.concatenate([self.value, *self.flight], axis=1 if self.axis == "a" else 0)
+
+    def whole(self):
+        grid, places = self.grid, self.places
+        value = self.value.reshape(grid.b * grid.a, *self.shape)
+        owner = jnp.arange(grid.a * grid.b, dtype=jnp.int32)
+        step_a = (places[0] - owner // grid.b) % grid.a
+        step_b = (places[1] - owner % grid.b) % grid.b
+        value = jnp.take(value, step_b * grid.a + step_a, axis=0)
+        return value.transpose(1, 0, 2).reshape(self.shape[0], -1)
 
 
 def layer_norm(values, scale_row, shift_row):
@@ -511,17 +723,33 @@
     return (times_transpose(grad_low, weight), grad_low)
 
 
-def ffn_forward(values, scale_row, shift_row, weight_in, weight_out):
+def ffn_enter(values, scale_row, shift_row, weight_in):
     normed_low = layer_norm(values, scale_row, shift_row).astype(jnp.bfloat16)
     hidden_pre = matmul_rows(normed_low, weight_in)
     hidden_low = jax.nn.silu(hidden_pre).astype(jnp.bfloat16)
-    return (matmul_rows(hidden_low, weight_out), (normed_low, hidden_pre, hidden_low))
+    return (normed_low, hidden_pre.astype(jnp.bfloat16), hidden_low)
+
+
+def ffn_forward(values, scale_row, shift_row, weight_in, weight_out):
+    saved = ffn_enter(values, scale_row, shift_row, weight_in)
+    return (matmul_rows(saved[2], weight_out), saved)
+
+
+def ffn_backward_exit(grad_rows, weight_out, saved_parts):
+    grad_hidden, grad_out_low = linear_back(grad_rows, weight_out)
+    silu_value, silu_back = jax.vjp(jax.nn.silu, saved_parts[1].astype(jnp.float32))
+    return (silu_back(grad_hidden)[0].astype(jnp.bfloat16), grad_out_low)
+
+
+def ffn_backward_entry(grad_pre_low, values, scale_row, shift_row, weight_in):
+    norm_value, norm_back = jax.vjp(layer_norm, values, scale_row, shift_row)
+    return norm_back(times_transpose(grad_pre_low, weight_in))
 
 
 def ffn_backward(grad_rows, values, scale_row, shift_row, weight_in, weight_out, saved_parts):
     normed_low, hidden_pre, hidden_low = saved_parts
     grad_hidden, grad_out_low = linear_back(grad_rows, weight_out)
-    silu_value, silu_back = jax.vjp(jax.nn.silu, hidden_pre)
+    silu_value, silu_back = jax.vjp(jax.nn.silu, hidden_pre.astype(jnp.float32))
     grad_pre = silu_back(grad_hidden)[0]
     grad_normed, grad_pre_low = linear_back(grad_pre, weight_in)
     norm_value, norm_back = jax.vjp(layer_norm, values, scale_row, shift_row)
@@ -536,17 +764,6 @@
             value = value + lax.ppermute(value, axis, [(i, i ^ step) for i in range(size)])
             step *= 2
     return value
-
-
-def gather_small(grid, places, shard):
-    value = jnp.stack(spread(grid, shard, "a"))
-    value = jnp.concatenate(spread(grid, value[None], "b"))
-    value = value.reshape(grid.b * grid.a, *shard.shape)
-    owner = jnp.arange(grid.a * grid.b, dtype=jnp.int32)
-    step_a = (places[0] - owner // grid.b) % grid.a
-    step_b = (places[1] - owner % grid.b) % grid.b
-    value = jnp.take(value, step_b * grid.a + step_a, axis=0)
-    return value.transpose(1, 0, 2).reshape(shard.shape[0], -1)
 
 
 def per_device(
@@ -575,57 +792,63 @@
     discrete_label_adjoint,
 ):
     places = grid.places()
-    small_all = gather_small(
+    small = Collect(
         grid,
         places,
         jnp.concatenate([normalizer_affine_rows, channelwise_filter_coefficients], axis=0),
     )
     vector_rows = normalizer_affine_rows.shape[0]
-    vectors_all, depth_all = small_all[:vector_rows], small_all[vector_rows:]
-    piece_width = acoustic_sequence.shape[2] // (grid.y * grid.c)
-    gather = partial(gather_weights, grid, places)
-    (macaron_in_all,), token = gather(
-        [opening_dense_entry_projection], piece_width, True, "gather_opening_entry"
-    )
-    (macaron_out_all,), token = gather(
-        [opening_dense_exit_projection], piece_width, True, "gather_opening_exit", token
-    )
-    (query_all, key_all, value_all, pos_all), token = gather(
+    model_width = acoustic_sequence.shape[2]
+    piece_width = model_width // (grid.y * grid.c)
+    gather = partial(Gather, grid, places)
+    first = gather([opening_dense_entry_projection], piece_width, True, "gather_opening_entry")
+    second = gather([opening_dense_exit_projection], piece_width, True, "gather_opening_exit")
+    third = gather(
         [request_projection, lookup_projection, content_projection_kernel, relative_offset_projection],
         piece_width,
-        True,
+        False,
         "gather_attention",
-        token,
-    )
-    (out_all, conv_in_all, conv_out_all, quant_all, codebook_all), token = gather(
-        [
-            mixing_exit_projection,
-            unit_kernel_before_gating,
-            unit_kernel_after_normalizing,
+    )
+    first.send("a")
+    small.send("a")
+    settle([first, small])
+    first.send("b")
+    small.send("b")
+    second.send("a")
+    settle([first, small, second])
+    conv_shards, entry_shard, exit_shard, quant_shard, lexicon_shard, first.value = lax.optimization_barrier(
+        (
+            (mixing_exit_projection, unit_kernel_after_normalizing, unit_kernel_before_gating),
+            closing_dense_entry_projection,
+            closing_dense_exit_projection,
             discretizer_score_projection,
             lexicon_vectors,
-        ],
-        piece_width,
-        True,
-        "gather_convolution",
-        token,
-    )
-    (closing_in_all, closing_out_all), token = gather(
-        [closing_dense_entry_projection, closing_dense_exit_projection],
-        piece_width,
-        False,
-        "gather_closing",
-        token,
-    )
+            first.value,
+        )
+    )
+    convolution_all = gather_everywhere(jnp.concatenate(conv_shards, axis=1))
+    out_all, conv_out_all, conv_in_all = jnp.split(
+        convolution_all, [model_width, 2 * model_width], axis=1
+    )
+    closing_in_all = gather_everywhere(entry_shard)
+    closing_out_all = gather_everywhere(exit_shard)
+    quantizer_all = gather_everywhere(jnp.concatenate([quant_shard, lexicon_shard], axis=1))
+    small_all = small.whole()
+    vectors_all, depth_all = small_all[:vector_rows], small_all[vector_rows:]
+    first.send("y")
+    second.send("b")
+    third.send("a")
+    settle([first, second, third])
     groups, local_len, model_width = acoustic_sequence.shape
     seq_count = lax.axis_size("seq")
     seq_place = lax.axis_index("seq")
     full_len = local_len * seq_count
-    entries = codebook_all.shape[0]
+    entries = lexicon_vectors.shape[0] * grid.a * grid.b
     total_rows = groups * local_len
     local_width = model_width // seq_count
     kernel_size = depth_all.shape[0]
     rim_width = kernel_size // 2
+    height = model_width // (grid.a * grid.b)
     params_f = vectors_all.astype(jnp.float32)
     depth_f = depth_all.astype(jnp.float32)
     positions = seq_place * local_len + jnp.arange(local_len, dtype=jnp.int32)
@@ -633,6 +856,58 @@
     valid_rows = valid_mask.reshape(total_rows, 1)
     inputs_low = acoustic_sequence.reshape(total_rows, model_width)
     inputs_f = inputs_low.astype(jnp.float32)
+    second.send("y")
+    third.send("b")
+    (macaron_in_all,) = first.whole()
+    macaron_saved = ffn_enter(inputs_f, params_f[0], params_f[5], macaron_in_all)
+    macaron_hidden = settle([second, third], macaron_saved[2])
+    macaron_saved = (*macaron_saved[:2], macaron_hidden)
+    (macaron_out_all,) = second.whole()
+    query_all, key_all, value_all, pos_all = third.whole()
+    macaron_value = matmul_rows(macaron_hidden, macaron_out_all)
+    first_mid = inputs_f + 0.5 * macaron_value
+    attn_normed = layer_norm(first_mid, params_f[1], params_f[6]).astype(jnp.bfloat16)
+    stacked = project_heads(attn_normed, [query_all, key_all, value_all], groups, seq_count)
+    by_heads = lax.all_to_all(stacked, "seq", split_axis=0, concat_axis=0, tiled=True)
+    table_low = position_table(full_len, model_width)
+    pos_columns = lax.dynamic_slice_in_dim(pos_all, seq_place * local_width, local_width, 1)
+    position_low = matmul_rows(table_low, pos_columns).astype(jnp.bfloat16)
+    biases = lax.dynamic_slice_in_dim(params_f[12:14], seq_place * local_width, local_width, 1)
+    by_heads, position_low = lax.optimization_barrier((by_heads, position_low))
+    attended_low, probs = attend_forward(by_heads, position_low, biases, utterance_durations)
+    back_time = lax.all_to_all(
+        attended_low, "seq", split_axis=0, concat_axis=0, tiled=True
+    )
+    attended_rows = back_time.transpose(1, 2, 0, 3).reshape(total_rows, model_width)
+    second_mid = first_mid + matmul_rows(attended_rows, out_all)
+    conv_normed = layer_norm(second_mid, params_f[2], params_f[7]).astype(jnp.bfloat16)
+    gated_rows = matmul_rows(conv_normed, conv_in_all)
+    glu_low = (
+        (valid_rows * glu_gate(gated_rows))
+        .astype(jnp.bfloat16)
+        .reshape(groups, local_len, model_width)
+    )
+    padded_glu = extended(glu_low, (("seq", 1),), rim_width)
+    conv_value = depth_conv(padded_glu, depth_f, local_len).reshape(total_rows, model_width)
+    masked_conv = valid_rows * conv_value
+    sums = sum_everywhere(
+        jnp.stack(
+            [
+                jnp.sum(masked_conv, axis=0),
+                jnp.sum(masked_conv * conv_value, axis=0),
+                jnp.broadcast_to(jnp.sum(valid_mask), (model_width,)),
+            ]
+        )
+    )
+    sum_first, sum_second, count_all = sums[0], sums[1], sums[2]
+    bound_norm = partial(batch_norm, count_all=count_all)
+    normalized = bound_norm(conv_value, sum_first, sum_second, params_f[10], params_f[11])
+    act_low = jax.nn.silu(normalized).astype(jnp.bfloat16)
+    third_mid = second_mid + matmul_rows(act_low, conv_out_all)
+    closing_value, closing_saved = ffn_forward(
+        third_mid, params_f[3], params_f[8], closing_in_all, closing_out_all
+    )
+    quant_all, codebook_all = quantizer_all[:, :entries], quantizer_all[:, entries:]
     quant_logits = matmul_rows(inputs_low, quant_all)
     scaled_logits = (
         quant_logits
@@ -646,64 +921,15 @@
     codes_value = valid_rows * (
         matmul_rows(one_hot, codebook_all) + matmul_rows(soft_low, codebook_all)
     )
-    macaron_value, macaron_saved = ffn_forward(
-        inputs_f, params_f[0], params_f[5], macaron_in_all, macaron_out_all
-    )
-    first_mid = inputs_f + 0.5 * macaron_value
-    attn_normed = layer_norm(first_mid, params_f[1], params_f[6]).astype(jnp.bfloat16)
-    stacked = (
-        jnp.stack(
-            [
-                matmul_rows(attn_normed, query_all),
-                matmul_rows(attn_normed, key_all),
-                matmul_rows(attn_normed, value_all),
-            ]
-        )
-        .astype(jnp.bfloat16)
-        .reshape(3, groups, local_len, model_width)
-    )
-    by_heads = lax.all_to_all(stacked, "seq", split_axis=3, concat_axis=2, tiled=True)
-    table_low = position_table(full_len, model_width)
-    pos_columns = lax.dynamic_slice_in_dim(pos_all, seq_place * local_width, local_width, 1)
-    position_low = matmul_rows(table_low, pos_columns).astype(jnp.bfloat16)
-    biases = lax.dynamic_slice_in_dim(params_f[12:14], seq_place * local_width, local_width, 1)
-    attended_low, probs = attend_forward(by_heads, position_low, biases, utterance_durations)
-    back_time = lax.all_to_all(
-        attended_low,
-        "seq",
-        split_axis=1,
-        concat_axis=2,
-        tiled=True,
-    )
-    attended_rows = back_time.reshape(total_rows, model_width)
-    second_mid = first_mid + matmul_rows(attended_rows, out_all)
-    conv_normed = layer_norm(second_mid, params_f[2], params_f[7]).astype(jnp.bfloat16)
-    gated_rows = matmul_rows(conv_normed, conv_in_all)
-    glu_low = (
-        (valid_rows * glu_gate(gated_rows))
-        .astype(jnp.bfloat16)
-        .reshape(groups, local_len, model_width)
-    )
-    padded_glu = extended(glu_low, (("seq", 1),), rim_width)
-    conv_value = depth_conv(padded_glu, depth_f, local_len).reshape(total_rows, model_width)
-    masked_conv = valid_rows * conv_value
-    sums = sum_everywhere(
-        jnp.stack(
-            [
-                jnp.sum(masked_conv, axis=0),
-                jnp.sum(masked_conv * conv_value, axis=0),
-                jnp.broadcast_to(jnp.sum(valid_mask), (model_width,)),
-            ]
-        )
-    )
-    sum_first, sum_second, count_all = sums[0], sums[1], sums[2]
-    bound_norm = partial(batch_norm, count_all=count_all)
-    normalized = bound_norm(conv_value, sum_first, sum_second, params_f[10], params_f[11])
-    act_low = jax.nn.silu(normalized).astype(jnp.bfloat16)
-    third_mid = second_mid + matmul_rows(act_low, conv_out_all)
-    closing_value, closing_saved = ffn_forward(
-        third_mid, params_f[3], params_f[8], closing_in_all, closing_out_all
-    )
+    grad_codes = (
+        valid_rows * discrete_label_adjoint.reshape(total_rows, model_width).astype(jnp.float32)
+    ).astype(jnp.bfloat16)
+    grad_soft = times_transpose(grad_codes, codebook_all)
+    rescaled_derivative = relaxed_assignments * (
+        grad_soft - jnp.sum(grad_soft * relaxed_assignments, axis=-1, keepdims=True)
+    )
+    score_derivative_lowprecision = (rescaled_derivative / softmax_heat).astype(jnp.bfloat16)
+    grad_quant_in = times_transpose(score_derivative_lowprecision, quant_all)
     fourth_mid = third_mid + 0.5 * closing_value
     final_value, final_back = jax.vjp(layer_norm, fourth_mid, params_f[4], params_f[9])
     output = (valid_rows * final_value).astype(jnp.bfloat16).reshape(groups, local_len, model_width)
@@ -720,6 +946,13 @@
         closing_saved,
     )
     grad_third = grad_fourth + grad_closing
+    close_normed, close_pre, close_hidden = closing_saved
+    reduce = partial(Reduce, grid, places)
+    closing_job = reduce(
+        [(close_hidden, close_out_low), (close_normed, close_pre_low)], piece_width, "by", "closing"
+    )
+    closing_job.far()
+    closing_job.ship()
     grad_act, grad_third_low = linear_back(grad_third, conv_out_all)
     silu_value, silu_back = jax.vjp(jax.nn.silu, normalized)
     grad_normalized = silu_back(grad_act)[0]
@@ -729,7 +962,26 @@
     grad_conv_direct, part_first, part_second, grad_bn_scale, grad_bn_shift = norm_back(
         grad_normalized
     )
-    total_first, total_second = sum_everywhere(jnp.stack([part_first, part_second]))
+    totals = sum_everywhere(jnp.stack([part_first, part_second]))
+    chosen_soft = one_hot + soft_low
+    early_job = reduce(
+        [
+            (act_low, grad_third_low),
+            (inputs_low, score_derivative_lowprecision),
+            (chosen_soft, grad_codes),
+        ],
+        piece_width,
+        "yb",
+        "early",
+    )
+    early_job.far()
+    early_job.ship()
+    closing_job.near()
+    early_job.near()
+    totals = settle([], totals, hold=[closing_job, early_job])
+    closing_job.send(0)
+    early_job.send(0)
+    total_first, total_second = totals[0], totals[1]
     grad_conv = grad_conv_direct + valid_rows * (total_first + 2.0 * conv_value * total_second)
     grad_conv_low = grad_conv.astype(jnp.bfloat16).reshape(groups, local_len, model_width)
     padded_grad = extended(grad_conv_low, (("seq", 1),), rim_width)
@@ -752,51 +1004,77 @@
     conv_norm_value, conv_norm_back = jax.vjp(layer_norm, second_mid, params_f[2], params_f[7])
     grad_from_conv, scale_two, shift_two = conv_norm_back(grad_conv_normed)
     grad_second = grad_third + grad_from_conv
-    grad_attended, grad_second_low = linear_back(grad_second, out_all)
-    grad_heads = lax.all_to_all(
-        grad_second_low_heads(grad_attended, groups, local_len, model_width),
-        "seq",
-        split_axis=2,
-        concat_axis=1,
-        tiled=True,
-    )
-
+    grad_second_low = grad_second.astype(jnp.bfloat16)
+    grad_attended = unproject_heads(grad_second_low, out_all, groups, seq_count)
+    grad_heads = lax.all_to_all(grad_attended, "seq", split_axis=0, concat_axis=0, tiled=True)
+
+    middle_job = reduce(
+        [(conv_normed, grad_gated_low), (attended_rows, grad_second_low)],
+        piece_width,
+        "by",
+        "middle",
+    )
+    middle_job.far()
+    grad_heads = settle([], grad_heads, hold=[middle_job])
+    middle_job.ship()
     grad_stack, grad_position_low, grad_biases = attend_backward(
         probs, by_heads, grad_heads, position_low, biases
     )
-    grad_time = lax.all_to_all(grad_stack, "seq", split_axis=2, concat_axis=3, tiled=True).reshape(
-        3, total_rows, model_width
-    )
-    grad_attn_normed = (
-        times_transpose(grad_time[0], query_all)
-        + times_transpose(grad_time[1], key_all)
-        + times_transpose(grad_time[2], value_all)
-    )
+    grad_stack = settle([closing_job, early_job], grad_stack)
+    grad_time = lax.all_to_all(grad_stack, "seq", split_axis=0, concat_axis=0, tiled=True)
+    position_parts = weight_grad(
+        grid, places, table_low, grad_position_low, piece_width, 0, height, 0, None, "b",
+        name="position_grad", local=True,
+    )
+    middle_job.near()
+    grad_time, *position_parts = settle([], grad_time, *position_parts, hold=[middle_job])
+    closing_job.send(1)
+    early_job.send(1)
+    middle_job.send(0)
+    grad_attn_normed = join_heads(grad_time, [query_all, key_all, value_all])
     attn_norm_value, attn_norm_back = jax.vjp(layer_norm, first_mid, params_f[1], params_f[6])
     grad_from_attn, scale_one, shift_one = attn_norm_back(grad_attn_normed)
     grad_first = grad_second + grad_from_attn
+    attention_job = reduce(
+        [(attn_normed, grad_time)], piece_width, "yb", "attention"
+    )
+    attention_job.extra = [part[0] for part in position_parts]
+    attention_job.far()
+    attention_job.ship()
     content_full, position_full = lax.dynamic_update_slice_in_dim(
         jnp.zeros((2, model_width), jnp.float32), grad_biases, seq_place * local_width, 1
     )
-    grad_macaron, scale_zero, shift_zero, mac_pre_low, mac_out_low = ffn_backward(
-        0.5 * grad_first,
-        inputs_f,
-        params_f[0],
-        params_f[5],
-        macaron_in_all,
-        macaron_out_all,
-        macaron_saved,
+    mac_normed, mac_pre, mac_hidden = macaron_saved
+    mac_out_low = (0.5 * grad_first).astype(jnp.bfloat16)
+    macaron_out_job = reduce([(mac_hidden, mac_out_low)], piece_width, "by", "opening_exit")
+    macaron_out_job.far()
+    macaron_out_job.ship()
+    attention_job.near()
+    macaron_out_job.near()
+    mac_out_low = settle(
+        [closing_job, early_job], mac_out_low, hold=[attention_job, macaron_out_job]
+    )
+    first_tails = Bundle(closing_job, early_job)
+    first_tails.send()
+    attention_job.send(0)
+    mac_pre_low, mac_out_low = ffn_backward_exit(mac_out_low, macaron_out_all, macaron_saved)
+    halves = mac_pre_low.shape[1] // model_width // 2
+    macaron_in_jobs = [
+        reduce([(mac_normed, mac_pre_low)], piece_width, order, name, sub=(i * halves, halves))
+        for i, (order, name) in enumerate((("yb", "opening_entry"), ("by", "opening_entry_more")))
+    ]
+    for job in macaron_in_jobs:
+        job.far()
+    mac_pre_low = settle([middle_job, first_tails], mac_pre_low, hold=macaron_in_jobs)
+    for job in macaron_in_jobs:
+        job.ship()
+    first_tails.send()
+    middle_job.send(1)
+    macaron_out_job.send(0)
+    grad_macaron, scale_zero, shift_zero = ffn_backward_entry(
+        mac_pre_low, inputs_f, params_f[0], params_f[5], macaron_in_all
     )
     grad_layer_in = grad_first + grad_macaron
-    grad_codes = (
-        valid_rows * discrete_label_adjoint.reshape(total_rows, model_width).astype(jnp.float32)
-    ).astype(jnp.bfloat16)
-    grad_soft = times_transpose(grad_codes, codebook_all)
-    rescaled_derivative = relaxed_assignments * (
-        grad_soft - jnp.sum(grad_soft * relaxed_assignments, axis=-1, keepdims=True)
-    )
-    score_derivative_lowprecision = (rescaled_derivative / softmax_heat).astype(jnp.bfloat16)
-    grad_quant_in = times_transpose(score_derivative_lowprecision, quant_all)
     frames_grad = (
         (grad_layer_in + grad_quant_in).astype(jnp.bfloat16).reshape(groups, local_len, model_width)
     )
@@ -818,48 +1096,54 @@
             position_full,
         ]
     )
-    small_sums = sum_everywhere(jnp.concatenate([vectors_grad, grad_depth], axis=0))
+    small = Share(grid, jnp.concatenate([vectors_grad, grad_depth], axis=0))
+    small.send("c")
+    small.land()
+    for job in macaron_in_jobs:
+        job.near()
+    small.value = settle(
+        [first_tails, middle_job, attention_job, macaron_out_job],
+        small.value,
+        hold=macaron_in_jobs,
+    )
+    for job in macaron_in_jobs:
+        job.send(0)
+    attention_job.send(1)
+    macaron_out_job.send(1)
+    middle_tails = Bundle(middle_job)
+    middle_tails.send()
+    small.send("y")
+    settle([small, middle_tails, attention_job, macaron_out_job, *macaron_in_jobs])
+    for job in macaron_in_jobs:
+        job.send(1)
+    middle_tails.send()
+    late_tails = Bundle(attention_job, macaron_out_job)
+    late_tails.send()
+    small.send("b")
+    settle([small, middle_tails, late_tails, *macaron_in_jobs])
+    late_tails.send()
+    last_tails = Bundle(*macaron_in_jobs)
+    last_tails.send()
+    small.send("a")
+    settle([small, last_tails, late_tails])
+    last_tails.send()
+    settle([last_tails])
     small_width = model_width // (grid.a * grid.b)
     small_sums = lax.dynamic_slice_in_dim(
-        small_sums, lax.axis_index("batch") * small_width, small_width, 1
+        small.value, lax.axis_index("batch") * small_width, small_width, 1
     )
     vectors_sum, depth_sum = small_sums[:vector_rows], small_sums[vector_rows:]
-    mac_normed, mac_pre, mac_hidden = macaron_saved
-    close_normed, close_pre, close_hidden = closing_saved
-    reduce = partial(reduce_group, grid, places)
-    height = model_width // (grid.a * grid.b)
-    closing_out_sum = reduce([(close_hidden, close_out_low)], piece_width, "y", "closing_exit")
-    closing_in_sum = reduce([(close_normed, close_pre_low)], piece_width, "b", "closing_entry")
-    chosen_soft = one_hot + soft_low
-    first_sums = reduce(
-        [
-            (inputs_low, score_derivative_lowprecision),
-            (chosen_soft, grad_codes),
-            (act_low, grad_third_low),
-        ],
-        piece_width,
-        "y",
-        "quantizer",
-    )
-    quant_sum, codebook_sum, conv_out_sum = (first_sums[i * height : (i + 1) * height] for i in range(3))
-    second_sums = reduce(
-        [(conv_normed, grad_gated_low), (attended_rows, grad_second_low)], piece_width, "b", "convolution"
-    )
-    conv_in_sum, out_sum = second_sums[: 2 * height], second_sums[2 * height :]
-    position_parts = weight_grad(
-        grid, places, table_low, grad_position_low, piece_width, 0, height, 0, None, "b",
-        name="position_grad", local=True,
-    )
-    third_sums = reduce(
-        [(attn_normed, grad_time[i]) for i in range(3)],
-        piece_width,
-        "y",
-        "attention",
-        extra=[part[0] for part in position_parts],
-    )
-    query_sum, key_sum, value_sum, pos_sum = (third_sums[i * height : (i + 1) * height] for i in range(4))
-    macaron_out_sum = reduce([(mac_hidden, mac_out_low)], piece_width, "b", "opening_exit")
-    macaron_in_sum = reduce([(mac_normed, mac_pre_low)], piece_width, "y", "opening_entry")
+
+    def rows_of(job, count):
+        return (job.result[i * height : (i + 1) * height] for i in range(count))
+
+    exit_rows = close_hidden.shape[1] // (grid.a * grid.b)
+    closing_out_sum, closing_in_sum = closing_job.result[:exit_rows], closing_job.result[exit_rows:]
+    conv_out_sum, quant_sum, codebook_sum = rows_of(early_job, 3)
+    conv_in_sum, out_sum = middle_job.result[: 2 * height], middle_job.result[2 * height :]
+    query_sum, key_sum, value_sum, pos_sum = rows_of(attention_job, 4)
+    macaron_out_sum = macaron_out_job.result
+    macaron_in_sum = jnp.concatenate([job.result for job in macaron_in_jobs])
 
     def side_by_side(blocks):
         return jnp.concatenate(
@@ -891,10 +1175,6 @@
         closing_in_sum,
         closing_out_sum,
     )
-
-
-def grad_second_low_heads(grad_attended, groups, local_len, model_width):
-    return grad_attended.astype(jnp.bfloat16).reshape(groups, local_len, model_width)
 
 
 def solution(mesh):

time: 1130 us -> 986 us (0.87)
  local copies, waits for them, and re-layouts: 97.3 us -> 53.1 us
  other arithmetic: 122 us -> 83 us
  starting transfers between devices: 137 us -> 103 us
  Pallas kernels: 234 us -> 215 us
  between operations: 3.63 us -> 16.8 us
    ppermute x75 -> x48, waiting for transfers between devices: 347 us -> 216 us  [shift(): return lax.ppermute(value, name, pairs)]
    ppermute x0 -> x8, waiting for transfers between devices: none -> 65.4 us  [swap(): return lax.ppermute(value, 'batch', pairs)]
    all_to_all x4, waiting for transfers between devices: 28.9 us -> 79.3 us  [the longest x1 41.6 us: per_device(): lax.all_to_all(stacked, 'seq', split_axis=0, concat_axis=0, tiled=True)]
    ppermute x75 -> x48, starting transfers between devices: 93.2 us -> 50.5 us  [shift(): return lax.ppermute(value, name, pairs)]
    pallas_call x5 -> x3, Pallas kernels: 52.5 us -> 26.9 us  [assemble(): pl.pallas_call(partial(_assemble_body, grid=grid, plan=plan, split=split)...]
    concatenate x11 -> x10, other arithmetic: 31.2 us -> 9.62 us  [the longest x2 7.09 us: land(): self.value = jnp.concatenate(parts, axis=0)]
    all_to_all x6 -> x0, local copies, waits for them, and re-layouts: 18.4 us -> none  [the longest x2 8.64 us: per_device(): lax.all_to_all(stacked, 'seq', split_axis=3, concat_axis=2, tiled=True)]
    pallas_call x0 -> x3, Pallas kernels: none -> 14.9 us  [the longest x1 6.54 us: project_heads(): pl.pallas_call(_project_body, grid=(parts,), in_specs=[pl.BlockSpec((rows...]
  transfers between devices with their start and end apart: 98 -> 78, of which waited for: 41 -> 39; matrix products, arithmetic and copies ran while one was open for 22% -> 20% of each run, Pallas kernels for 20% -> 19%
where the time goes in v3:
time: 986 us; the launch traced here: 981 us
  waiting for transfers between devices  397 us (40%)
  Pallas kernels  215 us (22%)
  matrix products  112 us (11%)
  starting transfers between devices  103 us (10%)
  other arithmetic  83 us (8%)
  local copies, waits for them, and re-layouts  53.1 us (5%)
  between operations  16.8 us (2%)
    ppermute x48, waiting for transfers between devices, shift(): return lax.ppermute(value, name, pairs)  216 us
    pallas_call x23, Pallas kernels, weight_grad(): pl.pallas_call(body, grid_spec=pltpu.PrefetchScalarGridSpec(num_scalar_pr...  119 us
    ppermute x8, waiting for transfers between devices, swap(): return lax.ppermute(value, 'batch', pairs)  65.4 us
    dot_general x11, matrix products, matmul_rows(): return jnp.dot(left_side, right_side, preferred_element_type=jnp.float32)  56.9 us
    dot_general x8, matrix products, times_transpose(): lax.dot_general(left_side, right_side, (((1,), (1,)), ((), ())), preferre...  55.2 us
    ppermute x48, starting transfers between devices, shift(): return lax.ppermute(value, name, pairs)  50.5 us
    all_to_all x1, waiting for transfers between devices, per_device(): lax.all_to_all(stacked, 'seq', split_axis=0, concat_axis=0, tiled=True)  41.6 us
    unnamed x291, local copies, waits for them, and re-layouts  36.5 us
  transfers between devices with their start and end apart: 78, of which 39 were waited for; matrix products, arithmetic and copies ran while one was open for 20% of the time, Pallas kernels for 19%

profile of v3, /device:TPU:0, one launch (start us, length us, event | category | flops | bytes accessed | tf_op | source)
XLA Modules:
  0.0 980.6 jit_solution(10567689220595274585)
XLA Ops:
  17.1 14.3 %collective-permute-done.3 = bf16[1,1,19,128]{3,2,1,0:T(8,128)(2,1)S(1)} collective-permute-done((bf16[1,1,19,128]{3,2,1,0:T(8,128)(2,1)S(1)}, bf16[1,1,19,128]{3,2,1,0:T(8,128)(2,1)S(1)}, u32[]{:S(2)}, u32[]{:S(2)}) %collective-permute-start.3) | collective-permute-done | bytes 4896 | tf_op jit(solution)/shard_map/ppermute | solution.py:288
  31.4 5.7 collective-permute-done.4
  47.5 6.1 collective-permute-done.10
  53.6 4.9 collective-permute-done.8
  58.5 7.2 collective-permute-done.9
  79.9 18.0 %collective-permute-done.13 = bf16[2,512,256]{2,1,0:T(8,128)(2,1)S(1)} collective-permute-done((bf16[2,512,256]{2,1,0:T(8,128)(2,1)S(1)}, bf16[2,512,256]{2,1,0:T(8,128)(2,1)S(1)}, u32[]{:S(2)}, u32[]{:S(2)}) %collective-permute-start.13) | collective-permute-done | bytes 524320 | tf_op jit(solution)/shard_map/ppermute | solution.py:288
  97.9 19.2 %collective-permute-done.14 = bf16[2,512,256]{2,1,0:T(8,128)(2,1)S(1)} collective-permute-done((bf16[2,512,256]{2,1,0:T(8,128)(2,1)S(1)}, bf16[2,512,256]{2,1,0:T(8,128)(2,1)S(1)}, u32[]{:S(2)}, u32[]{:S(2)}) %collective-permute-start.14) | collective-permute-done | bytes 524320 | tf_op jit(solution)/shard_map/ppermute | solution.py:288
  118.0 5.2 pad_maximum_fusion
  131.7 9.6 gather_opening_entry.1
  141.3 10.4 %multiply_convert_fusion.1 = (bf16[512,4096]{1,0:T(8,128)(2,1)S(1)}, bf16[512,4096]{1,0:T(8,128)(2,1)}) fusion(bf16[512,1024]{1,0:T(8,128)(2,1)S(1)} %fusion.22.refs_0_, bf16[1024,4096]{1,0:T(8,128)(2,1)} %gather_opening_entry.1), kind=kOutput, calls=%fused_computation.21 | convolution fusion | flops 4307550208 | bytes 17825792 | tf_op jit(solution)/shard_map/dot_general | solution.py:706
  151.7 39.8 %collective-permute-done.17 = bf16[2,4,512,256]{3,2,0,1:T(8,128)(2,1)} collective-permute-done((bf16[2,4,512,256]{3,2,0,1:T(8,128)(2,1)S(1)}, bf16[2,4,512,256]{3,2,0,1:T(8,128)(2,1)}, u32[]{:S(2)}, u32[]{:S(2)}) %collective-permute-start.17) | collective-permute-done | bytes 2097184 | tf_op jit(solution)/shard_map/ppermute | solution.py:288
  203.9 8.6 gather_attention.1
  212.5 8.7 gather_opening_exit.1
  221.2 7.0 fusion.179
  229.5 6.5 project_heads.1
  237.0 4.8 all-to-all-start
  249.2 41.6 %all-to-all-done.q_ref.k_ref.v_ref = bf16[4,3,2,256,256]{4,3,2,1,0:T(8,128)(2,1)} async-done(((bf16[4,3,2,256,256]{4,3,2,1,0:T(8,128)(2,1)}), bf16[4,3,2,256,256]{4,3,2,1,0:T(8,128)(2,1)}, u32[]{:S(2)}, u32[]{:S(2)}) %all-to-all-start) | async-done | bytes 3145760 | tf_op jit(solution)/shard_map/all_to_all | solution.py:871
  290.8 21.0 %attend_forward.1 = (bf16[4,2,256,256]{3,2,1,0:T(8,128)(2,1)}, bf16[2,2,1024,1024]{3,2,1,0:T(8,128)(2,1)}) custom-call(s32[2]{0:T(128)S(1)} %copy-done.47, bf16[4,3,2,256,256]{4,3,2,1,0:T(8,128)(2,1)} %all-to-all-done.q_ref.k_ref.v_ref, bf16[4,3,2,256,256]{4,3,2,1,0:T(8,128)(2,1)} %all-to-all-done.q_ref.k_ref.v_ref, ...), custom_call_target="tpu_custom_call" | custom-call | flops 3489660928 | bytes 13631488 | tf_op jit(solution)/shard_map/attend_forward/pallas_call | solution.py:48
  316.9 12.9 %all-to-all-done.1 = bf16[4,2,256,256]{3,2,1,0:T(8,128)(2,1)S(1)} async-done(((bf16[4,2,256,256]{3,2,1,0:T(8,128)(2,1)}), bf16[4,2,256,256]{3,2,1,0:T(8,128)(2,1)S(1)}, u32[]{:S(2)}, u32[]{:S(2)}) %all-to-all-start.1) | async-done | bytes 1048608 | tf_op jit(solution)/shard_map/all_to_all | solution.py:878
  330.9 4.0 fusion.180
  375.7 10.4 %multiply_convert_fusion = (bf16[512,4096]{1,0:T(8,128)(2,1)}, bf16[512,4096]{1,0:T(8,128)(2,1)}) fusion(bf16[512,1024]{1,0:T(8,128)(2,1)S(1)} %add_convert_fusion.7.refs_0_, bf16[1024,4096]{1,0:T(8,128)(2,1)} %all-gather.7.cloned.1.call-done), kind=kOutput, calls=%fused_computation.19 | convolution fusion | flops 4307550208 | bytes 17825792 | tf_op jit(solution)/shard_map/dot_general | solution.py:706
  386.1 10.0 %fusion.182 = (f32[512]{0:T(512)S(1)}, f32[512,1024]{1,0:T(8,128)S(1)}) fusion(f32[512,1024]{1,0:T(8,128)} %copy-done.72, bf16[512,4096]{1,0:T(8,128)(2,1)} %get-tuple-element.418.refs_0_, bf16[4096,1024]{1,0:T(8,128)(2,1)} %all-gather.9.cloned.1.call-done), kind=kOutput, calls=%fused_computation.463 | convolution fusion | flops 4296539648 | bytes 16779264 | tf_op jit(solution)/shard_map/dot_general | solution.py:706
  401.1 6.1 closing_0_1.1.refs_2_
  407.3 10.1 %fusion.5.refs_1_ = bf16[512,4096]{1,0:T(8,128)(2,1)S(1)} fusion(bf16[512,4096]{1,0:T(8,128)(2,1)S(1)} %copy-done.140, bf16[512,1024]{1,0:T(8,128)(2,1)S(1)} %multiply_convert_fusion.3.refs_1_, bf16[4096,1024]{1,0:T(8,128)(2,1)} %all-gather.9.cloned.1.call-done), kind=kOutput, calls=%fused_computation.12 | convolution fusion | flops 4318035968 | bytes 17825792 | tf_op jit(solution)/shard_map/dot_general | solution.py:710
  417.5 6.6 closing_1_1.1
  424.1 14.4 %all-gather.11.cloned.1.call-done = bf16[1024,2048]{1,0:T(8,128)(2,1)} async-done(((bf16[32,2048]{1,0:T(8,128)(2,1)}), bf16[1024,2048]{1,0:T(8,128)(2,1)}) %all-gather.11.cloned.1.call-update) | async-done | bytes 4194320 | tf_op jit(solution)/shard_map/all_gather | solution.py:619
  444.8 8.0 multiply_reduce_fusion.5
  466.2 6.6 multiply_reduce_fusion.2
  491.6 3.9 early_0_0.1
  495.5 3.9 early_1_0.1
  499.4 3.9 early_2_0.1
  503.3 8.6 closing_0_0.1
  511.9 9.3 closing_1_0.1
  521.3 4.2 multiply_reduce_fusion.1
  547.3 4.2 all-to-all-start.2
  554.8 4.0 middle_0_1.1.refs_2_
  567.8 34.2 %attend_backward.1 = (bf16[4,3,2,256,256]{4,3,2,1,0:T(8,128)(2,1)}, bf16[2048,256]{1,0:T(8,128)(2,1)S(1)}, f32[2,256]{1,0:T(2,128)S(1)}) custom-call(bf16[2,2,1024,1024]{3,2,1,0:T(8,128)(2,1)} %get-tuple-element.179.p_ref, bf16[4,3,2,256,256]{4,3,2,1,0:T(8,128)(2,1)} %all-to-all-done.q_ref.k_ref.v_ref, ...), custom_call_target="tpu_custom_call" | custom-call | flops 8321499136 | bytes 16777216 | tf_op jit(solution)/shard_map/attend_backward/pallas_call | solution.py:134
  602.0 22.7 %collective-permute-done.37 = bf16[2,4,1024,256]{3,2,1,0:T(8,128)(2,1)} collective-permute-done((bf16[2,4,1024,256]{3,2,1,0:T(8,128)(2,1)}, bf16[2,4,1024,256]{3,2,1,0:T(8,128)(2,1)}, u32[]{:S(2)}, u32[]{:S(2)}) %collective-permute-start.37) | collective-permute-done | bytes 4194336 | tf_op jit(solution)/shard_map/ppermute | solution.py:288
  624.7 4.8 all-to-all-start.3
  633.6 4.9 middle_0_0.1
  643.8 22.6 %all-to-all-done.3.grad_ref.refs_1_ = bf16[4,3,2,256,256]{4,3,2,1,0:T(8,128)(2,1)} async-done(((bf16[4,3,2,256,256]{4,3,2,1,0:T(8,128)(2,1)}), bf16[4,3,2,256,256]{4,3,2,1,0:T(8,128)(2,1)}, u32[]{:S(2)}, u32[]{:S(2)}) %all-to-all-start.3) | async-done | bytes 3145760 | tf_op jit(solution)/shard_map/all_to_all | solution.py:1024
  666.5 6.4 join_heads.1
  678.3 7.8 opening_exit_0_1.1
  686.1 6.9 attention_0_1.1
  693.5 5.0 add_convert_fusion.2
  709.8 9.1 attention_0_0.1
  720.1 8.1 opening_exit_0_0.1
  728.2 18.0 %collective-permute-done.41 = bf16[4,1024,256]{2,1,0:T(8,128)(2,1)S(1)} collective-permute-done((bf16[4,1024,256]{2,1,0:T(8,128)(2,1)}, bf16[4,1024,256]{2,1,0:T(8,128)(2,1)S(1)}, u32[]{:S(2)}, u32[]{:S(2)}) %collective-permute-start.41) | collective-permute-done | bytes 2097184 | tf_op jit(solution)/shard_map/ppermute | solution.py:288
  753.5 11.5 %fusion.11.refs_1_ = bf16[512,4096]{1,0:T(8,128)(2,1)} fusion(bf16[512,4096]{1,0:T(8,128)(2,1)S(1)} %copy-done.139, bf16[512,1024]{1,0:T(8,128)(2,1)S(1)} %get-tuple-element.203.refs_1_, bf16[4096,1024]{1,0:T(8,128)(2,1)} %gather_opening_exit.1), kind=kOutput, calls=%fused_computation.18 | convolution fusion | flops 4318035968 | bytes 17825792 | tf_op jit(solution)/shard_map/dot_general | solution.py:710
  765.1 5.3 opening_entry_more_0_1.1
  770.4 6.0 opening_entry_0_1.1
  776.4 6.6 collective-permute-done.45
  783.5 10.2 %fusion.23 = (f32[1024]{0:T(1024)}, f32[512]{0:T(512)}, f32[1024]{0:T(1024)}, f32[512,1024]{1,0:T(8,128)}) fusion(f32[512]{0:T(512)S(1)} %copy-done.128, f32[512]{0:T(512)S(1)} %bitcast.395, bf16[2,256,1024]{2,1,0:T(8,128)(2,1)S(1)} %copy-done.2, f32[1024]{0:T(1024)S(1)} %bitcast.374, bf16[512,4096]{1,0:T(8,128)(2,1)S(1)} %copy-done.53, ...), kind=kOutput, calls=%fused_computation.62 | convolution fusion | flops 4299683328 | bytes 15747072 | tf_op jit(solution)/shard_map/dot_general | solution.py:710
  807.6 4.8 opening_entry_more_0_0.1
  812.4 6.3 opening_entry_0_0.1
  818.8 19.2 %collective-permute-done.46 = bf16[1,1408,256]{2,1,0:T(8,128)(2,1)} collective-permute-done((bf16[1,1408,256]{2,1,0:T(8,128)(2,1)}, bf16[1,1408,256]{2,1,0:T(8,128)(2,1)}, u32[]{:S(2)}, u32[]{:S(2)}) %collective-permute-start.46) | collective-permute-done | bytes 720928 | tf_op jit(solution)/shard_map/ppermute | solution.py:294
  851.5 37.9 %collective-permute-done.53 = f32[19,1024]{1,0:T(8,128)S(1)} collective-permute-done((f32[19,1024]{1,0:T(8,128)S(1)}, f32[19,1024]{1,0:T(8,128)S(1)}, u32[]{:S(2)}, u32[]{:S(2)}) %collective-permute-start.53) | collective-permute-done | bytes 77856 | tf_op jit(solution)/shard_map/ppermute | solution.py:288
  891.2 7.7 collective-permute-done.54
  910.9 6.4 collective-permute-done.59
  917.3 9.1 collective-permute-done.60
  927.1 3.9 collective-permute-start.64
  938.2 9.4 collective-permute-done.65
  947.7 13.4 %collective-permute-done.68 = bf16[1,1024,256]{2,1,0:T(8,128)(2,1)S(1)} collective-permute-done((bf16[1,1024,256]{2,1,0:T(8,128)(2,1)S(1)}, bf16[1,1024,256]{2,1,0:T(8,128)(2,1)S(1)}, u32[]{:S(2)}, u32[]{:S(2)}) %collective-permute-start.68) | collective-permute-done | bytes 524320 | tf_op jit(solution)/shard_map/ppermute | solution.py:294
  964.2 8.7 collective-permute-done.69
  (605 shorter events, 277.1 us)
Async XLA Ops:
  7.2 323.7 %all-gather.5.cloned.1.call-start = ((), (), s32[]{:S(2)}) async-start(), calls=%async_computation.4 | async-start | bytes 8650752 | tf_op jit(solution)/shard_map/all_gather | solution.py:619
  8.3 29.1 %collective-permute-start = (bf16[1,512,256]{2,1,0:T(8,128)(2,1)S(1)}, bf16[1,512,256]{2,1,0:T(8,128)(2,1)S(1)}, u32[]{:S(2)}, u32[]{:S(2)}) collective-permute-start(bf16[1,512,256]{2,1,0:T(8,128)(2,1)S(1)} %get-tuple-element.381), channel_id=1, source_target_pairs={{0,8},{4,12},{8,16},{12,20},{16,24},{20,28},{24,0},{28,4},{1,9},{5... | collective-permute-start | bytes 786440 | tf_op jit(solution)/shard_map/ppermute | solution.py:288
  11.4 26.1 %collective-permute-start.1 = (bf16[1,512,256]{2,1,0:T(8,128)(2,1)S(1)}, bf16[1,512,256]{2,1,0:T(8,128)(2,1)S(1)}, u32[]{:S(2)}, u32[]{:S(2)}) collective-permute-start(bf16[1,512,256]{2,1,0:T(8,128)(2,1)S(1)} %get-tuple-element.381), channel_id=1, source_target_pairs={{0,16},{4,20},{8,24},{12,28},{16,0},{20,4},{24,8},{28,12},{1,17},{... | collective-permute-start | bytes 786440 | tf_op jit(solution)/shard_map/ppermute | solution.py:288
  14.0 23.5 %collective-permute-start.2 = (bf16[1,512,256]{2,1,0:T(8,128)(2,1)S(1)}, bf16[1,512,256]{2,1,0:T(8,128)(2,1)S(1)}, u32[]{:S(2)}, u32[]{:S(2)}) collective-permute-start(bf16[1,512,256]{2,1,0:T(8,128)(2,1)S(1)} %get-tuple-element.381), channel_id=1, source_target_pairs={{0,24},{4,28},{8,0},{12,4},{16,8},{20,12},{24,16},{28,20},{1,25},{... | collective-permute-start | bytes 786440 | tf_op jit(solution)/shard_map/ppermute | solution.py:288
  16.1 15.3 %collective-permute-start.3 = (bf16[1,1,19,128]{3,2,1,0:T(8,128)(2,1)S(1)}, bf16[1,1,19,128]{3,2,1,0:T(8,128)(2,1)S(1)}, u32[]{:S(2)}, u32[]{:S(2)}) collective-permute-start(bf16[1,1,19,128]{3,2,1,0:T(8,128)(2,1)S(1)} %maximum_bitcast_fusion.2), channel_id=1, source_target_pairs={{0,8},{4,12},{8,16},{12,20},{16,24},{20,28},{24,0},{28,4},{1,9},{5... | collective-permute-start | bytes 14600 | tf_op jit(solution)/shard_map/ppermute | solution.py:288
  16.8 20.3 %collective-permute-start.4 = (bf16[1,1,19,128]{3,2,1,0:T(8,128)(2,1)S(1)}, bf16[1,1,19,128]{3,2,1,0:T(8,128)(2,1)S(1)}, u32[]{:S(2)}, u32[]{:S(2)}) collective-permute-start(bf16[1,1,19,128]{3,2,1,0:T(8,128)(2,1)S(1)} %maximum_bitcast_fusion.2), channel_id=1, source_target_pairs={{0,16},{4,20},{8,24},{12,28},{16,0},{20,4},{24,8},{28,12},{1,17},{... | collective-permute-start | bytes 14600 | tf_op jit(solution)/shard_map/ppermute | solution.py:288
  37.7 28.0 %collective-permute-start.6 = (bf16[1,4,512,256]{3,2,1,0:T(8,128)(2,1)S(1)}, bf16[1,4,512,256]{3,2,1,0:T(8,128)(2,1)}, u32[]{:S(2)}, u32[]{:S(2)}) collective-permute-start(bf16[1,4,512,256]{3,2,1,0:T(8,128)(2,1)S(1)} %get-tuple-element.349), channel_id=1, source_target_pairs={{0,4},{4,0},{8,12},{12,8},{16,20},{20,16},{24,28},{28,24},{1,5},{5... | collective-permute-start | bytes 3145736 | tf_op jit(solution)/shard_map/ppermute | solution.py:288
  40.9 12.7 %collective-permute-start.10 = (bf16[1,512,256]{2,1,0:T(8,128)(2,1)}, bf16[1,512,256]{2,1,0:T(8,128)(2,1)}, u32[]{:S(2)}, u32[]{:S(2)}) collective-permute-start(bf16[1,512,256]{2,1,0:T(8,128)(2,1)} %get-tuple-element.347), channel_id=1, source_target_pairs={{0,24},{4,28},{8,0},{12,4},{16,8},{20,12},{24,16},{28,20},{1,25},{... | collective-permute-start | bytes 786440 | tf_op jit(solution)/shard_map/ppermute | solution.py:288
  44.0 14.4 %collective-permute-start.8 = (bf16[1,512,256]{2,1,0:T(8,128)(2,1)}, bf16[1,512,256]{2,1,0:T(8,128)(2,1)}, u32[]{:S(2)}, u32[]{:S(2)}) collective-permute-start(bf16[1,512,256]{2,1,0:T(8,128)(2,1)} %get-tuple-element.347), channel_id=1, source_target_pairs={{0,8},{4,12},{8,16},{12,20},{16,24},{20,28},{24,0},{28,4},{1,9},{5... | collective-permute-start | bytes 786440 | tf_op jit(solution)/shard_map/ppermute | solution.py:288
  44.0 21.6 %collective-permute-start.9 = (bf16[1,512,256]{2,1,0:T(8,128)(2,1)}, bf16[1,512,256]{2,1,0:T(8,128)(2,1)}, u32[]{:S(2)}, u32[]{:S(2)}) collective-permute-start(bf16[1,512,256]{2,1,0:T(8,128)(2,1)} %get-tuple-element.347), channel_id=1, source_target_pairs={{0,16},{4,20},{8,24},{12,28},{16,0},{20,4},{24,8},{28,12},{1,17},{... | collective-permute-start | bytes 786440 | tf_op jit(solution)/shard_map/ppermute | solution.py:288
  46.9 18.8 %collective-permute-start.7 = (bf16[1,4,19,128]{3,2,1,0:T(8,128)(2,1)S(1)}, bf16[1,4,19,128]{3,2,1,0:T(8,128)(2,1)S(1)}, u32[]{:S(2)}, u32[]{:S(2)}) collective-permute-start(bf16[1,4,19,128]{3,2,1,0:T(8,128)(2,1)S(1)} %pad_maximum_fusion.26), channel_id=1, source_target_pairs={{0,4},{4,0},{8,12},{12,8},{16,20},{20,16},{24,28},{28,24},{1,5},{5... | collective-permute-start | bytes 58376 | tf_op jit(solution)/shard_map/ppermute | solution.py:288
  69.3 306.5 %all-gather.7.cloned.1.call-start = ((), (), s32[]{:S(2)}) async-start(), calls=%async_computation.5 | async-start | bytes 8650752 | tf_op jit(solution)/shard_map/all_gather | solution.py:619
  70.1 316.0 %all-gather.9.cloned.1.call-start = ((), (), s32[]{:S(2)}) async-start(), calls=%async_computation.6 | async-start | bytes 8650752 | tf_op jit(solution)/shard_map/all_gather | solution.py:619
  70.1 47.9 %collective-permute-start.11 = (bf16[1,2,4,512,256]{4,3,2,1,0:T(8,128)(2,1)}, bf16[1,2,4,512,256]{4,3,2,1,0:T(8,128)(2,1)}, u32[]{:S(2)}, u32[]{:S(2)}) collective-permute-start(bf16[1,2,4,512,256]{4,3,2,1,0:T(8,128)(2,1)} %pad_maximum_fusion.3), channel_id=1, source_target_pairs={{0,2},{1,3},{2,0},{3,1},{4,6},{5,7},{6,4},{7,5},{8,10},{9,11},{10,... | collective-permute-start | bytes 6291464 | tf_op jit(solution)/shard_map/ppermute | solution.py:288
  73.0 44.0 %collective-permute-start.12 = (bf16[1,4,512,256]{3,2,1,0:T(8,128)(2,1)S(1)}, bf16[1,4,512,256]{3,2,1,0:T(8,128)(2,1)S(1)}, u32[]{:S(2)}, u32[]{:S(2)}) collective-permute-start(bf16[1,4,512,256]{3,2,1,0:T(8,128)(2,1)S(1)} %get-tuple-element.345), channel_id=1, source_target_pairs={{0,4},{4,0},{8,12},{12,8},{16,20},{20,16},{24,28},{28,24},{1,5},{5... | collective-permute-start | bytes 3145736 | tf_op jit(solution)/shard_map/ppermute | solution.py:288
  75.6 22.3 %collective-permute-start.13 = (bf16[2,512,256]{2,1,0:T(8,128)(2,1)S(1)}, bf16[2,512,256]{2,1,0:T(8,128)(2,1)S(1)}, u32[]{:S(2)}, u32[]{:S(2)}) collective-permute-start(bf16[2,512,256]{2,1,0:T(8,128)(2,1)S(1)} %get-tuple-element.361), channel_id=1, source_target_pairs={{0,8},{4,12},{8,16},{12,20},{16,24},{20,28},{24,0},{28,4},{1,9},{5... | collective-permute-start | bytes 1572872 | tf_op jit(solution)/shard_map/ppermute | solution.py:288
  75.6 41.5 %collective-permute-start.14 = (bf16[2,512,256]{2,1,0:T(8,128)(2,1)S(1)}, bf16[2,512,256]{2,1,0:T(8,128)(2,1)S(1)}, u32[]{:S(2)}, u32[]{:S(2)}) collective-permute-start(bf16[2,512,256]{2,1,0:T(8,128)(2,1)S(1)} %get-tuple-element.361), channel_id=1, source_target_pairs={{0,16},{4,20},{8,24},{12,28},{16,0},{20,4},{24,8},{28,12},{1,17},{... | collective-permute-start | bytes 1572872 | tf_op jit(solution)/shard_map/ppermute | solution.py:288
  78.8 38.3 %collective-permute-start.15 = (bf16[2,512,256]{2,1,0:T(8,128)(2,1)S(1)}, bf16[2,512,256]{2,1,0:T(8,128)(2,1)S(1)}, u32[]{:S(2)}, u32[]{:S(2)}) collective-permute-start(bf16[2,512,256]{2,1,0:T(8,128)(2,1)S(1)} %get-tuple-element.361), channel_id=1, source_target_pairs={{0,24},{4,28},{8,0},{12,4},{16,8},{20,12},{24,16},{28,20},{1,25},{... | collective-permute-start | bytes 1572872 | tf_op jit(solution)/shard_map/ppermute | solution.py:288
  123.3 8.5 collective-permute-start.18
  128.3 63.1 %collective-permute-start.17 = (bf16[2,4,512,256]{3,2,0,1:T(8,128)(2,1)S(1)}, bf16[2,4,512,256]{3,2,0,1:T(8,128)(2,1)}, u32[]{:S(2)}, u32[]{:S(2)}) collective-permute-start(bf16[2,4,512,256]{3,2,0,1:T(8,128)(2,1)S(1)} %get-tuple-element.323), channel_id=1, source_target_pairs={{0,4},{4,0},{8,12},{12,8},{16,20},{20,16},{24,28},{28,24},{1,5},{5... | collective-permute-start | bytes 6291464 | tf_op jit(solution)/shard_map/ppermute | solution.py:288
  131.2 63.0 %collective-permute-start.16 = (bf16[1,2,4,512,256]{4,3,2,1,0:T(8,128)(2,1)}, bf16[1,2,4,512,256]{4,3,2,1,0:T(8,128)(2,1)}, u32[]{:S(2)}, u32[]{:S(2)}) collective-permute-start(bf16[1,2,4,512,256]{4,3,2,1,0:T(8,128)(2,1)} %pad_maximum_fusion.4), channel_id=1, source_target_pairs={{0,2},{1,3},{2,0},{3,1},{4,6},{5,7},{6,4},{7,5},{8,10},{9,11},{10,... | collective-permute-start | bytes 6291464 | tf_op jit(solution)/shard_map/ppermute | solution.py:288
  196.5 7.4 collective-permute-start.20
  200.3 12.1 %collective-permute-start.19 = (bf16[2,8,512,256]{3,2,1,0:T(8,128)(2,1)S(1)}, bf16[2,8,512,256]{3,2,1,0:T(8,128)(2,1)}, u32[]{:S(2)}, u32[]{:S(2)}) collective-permute-start(bf16[2,8,512,256]{3,2,1,0:T(8,128)(2,1)S(1)} %bitcast.318), channel_id=1, source_target_pairs={{0,1},{1,0},{2,3},{3,2},{4,5},{5,4},{6,7},{7,6},{8,9},{9,8},{10,11... | collective-permute-start | bytes 12582920 | tf_op jit(solution)/shard_map/ppermute | solution.py:288
  237.0 53.8 %all-to-all-start = ((bf16[4,3,2,256,256]{4,3,2,1,0:T(8,128)(2,1)}), bf16[4,3,2,256,256]{4,3,2,1,0:T(8,128)(2,1)}, u32[]{:S(2)}, u32[]{:S(2)}) async-start(bf16[4,3,2,256,256]{4,3,2,1,0:T(8,128)(2,1)} %project_heads.1), calls=%async_computation | async-start | bytes 6291456 | tf_op jit(solution)/shard_map/all_to_all | solution.py:871
  311.9 18.0 %all-to-all-start.1 = ((bf16[4,2,256,256]{3,2,1,0:T(8,128)(2,1)}), bf16[4,2,256,256]{3,2,1,0:T(8,128)(2,1)S(1)}, u32[]{:S(2)}, u32[]{:S(2)}) async-start(bf16[4,2,256,256]{3,2,1,0:T(8,128)(2,1)} %get-tuple-element.158), calls=%async_computation.1 | async-start | bytes 2097152 | tf_op jit(solution)/shard_map/all_to_all | solution.py:878
  315.4 123.0 %all-gather.11.cloned.1.call-start = ((), (), s32[]{:S(2)}) async-start(), calls=%async_computation.7 | async-start | bytes 4325376 | tf_op jit(solution)/shard_map/all_gather | solution.py:619
  424.1 79.2 %collective-permute-start.33 = (bf16[2,2,4,1024,256]{4,3,2,1,0:T(8,128)(2,1)}, bf16[2,2,4,1024,256]{4,3,2,1,0:T(8,128)(2,1)}, u32[]{:S(2)}, u32[]{:S(2)}) collective-permute-start(bf16[2,2,4,1024,256]{4,3,2,1,0:T(8,128)(2,1)} %closing_1_1.1), channel_id=1, source_target_pairs={{0,1},{1,0},{2,3},{3,2},{4,5},{5,4},{6,7},{7,6},{8,9},{9,8},{10,11... | collective-permute-start | bytes 25165832 | tf_op jit(solution)/shard_map/ppermute | solution.py:288
  465.9 24.0 %collective-permute-start.34 = (bf16[2,2,4,384,256]{4,3,2,1,0:T(8,128)(2,1)S(1)}, bf16[2,2,4,384,256]{4,3,2,1,0:T(8,128)(2,1)S(1)}, u32[]{:S(2)}, u32[]{:S(2)}) collective-permute-start(bf16[2,2,4,384,256]{4,3,2,1,0:T(8,128)(2,1)S(1)} %early_2_1.1), channel_id=1, source_target_pairs={{0,1},{1,0},{2,3},{3,2},{4,5},{5,4},{6,7},{7,6},{8,9},{9,8},{10,11... | collective-permute-start | bytes 9437192 | tf_op jit(solution)/shard_map/ppermute | solution.py:288
  525.5 7.9 collective-permute-start.35
  531.8 92.9 %collective-permute-start.37 = (bf16[2,4,1024,256]{3,2,1,0:T(8,128)(2,1)}, bf16[2,4,1024,256]{3,2,1,0:T(8,128)(2,1)}, u32[]{:S(2)}, u32[]{:S(2)}) collective-permute-start(bf16[2,4,1024,256]{3,2,1,0:T(8,128)(2,1)} %get-tuple-element.177), channel_id=1, source_target_pairs={{0,4},{4,0},{8,12},{12,8},{16,20},{20,16},{24,28},{28,24},{1,5},{5... | collective-permute-start | bytes 12582920 | tf_op jit(solution)/shard_map/ppermute | solution.py:288
  547.3 19.2 %all-to-all-start.2 = ((bf16[4,2,256,256]{3,2,1,0:T(8,128)(2,1)}), bf16[4,2,256,256]{3,2,1,0:T(8,128)(2,1)}, u32[]{:S(2)}, u32[]{:S(2)}) async-start(bf16[4,2,256,256]{3,2,1,0:T(8,128)(2,1)} %copy-done.36), calls=%async_computation.2 | async-start | bytes 2097152 | tf_op jit(solution)/shard_map/all_to_all | solution.py:1009
  551.6 50.4 %collective-permute-start.38 = (bf16[2,4,384,256]{3,2,1,0:T(8,128)(2,1)}, bf16[2,4,384,256]{3,2,1,0:T(8,128)(2,1)}, u32[]{:S(2)}, u32[]{:S(2)}) collective-permute-start(bf16[2,4,384,256]{3,2,1,0:T(8,128)(2,1)} %copy-done.33), channel_id=1, source_target_pairs={{0,2},{1,3},{2,0},{3,1},{4,6},{5,7},{6,4},{7,5},{8,10},{9,11},{10,... | collective-permute-start | bytes 4718600 | tf_op jit(solution)/shard_map/ppermute | solution.py:288
  566.5 67.1 %collective-permute-start.39 = (bf16[2,2,4,384,256]{4,3,2,1,0:T(8,128)(2,1)}, bf16[2,2,4,384,256]{4,3,2,1,0:T(8,128)(2,1)}, u32[]{:S(2)}, u32[]{:S(2)}) collective-permute-start(bf16[2,2,4,384,256]{4,3,2,1,0:T(8,128)(2,1)} %copy-done.18), channel_id=1, source_target_pairs={{0,1},{1,0},{2,3},{3,2},{4,5},{5,4},{6,7},{7,6},{8,9},{9,8},{10,11... | collective-permute-start | bytes 9437192 | tf_op jit(solution)/shard_map/ppermute | solution.py:288
  624.7 41.8 %all-to-all-start.3 = ((bf16[4,3,2,256,256]{4,3,2,1,0:T(8,128)(2,1)}), bf16[4,3,2,256,256]{4,3,2,1,0:T(8,128)(2,1)}, u32[]{:S(2)}, u32[]{:S(2)}) async-start(bf16[4,3,2,256,256]{4,3,2,1,0:T(8,128)(2,1)} %get-tuple-element.182), calls=%async_computation.3 | async-start | bytes 6291456 | tf_op jit(solution)/shard_map/all_to_all | solution.py:1024
  686.1 34.1 %collective-permute-start.44 = (bf16[2,2,4,512,256]{4,3,2,1,0:T(8,128)(2,1)}, bf16[2,2,4,512,256]{4,3,2,1,0:T(8,128)(2,1)}, u32[]{:S(2)}, u32[]{:S(2)}) collective-permute-start(bf16[2,2,4,512,256]{4,3,2,1,0:T(8,128)(2,1)} %opening_exit_0_1.1), channel_id=1, source_target_pairs={{0,1},{1,0},{2,3},{3,2},{4,5},{5,4},{6,7},{7,6},{8,9},{9,8},{10,11... | collective-permute-start | bytes 12582920 | tf_op jit(solution)/shard_map/ppermute | solution.py:288
  693.0 16.8 %collective-permute-start.43 = (bf16[2,2,4,384,256]{4,3,2,1,0:T(8,128)(2,1)}, bf16[2,2,4,384,256]{4,3,2,1,0:T(8,128)(2,1)}, u32[]{:S(2)}, u32[]{:S(2)}) collective-permute-start(bf16[2,2,4,384,256]{4,3,2,1,0:T(8,128)(2,1)} %attention_0_1.1), channel_id=1, source_target_pairs={{0,1},{1,0},{2,3},{3,2},{4,5},{5,4},{6,7},{7,6},{8,9},{9,8},{10,11... | collective-permute-start | bytes 9437192 | tf_op jit(solution)/shard_map/ppermute | solution.py:288
  698.5 47.8 %collective-permute-start.41 = (bf16[4,1024,256]{2,1,0:T(8,128)(2,1)}, bf16[4,1024,256]{2,1,0:T(8,128)(2,1)S(1)}, u32[]{:S(2)}, u32[]{:S(2)}) collective-permute-start(bf16[4,1024,256]{2,1,0:T(8,128)(2,1)} %get-tuple-element.296), channel_id=1, source_target_pairs={{0,2},{1,3},{2,0},{3,1},{4,6},{5,7},{6,4},{7,5},{8,10},{9,11},{10,... | collective-permute-start | bytes 6291464 | tf_op jit(solution)/shard_map/ppermute | solution.py:288
  705.3 22.9 %collective-permute-start.42 = (bf16[4,384,256]{2,1,0:T(8,128)(2,1)S(1)}, bf16[4,384,256]{2,1,0:T(8,128)(2,1)}, u32[]{:S(2)}, u32[]{:S(2)}) collective-permute-start(bf16[4,384,256]{2,1,0:T(8,128)(2,1)S(1)} %get-tuple-element.307), channel_id=1, source_target_pairs={{0,4},{4,0},{8,12},{12,8},{16,20},{20,16},{24,28},{28,24},{1,5},{5... | collective-permute-start | bytes 2359304 | tf_op jit(solution)/shard_map/ppermute | solution.py:288
  709.3 67.1 %collective-permute-start.40 = (bf16[2,4,384,256]{3,2,1,0:T(8,128)(2,1)S(1)}, bf16[2,4,384,256]{3,2,1,0:T(8,128)(2,1)}, u32[]{:S(2)}, u32[]{:S(2)}) collective-permute-start(bf16[2,4,384,256]{3,2,1,0:T(8,128)(2,1)S(1)} %copy-done.40), channel_id=1, source_target_pairs={{0,4},{4,0},{8,12},{12,8},{16,20},{20,16},{24,28},{28,24},{1,5},{5... | collective-permute-start | bytes 4718600 | tf_op jit(solution)/shard_map/ppermute | solution.py:288
  750.1 32.8 %collective-permute-start.45 = (bf16[2,1408,256]{2,1,0:T(8,128)(2,1)S(1)}, bf16[2,1408,256]{2,1,0:T(8,128)(2,1)S(1)}, u32[]{:S(2)}, u32[]{:S(2)}) collective-permute-start(bf16[2,1408,256]{2,1,0:T(8,128)(2,1)S(1)} %pad_maximum_fusion.6), channel_id=1, source_target_pairs={{0,8},{4,12},{8,0},{12,4},{16,24},{20,28},{24,16},{28,20},{1,9},{5... | collective-permute-start | bytes 4325384 | tf_op jit(solution)/shard_map/ppermute | solution.py:294
  751.9 66.9 %collective-permute-start.49 = (bf16[2,4,512,256]{3,2,1,0:T(8,128)(2,1)}, bf16[2,4,512,256]{3,2,1,0:T(8,128)(2,1)}, u32[]{:S(2)}, u32[]{:S(2)}) collective-permute-start(bf16[2,4,512,256]{3,2,1,0:T(8,128)(2,1)} %get-tuple-element.209), channel_id=1, source_target_pairs={{0,4},{4,0},{8,12},{12,8},{16,20},{20,16},{24,28},{28,24},{1,5},{5... | collective-permute-start | bytes 6291464 | tf_op jit(solution)/shard_map/ppermute | solution.py:288
  753.2 65.6 %collective-permute-start.48 = (bf16[2,4,384,256]{3,2,1,0:T(8,128)(2,1)}, bf16[2,4,384,256]{3,2,1,0:T(8,128)(2,1)}, u32[]{:S(2)}, u32[]{:S(2)}) collective-permute-start(bf16[2,4,384,256]{3,2,1,0:T(8,128)(2,1)} %get-tuple-element.208), channel_id=1, source_target_pairs={{0,2},{1,3},{2,0},{3,1},{4,6},{5,7},{6,4},{7,5},{8,10},{9,11},{10,... | collective-permute-start | bytes 4718600 | tf_op jit(solution)/shard_map/ppermute | solution.py:288
  783.0 20.1 %collective-permute-start.52 = (bf16[2,2,4,256,256]{4,3,2,1,0:T(8,128)(2,1)}, bf16[2,2,4,256,256]{4,3,2,1,0:T(8,128)(2,1)}, u32[]{:S(2)}, u32[]{:S(2)}) collective-permute-start(bf16[2,2,4,256,256]{4,3,2,1,0:T(8,128)(2,1)} %opening_entry_more_0_1.1), channel_id=1, source_target_pairs={{0,1},{1,0},{2,3},{3,2},{4,5},{5,4},{6,7},{7,6},{8,9},{9,8},{10,11... | collective-permute-start | bytes 6291464 | tf_op jit(solution)/shard_map/ppermute | solution.py:288
  783.0 29.4 %collective-permute-start.51 = (bf16[2,2,4,256,256]{4,3,2,1,0:T(8,128)(2,1)}, bf16[2,2,4,256,256]{4,3,2,1,0:T(8,128)(2,1)}, u32[]{:S(2)}, u32[]{:S(2)}) collective-permute-start(bf16[2,2,4,256,256]{4,3,2,1,0:T(8,128)(2,1)} %opening_entry_0_1.1), channel_id=1, source_target_pairs={{0,1},{1,0},{2,3},{3,2},{4,5},{5,4},{6,7},{7,6},{8,9},{9,8},{10,11... | collective-permute-start | bytes 6291464 | tf_op jit(solution)/shard_map/ppermute | solution.py:288
  795.4 7.2 collective-permute-start.50
  802.6 35.4 %collective-permute-start.47 = (bf16[4,384,256]{2,1,0:T(8,128)(2,1)S(1)}, bf16[4,384,256]{2,1,0:T(8,128)(2,1)}, u32[]{:S(2)}, u32[]{:S(2)}) collective-permute-start(bf16[4,384,256]{2,1,0:T(8,128)(2,1)S(1)} %get-tuple-element.306), channel_id=1, source_target_pairs={{0,2},{1,3},{2,0},{3,1},{4,6},{5,7},{6,4},{7,5},{8,10},{9,11},{10,... | collective-permute-start | bytes 2359304 | tf_op jit(solution)/shard_map/ppermute | solution.py:288
  803.1 34.9 %collective-permute-start.46 = (bf16[1,1408,256]{2,1,0:T(8,128)(2,1)}, bf16[1,1408,256]{2,1,0:T(8,128)(2,1)}, u32[]{:S(2)}, u32[]{:S(2)}) collective-permute-start(bf16[1,1408,256]{2,1,0:T(8,128)(2,1)} %get-tuple-element.310), channel_id=1, source_target_pairs={{0,16},{4,20},{8,24},{12,28},{16,0},{20,4},{24,8},{28,12},{1,17},{... | collective-permute-start | bytes 2162696 | tf_op jit(solution)/shard_map/ppermute | solution.py:294
  840.3 58.6 %collective-permute-start.56 = (bf16[4,512,256]{2,1,0:T(8,128)(2,1)S(1)}, bf16[4,512,256]{2,1,0:T(8,128)(2,1)S(1)}, u32[]{:S(2)}, u32[]{:S(2)}) collective-permute-start(bf16[4,512,256]{2,1,0:T(8,128)(2,1)S(1)} %get-tuple-element.300), channel_id=1, source_target_pairs={{0,2},{1,3},{2,0},{3,1},{4,6},{5,7},{6,4},{7,5},{8,10},{9,11},{10,... | collective-permute-start | bytes 3145736 | tf_op jit(solution)/shard_map/ppermute | solution.py:288
  843.9 55.0 %collective-permute-start.55 = (bf16[4,512,256]{2,1,0:T(8,128)(2,1)S(1)}, bf16[4,512,256]{2,1,0:T(8,128)(2,1)S(1)}, u32[]{:S(2)}, u32[]{:S(2)}) collective-permute-start(bf16[4,512,256]{2,1,0:T(8,128)(2,1)S(1)} %pad_maximum_fusion.13), channel_id=1, source_target_pairs={{0,4},{4,0},{8,12},{12,8},{16,20},{20,16},{24,28},{28,24},{1,5},{5... | collective-permute-start | bytes 3145736 | tf_op jit(solution)/shard_map/ppermute | solution.py:288
  845.5 53.4 %collective-permute-start.57 = (bf16[2,4,256,256]{3,2,1,0:T(8,128)(2,1)S(1)}, bf16[2,4,256,256]{3,2,1,0:T(8,128)(2,1)S(1)}, u32[]{:S(2)}, u32[]{:S(2)}) collective-permute-start(bf16[2,4,256,256]{3,2,1,0:T(8,128)(2,1)S(1)} %get-tuple-element.224), channel_id=1, source_target_pairs={{0,2},{1,3},{2,0},{3,1},{4,6},{5,7},{6,4},{7,5},{8,10},{9,11},{10,... | collective-permute-start | bytes 3145736 | tf_op jit(solution)/shard_map/ppermute | solution.py:288
  845.9 53.0 %collective-permute-start.58 = (bf16[2,4,256,256]{3,2,1,0:T(8,128)(2,1)S(1)}, bf16[2,4,256,256]{3,2,1,0:T(8,128)(2,1)S(1)}, u32[]{:S(2)}, u32[]{:S(2)}) collective-permute-start(bf16[2,4,256,256]{3,2,1,0:T(8,128)(2,1)S(1)} %get-tuple-element.225), channel_id=1, source_target_pairs={{0,4},{4,0},{8,12},{12,8},{16,20},{20,16},{24,28},{28,24},{1,5},{5... | collective-permute-start | bytes 3145736 | tf_op jit(solution)/shard_map/ppermute | solution.py:288
  846.3 43.0 %collective-permute-start.53 = (f32[19,1024]{1,0:T(8,128)S(1)}, f32[19,1024]{1,0:T(8,128)S(1)}, u32[]{:S(2)}, u32[]{:S(2)}) collective-permute-start(f32[19,1024]{1,0:T(8,128)S(1)} %add.689), channel_id=1, source_target_pairs={{0,2},{1,3},{2,0},{3,1},{4,6},{5,7},{6,4},{7,5},{8,10},{9,11},{10,... | collective-permute-start | bytes 233480 | tf_op jit(solution)/shard_map/ppermute | solution.py:288
  889.4 9.5 collective-permute-start.54
  899.5 27.6 %collective-permute-start.61 = (bf16[2,1024,256]{2,1,0:T(8,128)(2,1)S(1)}, bf16[2,1024,256]{2,1,0:T(8,128)(2,1)S(1)}, u32[]{:S(2)}, u32[]{:S(2)}) collective-permute-start(bf16[2,1024,256]{2,1,0:T(8,128)(2,1)S(1)} %pad_maximum_fusion.14), channel_id=1, source_target_pairs={{0,8},{4,12},{8,0},{12,4},{16,24},{20,28},{24,16},{28,20},{1,9},{5... | collective-permute-start | bytes 3145736 | tf_op jit(solution)/shard_map/ppermute | solution.py:294
  901.6 24.8 %collective-permute-start.63 = (bf16[4,256,256]{2,1,0:T(8,128)(2,1)S(1)}, bf16[4,256,256]{2,1,0:T(8,128)(2,1)S(1)}, u32[]{:S(2)}, u32[]{:S(2)}) collective-permute-start(bf16[4,256,256]{2,1,0:T(8,128)(2,1)S(1)} %get-tuple-element.321), channel_id=1, source_target_pairs={{0,2},{1,3},{2,0},{3,1},{4,6},{5,7},{6,4},{7,5},{8,10},{9,11},{10,... | collective-permute-start | bytes 1572872 | tf_op jit(solution)/shard_map/ppermute | solution.py:288
  903.6 22.8 %collective-permute-start.62 = (bf16[4,256,256]{2,1,0:T(8,128)(2,1)S(1)}, bf16[4,256,256]{2,1,0:T(8,128)(2,1)S(1)}, u32[]{:S(2)}, u32[]{:S(2)}) collective-permute-start(bf16[4,256,256]{2,1,0:T(8,128)(2,1)S(1)} %get-tuple-element.319), channel_id=1, source_target_pairs={{0,4},{4,0},{8,12},{12,8},{16,20},{20,16},{24,28},{28,24},{1,5},{5... | collective-permute-start | bytes 1572872 | tf_op jit(solution)/shard_map/ppermute | solution.py:288
  903.8 22.5 %collective-permute-start.60 = (bf16[1,384,256]{2,1,0:T(8,128)(2,1)S(1)}, bf16[1,384,256]{2,1,0:T(8,128)(2,1)S(1)}, u32[]{:S(2)}, u32[]{:S(2)}) collective-permute-start(bf16[1,384,256]{2,1,0:T(8,128)(2,1)S(1)} %add_convert_fusion.29), channel_id=1, source_target_pairs={{0,16},{4,20},{8,24},{12,28},{16,0},{20,4},{24,8},{28,12},{1,17},{... | collective-permute-start | bytes 589832 | tf_op jit(solution)/shard_map/ppermute | solution.py:294
  907.9 9.4 collective-permute-start.59
  927.1 11.1 %collective-permute-start.64 = (f32[19,1024]{1,0:T(8,128)S(1)}, f32[19,1024]{1,0:T(8,128)S(1)}, u32[]{:S(2)}, u32[]{:S(2)}) collective-permute-start(f32[19,1024]{1,0:T(8,128)S(1)} %add.703), channel_id=1, source_target_pairs={{0,8},{4,12},{8,16},{12,20},{16,24},{20,28},{24,0},{28,4},{1,9},{5... | collective-permute-start | bytes 233480 | tf_op jit(solution)/shard_map/ppermute | solution.py:288
  931.0 16.6 %collective-permute-start.65 = (f32[19,1024]{1,0:T(8,128)S(1)}, f32[19,1024]{1,0:T(8,128)S(1)}, u32[]{:S(2)}, u32[]{:S(2)}) collective-permute-start(f32[19,1024]{1,0:T(8,128)S(1)} %add.703), channel_id=1, source_target_pairs={{0,16},{4,20},{8,24},{12,28},{16,0},{20,4},{24,8},{28,12},{1,17},{... | collective-permute-start | bytes 233480 | tf_op jit(solution)/shard_map/ppermute | solution.py:288
  932.3 15.4 %collective-permute-start.66 = (f32[19,1024]{1,0:T(8,128)S(1)}, f32[19,1024]{1,0:T(8,128)S(1)}, u32[]{:S(2)}, u32[]{:S(2)}) collective-permute-start(f32[19,1024]{1,0:T(8,128)S(1)} %add.703), channel_id=1, source_target_pairs={{0,24},{4,28},{8,0},{12,4},{16,8},{20,12},{24,16},{28,20},{1,25},{... | collective-permute-start | bytes 233480 | tf_op jit(solution)/shard_map/ppermute | solution.py:288
  933.8 27.3 %collective-permute-start.68 = (bf16[1,1024,256]{2,1,0:T(8,128)(2,1)S(1)}, bf16[1,1024,256]{2,1,0:T(8,128)(2,1)S(1)}, u32[]{:S(2)}, u32[]{:S(2)}) collective-permute-start(bf16[1,1024,256]{2,1,0:T(8,128)(2,1)S(1)} %get-tuple-element.313), channel_id=1, source_target_pairs={{0,16},{4,20},{8,24},{12,28},{16,0},{20,4},{24,8},{28,12},{1,17},{... | collective-permute-start | bytes 1572872 | tf_op jit(solution)/shard_map/ppermute | solution.py:294
  934.7 26.4 %collective-permute-start.67 = (bf16[2,512,256]{2,1,0:T(8,128)(2,1)S(1)}, bf16[2,512,256]{2,1,0:T(8,128)(2,1)S(1)}, u32[]{:S(2)}, u32[]{:S(2)}) collective-permute-start(bf16[2,512,256]{2,1,0:T(8,128)(2,1)S(1)} %pad_maximum_fusion.19), channel_id=1, source_target_pairs={{0,8},{4,12},{8,0},{12,4},{16,24},{20,28},{24,16},{28,20},{1,9},{5... | collective-permute-start | bytes 1572872 | tf_op jit(solution)/shard_map/ppermute | solution.py:294
  961.2 11.7 %collective-permute-start.69 = (bf16[1,512,256]{2,1,0:T(8,128)(2,1)S(1)}, bf16[1,512,256]{2,1,0:T(8,128)(2,1)S(1)}, u32[]{:S(2)}, u32[]{:S(2)}) collective-permute-start(bf16[1,512,256]{2,1,0:T(8,128)(2,1)S(1)} %get-tuple-element.335), channel_id=1, source_target_pairs={{0,16},{4,20},{8,24},{12,28},{16,0},{20,4},{24,8},{28,12},{1,17},{... | collective-permute-start | bytes 786440 | tf_op jit(solution)/shard_map/ppermute | solution.py:294
  (157 other events, 1579.9 us)
Sparse Core Ops, SparseCore 0:
  69.4 115.1 all-gather.4
  188.0 88.9 all-gather.6
  279.9 80.1 all-gather.8
  369.2 69.1 all-gather.10

commit v4 on v3

--- a/solution.py
+++ b/solution.py
@@ -14,6 +14,16 @@
 epsilon = 1e-05
 
 F32, BF16 = jnp.float32, jnp.bfloat16
+SHARE = 4
+
+
+def cost(flops, transcendentals, bytes_accessed):
+    return pl.CostEstimate(
+        flops=flops // SHARE,
+        transcendentals=transcendentals // SHARE,
+        bytes_accessed=bytes_accessed // SHARE,
+    )
+
 
 def dot(a, b, ca, cb):
     return lax.dot_general(a, b, (((ca,), (cb,)), ((), ())), preferred_element_type=F32)
@@ -67,7 +77,7 @@
             jax.ShapeDtypeStruct((groups, heads, full, full), BF16),
         ],
         compiler_params=pltpu.CompilerParams(vmem_limit_bytes=48 << 20),
-        cost_estimate=pl.CostEstimate(flops=flops, transcendentals=groups * heads * full * full, bytes_accessed=groups * heads * full * full * 2 + 5 * groups * full * width * 2),
+        cost_estimate=cost(flops=flops, transcendentals=groups * heads * full * full, bytes_accessed=groups * heads * full * full * 2 + 5 * groups * full * width * 2),
         name="attend_forward",
     )(lengths, by_heads, by_heads, by_heads, position, bias)
 
@@ -163,7 +173,7 @@
             jax.ShapeDtypeStruct((2, width), F32),
         ],
         compiler_params=pltpu.CompilerParams(vmem_limit_bytes=48 << 20),
-        cost_estimate=pl.CostEstimate(flops=flops, transcendentals=0, bytes_accessed=groups * heads * full * full * 2 + 8 * groups * full * width * 2),
+        cost_estimate=cost(flops=flops, transcendentals=0, bytes_accessed=groups * heads * full * full * 2 + 8 * groups * full * width * 2),
         name="attend_backward",
     )(probs, by_heads, by_heads, by_heads, grad_heads, position, bias)
 
@@ -199,7 +209,7 @@
         out_specs=pl.BlockSpec((1, *shape[1:]), lambda s: (s, 0, 0, 0, 0)),
         out_shape=jax.ShapeDtypeStruct(shape, BF16),
         compiler_params=pltpu.CompilerParams(vmem_limit_bytes=48 << 20),
-        cost_estimate=pl.CostEstimate(flops=2 * rows * depth * width * parts * len(weights), transcendentals=0, bytes_accessed=2 * len(weights) * (rows + depth) * width * parts + 2 * rows * depth),
+        cost_estimate=cost(flops=2 * rows * depth * width * parts * len(weights), transcendentals=0, bytes_accessed=2 * len(weights) * (rows + depth) * width * parts + 2 * rows * depth),
         name="project_heads",
     )(left, *weights)
 
@@ -222,7 +232,7 @@
         out_specs=pl.BlockSpec((1, *shape[1:]), lambda s: (s, 0, 0, 0)),
         out_shape=jax.ShapeDtypeStruct(shape, BF16),
         compiler_params=pltpu.CompilerParams(vmem_limit_bytes=48 << 20),
-        cost_estimate=pl.CostEstimate(flops=2 * rows * depth * width * parts, transcendentals=0, bytes_accessed=2 * (rows + depth) * width * parts + 2 * rows * depth),
+        cost_estimate=cost(flops=2 * rows * depth * width * parts, transcendentals=0, bytes_accessed=2 * (rows + depth) * width * parts + 2 * rows * depth),
         name="unproject_heads",
     )(left, weight)
 
@@ -251,7 +261,7 @@
         out_specs=pl.BlockSpec((rows, depth), lambda s: (0, 0)),
         out_shape=jax.ShapeDtypeStruct((rows, depth), F32),
         compiler_params=pltpu.CompilerParams(vmem_limit_bytes=48 << 20),
-        cost_estimate=pl.CostEstimate(flops=2 * rows * depth * width * parts * count, transcendentals=0, bytes_accessed=2 * count * (rows + depth) * width * parts + 4 * rows * depth),
+        cost_estimate=cost(flops=2 * rows * depth * width * parts * count, transcendentals=0, bytes_accessed=2 * count * (rows + depth) * width * parts + 4 * rows * depth),
         name="join_heads",
     )(grads, *weights)
 
@@ -307,6 +317,12 @@
     for job, flight in zip(jobs, landed):
         job.flight = list(flight)
         job.land()
+    moving = [job for job in jobs if isinstance(job, (Reduce, Bundle)) and job.result is None]
+    if tokens and moving:
+        parts = tuple(tuple(job.parts) for job in moving)
+        tokens, parts = lax.optimization_barrier((tokens, parts))
+        for job, held in zip(moving, parts):
+            job.parts = list(held)
     return tokens[0] if len(tokens) == 1 else tokens
 
 
@@ -365,7 +381,7 @@
         ),
         out_shape=[jax.ShapeDtypeStruct(shape, BF16) for shape in shapes],
         compiler_params=pltpu.CompilerParams(vmem_limit_bytes=48 << 20),
-        cost_estimate=pl.CostEstimate(flops=0, transcendentals=0, bytes_accessed=4 * sum(h * w for h, w in shapes)),
+        cost_estimate=cost(flops=0, transcendentals=0, bytes_accessed=4 * sum(h * w for h, w in shapes)),
         name=name,
     )(places, mine, theirs)
 
@@ -519,7 +535,7 @@
         out_shape=[jax.ShapeDtypeStruct(shape, BF16)] * number,
         input_output_aliases=aliases,
         compiler_params=pltpu.CompilerParams(vmem_limit_bytes=48 << 20),
-        cost_estimate=pl.CostEstimate(flops=2 * samples * depth * work, transcendentals=0, bytes_accessed=2 * (samples * (depth + work) + depth * work)),
+        cost_estimate=cost(flops=2 * samples * depth * work, transcendentals=0, bytes_accessed=2 * (samples * (depth + work) + depth * work)),
         name=name,
     )(places, *operands)
 
@@ -535,7 +551,7 @@
     def __init__(self, grid, places, pairs, width, order, name, sub=None):
         self.grid, self.places, self.pairs, self.width = grid, places, pairs, width
         self.axes, self.name, self.sub = tuple(order), name, sub
-        self.extra = None
+        self.extra, self.result = None, None
         self.heights = [left.shape[1] // (grid.a * grid.b) for left, _ in pairs]
         columns = grid.y * grid.c
         self.counts = [
@@ -587,30 +603,29 @@
 
 class Bundle:
     def __init__(self, *jobs):
-        self.jobs, self.stage = jobs, 0
+        self.jobs, self.stage, self.result = jobs, 0, None
         self.grid = jobs[0].grid
-        self.near, self.away = (
-            jnp.concatenate([job.parts[k] for job in jobs], axis=1) for k in range(2)
-        )
+        self.parts = [jnp.concatenate([job.parts[k] for job in jobs], axis=1) for k in range(2)]
 
     def send(self):
-        self.flight = [self.grid.swap(self.away, 1 << self.stage)]
+        self.flight = [self.grid.swap(self.parts[1], 1 << self.stage)]
 
     def land(self):
-        total = [self.near, self.flight[0]]
+        total = [self.parts[0], self.flight[0]]
         self.stage += 1
         if self.stage < self.grid.bits:
-            half = self.near.shape[0] // 2
-            self.near, self.away = (
+            half = self.parts[0].shape[0] // 2
+            self.parts = [
                 added([part[k * half : (k + 1) * half] for part in total]).astype(BF16)
                 for k in range(2)
-            )
+            ]
             return
         row = 0
         for job in self.jobs:
             height = job.parts[0].shape[1]
             job.result = added([part[0, row : row + height] for part in total])
             row += height
+        self.result = True
 
 
 def gather_everywhere(shard):
@@ -801,44 +816,39 @@
     model_width = acoustic_sequence.shape[2]
     piece_width = model_width // (grid.y * grid.c)
     gather = partial(Gather, grid, places)
-    first = gather([opening_dense_entry_projection], piece_width, True, "gather_opening_entry")
     second = gather([opening_dense_exit_projection], piece_width, True, "gather_opening_exit")
+    sixth = gather([closing_dense_exit_projection], piece_width, False, "gather_closing_exit")
     third = gather(
         [request_projection, lookup_projection, content_projection_kernel, relative_offset_projection],
         piece_width,
         False,
         "gather_attention",
     )
-    first.send("a")
+    macaron_in_all = gather_everywhere(opening_dense_entry_projection)
     small.send("a")
-    settle([first, small])
-    first.send("b")
+    second.send("a")
+    settle([small, second])
     small.send("b")
-    second.send("a")
-    settle([first, small, second])
-    conv_shards, entry_shard, exit_shard, quant_shard, lexicon_shard, first.value = lax.optimization_barrier(
-        (
-            (mixing_exit_projection, unit_kernel_after_normalizing, unit_kernel_before_gating),
-            closing_dense_entry_projection,
-            closing_dense_exit_projection,
-            discretizer_score_projection,
-            lexicon_vectors,
-            first.value,
-        )
-    )
-    convolution_all = gather_everywhere(jnp.concatenate(conv_shards, axis=1))
-    out_all, conv_out_all, conv_in_all = jnp.split(
-        convolution_all, [model_width, 2 * model_width], axis=1
-    )
-    closing_in_all = gather_everywhere(entry_shard)
-    closing_out_all = gather_everywhere(exit_shard)
-    quantizer_all = gather_everywhere(jnp.concatenate([quant_shard, lexicon_shard], axis=1))
+    second.send("b")
+    third.send("a")
+    settle([small, second, third])
     small_all = small.whole()
     vectors_all, depth_all = small_all[:vector_rows], small_all[vector_rows:]
-    first.send("y")
-    second.send("b")
-    third.send("a")
-    settle([first, second, third])
+    middle_shards = (
+        mixing_exit_projection,
+        unit_kernel_after_normalizing,
+        unit_kernel_before_gating,
+        discretizer_score_projection,
+        lexicon_vectors,
+    )
+    middle_shards, entry_shard, second.value = lax.optimization_barrier(
+        (middle_shards, closing_dense_entry_projection, second.value)
+    )
+    middle_all = gather_everywhere(jnp.concatenate(middle_shards, axis=1))
+    out_all, conv_out_all, conv_in_all, quant_all, codebook_all = jnp.split(
+        middle_all, [model_width * i for i in (1, 2, 4, 5)], axis=1
+    )
+    closing_in_all = gather_everywhere(entry_shard)
     groups, local_len, model_width = acoustic_sequence.shape
     seq_count = lax.axis_size("seq")
     seq_place = lax.axis_index("seq")
@@ -858,9 +868,10 @@
     inputs_f = inputs_low.astype(jnp.float32)
     second.send("y")
     third.send("b")
-    (macaron_in_all,) = first.whole()
     macaron_saved = ffn_enter(inputs_f, params_f[0], params_f[5], macaron_in_all)
-    macaron_hidden = settle([second, third], macaron_saved[2])
+    sixth.send("a")
+    macaron_hidden = settle([second, third, sixth], macaron_saved[2])
+    sixth.send("b")
     macaron_saved = (*macaron_saved[:2], macaron_hidden)
     (macaron_out_all,) = second.whole()
     query_all, key_all, value_all, pos_all = third.whole()
@@ -873,8 +884,9 @@
     pos_columns = lax.dynamic_slice_in_dim(pos_all, seq_place * local_width, local_width, 1)
     position_low = matmul_rows(table_low, pos_columns).astype(jnp.bfloat16)
     biases = lax.dynamic_slice_in_dim(params_f[12:14], seq_place * local_width, local_width, 1)
-    by_heads, position_low = lax.optimization_barrier((by_heads, position_low))
+    by_heads, position_low = settle([], by_heads, position_low)
     attended_low, probs = attend_forward(by_heads, position_low, biases, utterance_durations)
+    attended_low = settle([sixth], attended_low)
     back_time = lax.all_to_all(
         attended_low, "seq", split_axis=0, concat_axis=0, tiled=True
     )
@@ -903,11 +915,11 @@
     bound_norm = partial(batch_norm, count_all=count_all)
     normalized = bound_norm(conv_value, sum_first, sum_second, params_f[10], params_f[11])
     act_low = jax.nn.silu(normalized).astype(jnp.bfloat16)
+    (closing_out_all,) = sixth.whole()
     third_mid = second_mid + matmul_rows(act_low, conv_out_all)
     closing_value, closing_saved = ffn_forward(
         third_mid, params_f[3], params_f[8], closing_in_all, closing_out_all
     )
-    quant_all, codebook_all = quantizer_all[:, :entries], quantizer_all[:, entries:]
     quant_logits = matmul_rows(inputs_low, quant_all)
     scaled_logits = (
         quant_logits
@@ -1020,14 +1032,16 @@
     grad_stack, grad_position_low, grad_biases = attend_backward(
         probs, by_heads, grad_heads, position_low, biases
     )
-    grad_stack = settle([closing_job, early_job], grad_stack)
+    grad_stack = settle([early_job], grad_stack)
     grad_time = lax.all_to_all(grad_stack, "seq", split_axis=0, concat_axis=0, tiled=True)
     position_parts = weight_grad(
         grid, places, table_low, grad_position_low, piece_width, 0, height, 0, None, "b",
         name="position_grad", local=True,
     )
     middle_job.near()
-    grad_time, *position_parts = settle([], grad_time, *position_parts, hold=[middle_job])
+    grad_time, *position_parts = settle(
+        [closing_job], grad_time, *position_parts, hold=[middle_job]
+    )
     closing_job.send(1)
     early_job.send(1)
     middle_job.send(0)
@@ -1051,12 +1065,9 @@
     macaron_out_job.ship()
     attention_job.near()
     macaron_out_job.near()
-    mac_out_low = settle(
-        [closing_job, early_job], mac_out_low, hold=[attention_job, macaron_out_job]
-    )
-    first_tails = Bundle(closing_job, early_job)
-    first_tails.send()
+    mac_out_low = settle([], mac_out_low, hold=[attention_job, macaron_out_job])
     attention_job.send(0)
+    macaron_out_job.send(0)
     mac_pre_low, mac_out_low = ffn_backward_exit(mac_out_low, macaron_out_all, macaron_saved)
     halves = mac_pre_low.shape[1] // model_width // 2
     macaron_in_jobs = [
@@ -1065,12 +1076,14 @@
     ]
     for job in macaron_in_jobs:
         job.far()
-    mac_pre_low = settle([middle_job, first_tails], mac_pre_low, hold=macaron_in_jobs)
+    mac_pre_low = settle(
+        [closing_job, early_job, middle_job], mac_pre_low, hold=macaron_in_jobs
+    )
     for job in macaron_in_jobs:
         job.ship()
+    first_tails = Bundle(closing_job, early_job)
     first_tails.send()
     middle_job.send(1)
-    macaron_out_job.send(0)
     grad_macaron, scale_zero, shift_zero = ffn_backward_entry(
         mac_pre_low, inputs_f, params_f[0], params_f[5], macaron_in_all
     )
@@ -1110,15 +1123,16 @@
         job.send(0)
     attention_job.send(1)
     macaron_out_job.send(1)
+    first_tails.send()
     middle_tails = Bundle(middle_job)
     middle_tails.send()
     small.send("y")
-    settle([small, middle_tails, attention_job, macaron_out_job, *macaron_in_jobs])
+    settle([small, first_tails, middle_tails, attention_job, macaron_out_job, *macaron_in_jobs])
     for job in macaron_in_jobs:
         job.send(1)
-    middle_tails.send()
     late_tails = Bundle(attention_job, macaron_out_job)
     late_tails.send()
+    middle_tails.send()
     small.send("b")
     settle([small, middle_tails, late_tails, *macaron_in_jobs])
     late_tails.send()

time: 986 us -> 959 us (0.973)
  waiting for transfers between devices: 397 us -> 358 us
  starting transfers between devices: 103 us -> 88.4 us
  matrix products: 112 us -> 124 us
    ppermute x48 -> x47, waiting for transfers between devices: 216 us -> 169 us  [shift(): return lax.ppermute(value, name, pairs)]
    all_to_all x1, waiting for transfers between devices: 41.6 us -> 24.8 us  [per_device(): lax.all_to_all(stacked, 'seq', split_axis=0, concat_axis=0, tiled=True)]
    all_to_all x1, waiting for transfers between devices: 2.19 us -> 16 us  [per_device(): lax.all_to_all(grad_attended, 'seq', split_axis=0, concat_axis=0, tiled=T...]
    ppermute x48 -> x47, starting transfers between devices: 50.5 us -> 43 us  [shift(): return lax.ppermute(value, name, pairs)]
    unnamed x291 -> x306, local copies, waits for them, and re-layouts: 36.5 us -> 39.1 us
  transfers between devices with their start and end apart: 78 -> 76, of which waited for: 39 -> 36; matrix products, arithmetic and copies ran while one was open for 20% -> 19% of each run, Pallas kernels for 19% -> 17%
where the time goes in v4:
time: 959 us; the launch traced here: 947 us
  waiting for transfers between devices  358 us (37%)
  Pallas kernels  219 us (23%)
  matrix products  124 us (13%)
  starting transfers between devices  88.4 us (9%)
  other arithmetic  84.7 us (9%)
  local copies, waits for them, and re-layouts  56.5 us (6%)
  between operations  16.8 us (2%)
    ppermute x47, waiting for transfers between devices, shift(): return lax.ppermute(value, name, pairs)  169 us
    pallas_call x23, Pallas kernels, weight_grad(): pl.pallas_call(body, grid_spec=pltpu.PrefetchScalarGridSpec(num_scalar_pr...  119 us
    ppermute x8, waiting for transfers between devices, swap(): return lax.ppermute(value, 'batch', pairs)  67.7 us
    dot_general x11, matrix products, matmul_rows(): return jnp.dot(left_side, right_side, preferred_element_type=jnp.float32)  63.1 us
    dot_general x8, matrix products, times_transpose(): lax.dot_general(left_side, right_side, (((1,), (1,)), ((), ())), preferre...  61.1 us
    ppermute x47, starting transfers between devices, shift(): return lax.ppermute(value, name, pairs)  43 us
    unnamed x306, local copies, waits for them, and re-layouts  39.1 us
    pallas_call x1, Pallas kernels, attend_backward(): pl.pallas_call(body, grid_spec=pltpu.PrefetchScalarGridSpec(num_scalar_pr...  34.4 us
  transfers between devices with their start and end apart: 76, of which 36 were waited for; matrix products, arithmetic and copies ran while one was open for 19% of the time, Pallas kernels for 17%

profile of v4, /device:TPU:0, one launch (start us, length us, event | category | flops | bytes accessed | tf_op | source)
XLA Modules:
  0.0 947.0 jit_solution(5211163957431207265)
XLA Ops:
  19.1 17.4 %collective-permute-done = bf16[1,1,19,128]{3,2,1,0:T(8,128)(2,1)S(1)} collective-permute-done((bf16[1,1,19,128]{3,2,1,0:T(8,128)(2,1)S(1)}, bf16[1,1,19,128]{3,2,1,0:T(8,128)(2,1)S(1)}, u32[]{:S(2)}, u32[]{:S(2)}) %collective-permute-start) | collective-permute-done | bytes 4896 | tf_op jit(solution)/shard_map/ppermute | solution.py:298
  36.4 8.2 collective-permute-done.1
  53.7 24.0 %collective-permute-done.6 = bf16[1,4,19,128]{3,2,1,0:T(8,128)(2,1)S(1)} collective-permute-done((bf16[1,4,19,128]{3,2,1,0:T(8,128)(2,1)S(1)}, bf16[1,4,19,128]{3,2,1,0:T(8,128)(2,1)S(1)}, u32[]{:S(2)}, u32[]{:S(2)}) %collective-permute-start.6) | collective-permute-done | bytes 19488 | tf_op jit(solution)/shard_map/ppermute | solution.py:298
  77.7 8.1 collective-permute-done.8
  85.8 32.2 %collective-permute-done.9 = bf16[2,512,256]{2,1,0:T(8,128)(2,1)S(1)} collective-permute-done((bf16[2,512,256]{2,1,0:T(8,128)(2,1)S(1)}, bf16[2,512,256]{2,1,0:T(8,128)(2,1)S(1)}, u32[]{:S(2)}, u32[]{:S(2)}) %collective-permute-start.9) | collective-permute-done | bytes 524320 | tf_op jit(solution)/shard_map/ppermute | solution.py:298
  135.0 18.3 %all-gather.4.cloned.1.call-done = bf16[1024,4096]{1,0:T(8,128)(2,1)} async-done(((bf16[32,4096]{1,0:T(8,128)(2,1)}), bf16[1024,4096]{1,0:T(8,128)(2,1)}) %all-gather.4.cloned.1.call-update) | async-done | bytes 8388624 | tf_op jit(solution)/shard_map/all_gather | solution.py:634
  153.3 10.5 %multiply_convert_fusion.1 = (bf16[512,4096]{1,0:T(8,128)(2,1)}, bf16[512,4096]{1,0:T(8,128)(2,1)}) fusion(bf16[512,1024]{1,0:T(8,128)(2,1)S(1)} %fusion.22.refs_0_, bf16[1024,4096]{1,0:T(8,128)(2,1)} %all-gather.4.cloned.1.call-done), kind=kOutput, calls=%fused_computation.21 | convolution fusion | flops 4307550208 | bytes 17825792 | tf_op jit(solution)/shard_map/dot_general | solution.py:721
  163.9 16.2 %collective-permute-done.12 = bf16[2,4,512,256]{3,2,0,1:T(8,128)(2,1)} collective-permute-done((bf16[2,4,512,256]{3,2,0,1:T(8,128)(2,1)}, bf16[2,4,512,256]{3,2,0,1:T(8,128)(2,1)}, u32[]{:S(2)}, u32[]{:S(2)}) %collective-permute-start.12) | collective-permute-done | bytes 2097184 | tf_op jit(solution)/shard_map/ppermute | solution.py:298
  184.5 4.9 pad_maximum_fusion
  192.0 8.6 gather_attention.1
  200.6 10.5 %gather_opening_exit.1 = bf16[4096,1024]{1,0:T(8,128)(2,1)} custom-call(s32[4]{0:T(128)S(1)} %pad_add_fusion.place_ref, bf16[2,8,512,256]{3,2,1,0:T(8,128)(2,1)} %bitcast.26.mine_ref, bf16[2,8,512,256]{3,2,1,0:T(8,128)(2,1)} %collective-permute-done.16.theirs_ref), custom_call_target="tpu_custom_call" | custom-call | bytes 4194304 | tf_op jit(solution)/shard_map/gather_opening_exit/pallas_call | solution.py:374
  211.1 10.0 %fusion.170 = (f32[512]{0:T(512)S(1)}, f32[512,1024]{1,0:T(8,128)S(1)}) fusion(bf16[512,4096]{1,0:T(8,128)(2,1)} %get-tuple-element.167.refs_0_, bf16[4096,1024]{1,0:T(8,128)(2,1)} %gather_opening_exit.1, bf16[512,1024]{1,0:T(8,128)(2,1)S(1)} %bitcast.292), kind=kOutput, calls=%fused_computation.440 | convolution fusion | flops 4297063936 | bytes 15730688 | tf_op jit(solution)/shard_map/dot_general | solution.py:721
  222.4 6.5 project_heads.1
  229.9 4.2 all-to-all-start
  234.2 4.0 fusion.152
  248.1 24.8 %all-to-all-done.q_ref.k_ref.v_ref = bf16[4,3,2,256,256]{4,3,2,1,0:T(8,128)(2,1)S(1)} async-done(((bf16[4,3,2,256,256]{4,3,2,1,0:T(8,128)(2,1)}), bf16[4,3,2,256,256]{4,3,2,1,0:T(8,128)(2,1)S(1)}, u32[]{:S(2)}, u32[]{:S(2)}) %all-to-all-start) | async-done | bytes 3145760 | tf_op jit(solution)/shard_map/all_to_all | solution.py:882
  274.2 20.7 %attend_forward.1 = (bf16[4,2,256,256]{3,2,1,0:T(8,128)(2,1)S(1)}, bf16[2,2,1024,1024]{3,2,1,0:T(8,128)(2,1)}) custom-call(s32[2]{0:T(128)S(1)} %copy-done.51, bf16[4,3,2,256,256]{4,3,2,1,0:T(8,128)(2,1)S(1)} %all-to-all-done.q_ref.k_ref.v_ref, bf16[4,3,2,256,256]{4,3,2,1,0:T(8,128)(2,1)S(1)} %all-to-all-done.q_ref.k_ref.v_ref, ...), custom_call_target="tpu_custom_call" | custom-call | flops 872415232 | bytes 3407872 | tf_op jit(solution)/shard_map/attend_forward/pallas_call | solution.py:58
  300.8 16.3 %all-to-all-done.1 = bf16[4,2,256,256]{3,2,1,0:T(8,128)(2,1)S(1)} async-done(((bf16[4,2,256,256]{3,2,1,0:T(8,128)(2,1)}), bf16[4,2,256,256]{3,2,1,0:T(8,128)(2,1)S(1)}, u32[]{:S(2)}, u32[]{:S(2)}) %all-to-all-start.1) | async-done | bytes 1048608 | tf_op jit(solution)/shard_map/all_to_all | solution.py:890
  323.4 4.9 fusion.14
  355.3 4.6 pad_maximum_fusion.2
  366.6 9.7 %multiply_convert_fusion = (bf16[512,4096]{1,0:T(8,128)(2,1)S(1)}, bf16[512,4096]{1,0:T(8,128)(2,1)}) fusion(bf16[512,1024]{1,0:T(8,128)(2,1)S(1)} %add_convert_fusion.9.refs_0_, bf16[1024,4096]{1,0:T(8,128)(2,1)} %all-gather.8.cloned.1.call-done), kind=kOutput, calls=%fused_computation.19 | convolution fusion | flops 4307550208 | bytes 17825792 | tf_op jit(solution)/shard_map/dot_general | solution.py:721
  376.2 10.6 %gather_closing_exit.1 = bf16[4096,1024]{1,0:T(8,128)(2,1)} custom-call(s32[4]{0:T(128)S(1)} %pad_add_fusion.place_ref, bf16[2,8,512,256]{3,2,1,0:T(8,128)(2,1)} %bitcast.62.mine_ref, bf16[2,8,512,256]{3,2,1,0:T(8,128)(2,1)} %collective-permute-done.26.theirs_ref), custom_call_target="tpu_custom_call" | custom-call | bytes 4194304 | tf_op jit(solution)/shard_map/gather_closing_exit/pallas_call | solution.py:374
  386.8 8.6 fusion.173
  399.9 5.7 closing_0_1.1.refs_2_
  405.7 10.8 %fusion.5.refs_1_ = bf16[512,4096]{1,0:T(8,128)(2,1)S(1)} fusion(bf16[512,4096]{1,0:T(8,128)(2,1)} %get-tuple-element.463, bf16[512,1024]{1,0:T(8,128)(2,1)S(1)} %multiply_convert_fusion.3.refs_1_, bf16[4096,1024]{1,0:T(8,128)(2,1)} %gather_closing_exit.1), kind=kOutput, calls=%fused_computation.12 | convolution fusion | flops 4318035968 | bytes 17825792 | tf_op jit(solution)/shard_map/dot_general | solution.py:725
  416.5 6.7 closing_1_1.1
  428.5 8.6 multiply_reduce_fusion.5
  449.8 6.0 multiply_reduce_fusion.2
  472.8 4.6 early_0_0.1
  477.5 4.6 early_1_0.1
  482.1 4.6 early_2_0.1
  486.7 8.4 closing_0_0.1
  495.1 9.3 closing_1_0.1
  504.5 4.3 multiply_reduce_fusion.1
  519.5 6.3 multiply_reduce_fusion.6
  531.8 4.2 all-to-all-start.2
  537.3 4.1 middle_0_1.1.refs_2_
  547.0 16.0 %all-to-all-done.2.g_ref = bf16[4,2,256,256]{3,2,1,0:T(8,128)(2,1)} async-done(((bf16[4,2,256,256]{3,2,1,0:T(8,128)(2,1)}), bf16[4,2,256,256]{3,2,1,0:T(8,128)(2,1)}, u32[]{:S(2)}, u32[]{:S(2)}) %all-to-all-start.2) | async-done | bytes 1048608 | tf_op jit(solution)/shard_map/all_to_all | solution.py:1021
  563.0 34.4 %attend_backward.1 = (bf16[4,3,2,256,256]{4,3,2,1,0:T(8,128)(2,1)}, bf16[2048,256]{1,0:T(8,128)(2,1)S(1)}, f32[2,256]{1,0:T(2,128)S(1)}) custom-call(bf16[2,2,1024,1024]{3,2,1,0:T(8,128)(2,1)} %get-tuple-element.201.p_ref, bf16[4,3,2,256,256]{4,3,2,1,0:T(8,128)(2,1)} %copy-done.2, bf16[4,3,2,256,256]{4,3,2,1,0:T(8,128)(2,1)} %copy-done.2, ...), custom_call_target="tpu_custom_call" | custom-call | flops 2080374784 | bytes 4194304 | tf_op jit(solution)/shard_map/attend_backward/pallas_call | solution.py:144
  600.3 4.8 all-to-all-start.3
  609.3 4.9 middle_0_0.1
  619.6 22.6 %all-to-all-done.3.grad_ref.refs_1_ = bf16[4,3,2,256,256]{4,3,2,1,0:T(8,128)(2,1)} async-done(((bf16[4,3,2,256,256]{4,3,2,1,0:T(8,128)(2,1)}), bf16[4,3,2,256,256]{4,3,2,1,0:T(8,128)(2,1)}, u32[]{:S(2)}, u32[]{:S(2)}) %all-to-all-start.3) | async-done | bytes 3145760 | tf_op jit(solution)/shard_map/all_to_all | solution.py:1036
  642.2 5.4 fusion.43
  647.6 6.4 join_heads.1
  659.3 7.8 opening_exit_0_1.1
  667.2 6.9 attention_0_1.1
  674.6 4.2 fusion.41
  681.3 8.3 attention_0_0.1
  691.8 8.5 opening_exit_0_0.1
  701.6 12.1 %fusion.11.refs_1_ = bf16[512,4096]{1,0:T(8,128)(2,1)} fusion(bf16[512,4096]{1,0:T(8,128)(2,1)} %get-tuple-element.455, bf16[512,1024]{1,0:T(8,128)(2,1)S(1)} %get-tuple-element.229.refs_1_, bf16[4096,1024]{1,0:T(8,128)(2,1)} %gather_opening_exit.1), kind=kOutput, calls=%fused_computation.18 | convolution fusion | flops 4318035968 | bytes 17825792 | tf_op jit(solution)/shard_map/dot_general | solution.py:725
  713.8 5.4 opening_entry_more_0_1.1
  719.2 5.5 opening_entry_0_1.1
  724.7 7.5 collective-permute-done.41
  738.8 10.2 %fusion.23 = (f32[1024]{0:T(1024)}, f32[512]{0:T(512)}, f32[1024]{0:T(1024)}, f32[512,1024]{1,0:T(8,128)}) fusion(f32[512]{0:T(512)S(1)} %copy-done.135, f32[512]{0:T(512)S(1)} %bitcast.368, bf16[2,256,1024]{2,1,0:T(8,128)(2,1)S(1)} %copy-done.4, f32[1024]{0:T(1024)S(1)} %bitcast.347, bf16[512,4096]{1,0:T(8,128)(2,1)S(1)} %copy-done.53, ...), kind=kOutput, calls=%fused_computation.62 | convolution fusion | flops 4299683328 | bytes 15747072 | tf_op jit(solution)/shard_map/dot_general | solution.py:725
  766.2 4.8 opening_entry_more_0_0.1
  771.0 6.4 opening_entry_0_0.1
  777.4 28.0 %collective-permute-done.45 = bf16[4,384,256]{2,1,0:T(8,128)(2,1)} collective-permute-done((bf16[4,384,256]{2,1,0:T(8,128)(2,1)S(1)}, bf16[4,384,256]{2,1,0:T(8,128)(2,1)}, u32[]{:S(2)}, u32[]{:S(2)}) %collective-permute-start.45) | collective-permute-done | bytes 786464 | tf_op jit(solution)/shard_map/ppermute | solution.py:298
  828.4 28.1 %collective-permute-done.52 = bf16[1,1408,256]{2,1,0:T(8,128)(2,1)S(1)} collective-permute-done((bf16[1,1408,256]{2,1,0:T(8,128)(2,1)S(1)}, bf16[1,1408,256]{2,1,0:T(8,128)(2,1)S(1)}, u32[]{:S(2)}, u32[]{:S(2)}) %collective-permute-start.52) | collective-permute-done | bytes 720928 | tf_op jit(solution)/shard_map/ppermute | solution.py:304
  856.5 6.6 collective-permute-done.56
  871.8 6.8 collective-permute-done.58
  878.6 13.0 %collective-permute-done.59 = bf16[1,384,256]{2,1,0:T(8,128)(2,1)S(1)} collective-permute-done((bf16[1,384,256]{2,1,0:T(8,128)(2,1)S(1)}, bf16[1,384,256]{2,1,0:T(8,128)(2,1)S(1)}, u32[]{:S(2)}, u32[]{:S(2)}) %collective-permute-start.59) | collective-permute-done | bytes 196640 | tf_op jit(solution)/shard_map/ppermute | solution.py:304
  902.0 10.7 %collective-permute-done.64 = f32[19,1024]{1,0:T(8,128)S(1)} collective-permute-done((f32[19,1024]{1,0:T(8,128)S(1)}, f32[19,1024]{1,0:T(8,128)S(1)}, u32[]{:S(2)}, u32[]{:S(2)}) %collective-permute-start.64) | collective-permute-done | bytes 77856 | tf_op jit(solution)/shard_map/ppermute | solution.py:298
  912.8 14.0 %collective-permute-done.67 = bf16[1,1024,256]{2,1,0:T(8,128)(2,1)S(1)} collective-permute-done((bf16[1,1024,256]{2,1,0:T(8,128)(2,1)S(1)}, bf16[1,1024,256]{2,1,0:T(8,128)(2,1)S(1)}, u32[]{:S(2)}, u32[]{:S(2)}) %collective-permute-start.67) | collective-permute-done | bytes 524320 | tf_op jit(solution)/shard_map/ppermute | solution.py:304
  929.9 9.4 collective-permute-done.68
  (614 shorter events, 259.5 us)
Async XLA Ops:
  7.2 146.1 %all-gather.4.cloned.1.call-start = ((), (), s32[]{:S(2)}) async-start(), calls=%async_computation.4 | async-start | bytes 8650752 | tf_op jit(solution)/shard_map/all_gather | solution.py:634
  9.2 309.0 %all-gather.6.cloned.1.call-start = ((), (), s32[]{:S(2)}) async-start(), calls=%async_computation.5 | async-start | bytes 12976128 | tf_op jit(solution)/shard_map/all_gather | solution.py:634
  10.3 34.7 %collective-permute-start.3 = (bf16[1,512,256]{2,1,0:T(8,128)(2,1)S(1)}, bf16[1,512,256]{2,1,0:T(8,128)(2,1)S(1)}, u32[]{:S(2)}, u32[]{:S(2)}) collective-permute-start(bf16[1,512,256]{2,1,0:T(8,128)(2,1)S(1)} %get-tuple-element.397), channel_id=1, source_target_pairs={{0,8},{4,12},{8,16},{12,20},{16,24},{20,28},{24,0},{28,4},{1,9},{5... | collective-permute-start | bytes 786440 | tf_op jit(solution)/shard_map/ppermute | solution.py:298
  13.4 31.7 %collective-permute-start.4 = (bf16[1,512,256]{2,1,0:T(8,128)(2,1)S(1)}, bf16[1,512,256]{2,1,0:T(8,128)(2,1)S(1)}, u32[]{:S(2)}, u32[]{:S(2)}) collective-permute-start(bf16[1,512,256]{2,1,0:T(8,128)(2,1)S(1)} %get-tuple-element.397), channel_id=1, source_target_pairs={{0,16},{4,20},{8,24},{12,28},{16,0},{20,4},{24,8},{28,12},{1,17},{... | collective-permute-start | bytes 786440 | tf_op jit(solution)/shard_map/ppermute | solution.py:298
  16.0 29.1 %collective-permute-start.5 = (bf16[1,512,256]{2,1,0:T(8,128)(2,1)S(1)}, bf16[1,512,256]{2,1,0:T(8,128)(2,1)S(1)}, u32[]{:S(2)}, u32[]{:S(2)}) collective-permute-start(bf16[1,512,256]{2,1,0:T(8,128)(2,1)S(1)} %get-tuple-element.397), channel_id=1, source_target_pairs={{0,24},{4,28},{8,0},{12,4},{16,8},{20,12},{24,16},{28,20},{1,25},{... | collective-permute-start | bytes 786440 | tf_op jit(solution)/shard_map/ppermute | solution.py:298
  18.0 18.4 %collective-permute-start = (bf16[1,1,19,128]{3,2,1,0:T(8,128)(2,1)S(1)}, bf16[1,1,19,128]{3,2,1,0:T(8,128)(2,1)S(1)}, u32[]{:S(2)}, u32[]{:S(2)}) collective-permute-start(bf16[1,1,19,128]{3,2,1,0:T(8,128)(2,1)S(1)} %maximum_bitcast_fusion.2), channel_id=1, source_target_pairs={{0,8},{4,12},{8,16},{12,20},{16,24},{20,28},{24,0},{28,4},{1,9},{5... | collective-permute-start | bytes 14600 | tf_op jit(solution)/shard_map/ppermute | solution.py:298
  18.7 25.9 %collective-permute-start.1 = (bf16[1,1,19,128]{3,2,1,0:T(8,128)(2,1)S(1)}, bf16[1,1,19,128]{3,2,1,0:T(8,128)(2,1)S(1)}, u32[]{:S(2)}, u32[]{:S(2)}) collective-permute-start(bf16[1,1,19,128]{3,2,1,0:T(8,128)(2,1)S(1)} %maximum_bitcast_fusion.2), channel_id=1, source_target_pairs={{0,16},{4,20},{8,24},{12,28},{16,0},{20,4},{24,8},{28,12},{1,17},{... | collective-permute-start | bytes 14600 | tf_op jit(solution)/shard_map/ppermute | solution.py:298
  36.4 8.6 collective-permute-start.2
  45.2 72.8 %collective-permute-start.7 = (bf16[1,4,512,256]{3,2,1,0:T(8,128)(2,1)S(1)}, bf16[1,4,512,256]{3,2,1,0:T(8,128)(2,1)S(1)}, u32[]{:S(2)}, u32[]{:S(2)}) collective-permute-start(bf16[1,4,512,256]{3,2,1,0:T(8,128)(2,1)S(1)} %get-tuple-element.395), channel_id=1, source_target_pairs={{0,4},{4,0},{8,12},{12,8},{16,20},{20,16},{24,28},{28,24},{1,5},{5... | collective-permute-start | bytes 3145736 | tf_op jit(solution)/shard_map/ppermute | solution.py:298
  47.0 30.6 %collective-permute-start.10 = (bf16[2,512,256]{2,1,0:T(8,128)(2,1)S(1)}, bf16[2,512,256]{2,1,0:T(8,128)(2,1)S(1)}, u32[]{:S(2)}, u32[]{:S(2)}) collective-permute-start(bf16[2,512,256]{2,1,0:T(8,128)(2,1)S(1)} %get-tuple-element.407), channel_id=1, source_target_pairs={{0,24},{4,28},{8,0},{12,4},{16,8},{20,12},{24,16},{28,20},{1,25},{... | collective-permute-start | bytes 1572872 | tf_op jit(solution)/shard_map/ppermute | solution.py:298
  50.2 35.6 %collective-permute-start.8 = (bf16[2,512,256]{2,1,0:T(8,128)(2,1)S(1)}, bf16[2,512,256]{2,1,0:T(8,128)(2,1)S(1)}, u32[]{:S(2)}, u32[]{:S(2)}) collective-permute-start(bf16[2,512,256]{2,1,0:T(8,128)(2,1)S(1)} %get-tuple-element.407), channel_id=1, source_target_pairs={{0,8},{4,12},{8,16},{12,20},{16,24},{20,28},{24,0},{28,4},{1,9},{5... | collective-permute-start | bytes 1572872 | tf_op jit(solution)/shard_map/ppermute | solution.py:298
  50.2 67.8 %collective-permute-start.9 = (bf16[2,512,256]{2,1,0:T(8,128)(2,1)S(1)}, bf16[2,512,256]{2,1,0:T(8,128)(2,1)S(1)}, u32[]{:S(2)}, u32[]{:S(2)}) collective-permute-start(bf16[2,512,256]{2,1,0:T(8,128)(2,1)S(1)} %get-tuple-element.407), channel_id=1, source_target_pairs={{0,16},{4,20},{8,24},{12,28},{16,0},{20,4},{24,8},{28,12},{1,17},{... | collective-permute-start | bytes 1572872 | tf_op jit(solution)/shard_map/ppermute | solution.py:298
  53.1 24.6 %collective-permute-start.6 = (bf16[1,4,19,128]{3,2,1,0:T(8,128)(2,1)S(1)}, bf16[1,4,19,128]{3,2,1,0:T(8,128)(2,1)S(1)}, u32[]{:S(2)}, u32[]{:S(2)}) collective-permute-start(bf16[1,4,19,128]{3,2,1,0:T(8,128)(2,1)S(1)} %pad_maximum_fusion.24), channel_id=1, source_target_pairs={{0,4},{4,0},{8,12},{12,8},{16,20},{20,16},{24,28},{28,24},{1,5},{5... | collective-permute-start | bytes 58376 | tf_op jit(solution)/shard_map/ppermute | solution.py:298
  122.3 244.3 %all-gather.8.cloned.1.call-start = ((), (), s32[]{:S(2)}) async-start(), calls=%async_computation.6 | async-start | bytes 8650752 | tf_op jit(solution)/shard_map/all_gather | solution.py:634
  123.4 40.4 %collective-permute-start.13 = (bf16[2,512,256]{2,1,0:T(8,128)(2,1)}, bf16[2,512,256]{2,1,0:T(8,128)(2,1)S(1)}, u32[]{:S(2)}, u32[]{:S(2)}) collective-permute-start(bf16[2,512,256]{2,1,0:T(8,128)(2,1)} %get-tuple-element.405), channel_id=1, source_target_pairs={{0,8},{4,12},{8,16},{12,20},{16,24},{20,28},{24,0},{28,4},{1,9},{5... | collective-permute-start | bytes 1572872 | tf_op jit(solution)/shard_map/ppermute | solution.py:298
  123.4 40.4 %collective-permute-start.14 = (bf16[2,512,256]{2,1,0:T(8,128)(2,1)}, bf16[2,512,256]{2,1,0:T(8,128)(2,1)S(1)}, u32[]{:S(2)}, u32[]{:S(2)}) collective-permute-start(bf16[2,512,256]{2,1,0:T(8,128)(2,1)} %get-tuple-element.405), channel_id=1, source_target_pairs={{0,16},{4,20},{8,24},{12,28},{16,0},{20,4},{24,8},{28,12},{1,17},{... | collective-permute-start | bytes 1572872 | tf_op jit(solution)/shard_map/ppermute | solution.py:298
  126.2 37.6 %collective-permute-start.15 = (bf16[2,512,256]{2,1,0:T(8,128)(2,1)}, bf16[2,512,256]{2,1,0:T(8,128)(2,1)}, u32[]{:S(2)}, u32[]{:S(2)}) collective-permute-start(bf16[2,512,256]{2,1,0:T(8,128)(2,1)} %get-tuple-element.405), channel_id=1, source_target_pairs={{0,24},{4,28},{8,0},{12,4},{16,8},{20,12},{24,16},{28,20},{1,25},{... | collective-permute-start | bytes 1572872 | tf_op jit(solution)/shard_map/ppermute | solution.py:298
  132.1 47.9 %collective-permute-start.12 = (bf16[2,4,512,256]{3,2,0,1:T(8,128)(2,1)}, bf16[2,4,512,256]{3,2,0,1:T(8,128)(2,1)}, u32[]{:S(2)}, u32[]{:S(2)}) collective-permute-start(bf16[2,4,512,256]{3,2,0,1:T(8,128)(2,1)} %get-tuple-element.371), channel_id=1, source_target_pairs={{0,4},{4,0},{8,12},{12,8},{16,20},{20,16},{24,28},{28,24},{1,5},{5... | collective-permute-start | bytes 6291464 | tf_op jit(solution)/shard_map/ppermute | solution.py:298
  132.1 48.0 %collective-permute-start.11 = (bf16[1,2,4,512,256]{4,3,2,1,0:T(8,128)(2,1)}, bf16[1,2,4,512,256]{4,3,2,1,0:T(8,128)(2,1)}, u32[]{:S(2)}, u32[]{:S(2)}) collective-permute-start(bf16[1,2,4,512,256]{4,3,2,1,0:T(8,128)(2,1)} %pad_maximum_fusion.3), channel_id=1, source_target_pairs={{0,2},{1,3},{2,0},{3,1},{4,6},{5,7},{6,4},{7,5},{8,10},{9,11},{10,... | collective-permute-start | bytes 6291464 | tf_op jit(solution)/shard_map/ppermute | solution.py:298
  184.5 7.5 collective-permute-start.18
  189.4 11.1 %collective-permute-start.16 = (bf16[2,8,512,256]{3,2,1,0:T(8,128)(2,1)}, bf16[2,8,512,256]{3,2,1,0:T(8,128)(2,1)}, u32[]{:S(2)}, u32[]{:S(2)}) collective-permute-start(bf16[2,8,512,256]{3,2,1,0:T(8,128)(2,1)} %bitcast.26.mine_ref), channel_id=1, source_target_pairs={{0,1},{1,0},{2,3},{3,2},{4,5},{5,4},{6,7},{7,6},{8,9},{9,8},{10,11... | collective-permute-start | bytes 12582920 | tf_op jit(solution)/shard_map/ppermute | solution.py:298
  229.9 43.0 %all-to-all-start = ((bf16[4,3,2,256,256]{4,3,2,1,0:T(8,128)(2,1)}), bf16[4,3,2,256,256]{4,3,2,1,0:T(8,128)(2,1)S(1)}, u32[]{:S(2)}, u32[]{:S(2)}) async-start(bf16[4,3,2,256,256]{4,3,2,1,0:T(8,128)(2,1)} %project_heads.1), calls=%async_computation | async-start | bytes 6291456 | tf_op jit(solution)/shard_map/all_to_all | solution.py:882
  238.2 56.7 %collective-permute-start.17 = (bf16[2,4,512,256]{3,2,1,0:T(8,128)(2,1)}, bf16[2,4,512,256]{3,2,1,0:T(8,128)(2,1)}, u32[]{:S(2)}, u32[]{:S(2)}) collective-permute-start(bf16[2,4,512,256]{3,2,1,0:T(8,128)(2,1)} %get-tuple-element.369), channel_id=1, source_target_pairs={{0,4},{4,0},{8,12},{12,8},{16,20},{20,16},{24,28},{28,24},{1,5},{5... | collective-permute-start | bytes 6291464 | tf_op jit(solution)/shard_map/ppermute | solution.py:298
  295.8 21.3 %all-to-all-start.1 = ((bf16[4,2,256,256]{3,2,1,0:T(8,128)(2,1)}), bf16[4,2,256,256]{3,2,1,0:T(8,128)(2,1)S(1)}, u32[]{:S(2)}, u32[]{:S(2)}) async-start(bf16[4,2,256,256]{3,2,1,0:T(8,128)(2,1)} %copy-done.48), calls=%async_computation.1 | async-start | bytes 2097152 | tf_op jit(solution)/shard_map/all_to_all | solution.py:890
  353.1 6.8 collective-permute-start.25
  359.9 16.3 %collective-permute-start.26 = (bf16[2,8,512,256]{3,2,1,0:T(8,128)(2,1)}, bf16[2,8,512,256]{3,2,1,0:T(8,128)(2,1)}, u32[]{:S(2)}, u32[]{:S(2)}) collective-permute-start(bf16[2,8,512,256]{3,2,1,0:T(8,128)(2,1)} %bitcast.62.mine_ref), channel_id=1, source_target_pairs={{0,1},{1,0},{2,3},{3,2},{4,5},{5,4},{6,7},{7,6},{8,9},{9,8},{10,11... | collective-permute-start | bytes 12582920 | tf_op jit(solution)/shard_map/ppermute | solution.py:298
  423.2 63.5 %collective-permute-start.32 = (bf16[2,2,4,1024,256]{4,3,2,1,0:T(8,128)(2,1)}, bf16[2,2,4,1024,256]{4,3,2,1,0:T(8,128)(2,1)}, u32[]{:S(2)}, u32[]{:S(2)}) collective-permute-start(bf16[2,2,4,1024,256]{4,3,2,1,0:T(8,128)(2,1)} %closing_1_1.1), channel_id=1, source_target_pairs={{0,1},{1,0},{2,3},{3,2},{4,5},{5,4},{6,7},{7,6},{8,9},{9,8},{10,11... | collective-permute-start | bytes 25165832 | tf_op jit(solution)/shard_map/ppermute | solution.py:298
  449.2 23.6 %collective-permute-start.33 = (bf16[2,2,4,384,256]{4,3,2,1,0:T(8,128)(2,1)S(1)}, bf16[2,2,4,384,256]{4,3,2,1,0:T(8,128)(2,1)}, u32[]{:S(2)}, u32[]{:S(2)}) collective-permute-start(bf16[2,2,4,384,256]{4,3,2,1,0:T(8,128)(2,1)S(1)} %early_2_1.1), channel_id=1, source_target_pairs={{0,1},{1,0},{2,3},{3,2},{4,5},{5,4},{6,7},{7,6},{8,9},{9,8},{10,11... | collective-permute-start | bytes 9437192 | tf_op jit(solution)/shard_map/ppermute | solution.py:298
  508.8 6.7 collective-permute-start.34
  510.1 5.4 collective-permute-start.35
  515.1 82.3 %collective-permute-start.37 = (bf16[2,4,384,256]{3,2,1,0:T(8,128)(2,1)}, bf16[2,4,384,256]{3,2,1,0:T(8,128)(2,1)}, u32[]{:S(2)}, u32[]{:S(2)}) collective-permute-start(bf16[2,4,384,256]{3,2,1,0:T(8,128)(2,1)} %get-tuple-element.200), channel_id=1, source_target_pairs={{0,2},{1,3},{2,0},{3,1},{4,6},{5,7},{6,4},{7,5},{8,10},{9,11},{10,... | collective-permute-start | bytes 4718600 | tf_op jit(solution)/shard_map/ppermute | solution.py:298
  515.4 126.8 %collective-permute-start.36 = (bf16[2,4,1024,256]{3,2,1,0:T(8,128)(2,1)}, bf16[2,4,1024,256]{3,2,1,0:T(8,128)(2,1)}, u32[]{:S(2)}, u32[]{:S(2)}) collective-permute-start(bf16[2,4,1024,256]{3,2,1,0:T(8,128)(2,1)} %get-tuple-element.199), channel_id=1, source_target_pairs={{0,4},{4,0},{8,12},{12,8},{16,20},{20,16},{24,28},{28,24},{1,5},{5... | collective-permute-start | bytes 12582920 | tf_op jit(solution)/shard_map/ppermute | solution.py:298
  531.8 31.3 %all-to-all-start.2 = ((bf16[4,2,256,256]{3,2,1,0:T(8,128)(2,1)}), bf16[4,2,256,256]{3,2,1,0:T(8,128)(2,1)}, u32[]{:S(2)}, u32[]{:S(2)}) async-start(bf16[4,2,256,256]{3,2,1,0:T(8,128)(2,1)} %copy-done.41), calls=%async_computation.2 | async-start | bytes 2097152 | tf_op jit(solution)/shard_map/all_to_all | solution.py:1021
  563.0 46.3 %collective-permute-start.38 = (bf16[2,2,4,384,256]{4,3,2,1,0:T(8,128)(2,1)}, bf16[2,2,4,384,256]{4,3,2,1,0:T(8,128)(2,1)}, u32[]{:S(2)}, u32[]{:S(2)}) collective-permute-start(bf16[2,2,4,384,256]{4,3,2,1,0:T(8,128)(2,1)} %copy-done.21), channel_id=1, source_target_pairs={{0,1},{1,0},{2,3},{3,2},{4,5},{5,4},{6,7},{7,6},{8,9},{9,8},{10,11... | collective-permute-start | bytes 9437192 | tf_op jit(solution)/shard_map/ppermute | solution.py:298
  600.3 41.8 %all-to-all-start.3 = ((bf16[4,3,2,256,256]{4,3,2,1,0:T(8,128)(2,1)}), bf16[4,3,2,256,256]{4,3,2,1,0:T(8,128)(2,1)}, u32[]{:S(2)}, u32[]{:S(2)}) async-start(bf16[4,3,2,256,256]{4,3,2,1,0:T(8,128)(2,1)} %get-tuple-element.207), calls=%async_computation.3 | async-start | bytes 6291456 | tf_op jit(solution)/shard_map/all_to_all | solution.py:1036
  667.2 24.7 %collective-permute-start.43 = (bf16[2,2,4,512,256]{4,3,2,1,0:T(8,128)(2,1)}, bf16[2,2,4,512,256]{4,3,2,1,0:T(8,128)(2,1)}, u32[]{:S(2)}, u32[]{:S(2)}) collective-permute-start(bf16[2,2,4,512,256]{4,3,2,1,0:T(8,128)(2,1)} %opening_exit_0_1.1), channel_id=1, source_target_pairs={{0,1},{1,0},{2,3},{3,2},{4,5},{5,4},{6,7},{7,6},{8,9},{9,8},{10,11... | collective-permute-start | bytes 12582920 | tf_op jit(solution)/shard_map/ppermute | solution.py:298
  674.1 7.1 collective-permute-start.42
  678.8 45.8 %collective-permute-start.40 = (bf16[4,384,256]{2,1,0:T(8,128)(2,1)}, bf16[4,384,256]{2,1,0:T(8,128)(2,1)S(1)}, u32[]{:S(2)}, u32[]{:S(2)}) collective-permute-start(bf16[4,384,256]{2,1,0:T(8,128)(2,1)} %get-tuple-element.223), channel_id=1, source_target_pairs={{0,4},{4,0},{8,12},{12,8},{16,20},{20,16},{24,28},{28,24},{1,5},{5... | collective-permute-start | bytes 2359304 | tf_op jit(solution)/shard_map/ppermute | solution.py:298
  679.1 53.1 %collective-permute-start.39 = (bf16[4,1024,256]{2,1,0:T(8,128)(2,1)}, bf16[4,1024,256]{2,1,0:T(8,128)(2,1)S(1)}, u32[]{:S(2)}, u32[]{:S(2)}) collective-permute-start(bf16[4,1024,256]{2,1,0:T(8,128)(2,1)} %get-tuple-element.222), channel_id=1, source_target_pairs={{0,2},{1,3},{2,0},{3,1},{4,6},{5,7},{6,4},{7,5},{8,10},{9,11},{10,... | collective-permute-start | bytes 6291464 | tf_op jit(solution)/shard_map/ppermute | solution.py:298
  679.5 52.7 %collective-permute-start.41 = (bf16[2,4,384,256]{3,2,1,0:T(8,128)(2,1)S(1)}, bf16[2,4,384,256]{3,2,1,0:T(8,128)(2,1)S(1)}, u32[]{:S(2)}, u32[]{:S(2)}) collective-permute-start(bf16[2,4,384,256]{3,2,1,0:T(8,128)(2,1)S(1)} %copy-done.45), channel_id=1, source_target_pairs={{0,4},{4,0},{8,12},{12,8},{16,20},{20,16},{24,28},{28,24},{1,5},{5... | collective-permute-start | bytes 4718600 | tf_op jit(solution)/shard_map/ppermute | solution.py:298
  732.2 27.4 %collective-permute-start.50 = (bf16[2,2,4,256,256]{4,3,2,1,0:T(8,128)(2,1)}, bf16[2,2,4,256,256]{4,3,2,1,0:T(8,128)(2,1)}, u32[]{:S(2)}, u32[]{:S(2)}) collective-permute-start(bf16[2,2,4,256,256]{4,3,2,1,0:T(8,128)(2,1)} %opening_entry_more_0_1.1), channel_id=1, source_target_pairs={{0,1},{1,0},{2,3},{3,2},{4,5},{5,4},{6,7},{7,6},{8,9},{9,8},{10,11... | collective-permute-start | bytes 6291464 | tf_op jit(solution)/shard_map/ppermute | solution.py:298
  732.2 38.8 %collective-permute-start.49 = (bf16[2,2,4,256,256]{4,3,2,1,0:T(8,128)(2,1)}, bf16[2,2,4,256,256]{4,3,2,1,0:T(8,128)(2,1)}, u32[]{:S(2)}, u32[]{:S(2)}) collective-permute-start(bf16[2,2,4,256,256]{4,3,2,1,0:T(8,128)(2,1)} %opening_entry_0_1.1), channel_id=1, source_target_pairs={{0,1},{1,0},{2,3},{3,2},{4,5},{5,4},{6,7},{7,6},{8,9},{9,8},{10,11... | collective-permute-start | bytes 6291464 | tf_op jit(solution)/shard_map/ppermute | solution.py:298
  737.8 67.6 %collective-permute-start.47 = (bf16[2,4,512,256]{3,2,1,0:T(8,128)(2,1)}, bf16[2,4,512,256]{3,2,1,0:T(8,128)(2,1)}, u32[]{:S(2)}, u32[]{:S(2)}) collective-permute-start(bf16[2,4,512,256]{3,2,1,0:T(8,128)(2,1)} %get-tuple-element.242), channel_id=1, source_target_pairs={{0,4},{4,0},{8,12},{12,8},{16,20},{20,16},{24,28},{28,24},{1,5},{5... | collective-permute-start | bytes 6291464 | tf_op jit(solution)/shard_map/ppermute | solution.py:298
  751.4 54.0 %collective-permute-start.46 = (bf16[2,4,384,256]{3,2,1,0:T(8,128)(2,1)}, bf16[2,4,384,256]{3,2,1,0:T(8,128)(2,1)S(1)}, u32[]{:S(2)}, u32[]{:S(2)}) collective-permute-start(bf16[2,4,384,256]{3,2,1,0:T(8,128)(2,1)} %copy-done.52), channel_id=1, source_target_pairs={{0,2},{1,3},{2,0},{3,1},{4,6},{5,7},{6,4},{7,5},{8,10},{9,11},{10,... | collective-permute-start | bytes 4718600 | tf_op jit(solution)/shard_map/ppermute | solution.py:298
  754.5 50.9 %collective-permute-start.44 = (bf16[2,1408,256]{2,1,0:T(8,128)(2,1)}, bf16[2,1408,256]{2,1,0:T(8,128)(2,1)S(1)}, u32[]{:S(2)}, u32[]{:S(2)}) collective-permute-start(bf16[2,1408,256]{2,1,0:T(8,128)(2,1)} %pad_maximum_fusion.6), channel_id=1, source_target_pairs={{0,8},{4,12},{8,0},{12,4},{16,24},{20,28},{24,16},{28,20},{1,9},{5... | collective-permute-start | bytes 4325384 | tf_op jit(solution)/shard_map/ppermute | solution.py:304
  759.6 45.8 %collective-permute-start.45 = (bf16[4,384,256]{2,1,0:T(8,128)(2,1)S(1)}, bf16[4,384,256]{2,1,0:T(8,128)(2,1)}, u32[]{:S(2)}, u32[]{:S(2)}) collective-permute-start(bf16[4,384,256]{2,1,0:T(8,128)(2,1)S(1)} %copy-done.87), channel_id=1, source_target_pairs={{0,2},{1,3},{2,0},{3,1},{4,6},{5,7},{6,4},{7,5},{8,10},{9,11},{10,... | collective-permute-start | bytes 2359304 | tf_op jit(solution)/shard_map/ppermute | solution.py:298
  812.0 11.0 %collective-permute-start.53 = (bf16[2,384,256]{2,1,0:T(8,128)(2,1)S(1)}, bf16[2,384,256]{2,1,0:T(8,128)(2,1)S(1)}, u32[]{:S(2)}, u32[]{:S(2)}) collective-permute-start(bf16[2,384,256]{2,1,0:T(8,128)(2,1)S(1)} %get-tuple-element.262), channel_id=1, source_target_pairs={{0,8},{4,12},{8,0},{12,4},{16,24},{20,28},{24,16},{28,20},{1,9},{5... | collective-permute-start | bytes 1179656 | tf_op jit(solution)/shard_map/ppermute | solution.py:304
  814.0 5.7 collective-permute-start.51
  814.5 42.0 %collective-permute-start.54 = (bf16[4,512,256]{2,1,0:T(8,128)(2,1)S(1)}, bf16[4,512,256]{2,1,0:T(8,128)(2,1)S(1)}, u32[]{:S(2)}, u32[]{:S(2)}) collective-permute-start(bf16[4,512,256]{2,1,0:T(8,128)(2,1)S(1)} %pad_maximum_fusion.12), channel_id=1, source_target_pairs={{0,4},{4,0},{8,12},{12,8},{16,20},{20,16},{24,28},{28,24},{1,5},{5... | collective-permute-start | bytes 3145736 | tf_op jit(solution)/shard_map/ppermute | solution.py:298
  815.6 40.8 %collective-permute-start.55 = (bf16[4,512,256]{2,1,0:T(8,128)(2,1)S(1)}, bf16[4,512,256]{2,1,0:T(8,128)(2,1)S(1)}, u32[]{:S(2)}, u32[]{:S(2)}) collective-permute-start(bf16[4,512,256]{2,1,0:T(8,128)(2,1)S(1)} %get-tuple-element.265), channel_id=1, source_target_pairs={{0,2},{1,3},{2,0},{3,1},{4,6},{5,7},{6,4},{7,5},{8,10},{9,11},{10,... | collective-permute-start | bytes 3145736 | tf_op jit(solution)/shard_map/ppermute | solution.py:298
  817.3 45.8 %collective-permute-start.56 = (bf16[2,4,256,256]{3,2,1,0:T(8,128)(2,1)S(1)}, bf16[2,4,256,256]{3,2,1,0:T(8,128)(2,1)S(1)}, u32[]{:S(2)}, u32[]{:S(2)}) collective-permute-start(bf16[2,4,256,256]{3,2,1,0:T(8,128)(2,1)S(1)} %get-tuple-element.266), channel_id=1, source_target_pairs={{0,2},{1,3},{2,0},{3,1},{4,6},{5,7},{6,4},{7,5},{8,10},{9,11},{10,... | collective-permute-start | bytes 3145736 | tf_op jit(solution)/shard_map/ppermute | solution.py:298
  819.8 43.3 %collective-permute-start.57 = (bf16[2,4,256,256]{3,2,1,0:T(8,128)(2,1)S(1)}, bf16[2,4,256,256]{3,2,1,0:T(8,128)(2,1)S(1)}, u32[]{:S(2)}, u32[]{:S(2)}) collective-permute-start(bf16[2,4,256,256]{3,2,1,0:T(8,128)(2,1)S(1)} %get-tuple-element.267), channel_id=1, source_target_pairs={{0,4},{4,0},{8,12},{12,8},{16,20},{20,16},{24,28},{28,24},{1,5},{5... | collective-permute-start | bytes 3145736 | tf_op jit(solution)/shard_map/ppermute | solution.py:298
  823.0 33.5 %collective-permute-start.52 = (bf16[1,1408,256]{2,1,0:T(8,128)(2,1)S(1)}, bf16[1,1408,256]{2,1,0:T(8,128)(2,1)S(1)}, u32[]{:S(2)}, u32[]{:S(2)}) collective-permute-start(bf16[1,1408,256]{2,1,0:T(8,128)(2,1)S(1)} %get-tuple-element.261), channel_id=1, source_target_pairs={{0,16},{4,20},{8,24},{12,28},{16,0},{20,4},{24,8},{28,12},{1,17},{... | collective-permute-start | bytes 2162696 | tf_op jit(solution)/shard_map/ppermute | solution.py:304
  863.4 28.2 %collective-permute-start.62 = (bf16[4,256,256]{2,1,0:T(8,128)(2,1)S(1)}, bf16[4,256,256]{2,1,0:T(8,128)(2,1)S(1)}, u32[]{:S(2)}, u32[]{:S(2)}) collective-permute-start(bf16[4,256,256]{2,1,0:T(8,128)(2,1)S(1)} %get-tuple-element.367), channel_id=1, source_target_pairs={{0,2},{1,3},{2,0},{3,1},{4,6},{5,7},{6,4},{7,5},{8,10},{9,11},{10,... | collective-permute-start | bytes 1572872 | tf_op jit(solution)/shard_map/ppermute | solution.py:298
  864.6 27.0 %collective-permute-start.61 = (bf16[4,256,256]{2,1,0:T(8,128)(2,1)S(1)}, bf16[4,256,256]{2,1,0:T(8,128)(2,1)S(1)}, u32[]{:S(2)}, u32[]{:S(2)}) collective-permute-start(bf16[4,256,256]{2,1,0:T(8,128)(2,1)S(1)} %get-tuple-element.365), channel_id=1, source_target_pairs={{0,4},{4,0},{8,12},{12,8},{16,20},{20,16},{24,28},{28,24},{1,5},{5... | collective-permute-start | bytes 1572872 | tf_op jit(solution)/shard_map/ppermute | solution.py:298
  866.4 27.1 %collective-permute-start.60 = (bf16[2,1024,256]{2,1,0:T(8,128)(2,1)S(1)}, bf16[2,1024,256]{2,1,0:T(8,128)(2,1)S(1)}, u32[]{:S(2)}, u32[]{:S(2)}) collective-permute-start(bf16[2,1024,256]{2,1,0:T(8,128)(2,1)S(1)} %pad_maximum_fusion.13), channel_id=1, source_target_pairs={{0,8},{4,12},{8,0},{12,4},{16,24},{20,28},{24,16},{28,20},{1,9},{5... | collective-permute-start | bytes 3145736 | tf_op jit(solution)/shard_map/ppermute | solution.py:304
  866.6 25.0 %collective-permute-start.59 = (bf16[1,384,256]{2,1,0:T(8,128)(2,1)S(1)}, bf16[1,384,256]{2,1,0:T(8,128)(2,1)S(1)}, u32[]{:S(2)}, u32[]{:S(2)}) collective-permute-start(bf16[1,384,256]{2,1,0:T(8,128)(2,1)S(1)} %add_convert_fusion.37), channel_id=1, source_target_pairs={{0,16},{4,20},{8,24},{12,28},{16,0},{20,4},{24,8},{28,12},{1,17},{... | collective-permute-start | bytes 589832 | tf_op jit(solution)/shard_map/ppermute | solution.py:304
  868.0 10.6 %collective-permute-start.58 = (f32[19,1024]{1,0:T(8,128)S(1)}, f32[19,1024]{1,0:T(8,128)S(1)}, u32[]{:S(2)}, u32[]{:S(2)}) collective-permute-start(f32[19,1024]{1,0:T(8,128)S(1)} %add.693), channel_id=1, source_target_pairs={{0,4},{4,0},{8,12},{12,8},{16,20},{20,16},{24,28},{28,24},{1,5},{5... | collective-permute-start | bytes 233480 | tf_op jit(solution)/shard_map/ppermute | solution.py:298
  893.6 8.5 collective-permute-start.63
  894.9 17.9 %collective-permute-start.64 = (f32[19,1024]{1,0:T(8,128)S(1)}, f32[19,1024]{1,0:T(8,128)S(1)}, u32[]{:S(2)}, u32[]{:S(2)}) collective-permute-start(f32[19,1024]{1,0:T(8,128)S(1)} %add.699), channel_id=1, source_target_pairs={{0,16},{4,20},{8,24},{12,28},{16,0},{20,4},{24,8},{28,12},{1,17},{... | collective-permute-start | bytes 233480 | tf_op jit(solution)/shard_map/ppermute | solution.py:298
  895.7 17.1 %collective-permute-start.65 = (f32[19,1024]{1,0:T(8,128)S(1)}, f32[19,1024]{1,0:T(8,128)S(1)}, u32[]{:S(2)}, u32[]{:S(2)}) collective-permute-start(f32[19,1024]{1,0:T(8,128)S(1)} %add.699), channel_id=1, source_target_pairs={{0,24},{4,28},{8,0},{12,4},{16,8},{20,12},{24,16},{28,20},{1,25},{... | collective-permute-start | bytes 233480 | tf_op jit(solution)/shard_map/ppermute | solution.py:298
  898.3 28.5 %collective-permute-start.67 = (bf16[1,1024,256]{2,1,0:T(8,128)(2,1)S(1)}, bf16[1,1024,256]{2,1,0:T(8,128)(2,1)S(1)}, u32[]{:S(2)}, u32[]{:S(2)}) collective-permute-start(bf16[1,1024,256]{2,1,0:T(8,128)(2,1)S(1)} %get-tuple-element.359), channel_id=1, source_target_pairs={{0,16},{4,20},{8,24},{12,28},{16,0},{20,4},{24,8},{28,12},{1,17},{... | collective-permute-start | bytes 1572872 | tf_op jit(solution)/shard_map/ppermute | solution.py:304
  900.1 26.6 %collective-permute-start.66 = (bf16[2,512,256]{2,1,0:T(8,128)(2,1)S(1)}, bf16[2,512,256]{2,1,0:T(8,128)(2,1)S(1)}, u32[]{:S(2)}, u32[]{:S(2)}) collective-permute-start(bf16[2,512,256]{2,1,0:T(8,128)(2,1)S(1)} %pad_maximum_fusion.18), channel_id=1, source_target_pairs={{0,8},{4,12},{8,0},{12,4},{16,24},{20,28},{24,16},{28,20},{1,9},{5... | collective-permute-start | bytes 1572872 | tf_op jit(solution)/shard_map/ppermute | solution.py:304
  926.9 12.4 %collective-permute-start.68 = (bf16[1,512,256]{2,1,0:T(8,128)(2,1)S(1)}, bf16[1,512,256]{2,1,0:T(8,128)(2,1)S(1)}, u32[]{:S(2)}, u32[]{:S(2)}) collective-permute-start(bf16[1,512,256]{2,1,0:T(8,128)(2,1)S(1)} %get-tuple-element.383), channel_id=1, source_target_pairs={{0,16},{4,20},{8,24},{12,28},{16,0},{20,4},{24,8},{28,12},{1,17},{... | collective-permute-start | bytes 786440 | tf_op jit(solution)/shard_map/ppermute | solution.py:304
  (160 other events, 1468.4 us)
Sparse Core Ops, SparseCore 0:
  11.5 141.7 all-gather.3
  156.8 98.0 all-gather.5
  258.3 83.2 all-gather.7

commit v5 on v4

--- a/solution.py
+++ b/solution.py
@@ -989,10 +989,8 @@
     early_job.far()
     early_job.ship()
     closing_job.near()
-    early_job.near()
-    totals = settle([], totals, hold=[closing_job, early_job])
+    totals = settle([], totals, hold=[closing_job])
     closing_job.send(0)
-    early_job.send(0)
     total_first, total_second = totals[0], totals[1]
     grad_conv = grad_conv_direct + valid_rows * (total_first + 2.0 * conv_value * total_second)
     grad_conv_low = grad_conv.astype(jnp.bfloat16).reshape(groups, local_len, model_width)
@@ -1027,7 +1025,9 @@
         "middle",
     )
     middle_job.far()
-    grad_heads = settle([], grad_heads, hold=[middle_job])
+    early_job.near()
+    grad_heads = settle([], grad_heads, hold=[early_job, middle_job])
+    early_job.send(0)
     middle_job.ship()
     grad_stack, grad_position_low, grad_biases = attend_backward(
         probs, by_heads, grad_heads, position_low, biases

time: 959 us -> 932 us (0.972)
  waiting for transfers between devices: 358 us -> 306 us
  starting transfers between devices: 88.4 us -> 115 us
    ppermute x47, starting transfers between devices: 43 us -> 69.1 us  [shift(): return lax.ppermute(value, name, pairs)]
    all_to_all x1, waiting for transfers between devices: 22.6 us -> 0.01 us  [per_device(): lax.all_to_all(grad_stack, 'seq', split_axis=0, concat_axis=0, tiled=True)]
    all_to_all x1, waiting for transfers between devices: 16 us -> 0.01 us  [per_device(): lax.all_to_all(grad_attended, 'seq', split_axis=0, concat_axis=0, tiled=T...]
    ppermute x47, waiting for transfers between devices: 169 us -> 153 us  [shift(): return lax.ppermute(value, name, pairs)]
    ppermute x10, waiting for transfers between devices: 21.2 us -> 9.53 us  [sum_everywhere(): lax.ppermute(value, axis, [(i, i ^ step) for i in range(size)])]
    ppermute x8, waiting for transfers between devices: 67.7 us -> 77.5 us  [swap(): return lax.ppermute(value, 'batch', pairs)]
    unnamed x306 -> x302, local copies, waits for them, and re-layouts: 39.1 us -> 46 us
  transfers between devices with their start and end apart: 76 -> 76, of which waited for: 36 -> 34; matrix products, arithmetic and copies ran while one was open for 19% -> 19% of each run, Pallas kernels for 17% -> 18%
where the time goes in v5:
time: 932 us; the launch traced here: 920 us
  waiting for transfers between devices  306 us (33%)
  Pallas kernels  219 us (23%)
  matrix products  117 us (13%)
  starting transfers between devices  115 us (12%)
  other arithmetic  83.2 us (9%)
  local copies, waits for them, and re-layouts  63.7 us (7%)
  between operations  16.8 us (2%)
    ppermute x47, waiting for transfers between devices, shift(): return lax.ppermute(value, name, pairs)  153 us
    pallas_call x23, Pallas kernels, weight_grad(): pl.pallas_call(body, grid_spec=pltpu.PrefetchScalarGridSpec(num_scalar_pr...  120 us
    ppermute x8, waiting for transfers between devices, swap(): return lax.ppermute(value, 'batch', pairs)  77.5 us
    ppermute x47, starting transfers between devices, shift(): return lax.ppermute(value, name, pairs)  69.1 us
    dot_general x8, matrix products, times_transpose(): lax.dot_general(left_side, right_side, (((1,), (1,)), ((), ())), preferre...  60.6 us
    dot_general x11, matrix products, matmul_rows(): return jnp.dot(left_side, right_side, preferred_element_type=jnp.float32)  56 us
    unnamed x302, local copies, waits for them, and re-layouts  46 us
    pallas_call x1, Pallas kernels, attend_backward(): pl.pallas_call(body, grid_spec=pltpu.PrefetchScalarGridSpec(num_scalar_pr...  34.4 us
  transfers between devices with their start and end apart: 76, of which 34 were waited for; matrix products, arithmetic and copies ran while one was open for 19% of the time, Pallas kernels for 18%

profile of v5, /device:TPU:0, one launch (start us, length us, event | category | flops | bytes accessed | tf_op | source)
XLA Modules:
  0.0 920.3 jit_solution(7683727137371182468)
XLA Ops:
  19.1 17.4 %collective-permute-done = bf16[1,1,19,128]{3,2,1,0:T(8,128)(2,1)S(1)} collective-permute-done((bf16[1,1,19,128]{3,2,1,0:T(8,128)(2,1)S(1)}, bf16[1,1,19,128]{3,2,1,0:T(8,128)(2,1)S(1)}, u32[]{:S(2)}, u32[]{:S(2)}) %collective-permute-start) | collective-permute-done | bytes 4896 | tf_op jit(solution)/shard_map/ppermute | solution.py:298
  36.4 8.2 collective-permute-done.1
  54.6 23.1 %collective-permute-done.6 = bf16[1,4,19,128]{3,2,1,0:T(8,128)(2,1)S(1)} collective-permute-done((bf16[1,4,19,128]{3,2,1,0:T(8,128)(2,1)S(1)}, bf16[1,4,19,128]{3,2,1,0:T(8,128)(2,1)S(1)}, u32[]{:S(2)}, u32[]{:S(2)}) %collective-permute-start.6) | collective-permute-done | bytes 19488 | tf_op jit(solution)/shard_map/ppermute | solution.py:298
  77.7 17.8 %collective-permute-done.9 = bf16[2,512,256]{2,1,0:T(8,128)(2,1)S(1)} collective-permute-done((bf16[2,512,256]{2,1,0:T(8,128)(2,1)S(1)}, bf16[2,512,256]{2,1,0:T(8,128)(2,1)S(1)}, u32[]{:S(2)}, u32[]{:S(2)}) %collective-permute-start.9) | collective-permute-done | bytes 524320 | tf_op jit(solution)/shard_map/ppermute | solution.py:298
  101.1 21.6 %collective-permute-start.13 = (bf16[2,512,256]{2,1,0:T(8,128)(2,1)}, bf16[2,512,256]{2,1,0:T(8,128)(2,1)S(1)}, u32[]{:S(2)}, u32[]{:S(2)}) collective-permute-start(bf16[2,512,256]{2,1,0:T(8,128)(2,1)} %get-tuple-element.405), channel_id=1, source_target_pairs={{0,8},{4,12},{8,16},{12,20},{16,24},{20,28},{24,0},{28,4},{1,9},{5... | collective-permute-start | bytes 1572872 | tf_op jit(solution)/shard_map/ppermute | solution.py:298
  132.8 23.5 %all-gather.4.cloned.1.call-done = bf16[1024,4096]{1,0:T(8,128)(2,1)} async-done(((bf16[32,4096]{1,0:T(8,128)(2,1)}), bf16[1024,4096]{1,0:T(8,128)(2,1)}) %all-gather.4.cloned.1.call-update) | async-done | bytes 8388624 | tf_op jit(solution)/shard_map/all_gather | solution.py:634
  156.3 10.3 %multiply_convert_fusion.1 = (bf16[512,4096]{1,0:T(8,128)(2,1)}, bf16[512,4096]{1,0:T(8,128)(2,1)}) fusion(bf16[512,1024]{1,0:T(8,128)(2,1)S(1)} %fusion.22.refs_0_, bf16[1024,4096]{1,0:T(8,128)(2,1)} %all-gather.4.cloned.1.call-done), kind=kOutput, calls=%fused_computation.21 | convolution fusion | flops 4307550208 | bytes 17825792 | tf_op jit(solution)/shard_map/dot_general | solution.py:721
  166.6 7.2 collective-permute-done.11
  173.8 6.0 collective-permute-done.12
  179.8 4.8 pad_maximum_fusion
  192.1 9.7 %gather_opening_exit.1 = bf16[4096,1024]{1,0:T(8,128)(2,1)} custom-call(s32[4]{0:T(128)S(1)} %pad_add_fusion.place_ref, bf16[2,8,512,256]{3,2,1,0:T(8,128)(2,1)} %bitcast.26.mine_ref, bf16[2,8,512,256]{3,2,1,0:T(8,128)(2,1)} %collective-permute-done.16.theirs_ref), custom_call_target="tpu_custom_call" | custom-call | bytes 4194304 | tf_op jit(solution)/shard_map/gather_opening_exit/pallas_call | solution.py:374
  201.8 8.8 gather_attention.1
  210.7 8.5 fusion.170
  220.5 6.6 project_heads.1
  228.1 4.2 all-to-all-start
  232.2 4.0 fusion.152
  244.8 28.3 %all-to-all-done.q_ref.k_ref.v_ref = bf16[4,3,2,256,256]{4,3,2,1,0:T(8,128)(2,1)S(1)} async-done(((bf16[4,3,2,256,256]{4,3,2,1,0:T(8,128)(2,1)}), bf16[4,3,2,256,256]{4,3,2,1,0:T(8,128)(2,1)S(1)}, u32[]{:S(2)}, u32[]{:S(2)}) %all-to-all-start) | async-done | bytes 3145760 | tf_op jit(solution)/shard_map/all_to_all | solution.py:882
  274.4 20.7 %attend_forward.1 = (bf16[4,2,256,256]{3,2,1,0:T(8,128)(2,1)S(1)}, bf16[2,2,1024,1024]{3,2,1,0:T(8,128)(2,1)}) custom-call(s32[2]{0:T(128)S(1)} %copy-done.61, bf16[4,3,2,256,256]{4,3,2,1,0:T(8,128)(2,1)S(1)} %all-to-all-done.q_ref.k_ref.v_ref, bf16[4,3,2,256,256]{4,3,2,1,0:T(8,128)(2,1)S(1)} %all-to-all-done.q_ref.k_ref.v_ref, ...), custom_call_target="tpu_custom_call" | custom-call | flops 872415232 | bytes 3407872 | tf_op jit(solution)/shard_map/attend_forward/pallas_call | solution.py:58
  301.1 12.9 %all-to-all-done.1 = bf16[4,2,256,256]{3,2,1,0:T(8,128)(2,1)S(1)} async-done(((bf16[4,2,256,256]{3,2,1,0:T(8,128)(2,1)}), bf16[4,2,256,256]{3,2,1,0:T(8,128)(2,1)S(1)}, u32[]{:S(2)}, u32[]{:S(2)}) %all-to-all-start.1) | async-done | bytes 1048608 | tf_op jit(solution)/shard_map/all_to_all | solution.py:890
  350.7 4.0 pad_maximum_fusion.2
  357.6 9.7 %multiply_convert_fusion = (bf16[512,4096]{1,0:T(8,128)(2,1)S(1)}, bf16[512,4096]{1,0:T(8,128)(2,1)}) fusion(bf16[512,1024]{1,0:T(8,128)(2,1)S(1)} %add_convert_fusion.9.refs_0_, bf16[1024,4096]{1,0:T(8,128)(2,1)} %all-gather.8.cloned.1.call-done), kind=kOutput, calls=%fused_computation.19 | convolution fusion | flops 4307550208 | bytes 17825792 | tf_op jit(solution)/shard_map/dot_general | solution.py:721
  367.3 10.5 %gather_closing_exit.1 = bf16[4096,1024]{1,0:T(8,128)(2,1)} custom-call(s32[4]{0:T(128)S(1)} %pad_add_fusion.place_ref, bf16[2,8,512,256]{3,2,1,0:T(8,128)(2,1)} %bitcast.62.mine_ref, bf16[2,8,512,256]{3,2,1,0:T(8,128)(2,1)} %collective-permute-done.26.theirs_ref), custom_call_target="tpu_custom_call" | custom-call | bytes 4194304 | tf_op jit(solution)/shard_map/gather_closing_exit/pallas_call | solution.py:374
  377.8 7.1 fusion.173
  390.1 6.0 closing_0_1.1.refs_2_
  396.1 10.3 %fusion.5.refs_1_ = bf16[512,4096]{1,0:T(8,128)(2,1)S(1)} fusion(bf16[512,4096]{1,0:T(8,128)(2,1)S(1)} %copy-done.145, bf16[512,1024]{1,0:T(8,128)(2,1)S(1)} %multiply_convert_fusion.3.refs_1_, bf16[4096,1024]{1,0:T(8,128)(2,1)} %gather_closing_exit.1), kind=kOutput, calls=%fused_computation.12 | convolution fusion | flops 4318035968 | bytes 17825792 | tf_op jit(solution)/shard_map/dot_general | solution.py:725
  406.4 6.7 closing_1_1.1
  420.1 8.5 multiply_reduce_fusion.5
  432.4 6.0 multiply_reduce_fusion.2
  459.3 8.2 closing_0_0.1
  467.5 9.3 %closing_1_0.1 = (bf16[2,4,1024,256]{3,2,1,0:T(8,128)(2,1)S(1)}, bf16[2,4,1024,256]{3,2,1,0:T(8,128)(2,1)}) custom-call(s32[4]{0:T(128)S(1)} %pad_add_fusion.place_ref, bf16[512,1024]{1,0:T(8,128)(2,1)S(1)} %add_convert_fusion.9.refs_0_, bf16[512,4096]{1,0:T(8,128)(2,1)} %copy-done.15, ...), custom_call_target="tpu_custom_call", output_to_operand_aliasing={{0}: (4, {}), {1}: (5, {})} | custom-call | flops 536870912 | bytes 1835008 | tf_op jit(solution)/shard_map/closing_1_0/pallas_call | solution.py:525
  478.8 4.0 multiply_reduce_fusion.1
  496.5 6.4 multiply_reduce_fusion.6
  508.8 4.4 all-to-all-start.2
  515.8 3.9 early_0_0.1
  519.7 3.9 early_1_0.1
  523.6 3.9 early_2_0.1
  528.7 4.1 middle_0_1.1.refs_2_
  542.0 34.4 %attend_backward.1 = (bf16[4,3,2,256,256]{4,3,2,1,0:T(8,128)(2,1)}, bf16[2048,256]{1,0:T(8,128)(2,1)S(1)}, f32[2,256]{1,0:T(2,128)S(1)}) custom-call(bf16[2,2,1024,1024]{3,2,1,0:T(8,128)(2,1)} %get-tuple-element.201.p_ref, bf16[4,3,2,256,256]{4,3,2,1,0:T(8,128)(2,1)} %copy-done.2, bf16[4,3,2,256,256]{4,3,2,1,0:T(8,128)(2,1)} %copy-done.2, ...), custom_call_target="tpu_custom_call" | custom-call | flops 2080374784 | bytes 4194304 | tf_op jit(solution)/shard_map/attend_backward/pallas_call | solution.py:144
  577.9 4.9 all-to-all-start.3
  587.0 4.9 middle_0_0.1
  597.2 36.0 %collective-permute-done.35 = bf16[2,4,1024,256]{3,2,1,0:T(8,128)(2,1)} collective-permute-done((bf16[2,4,1024,256]{3,2,1,0:T(8,128)(2,1)}, bf16[2,4,1024,256]{3,2,1,0:T(8,128)(2,1)}, u32[]{:S(2)}, u32[]{:S(2)}) %collective-permute-start.35) | collective-permute-done | bytes 4194336 | tf_op jit(solution)/shard_map/ppermute | solution.py:298
  633.2 5.4 fusion.43
  638.6 6.4 join_heads.1
  650.4 7.8 opening_exit_0_1.1
  658.2 6.9 attention_0_1.1
  665.6 4.7 fusion.41
  672.7 9.2 attention_0_0.1
  683.1 8.5 opening_exit_0_0.1
  693.0 12.2 %fusion.11.refs_1_ = bf16[512,4096]{1,0:T(8,128)(2,1)} fusion(bf16[512,4096]{1,0:T(8,128)(2,1)} %get-tuple-element.455, bf16[512,1024]{1,0:T(8,128)(2,1)S(1)} %get-tuple-element.229.refs_1_, bf16[4096,1024]{1,0:T(8,128)(2,1)} %gather_opening_exit.1), kind=kOutput, calls=%fused_computation.18 | convolution fusion | flops 4318035968 | bytes 17825792 | tf_op jit(solution)/shard_map/dot_general | solution.py:725
  705.1 5.3 opening_entry_0_1.1
  710.5 5.6 opening_entry_more_0_1.1
  716.1 7.7 collective-permute-done.41
  730.9 10.2 %fusion.23 = (f32[1024]{0:T(1024)}, f32[512]{0:T(512)}, f32[1024]{0:T(1024)}, f32[512,1024]{1,0:T(8,128)}) fusion(f32[512]{0:T(512)S(1)} %copy-done.133, f32[512]{0:T(512)S(1)} %bitcast.368, bf16[2,256,1024]{2,1,0:T(8,128)(2,1)S(1)} %copy-done.4, f32[1024]{0:T(1024)S(1)} %bitcast.347, bf16[512,4096]{1,0:T(8,128)(2,1)S(1)} %copy-done.62, ...), kind=kOutput, calls=%fused_computation.62 | convolution fusion | flops 4299683328 | bytes 15747072 | tf_op jit(solution)/shard_map/dot_general | solution.py:725
  750.9 3.9 multiply_convert_fusion.4
  755.9 6.1 opening_entry_0_0.1
  762.0 5.0 opening_entry_more_0_0.1
  767.0 14.1 %collective-permute-done.45 = bf16[4,384,256]{2,1,0:T(8,128)(2,1)S(1)} collective-permute-done((bf16[4,384,256]{2,1,0:T(8,128)(2,1)S(1)}, bf16[4,384,256]{2,1,0:T(8,128)(2,1)S(1)}, u32[]{:S(2)}, u32[]{:S(2)}) %collective-permute-start.45) | collective-permute-done | bytes 786464 | tf_op jit(solution)/shard_map/ppermute | solution.py:298
  799.3 3.9 add_convert_fusion.6
  803.2 27.2 %collective-permute-done.52 = bf16[1,1408,256]{2,1,0:T(8,128)(2,1)S(1)} collective-permute-done((bf16[1,1408,256]{2,1,0:T(8,128)(2,1)S(1)}, bf16[1,1408,256]{2,1,0:T(8,128)(2,1)S(1)}, u32[]{:S(2)}, u32[]{:S(2)}) %collective-permute-start.52) | collective-permute-done | bytes 720928 | tf_op jit(solution)/shard_map/ppermute | solution.py:304
  830.4 6.4 collective-permute-done.56
  848.3 4.8 collective-permute-done.61
  853.4 13.0 %collective-permute-done.60 = bf16[2,1024,256]{2,1,0:T(8,128)(2,1)S(1)} collective-permute-done((bf16[2,1024,256]{2,1,0:T(8,128)(2,1)S(1)}, bf16[2,1024,256]{2,1,0:T(8,128)(2,1)S(1)}, u32[]{:S(2)}, u32[]{:S(2)}) %collective-permute-start.60) | collective-permute-done | bytes 1048608 | tf_op jit(solution)/shard_map/ppermute | solution.py:304
  876.5 19.5 %collective-permute-done.66 = bf16[2,512,256]{2,1,0:T(8,128)(2,1)S(1)} collective-permute-done((bf16[2,512,256]{2,1,0:T(8,128)(2,1)S(1)}, bf16[2,512,256]{2,1,0:T(8,128)(2,1)S(1)}, u32[]{:S(2)}, u32[]{:S(2)}) %collective-permute-start.66) | collective-permute-done | bytes 524320 | tf_op jit(solution)/shard_map/ppermute | solution.py:304
  902.9 9.7 %collective-permute-done.68 = bf16[1,512,256]{2,1,0:T(8,128)(2,1)S(1)} collective-permute-done((bf16[1,512,256]{2,1,0:T(8,128)(2,1)S(1)}, bf16[1,512,256]{2,1,0:T(8,128)(2,1)S(1)}, u32[]{:S(2)}, u32[]{:S(2)}) %collective-permute-start.68) | collective-permute-done | bytes 262176 | tf_op jit(solution)/shard_map/ppermute | solution.py:304
  (610 shorter events, 259.6 us)
Async XLA Ops:
  7.2 149.1 %all-gather.4.cloned.1.call-start = ((), (), s32[]{:S(2)}) async-start(), calls=%async_computation.4 | async-start | bytes 8650752 | tf_op jit(solution)/shard_map/all_gather | solution.py:634
  9.2 305.9 %all-gather.6.cloned.1.call-start = ((), (), s32[]{:S(2)}) async-start(), calls=%async_computation.5 | async-start | bytes 12976128 | tf_op jit(solution)/shard_map/all_gather | solution.py:634
  10.3 34.7 %collective-permute-start.3 = (bf16[1,512,256]{2,1,0:T(8,128)(2,1)S(1)}, bf16[1,512,256]{2,1,0:T(8,128)(2,1)S(1)}, u32[]{:S(2)}, u32[]{:S(2)}) collective-permute-start(bf16[1,512,256]{2,1,0:T(8,128)(2,1)S(1)} %get-tuple-element.397), channel_id=1, source_target_pairs={{0,8},{4,12},{8,16},{12,20},{16,24},{20,28},{24,0},{28,4},{1,9},{5... | collective-permute-start | bytes 786440 | tf_op jit(solution)/shard_map/ppermute | solution.py:298
  13.4 31.7 %collective-permute-start.4 = (bf16[1,512,256]{2,1,0:T(8,128)(2,1)S(1)}, bf16[1,512,256]{2,1,0:T(8,128)(2,1)S(1)}, u32[]{:S(2)}, u32[]{:S(2)}) collective-permute-start(bf16[1,512,256]{2,1,0:T(8,128)(2,1)S(1)} %get-tuple-element.397), channel_id=1, source_target_pairs={{0,16},{4,20},{8,24},{12,28},{16,0},{20,4},{24,8},{28,12},{1,17},{... | collective-permute-start | bytes 786440 | tf_op jit(solution)/shard_map/ppermute | solution.py:298
  16.0 29.1 %collective-permute-start.5 = (bf16[1,512,256]{2,1,0:T(8,128)(2,1)S(1)}, bf16[1,512,256]{2,1,0:T(8,128)(2,1)S(1)}, u32[]{:S(2)}, u32[]{:S(2)}) collective-permute-start(bf16[1,512,256]{2,1,0:T(8,128)(2,1)S(1)} %get-tuple-element.397), channel_id=1, source_target_pairs={{0,24},{4,28},{8,0},{12,4},{16,8},{20,12},{24,16},{28,20},{1,25},{... | collective-permute-start | bytes 786440 | tf_op jit(solution)/shard_map/ppermute | solution.py:298
  18.0 18.4 %collective-permute-start = (bf16[1,1,19,128]{3,2,1,0:T(8,128)(2,1)S(1)}, bf16[1,1,19,128]{3,2,1,0:T(8,128)(2,1)S(1)}, u32[]{:S(2)}, u32[]{:S(2)}) collective-permute-start(bf16[1,1,19,128]{3,2,1,0:T(8,128)(2,1)S(1)} %maximum_bitcast_fusion.2), channel_id=1, source_target_pairs={{0,8},{4,12},{8,16},{12,20},{16,24},{20,28},{24,0},{28,4},{1,9},{5... | collective-permute-start | bytes 14600 | tf_op jit(solution)/shard_map/ppermute | solution.py:298
  18.7 25.9 %collective-permute-start.1 = (bf16[1,1,19,128]{3,2,1,0:T(8,128)(2,1)S(1)}, bf16[1,1,19,128]{3,2,1,0:T(8,128)(2,1)S(1)}, u32[]{:S(2)}, u32[]{:S(2)}) collective-permute-start(bf16[1,1,19,128]{3,2,1,0:T(8,128)(2,1)S(1)} %maximum_bitcast_fusion.2), channel_id=1, source_target_pairs={{0,16},{4,20},{8,24},{12,28},{16,0},{20,4},{24,8},{28,12},{1,17},{... | collective-permute-start | bytes 14600 | tf_op jit(solution)/shard_map/ppermute | solution.py:298
  36.4 8.6 collective-permute-start.2
  45.2 50.3 %collective-permute-start.7 = (bf16[1,4,512,256]{3,2,1,0:T(8,128)(2,1)S(1)}, bf16[1,4,512,256]{3,2,1,0:T(8,128)(2,1)S(1)}, u32[]{:S(2)}, u32[]{:S(2)}) collective-permute-start(bf16[1,4,512,256]{3,2,1,0:T(8,128)(2,1)S(1)} %get-tuple-element.395), channel_id=1, source_target_pairs={{0,4},{4,0},{8,12},{12,8},{16,20},{20,16},{24,28},{28,24},{1,5},{5... | collective-permute-start | bytes 3145736 | tf_op jit(solution)/shard_map/ppermute | solution.py:298
  47.0 30.6 %collective-permute-start.8 = (bf16[2,512,256]{2,1,0:T(8,128)(2,1)S(1)}, bf16[2,512,256]{2,1,0:T(8,128)(2,1)S(1)}, u32[]{:S(2)}, u32[]{:S(2)}) collective-permute-start(bf16[2,512,256]{2,1,0:T(8,128)(2,1)S(1)} %get-tuple-element.407), channel_id=1, source_target_pairs={{0,8},{4,12},{8,16},{12,20},{16,24},{20,28},{24,0},{28,4},{1,9},{5... | collective-permute-start | bytes 1572872 | tf_op jit(solution)/shard_map/ppermute | solution.py:298
  49.6 45.9 %collective-permute-start.9 = (bf16[2,512,256]{2,1,0:T(8,128)(2,1)S(1)}, bf16[2,512,256]{2,1,0:T(8,128)(2,1)S(1)}, u32[]{:S(2)}, u32[]{:S(2)}) collective-permute-start(bf16[2,512,256]{2,1,0:T(8,128)(2,1)S(1)} %get-tuple-element.407), channel_id=1, source_target_pairs={{0,16},{4,20},{8,24},{12,28},{16,0},{20,4},{24,8},{28,12},{1,17},{... | collective-permute-start | bytes 1572872 | tf_op jit(solution)/shard_map/ppermute | solution.py:298
  51.1 44.4 %collective-permute-start.10 = (bf16[2,512,256]{2,1,0:T(8,128)(2,1)S(1)}, bf16[2,512,256]{2,1,0:T(8,128)(2,1)S(1)}, u32[]{:S(2)}, u32[]{:S(2)}) collective-permute-start(bf16[2,512,256]{2,1,0:T(8,128)(2,1)S(1)} %get-tuple-element.407), channel_id=1, source_target_pairs={{0,24},{4,28},{8,0},{12,4},{16,8},{20,12},{24,16},{28,20},{1,25},{... | collective-permute-start | bytes 1572872 | tf_op jit(solution)/shard_map/ppermute | solution.py:298
  54.0 23.7 %collective-permute-start.6 = (bf16[1,4,19,128]{3,2,1,0:T(8,128)(2,1)S(1)}, bf16[1,4,19,128]{3,2,1,0:T(8,128)(2,1)S(1)}, u32[]{:S(2)}, u32[]{:S(2)}) collective-permute-start(bf16[1,4,19,128]{3,2,1,0:T(8,128)(2,1)S(1)} %pad_maximum_fusion.24), channel_id=1, source_target_pairs={{0,4},{4,0},{8,12},{12,8},{16,20},{20,16},{24,28},{28,24},{1,5},{5... | collective-permute-start | bytes 58376 | tf_op jit(solution)/shard_map/ppermute | solution.py:298
  99.9 257.7 %all-gather.8.cloned.1.call-start = ((), (), s32[]{:S(2)}) async-start(), calls=%async_computation.6 | async-start | bytes 8650752 | tf_op jit(solution)/shard_map/all_gather | solution.py:634
  101.1 65.5 %collective-permute-start.13 = (bf16[2,512,256]{2,1,0:T(8,128)(2,1)}, bf16[2,512,256]{2,1,0:T(8,128)(2,1)S(1)}, u32[]{:S(2)}, u32[]{:S(2)}) collective-permute-start(bf16[2,512,256]{2,1,0:T(8,128)(2,1)} %get-tuple-element.405), channel_id=1, source_target_pairs={{0,8},{4,12},{8,16},{12,20},{16,24},{20,28},{24,0},{28,4},{1,9},{5... | collective-permute-start | bytes 1572872 | tf_op jit(solution)/shard_map/ppermute | solution.py:298
  122.7 43.9 %collective-permute-start.14 = (bf16[2,512,256]{2,1,0:T(8,128)(2,1)}, bf16[2,512,256]{2,1,0:T(8,128)(2,1)S(1)}, u32[]{:S(2)}, u32[]{:S(2)}) collective-permute-start(bf16[2,512,256]{2,1,0:T(8,128)(2,1)} %get-tuple-element.405), channel_id=1, source_target_pairs={{0,16},{4,20},{8,24},{12,28},{16,0},{20,4},{24,8},{28,12},{1,17},{... | collective-permute-start | bytes 1572872 | tf_op jit(solution)/shard_map/ppermute | solution.py:298
  124.8 41.8 %collective-permute-start.15 = (bf16[2,512,256]{2,1,0:T(8,128)(2,1)}, bf16[2,512,256]{2,1,0:T(8,128)(2,1)}, u32[]{:S(2)}, u32[]{:S(2)}) collective-permute-start(bf16[2,512,256]{2,1,0:T(8,128)(2,1)} %get-tuple-element.405), channel_id=1, source_target_pairs={{0,24},{4,28},{8,0},{12,4},{16,8},{20,12},{24,16},{28,20},{1,25},{... | collective-permute-start | bytes 1572872 | tf_op jit(solution)/shard_map/ppermute | solution.py:298
  126.3 47.5 %collective-permute-start.11 = (bf16[1,2,4,512,256]{4,3,2,1,0:T(8,128)(2,1)}, bf16[1,2,4,512,256]{4,3,2,1,0:T(8,128)(2,1)}, u32[]{:S(2)}, u32[]{:S(2)}) collective-permute-start(bf16[1,2,4,512,256]{4,3,2,1,0:T(8,128)(2,1)} %pad_maximum_fusion.3), channel_id=1, source_target_pairs={{0,2},{1,3},{2,0},{3,1},{4,6},{5,7},{6,4},{7,5},{8,10},{9,11},{10,... | collective-permute-start | bytes 6291464 | tf_op jit(solution)/shard_map/ppermute | solution.py:298
  131.5 48.3 %collective-permute-start.12 = (bf16[2,4,512,256]{3,2,0,1:T(8,128)(2,1)}, bf16[2,4,512,256]{3,2,0,1:T(8,128)(2,1)}, u32[]{:S(2)}, u32[]{:S(2)}) collective-permute-start(bf16[2,4,512,256]{3,2,0,1:T(8,128)(2,1)} %get-tuple-element.371), channel_id=1, source_target_pairs={{0,4},{4,0},{8,12},{12,8},{16,20},{20,16},{24,28},{28,24},{1,5},{5... | collective-permute-start | bytes 6291464 | tf_op jit(solution)/shard_map/ppermute | solution.py:298
  184.6 7.5 collective-permute-start.16
  188.8 13.0 %collective-permute-start.18 = (bf16[2,8,512,256]{3,2,1,0:T(8,128)(2,1)}, bf16[2,8,512,256]{3,2,1,0:T(8,128)(2,1)}, u32[]{:S(2)}, u32[]{:S(2)}) collective-permute-start(bf16[2,8,512,256]{3,2,1,0:T(8,128)(2,1)} %bitcast.38.mine_ref), channel_id=1, source_target_pairs={{0,1},{1,0},{2,3},{3,2},{4,5},{5,4},{6,7},{7,6},{8,9},{9,8},{10,11... | collective-permute-start | bytes 12582920 | tf_op jit(solution)/shard_map/ppermute | solution.py:298
  228.1 45.1 %all-to-all-start = ((bf16[4,3,2,256,256]{4,3,2,1,0:T(8,128)(2,1)}), bf16[4,3,2,256,256]{4,3,2,1,0:T(8,128)(2,1)S(1)}, u32[]{:S(2)}, u32[]{:S(2)}) async-start(bf16[4,3,2,256,256]{4,3,2,1,0:T(8,128)(2,1)} %project_heads.1), calls=%async_computation | async-start | bytes 6291456 | tf_op jit(solution)/shard_map/all_to_all | solution.py:882
  236.2 59.9 %collective-permute-start.17 = (bf16[2,4,512,256]{3,2,1,0:T(8,128)(2,1)}, bf16[2,4,512,256]{3,2,1,0:T(8,128)(2,1)}, u32[]{:S(2)}, u32[]{:S(2)}) collective-permute-start(bf16[2,4,512,256]{3,2,1,0:T(8,128)(2,1)} %get-tuple-element.369), channel_id=1, source_target_pairs={{0,4},{4,0},{8,12},{12,8},{16,20},{20,16},{24,28},{28,24},{1,5},{5... | collective-permute-start | bytes 6291464 | tf_op jit(solution)/shard_map/ppermute | solution.py:298
  296.1 18.0 %all-to-all-start.1 = ((bf16[4,2,256,256]{3,2,1,0:T(8,128)(2,1)}), bf16[4,2,256,256]{3,2,1,0:T(8,128)(2,1)S(1)}, u32[]{:S(2)}, u32[]{:S(2)}) async-start(bf16[4,2,256,256]{3,2,1,0:T(8,128)(2,1)} %copy-done.58), calls=%async_computation.1 | async-start | bytes 2097152 | tf_op jit(solution)/shard_map/all_to_all | solution.py:890
  348.2 6.5 collective-permute-start.25
  354.7 12.6 %collective-permute-start.26 = (bf16[2,8,512,256]{3,2,1,0:T(8,128)(2,1)}, bf16[2,8,512,256]{3,2,1,0:T(8,128)(2,1)}, u32[]{:S(2)}, u32[]{:S(2)}) collective-permute-start(bf16[2,8,512,256]{3,2,1,0:T(8,128)(2,1)} %bitcast.62.mine_ref), channel_id=1, source_target_pairs={{0,1},{1,0},{2,3},{3,2},{4,5},{5,4},{6,7},{7,6},{8,9},{9,8},{10,11... | collective-permute-start | bytes 12582920 | tf_op jit(solution)/shard_map/ppermute | solution.py:298
  413.1 46.1 %collective-permute-start.32 = (bf16[2,2,4,1024,256]{4,3,2,1,0:T(8,128)(2,1)}, bf16[2,2,4,1024,256]{4,3,2,1,0:T(8,128)(2,1)}, u32[]{:S(2)}, u32[]{:S(2)}) collective-permute-start(bf16[2,2,4,1024,256]{4,3,2,1,0:T(8,128)(2,1)} %closing_1_1.1), channel_id=1, source_target_pairs={{0,1},{1,0},{2,3},{3,2},{4,5},{5,4},{6,7},{7,6},{8,9},{9,8},{10,11... | collective-permute-start | bytes 25165832 | tf_op jit(solution)/shard_map/ppermute | solution.py:298
  482.8 7.3 collective-permute-start.34
  484.1 6.0 collective-permute-start.33
  488.2 25.1 %collective-permute-start.36 = (bf16[2,2,4,384,256]{4,3,2,1,0:T(8,128)(2,1)}, bf16[2,2,4,384,256]{4,3,2,1,0:T(8,128)(2,1)}, u32[]{:S(2)}, u32[]{:S(2)}) collective-permute-start(bf16[2,2,4,384,256]{4,3,2,1,0:T(8,128)(2,1)} %early_2_1.1), channel_id=1, source_target_pairs={{0,1},{1,0},{2,3},{3,2},{4,5},{5,4},{6,7},{7,6},{8,9},{9,8},{10,11... | collective-permute-start | bytes 9437192 | tf_op jit(solution)/shard_map/ppermute | solution.py:298
  508.8 29.7 %all-to-all-start.2 = ((bf16[4,2,256,256]{3,2,1,0:T(8,128)(2,1)}), bf16[4,2,256,256]{3,2,1,0:T(8,128)(2,1)}, u32[]{:S(2)}, u32[]{:S(2)}) async-start(bf16[4,2,256,256]{3,2,1,0:T(8,128)(2,1)} %copy-done.51), calls=%async_computation.2 | async-start | bytes 2097152 | tf_op jit(solution)/shard_map/all_to_all | solution.py:1019
  538.5 37.8 %collective-permute-start.37 = (bf16[2,4,384,256]{3,2,1,0:T(8,128)(2,1)}, bf16[2,4,384,256]{3,2,1,0:T(8,128)(2,1)S(1)}, u32[]{:S(2)}, u32[]{:S(2)}) collective-permute-start(bf16[2,4,384,256]{3,2,1,0:T(8,128)(2,1)} %copy-done.46), channel_id=1, source_target_pairs={{0,2},{1,3},{2,0},{3,1},{4,6},{5,7},{6,4},{7,5},{8,10},{9,11},{10,... | collective-permute-start | bytes 4718600 | tf_op jit(solution)/shard_map/ppermute | solution.py:298
  540.5 92.7 %collective-permute-start.35 = (bf16[2,4,1024,256]{3,2,1,0:T(8,128)(2,1)}, bf16[2,4,1024,256]{3,2,1,0:T(8,128)(2,1)}, u32[]{:S(2)}, u32[]{:S(2)}) collective-permute-start(bf16[2,4,1024,256]{3,2,1,0:T(8,128)(2,1)} %get-tuple-element.193), channel_id=1, source_target_pairs={{0,4},{4,0},{8,12},{12,8},{16,20},{20,16},{24,28},{28,24},{1,5},{5... | collective-permute-start | bytes 12582920 | tf_op jit(solution)/shard_map/ppermute | solution.py:298
  542.0 45.0 %collective-permute-start.38 = (bf16[2,2,4,384,256]{4,3,2,1,0:T(8,128)(2,1)}, bf16[2,2,4,384,256]{4,3,2,1,0:T(8,128)(2,1)}, u32[]{:S(2)}, u32[]{:S(2)}) collective-permute-start(bf16[2,2,4,384,256]{4,3,2,1,0:T(8,128)(2,1)} %copy-done.22), channel_id=1, source_target_pairs={{0,1},{1,0},{2,3},{3,2},{4,5},{5,4},{6,7},{7,6},{8,9},{9,8},{10,11... | collective-permute-start | bytes 9437192 | tf_op jit(solution)/shard_map/ppermute | solution.py:298
  577.9 55.2 %all-to-all-start.3 = ((bf16[4,3,2,256,256]{4,3,2,1,0:T(8,128)(2,1)}), bf16[4,3,2,256,256]{4,3,2,1,0:T(8,128)(2,1)}, u32[]{:S(2)}, u32[]{:S(2)}) async-start(bf16[4,3,2,256,256]{4,3,2,1,0:T(8,128)(2,1)} %get-tuple-element.207), calls=%async_computation.3 | async-start | bytes 6291456 | tf_op jit(solution)/shard_map/all_to_all | solution.py:1036
  658.2 24.9 %collective-permute-start.43 = (bf16[2,2,4,512,256]{4,3,2,1,0:T(8,128)(2,1)}, bf16[2,2,4,512,256]{4,3,2,1,0:T(8,128)(2,1)}, u32[]{:S(2)}, u32[]{:S(2)}) collective-permute-start(bf16[2,2,4,512,256]{4,3,2,1,0:T(8,128)(2,1)} %opening_exit_0_1.1), channel_id=1, source_target_pairs={{0,1},{1,0},{2,3},{3,2},{4,5},{5,4},{6,7},{7,6},{8,9},{9,8},{10,11... | collective-permute-start | bytes 12582920 | tf_op jit(solution)/shard_map/ppermute | solution.py:298
  665.1 7.6 collective-permute-start.42
  670.4 45.7 %collective-permute-start.40 = (bf16[4,384,256]{2,1,0:T(8,128)(2,1)}, bf16[4,384,256]{2,1,0:T(8,128)(2,1)S(1)}, u32[]{:S(2)}, u32[]{:S(2)}) collective-permute-start(bf16[4,384,256]{2,1,0:T(8,128)(2,1)} %get-tuple-element.223), channel_id=1, source_target_pairs={{0,4},{4,0},{8,12},{12,8},{16,20},{20,16},{24,28},{28,24},{1,5},{5... | collective-permute-start | bytes 2359304 | tf_op jit(solution)/shard_map/ppermute | solution.py:298
  671.8 51.9 %collective-permute-start.39 = (bf16[4,1024,256]{2,1,0:T(8,128)(2,1)}, bf16[4,1024,256]{2,1,0:T(8,128)(2,1)S(1)}, u32[]{:S(2)}, u32[]{:S(2)}) collective-permute-start(bf16[4,1024,256]{2,1,0:T(8,128)(2,1)} %get-tuple-element.222), channel_id=1, source_target_pairs={{0,2},{1,3},{2,0},{3,1},{4,6},{5,7},{6,4},{7,5},{8,10},{9,11},{10,... | collective-permute-start | bytes 6291464 | tf_op jit(solution)/shard_map/ppermute | solution.py:298
  672.2 51.6 %collective-permute-start.41 = (bf16[2,4,384,256]{3,2,1,0:T(8,128)(2,1)S(1)}, bf16[2,4,384,256]{3,2,1,0:T(8,128)(2,1)S(1)}, u32[]{:S(2)}, u32[]{:S(2)}) collective-permute-start(bf16[2,4,384,256]{3,2,1,0:T(8,128)(2,1)S(1)} %copy-done.55), channel_id=1, source_target_pairs={{0,4},{4,0},{8,12},{12,8},{16,20},{20,16},{24,28},{28,24},{1,5},{5... | collective-permute-start | bytes 4718600 | tf_op jit(solution)/shard_map/ppermute | solution.py:298
  728.6 52.5 %collective-permute-start.46 = (bf16[2,4,384,256]{3,2,1,0:T(8,128)(2,1)}, bf16[2,4,384,256]{3,2,1,0:T(8,128)(2,1)}, u32[]{:S(2)}, u32[]{:S(2)}) collective-permute-start(bf16[2,4,384,256]{3,2,1,0:T(8,128)(2,1)} %get-tuple-element.241), channel_id=1, source_target_pairs={{0,2},{1,3},{2,0},{3,1},{4,6},{5,7},{6,4},{7,5},{8,10},{9,11},{10,... | collective-permute-start | bytes 4718600 | tf_op jit(solution)/shard_map/ppermute | solution.py:298
  728.9 52.2 %collective-permute-start.47 = (bf16[2,4,512,256]{3,2,1,0:T(8,128)(2,1)}, bf16[2,4,512,256]{3,2,1,0:T(8,128)(2,1)}, u32[]{:S(2)}, u32[]{:S(2)}) collective-permute-start(bf16[2,4,512,256]{3,2,1,0:T(8,128)(2,1)} %get-tuple-element.242), channel_id=1, source_target_pairs={{0,4},{4,0},{8,12},{12,8},{16,20},{20,16},{24,28},{28,24},{1,5},{5... | collective-permute-start | bytes 6291464 | tf_op jit(solution)/shard_map/ppermute | solution.py:298
  730.4 18.7 %collective-permute-start.49 = (bf16[2,2,4,256,256]{4,3,2,1,0:T(8,128)(2,1)}, bf16[2,2,4,256,256]{4,3,2,1,0:T(8,128)(2,1)}, u32[]{:S(2)}, u32[]{:S(2)}) collective-permute-start(bf16[2,2,4,256,256]{4,3,2,1,0:T(8,128)(2,1)} %opening_entry_0_1.1), channel_id=1, source_target_pairs={{0,1},{1,0},{2,3},{3,2},{4,5},{5,4},{6,7},{7,6},{8,9},{9,8},{10,11... | collective-permute-start | bytes 6291464 | tf_op jit(solution)/shard_map/ppermute | solution.py:298
  730.4 31.6 %collective-permute-start.50 = (bf16[2,2,4,256,256]{4,3,2,1,0:T(8,128)(2,1)}, bf16[2,2,4,256,256]{4,3,2,1,0:T(8,128)(2,1)}, u32[]{:S(2)}, u32[]{:S(2)}) collective-permute-start(bf16[2,2,4,256,256]{4,3,2,1,0:T(8,128)(2,1)} %opening_entry_more_0_1.1), channel_id=1, source_target_pairs={{0,1},{1,0},{2,3},{3,2},{4,5},{5,4},{6,7},{7,6},{8,9},{9,8},{10,11... | collective-permute-start | bytes 6291464 | tf_op jit(solution)/shard_map/ppermute | solution.py:298
  745.2 35.9 %collective-permute-start.44 = (bf16[2,1408,256]{2,1,0:T(8,128)(2,1)S(1)}, bf16[2,1408,256]{2,1,0:T(8,128)(2,1)S(1)}, u32[]{:S(2)}, u32[]{:S(2)}) collective-permute-start(bf16[2,1408,256]{2,1,0:T(8,128)(2,1)S(1)} %pad_maximum_fusion.6), channel_id=1, source_target_pairs={{0,8},{4,12},{8,0},{12,4},{16,24},{20,28},{24,16},{28,20},{1,9},{5... | collective-permute-start | bytes 4325384 | tf_op jit(solution)/shard_map/ppermute | solution.py:304
  749.2 32.0 %collective-permute-start.45 = (bf16[4,384,256]{2,1,0:T(8,128)(2,1)S(1)}, bf16[4,384,256]{2,1,0:T(8,128)(2,1)S(1)}, u32[]{:S(2)}, u32[]{:S(2)}) collective-permute-start(bf16[4,384,256]{2,1,0:T(8,128)(2,1)S(1)} %copy-done.96), channel_id=1, source_target_pairs={{0,2},{1,3},{2,0},{3,1},{4,6},{5,7},{6,4},{7,5},{8,10},{9,11},{10,... | collective-permute-start | bytes 2359304 | tf_op jit(solution)/shard_map/ppermute | solution.py:298
  787.9 5.7 collective-permute-start.51
  788.3 9.8 %collective-permute-start.53 = (bf16[2,384,256]{2,1,0:T(8,128)(2,1)S(1)}, bf16[2,384,256]{2,1,0:T(8,128)(2,1)S(1)}, u32[]{:S(2)}, u32[]{:S(2)}) collective-permute-start(bf16[2,384,256]{2,1,0:T(8,128)(2,1)S(1)} %get-tuple-element.262), channel_id=1, source_target_pairs={{0,8},{4,12},{8,0},{12,4},{16,24},{20,28},{24,16},{28,20},{1,9},{5... | collective-permute-start | bytes 1179656 | tf_op jit(solution)/shard_map/ppermute | solution.py:304
  789.3 41.1 %collective-permute-start.54 = (bf16[4,512,256]{2,1,0:T(8,128)(2,1)S(1)}, bf16[4,512,256]{2,1,0:T(8,128)(2,1)S(1)}, u32[]{:S(2)}, u32[]{:S(2)}) collective-permute-start(bf16[4,512,256]{2,1,0:T(8,128)(2,1)S(1)} %pad_maximum_fusion.12), channel_id=1, source_target_pairs={{0,4},{4,0},{8,12},{12,8},{16,20},{20,16},{24,28},{28,24},{1,5},{5... | collective-permute-start | bytes 3145736 | tf_op jit(solution)/shard_map/ppermute | solution.py:298
  790.8 39.6 %collective-permute-start.55 = (bf16[4,512,256]{2,1,0:T(8,128)(2,1)S(1)}, bf16[4,512,256]{2,1,0:T(8,128)(2,1)S(1)}, u32[]{:S(2)}, u32[]{:S(2)}) collective-permute-start(bf16[4,512,256]{2,1,0:T(8,128)(2,1)S(1)} %get-tuple-element.265), channel_id=1, source_target_pairs={{0,2},{1,3},{2,0},{3,1},{4,6},{5,7},{6,4},{7,5},{8,10},{9,11},{10,... | collective-permute-start | bytes 3145736 | tf_op jit(solution)/shard_map/ppermute | solution.py:298
  792.5 44.3 %collective-permute-start.56 = (bf16[2,4,256,256]{3,2,1,0:T(8,128)(2,1)S(1)}, bf16[2,4,256,256]{3,2,1,0:T(8,128)(2,1)S(1)}, u32[]{:S(2)}, u32[]{:S(2)}) collective-permute-start(bf16[2,4,256,256]{3,2,1,0:T(8,128)(2,1)S(1)} %get-tuple-element.266), channel_id=1, source_target_pairs={{0,2},{1,3},{2,0},{3,1},{4,6},{5,7},{6,4},{7,5},{8,10},{9,11},{10,... | collective-permute-start | bytes 3145736 | tf_op jit(solution)/shard_map/ppermute | solution.py:298
  793.6 43.2 %collective-permute-start.57 = (bf16[2,4,256,256]{3,2,1,0:T(8,128)(2,1)S(1)}, bf16[2,4,256,256]{3,2,1,0:T(8,128)(2,1)S(1)}, u32[]{:S(2)}, u32[]{:S(2)}) collective-permute-start(bf16[2,4,256,256]{3,2,1,0:T(8,128)(2,1)S(1)} %get-tuple-element.267), channel_id=1, source_target_pairs={{0,4},{4,0},{8,12},{12,8},{16,20},{20,16},{24,28},{28,24},{1,5},{5... | collective-permute-start | bytes 3145736 | tf_op jit(solution)/shard_map/ppermute | solution.py:298
  798.1 32.2 %collective-permute-start.52 = (bf16[1,1408,256]{2,1,0:T(8,128)(2,1)S(1)}, bf16[1,1408,256]{2,1,0:T(8,128)(2,1)S(1)}, u32[]{:S(2)}, u32[]{:S(2)}) collective-permute-start(bf16[1,1408,256]{2,1,0:T(8,128)(2,1)S(1)} %get-tuple-element.261), channel_id=1, source_target_pairs={{0,16},{4,20},{8,24},{12,28},{16,0},{20,4},{24,8},{28,12},{1,17},{... | collective-permute-start | bytes 2162696 | tf_op jit(solution)/shard_map/ppermute | solution.py:304
  836.8 9.4 %collective-permute-start.58 = (f32[19,1024]{1,0:T(8,128)S(1)}, f32[19,1024]{1,0:T(8,128)S(1)}, u32[]{:S(2)}, u32[]{:S(2)}) collective-permute-start(f32[19,1024]{1,0:T(8,128)S(1)} %add.693), channel_id=1, source_target_pairs={{0,4},{4,0},{8,12},{12,8},{16,20},{20,16},{24,28},{28,24},{1,5},{5... | collective-permute-start | bytes 233480 | tf_op jit(solution)/shard_map/ppermute | solution.py:298
  838.3 10.0 %collective-permute-start.59 = (bf16[1,384,256]{2,1,0:T(8,128)(2,1)S(1)}, bf16[1,384,256]{2,1,0:T(8,128)(2,1)S(1)}, u32[]{:S(2)}, u32[]{:S(2)}) collective-permute-start(bf16[1,384,256]{2,1,0:T(8,128)(2,1)S(1)} %add_convert_fusion.37), channel_id=1, source_target_pairs={{0,16},{4,20},{8,24},{12,28},{16,0},{20,4},{24,8},{28,12},{1,17},{... | collective-permute-start | bytes 589832 | tf_op jit(solution)/shard_map/ppermute | solution.py:304
  840.2 26.3 %collective-permute-start.60 = (bf16[2,1024,256]{2,1,0:T(8,128)(2,1)S(1)}, bf16[2,1024,256]{2,1,0:T(8,128)(2,1)S(1)}, u32[]{:S(2)}, u32[]{:S(2)}) collective-permute-start(bf16[2,1024,256]{2,1,0:T(8,128)(2,1)S(1)} %pad_maximum_fusion.13), channel_id=1, source_target_pairs={{0,8},{4,12},{8,0},{12,4},{16,24},{20,28},{24,16},{28,20},{1,9},{5... | collective-permute-start | bytes 3145736 | tf_op jit(solution)/shard_map/ppermute | solution.py:304
  841.7 11.4 %collective-permute-start.61 = (bf16[4,256,256]{2,1,0:T(8,128)(2,1)S(1)}, bf16[4,256,256]{2,1,0:T(8,128)(2,1)S(1)}, u32[]{:S(2)}, u32[]{:S(2)}) collective-permute-start(bf16[4,256,256]{2,1,0:T(8,128)(2,1)S(1)} %get-tuple-element.365), channel_id=1, source_target_pairs={{0,4},{4,0},{8,12},{12,8},{16,20},{20,16},{24,28},{28,24},{1,5},{5... | collective-permute-start | bytes 1572872 | tf_op jit(solution)/shard_map/ppermute | solution.py:298
  842.7 10.7 %collective-permute-start.62 = (bf16[4,256,256]{2,1,0:T(8,128)(2,1)S(1)}, bf16[4,256,256]{2,1,0:T(8,128)(2,1)S(1)}, u32[]{:S(2)}, u32[]{:S(2)}) collective-permute-start(bf16[4,256,256]{2,1,0:T(8,128)(2,1)S(1)} %get-tuple-element.367), channel_id=1, source_target_pairs={{0,2},{1,3},{2,0},{3,1},{4,6},{5,7},{6,4},{7,5},{8,10},{9,11},{10,... | collective-permute-start | bytes 1572872 | tf_op jit(solution)/shard_map/ppermute | solution.py:298
  866.5 8.1 collective-permute-start.63
  866.9 8.6 collective-permute-start.64
  870.0 6.5 collective-permute-start.65
  871.2 24.8 %collective-permute-start.66 = (bf16[2,512,256]{2,1,0:T(8,128)(2,1)S(1)}, bf16[2,512,256]{2,1,0:T(8,128)(2,1)S(1)}, u32[]{:S(2)}, u32[]{:S(2)}) collective-permute-start(bf16[2,512,256]{2,1,0:T(8,128)(2,1)S(1)} %pad_maximum_fusion.18), channel_id=1, source_target_pairs={{0,8},{4,12},{8,0},{12,4},{16,24},{20,28},{24,16},{28,20},{1,9},{5... | collective-permute-start | bytes 1572872 | tf_op jit(solution)/shard_map/ppermute | solution.py:304
  872.7 27.1 %collective-permute-start.67 = (bf16[1,1024,256]{2,1,0:T(8,128)(2,1)S(1)}, bf16[1,1024,256]{2,1,0:T(8,128)(2,1)S(1)}, u32[]{:S(2)}, u32[]{:S(2)}) collective-permute-start(bf16[1,1024,256]{2,1,0:T(8,128)(2,1)S(1)} %get-tuple-element.359), channel_id=1, source_target_pairs={{0,16},{4,20},{8,24},{12,28},{16,0},{20,4},{24,8},{28,12},{1,17},{... | collective-permute-start | bytes 1572872 | tf_op jit(solution)/shard_map/ppermute | solution.py:304
  899.9 12.7 %collective-permute-start.68 = (bf16[1,512,256]{2,1,0:T(8,128)(2,1)S(1)}, bf16[1,512,256]{2,1,0:T(8,128)(2,1)S(1)}, u32[]{:S(2)}, u32[]{:S(2)}) collective-permute-start(bf16[1,512,256]{2,1,0:T(8,128)(2,1)S(1)} %get-tuple-element.383), channel_id=1, source_target_pairs={{0,16},{4,20},{8,24},{12,28},{16,0},{20,4},{24,8},{28,12},{1,17},{... | collective-permute-start | bytes 786440 | tf_op jit(solution)/shard_map/ppermute | solution.py:304
  (158 other events, 1602.8 us)
Sparse Core Ops, SparseCore 0:
  11.5 144.7 all-gather.3
  159.7 102.0 all-gather.5
  265.3 79.2 all-gather.7
